TPU v7x, 32 devices: a whole 2x2x4 slice. The times are simulated.
32 devices in a mesh: fsdp: 32 (over z, y, x, core).
Axes of the slice: x: 2, y: 2, z: 4, core: 2. Of those that a mesh axis runs over, the one named last changes fastest.
Arguments:
- hidden_in: bfloat16 [64, 320, 768], P('fsdp'), may hold values from -16 to 16
- encoder_states: bfloat16 [64, 128, 768], P('fsdp'), may hold values from -16 to 16
- lengths: int32 [64], P('fsdp'), may hold values from 60 to 320, as said below
- out_grad: bfloat16 [64, 320, 768], P('fsdp'), may hold values from -6 to 6
- attn_in: bfloat16 [6, 768, 768], P(None, 'fsdp'), may hold values from -0.21875 to 0.21875
- attn_out: bfloat16 [2, 768, 768], P(None, 'fsdp'), may hold values from -0.875 to 0.875
- fc_in: bfloat16 [768, 3072], P('fsdp'), may hold values from -0.21875 to 0.21875
- fc_out: bfloat16 [3072, 768], P('fsdp'), may hold values from -0.109375 to 0.109375
- gains: bfloat16 [3, 768], P(None, 'fsdp'), may hold values from 0.5 to 1.5
- biases: bfloat16 [10, 768], P(None, 'fsdp'), may hold values from -2 to 2
- ffn_bias: bfloat16 [3072], P('fsdp'), may hold values from -2 to 2
Outputs:
- layer_out: bfloat16 [64, 320, 768], P('fsdp')
- grad_in: bfloat16 [64, 320, 768], P('fsdp')
- grad_encoder: bfloat16 [64, 128, 768], P('fsdp')
- grad_attn_in: float32 [6, 768, 768], P(None, 'fsdp')
- grad_attn_out: float32 [2, 768, 768], P(None, 'fsdp')
- grad_fc_in: float32 [768, 3072], P('fsdp')
- grad_fc_out: float32 [3072, 768], P('fsdp')
- grad_gains: float32 [3, 768], P(None, 'fsdp')
- grad_biases: float32 [10, 768], P(None, 'fsdp')
- grad_ffn_bias: float32 [3072], P('fsdp')
- rms: float32 [4], replicated
Inputs may be any that keep to these rules, and one draw needn't show every extreme that they name: `lengths`: each transcript has 60 to 320 valid tokens, its first ones; some transcript has exactly 320.
All inputs are finite; a program needn't handle non-finite values.
Results may differ from a plain program's by a relative error of at most 0.017.
Values may be sent and summed in bfloat16 or wider, within the bound.
No kernel may reach another device: no remote copies, remote signals or barrier semaphores. Data moves between devices by JAX's collectives and lax.ppermute only.
A program may use at most 256 MiB of HBM per device.

v0:
```python
import math

import jax
import jax.numpy as jnp
from jax import lax
from jax.sharding import PartitionSpec as P

HEADS = 12
HEAD_FEATURES = 64


norm_eps = 1e-05
masked_score = -1e30


def layer_norm(inputs, gain_row, shift_row):
    center = inputs - jnp.mean(inputs, -1, keepdims=True)
    spread = jnp.mean(center * center, -1, keepdims=True)
    return center * lax.rsqrt(spread + norm_eps) * gain_row + shift_row


def gelu_exact(inputs):
    return jax.nn.gelu(inputs, approximate=False)


def matmul(left, right):
    return jnp.dot(left, right, preferred_element_type=jnp.float32)


def matmul_tn(left, right):
    return lax.dot_general(
        left, right, (((0,), (0,)), ((), ())), preferred_element_type=jnp.float32
    )


def matmul_nt(left, right):
    return lax.dot_general(
        left, right, (((1,), (1,)), ((), ())), preferred_element_type=jnp.float32
    )


def row_sum(values):
    return jnp.sum(values.astype(jnp.float32), 0)


def divide_into_heads(values):
    return values.reshape(values.shape[0], HEADS, HEAD_FEATURES)


def scores_of(query_matrix, key_matrix, causal):
    logit_scores = jnp.einsum(
        "sxc,oxc->xso",
        divide_into_heads(query_matrix),
        divide_into_heads(key_matrix),
        preferred_element_type=jnp.float32,
    ) * (1.0 / math.sqrt(HEAD_FEATURES))
    if causal:
        allowed = (
            jnp.arange(key_matrix.shape[0])[None, :] <= jnp.arange(query_matrix.shape[0])[:, None]
        )
        logit_scores = jnp.where(allowed[None], logit_scores, masked_score)
    return logit_scores


def attend_forward(query_matrix, key_matrix, value_matrix, causal):
    logit_scores = scores_of(query_matrix, key_matrix, causal)
    row_max = jnp.max(logit_scores, -1, keepdims=True)
    exponent = jnp.exp(logit_scores - row_max)
    row_total = jnp.sum(exponent, -1, keepdims=True)
    attention_weight = (exponent / row_total).astype(jnp.bfloat16)
    attended_rows = jnp.einsum(
        "opi,ioz->poz",
        attention_weight,
        divide_into_heads(value_matrix),
        preferred_element_type=jnp.float32,
    )
    return (
        attended_rows.reshape(query_matrix.shape[0], -1).astype(jnp.bfloat16),
        row_max + jnp.log(row_total),
    )


def attend_backward(query_matrix, key_matrix, value_matrix, log_totals, grad_attended, causal):
    logit_scores = scores_of(query_matrix, key_matrix, causal)
    softmax_rows = jnp.exp(logit_scores - log_totals)
    head_gradient = divide_into_heads(grad_attended)
    grad_value = jnp.einsum(
        "ebw,bef->wef",
        softmax_rows.astype(jnp.bfloat16),
        head_gradient,
        preferred_element_type=jnp.float32,
    )
    grad_probs = jnp.einsum(
        "sxc,oxc->xso",
        head_gradient,
        divide_into_heads(value_matrix),
        preferred_element_type=jnp.float32,
    )
    score_gradient = softmax_rows * (
        grad_probs - jnp.sum(softmax_rows * grad_probs, -1, keepdims=True)
    )
    score_gradient = score_gradient.astype(jnp.bfloat16)
    score_scale = 1.0 / math.sqrt(HEAD_FEATURES)
    grad_query = (
        jnp.einsum(
            "opi,ioz->poz",
            score_gradient,
            divide_into_heads(key_matrix),
            preferred_element_type=jnp.float32,
        )
        * score_scale
    )
    grad_key = (
        jnp.einsum(
            "ebw,bef->wef",
            score_gradient,
            divide_into_heads(query_matrix),
            preferred_element_type=jnp.float32,
        )
        * score_scale
    )
    return (
        grad_query.reshape(query_matrix.shape[0], -1).astype(jnp.bfloat16),
        grad_key.reshape(key_matrix.shape[0], -1).astype(jnp.bfloat16),
        grad_value.reshape(key_matrix.shape[0], -1).astype(jnp.bfloat16),
    )


def forward(attention_weight, stream_in, frames_in):
    attn_in, attn_out, fc_in, fc_out, gains, biases, ffn_bias = attention_weight
    gain_rows = gains.astype(jnp.float32)
    bias_rows = biases.astype(jnp.float32)
    stream = stream_in.astype(jnp.float32)
    norm_one = layer_norm(stream, gain_rows[0], bias_rows[7]).astype(jnp.bfloat16)
    query_matrix = (matmul(norm_one, attn_in[0]) + bias_rows[0]).astype(jnp.bfloat16)
    key_matrix = matmul(norm_one, attn_in[1]).astype(jnp.bfloat16)
    value_matrix = (matmul(norm_one, attn_in[2]) + bias_rows[1]).astype(jnp.bfloat16)
    attended_rows, self_totals = attend_forward(query_matrix, key_matrix, value_matrix, True)
    self_out = matmul(attended_rows, attn_out[0]) + bias_rows[2]
    stream_mid = stream + self_out
    norm_two = layer_norm(stream_mid, gain_rows[1], bias_rows[8]).astype(jnp.bfloat16)
    cross_query = (matmul(norm_two, attn_in[3]) + bias_rows[3]).astype(jnp.bfloat16)
    cross_key = matmul(frames_in, attn_in[4]).astype(jnp.bfloat16)
    cross_value = (matmul(frames_in, attn_in[5]) + bias_rows[4]).astype(jnp.bfloat16)
    cross_attended, cross_totals = attend_forward(cross_query, cross_key, cross_value, False)
    cross_out = matmul(cross_attended, attn_out[1]) + bias_rows[5]
    stream_late = stream_mid + cross_out
    norm_three = layer_norm(stream_late, gain_rows[2], bias_rows[9]).astype(jnp.bfloat16)
    ffn_input = matmul(norm_three, fc_in) + ffn_bias.astype(jnp.float32)
    ffn_hidden = gelu_exact(ffn_input).astype(jnp.bfloat16)
    ffn_out = matmul(ffn_hidden, fc_out) + bias_rows[6]
    result = stream_late + ffn_out
    saved = (
        stream,
        norm_one,
        query_matrix,
        key_matrix,
        value_matrix,
        self_totals,
        attended_rows,
        stream_mid,
        norm_two,
        cross_query,
        cross_key,
        cross_value,
        cross_totals,
        cross_attended,
        stream_late,
        norm_three,
        ffn_input,
        ffn_hidden,
        frames_in,
    )
    return (saved, result, (self_out, cross_out, ffn_out))


def backward(attention_weight, saved, cotangent, valid_rows):
    attn_in, attn_out, fc_in, fc_out, gains, biases, ffn_bias = attention_weight
    gain_rows = gains.astype(jnp.float32)
    bias_rows = biases.astype(jnp.float32)
    (
        stream,
        norm_one,
        query_matrix,
        key_matrix,
        value_matrix,
        self_totals,
        attended_rows,
        stream_mid,
        norm_two,
        cross_query,
        cross_key,
        cross_value,
        cross_totals,
        cross_attended,
        stream_late,
        norm_three,
        ffn_input,
        ffn_hidden,
        frames_in,
    ) = saved
    grad_result = cotangent.astype(jnp.float32) * valid_rows
    grad_ffn = grad_result.astype(jnp.bfloat16)
    grad_fc_out = matmul_tn(ffn_hidden, grad_ffn)
    grad_hidden = matmul_nt(grad_ffn, fc_out)
    gelu_value, gelu_pull = jax.vjp(gelu_exact, ffn_input)
    grad_pre = gelu_pull(grad_hidden)[0].astype(jnp.bfloat16)
    grad_fc_in = matmul_tn(norm_three, grad_pre)
    grad_norm_three = matmul_nt(grad_pre, fc_in)
    norm_value, norm_pull = jax.vjp(layer_norm, stream_late, gain_rows[2], bias_rows[9])
    grad_from_three, grad_gain_three, grad_shift_three = norm_pull(grad_norm_three)
    grad_late = grad_result + grad_from_three
    grad_cross = grad_late.astype(jnp.bfloat16)
    grad_cross_proj = matmul_tn(cross_attended, grad_cross)
    grad_cross_attended = matmul_nt(grad_cross, attn_out[1]).astype(jnp.bfloat16)
    grad_cq, grad_ck, grad_cv = attend_backward(
        cross_query, cross_key, cross_value, cross_totals, grad_cross_attended, False
    )
    grad_frames = (matmul_nt(grad_ck, attn_in[4]) + matmul_nt(grad_cv, attn_in[5])).astype(
        jnp.bfloat16
    )
    grad_norm_two = matmul_nt(grad_cq, attn_in[3])
    norm_value, norm_pull = jax.vjp(layer_norm, stream_mid, gain_rows[1], bias_rows[8])
    grad_from_two, grad_gain_two, grad_shift_two = norm_pull(grad_norm_two)
    grad_mid = grad_late + grad_from_two
    grad_self = grad_mid.astype(jnp.bfloat16)
    grad_self_proj = matmul_tn(attended_rows, grad_self)
    grad_attended = matmul_nt(grad_self, attn_out[0]).astype(jnp.bfloat16)
    grad_query, grad_key, grad_value = attend_backward(
        query_matrix, key_matrix, value_matrix, self_totals, grad_attended, True
    )
    grad_norm_one = (
        matmul_nt(grad_query, attn_in[0])
        + matmul_nt(grad_key, attn_in[1])
        + matmul_nt(grad_value, attn_in[2])
    )
    norm_value, norm_pull = jax.vjp(layer_norm, stream, gain_rows[0], bias_rows[7])
    grad_from_one, grad_gain_one, grad_shift_one = norm_pull(grad_norm_one)
    grad_stream = (grad_mid + grad_from_one).astype(jnp.bfloat16)
    grad_pieces = (
        matmul_tn(norm_one, grad_query),
        matmul_tn(norm_one, grad_key),
        matmul_tn(norm_one, grad_value),
        matmul_tn(norm_two, grad_cq),
        matmul_tn(frames_in, grad_ck),
        matmul_tn(frames_in, grad_cv),
        grad_self_proj,
        grad_cross_proj,
        grad_fc_in,
        grad_fc_out,
        grad_gain_one,
        grad_gain_two,
        grad_gain_three,
        row_sum(grad_query),
        row_sum(grad_value),
        row_sum(grad_self),
        row_sum(grad_cq),
        row_sum(grad_cv),
        row_sum(grad_cross),
        row_sum(grad_ffn),
        grad_shift_one,
        grad_shift_two,
        grad_shift_three,
        row_sum(grad_pre),
    )
    return (grad_pieces, grad_stream, grad_frames)


def fetch_forward(attn_in, attn_out, fc_in, fc_out, gains, biases, ffn_bias):
    return (
        lax.all_gather(attn_in, "fsdp", axis=1, tiled=True),
        lax.all_gather(attn_out, "fsdp", axis=1, tiled=True),
        lax.all_gather(fc_in, "fsdp", axis=0, tiled=True),
        lax.all_gather(fc_out, "fsdp", axis=0, tiled=True),
        lax.all_gather(gains, "fsdp", axis=1, tiled=True),
        lax.all_gather(biases, "fsdp", axis=1, tiled=True),
        lax.all_gather(ffn_bias, "fsdp", axis=0, tiled=True),
    )


def shards(
    hidden_in,
    encoder_states,
    lengths,
    out_grad,
    attn_in,
    attn_out,
    fc_in,
    fc_out,
    gains,
    biases,
    ffn_bias,
):
    micro_count = hidden_in.shape[0]
    length = hidden_in.shape[1]
    model_width = hidden_in.shape[2]
    totals = None
    square_sums = jnp.zeros((4,), jnp.float32)
    results, grad_streams, grad_frames = ([], [], [])
    for batch_index in range(micro_count):
        gathered = fetch_forward(attn_in, attn_out, fc_in, fc_out, gains, biases, ffn_bias)
        saved, result, branches = forward(
            gathered, hidden_in[batch_index], encoder_states[batch_index]
        )
        valid_rows = (jnp.arange(length) < lengths[batch_index]).astype(jnp.float32)[:, None]
        square_sums = square_sums + jnp.stack(
            [jnp.sum(valid_rows * branch * branch) for branch in (result,) + branches]
        )
        weights_back = (
            lax.all_gather(attn_in, "fsdp", axis=1, tiled=True),
            lax.all_gather(attn_out, "fsdp", axis=1, tiled=True),
            lax.all_gather(fc_in, "fsdp", axis=0, tiled=True),
            lax.all_gather(fc_out, "fsdp", axis=0, tiled=True),
            lax.all_gather(gains, "fsdp", axis=1, tiled=True),
            lax.all_gather(biases, "fsdp", axis=1, tiled=True),
            lax.all_gather(ffn_bias, "fsdp", axis=0, tiled=True),
        )
        grad_pieces, grad_stream, grad_frame = backward(
            weights_back, saved, out_grad[batch_index], valid_rows
        )
        totals = (
            list(grad_pieces)
            if totals is None
            else [old + new for old, new in zip(totals, grad_pieces)]
        )
        results.append(result.astype(jnp.bfloat16))
        grad_streams.append(grad_stream)
        grad_frames.append(grad_frame)
    totals = list(lax.psum_scatter(tuple(totals), "fsdp", scatter_dimension=0, tiled=True))
    stat_sums, valid_total = lax.psum((square_sums, jnp.sum(lengths).astype(jnp.float32)), "fsdp")
    rms = jnp.sqrt(stat_sums / (valid_total * model_width))
    grad_outputs = (
        jnp.stack(totals[0:6]),
        jnp.stack(totals[6:8]),
        totals[8],
        totals[9],
        jnp.stack(totals[10:13]),
        jnp.stack(totals[13:23]),
        totals[23],
    )
    return (
        (jnp.stack(results), jnp.stack(grad_streams), jnp.stack(grad_frames))
        + grad_outputs
        + (rms,)
    )


def solution(mesh):
    placed = (
        P("fsdp", None, None),
        P("fsdp", None, None),
        P("fsdp"),
        P("fsdp", None, None),
        P(None, "fsdp", None),
        P(None, "fsdp", None),
        P("fsdp", None),
        P("fsdp", None),
        P(None, "fsdp"),
        P(None, "fsdp"),
        P("fsdp"),
    )
    return jax.shard_map(
        shards,
        mesh=mesh,
        in_specs=placed,
        out_specs=(
            P("fsdp", None, None),
            P("fsdp", None, None),
            P("fsdp", None, None),
            P(None, "fsdp", None),
            P(None, "fsdp", None),
            P("fsdp", None),
            P("fsdp", None),
            P(None, "fsdp"),
            P(None, "fsdp"),
            P("fsdp"),
            P(),
        ),
        check_vma=False,
    )
```

profile of v0, /device:TPU:0, one launch (start us, length us, event | category | flops | bytes accessed | tf_op | source)
XLA Modules:
  0.0 1465.3 jit_solution(3921384584617405980)
XLA Ops:
  12.2 42.7 %all-reduce = bf16[3072]{0:T(1024)(128)(2,1)S(1)} all-reduce(bf16[3072]{0:T(1024)(128)(2,1)S(1)} %dynamic-update-slice), channel_id=1, replica_groups=mesh['fsdp'=32] {'fsdp'}, use_global_device_ids=true, to_apply=%add | all-reduce | flops 3072 | bytes 12288
  55.5 42.4 %all-gather.1 = bf16[32,24,10]{1,2,0:T(8,128)(2,1)S(1)} all-gather(bf16[1,24,10]{1,2,0:T(8,128)(2,1)} %bitcast.492), channel_id=1, replica_groups=mesh['fsdp'=32] {'fsdp'}, dimensions={0}, use_global_device_ids=true | all-gather | bytes 15840 | tf_op jit(solution)/shard_map/all_gather | solution.py:276
  98.3 37.2 %all-gather = bf16[32,24,3]{1,2,0:T(4,128)(2,1)S(1)} all-gather(bf16[1,24,3]{1,2,0:T(4,128)(2,1)} %bitcast.493), channel_id=1, replica_groups=mesh['fsdp'=32] {'fsdp'}, dimensions={0}, use_global_device_ids=true | all-gather | bytes 4752 | tf_op jit(solution)/shard_map/all_gather | solution.py:275
  210.5 13.8 multiply_convert_fusion.3
  224.4 50.9 %all-gather.13.cloned.1.call-done = bf16[3072,768]{1,0:T(8,128)(2,1)} async-done(((bf16[96,768]{1,0:T(8,128)(2,1)}), bf16[3072,768]{1,0:T(8,128)(2,1)}) %all-gather.13.cloned.1.call-update) | async-done | bytes 4718608 | tf_op jit(solution)/shard_map/all_gather | solution.py:274
  275.3 8.3 convert_reduce_fusion.1
  286.7 12.6 multiply_convert_fusion.2
  299.3 6.8 convert_reduce_fusion
  310.5 4.3 convert_reduce_fusion.10
  321.3 3.4 multiply_reduce_fusion.2
  333.8 3.1 multiply_reduce_fusion.3
  342.1 4.4 multiply_reduce_fusion.9
  364.9 7.1 multiply_reduce_fusion.1
  378.8 5.8 multiply_convert_fusion.1
  397.1 3.2 fusion.29
  406.7 4.5 convert_reduce_fusion.7
  412.3 4.4 convert_reduce_fusion.6
  421.7 3.0 convolution_add_fusion.6
  440.8 4.5 fusion.163
  445.3 5.6 convolution_add_fusion.1
  452.2 4.4 fusion.149
  456.6 5.4 convolution_add_fusion
  486.9 5.5 maximum_add_fusion
  492.5 42.2 %all-reduce.15 = (f32[768]{0:T(1024)}, f32[768]{0:T(1024)}, f32[768]{0:T(1024)}, f32[768]{0:T(1024)}, f32[768]{0:T(1024)}, /*index=5*/f32[768]{0:T(1024)}, f32[7...) all-reduce(f32[768]{0:T(1024)} %add.568, ...), channel_id=14, replica_groups=mesh['fsdp'=32] {'fsdp'}, use_global_device_ids=true, to_apply=%region_54.55.clone | all-reduce | flops 13061 | bytes 104488
  568.1 87.7 %reduce-scatter.11.cloned.1.call-done = f32[24,768]{1,0:T(8,128)} async-done(((f32[768,768]{1,0:T(8,128)}), f32[24,768]{1,0:T(8,128)}) %reduce-scatter.11.cloned.1.call-update) | async-done | bytes 73744 | tf_op jit(solution)/shard_map/reduce_scatter | solution.py:329
  656.7 103.1 %reduce-scatter.13.cloned.1.call-done = f32[24,768]{1,0:T(8,128)} async-done(((f32[768,768]{1,0:T(8,128)}), f32[24,768]{1,0:T(8,128)}) %reduce-scatter.13.cloned.1.call-update) | async-done | bytes 73744 | tf_op jit(solution)/shard_map/reduce_scatter | solution.py:329
  760.7 103.1 %reduce-scatter.15.cloned.1.call-done = f32[24,768]{1,0:T(8,128)} async-done(((f32[768,768]{1,0:T(8,128)}), f32[24,768]{1,0:T(8,128)}) %reduce-scatter.15.cloned.1.call-update) | async-done | bytes 73744 | tf_op jit(solution)/shard_map/reduce_scatter | solution.py:329
  864.7 102.9 %reduce-scatter.17.cloned.1.call-done = f32[24,768]{1,0:T(8,128)} async-done(((f32[768,768]{1,0:T(8,128)}), f32[24,768]{1,0:T(8,128)}) %reduce-scatter.17.cloned.1.call-update) | async-done | bytes 73744 | tf_op jit(solution)/shard_map/reduce_scatter | solution.py:329
  968.5 103.1 %reduce-scatter.19.cloned.1.call-done = f32[24,768]{1,0:T(8,128)} async-done(((f32[768,768]{1,0:T(8,128)}), f32[24,768]{1,0:T(8,128)}) %reduce-scatter.19.cloned.1.call-update) | async-done | bytes 73744 | tf_op jit(solution)/shard_map/reduce_scatter | solution.py:329
  1072.5 102.9 %reduce-scatter.21.cloned.1.call-done = f32[24,768]{1,0:T(8,128)} async-done(((f32[768,768]{1,0:T(8,128)}), f32[24,768]{1,0:T(8,128)}) %reduce-scatter.21.cloned.1.call-update) | async-done | bytes 73744 | tf_op jit(solution)/shard_map/reduce_scatter | solution.py:329
  1176.3 140.8 %reduce-scatter.27.cloned.1.call-done = f32[24,3072]{1,0:T(8,128)} async-done(((f32[768,3072]{1,0:T(8,128)}), f32[24,3072]{1,0:T(8,128)}) %reduce-scatter.27.cloned.1.call-update) | async-done | bytes 294928 | tf_op jit(solution)/shard_map/reduce_scatter | solution.py:329
  1317.1 141.5 %reduce-scatter.29.cloned.1.call-done = f32[96,768]{1,0:T(8,128)} async-done(((f32[3072,768]{1,0:T(8,128)}), f32[96,768]{1,0:T(8,128)}) %reduce-scatter.29.cloned.1.call-update) | async-done | bytes 294928 | tf_op jit(solution)/shard_map/reduce_scatter | solution.py:329
  (683 shorter events, 236.2 us)
Async XLA Ops:
  7.2 134.3 %all-gather.7.cloned.1.call-start = ((), (), s32[]{:S(2)}) async-start(), calls=%async_computation.10 | async-start | bytes 7299072 | tf_op jit(solution)/shard_map/all_gather | solution.py:271
  7.9 165.1 %all-gather.9.cloned.1.call-start = ((), (), s32[]{:S(2)}) async-start(), calls=%async_computation.11 | async-start | bytes 2433024 | tf_op jit(solution)/shard_map/all_gather | solution.py:272
  8.7 201.8 %all-gather.11.cloned.1.call-start = ((), (), s32[]{:S(2)}) async-start(), calls=%async_computation.12 | async-start | bytes 4866048 | tf_op jit(solution)/shard_map/all_gather | solution.py:273
  9.4 265.9 %all-gather.13.cloned.1.call-start = ((), (), s32[]{:S(2)}) async-start(), calls=%async_computation.13 | async-start | bytes 4866048 | tf_op jit(solution)/shard_map/all_gather | solution.py:274
  10.0 556.5 %reduce-scatter.25.cloned.1.call-start = ((), (), s32[]{:S(2)}) async-start(), calls=%async_computation.21 | async-start | bytes 2433024 | tf_op jit(solution)/shard_map/reduce_scatter | solution.py:329
  98.2 46.5 %copy-start.2 = (bf16[2,320,768]{2,1,0:T(8,128)(2,1)S(1)}, bf16[2,320,768]{2,1,0:T(8,128)(2,1)}, u32[]{:S(2)}) copy-start(bf16[2,320,768]{2,1,0:T(8,128)(2,1)} %param.11) | copy-start | bytes 2949124
  137.2 17.6 %copy-start.124 = (f32[320]{0:T(512)}, f32[320]{0:T(512)S(1)}, u32[]{:S(2)}) copy-start(f32[320]{0:T(512)S(1)} %get-tuple-element.180) | copy-start | bytes 3844
  138.9 15.9 %copy-start.138 = (f32[320]{0:T(512)}, f32[320]{0:T(512)S(1)}, u32[]{:S(2)}) copy-start(f32[320]{0:T(512)S(1)} %fusion.134) | copy-start | bytes 3844
  140.8 63.1 %copy-start.156 = (f32[320]{0:T(512)}, f32[320]{0:T(512)S(1)}, u32[]{:S(2)}) copy-start(f32[320]{0:T(512)S(1)} %get-tuple-element.185) | copy-start | bytes 3844
  141.5 13.4 copy-start.113
  141.5 13.4 copy-start.117
  141.5 44.6 %copy-start.147 = (f32[768]{0:T(1024)}, f32[768]{0:T(1024)S(1)}, u32[]{:S(2)}) copy-start(f32[768]{0:T(1024)S(1)} %get-tuple-element.51) | copy-start | bytes 9220
  146.9 16.6 %copy-start.47 = (bf16[320,768]{0,1:T(8,128)(2,1)}, bf16[320,768]{0,1:T(8,128)(2,1)S(1)}, u32[]{:S(2)}) copy-start(bf16[320,768]{0,1:T(8,128)(2,1)S(1)} %copy.138) | copy-start | bytes 1474564
  149.3 14.1 copy-start.50
  154.9 12.6 copy-start.49
  198.8 116.1 %copy-start.136 = (f32[320]{0:T(512)}, f32[320]{0:T(512)S(1)}, u32[]{:S(2)}) copy-start(f32[320]{0:T(512)S(1)} %broadcast_multiply_fusion.3) | copy-start | bytes 3844
  203.8 20.5 %copy-start.104 = (bf16[12,64,320]{2,1,0:T(8,128)(2,1)}, bf16[12,64,320]{2,1,0:T(8,128)(2,1)S(1)}, u32[]{:S(2)}) copy-start(bf16[12,64,320]{2,1,0:T(8,128)(2,1)S(1)} %convolution_convert_fusion) | copy-start | bytes 1474564
  205.2 109.7 %copy-start.144 = (f32[320]{0:T(512)}, f32[320]{0:T(512)S(1)}, u32[]{:S(2)}) copy-start(f32[320]{0:T(512)S(1)} %broadcast_multiply_fusion) | copy-start | bytes 3844
  284.9 14.4 slice-start.2
  349.4 217.1 %reduce-scatter.23.cloned.1.call-start = ((), (), s32[]{:S(2)}) async-start(), calls=%async_computation.20 | async-start | bytes 2433024 | tf_op jit(solution)/shard_map/reduce_scatter | solution.py:329
  372.1 283.7 %reduce-scatter.11.cloned.1.call-start = ((), (), s32[]{:S(2)}) async-start(), calls=%async_computation.14 | async-start | bytes 2433024 | tf_op jit(solution)/shard_map/reduce_scatter | solution.py:329
  397.0 362.7 %reduce-scatter.13.cloned.1.call-start = ((), (), s32[]{:S(2)}) async-start(), calls=%async_computation.15 | async-start | bytes 2433024 | tf_op jit(solution)/shard_map/reduce_scatter | solution.py:329
  406.4 457.3 %reduce-scatter.15.cloned.1.call-start = ((), (), s32[]{:S(2)}) async-start(), calls=%async_computation.16 | async-start | bytes 2433024 | tf_op jit(solution)/shard_map/reduce_scatter | solution.py:329
  419.1 548.5 %reduce-scatter.17.cloned.1.call-start = ((), (), s32[]{:S(2)}) async-start(), calls=%async_computation.17 | async-start | bytes 2433024 | tf_op jit(solution)/shard_map/reduce_scatter | solution.py:329
  424.7 646.9 %reduce-scatter.19.cloned.1.call-start = ((), (), s32[]{:S(2)}) async-start(), calls=%async_computation.18 | async-start | bytes 2433024 | tf_op jit(solution)/shard_map/reduce_scatter | solution.py:329
  432.5 742.9 %reduce-scatter.21.cloned.1.call-start = ((), (), s32[]{:S(2)}) async-start(), calls=%async_computation.19 | async-start | bytes 2433024 | tf_op jit(solution)/shard_map/reduce_scatter | solution.py:329
  440.7 876.4 %reduce-scatter.27.cloned.1.call-start = ((), (), s32[]{:S(2)}) async-start(), calls=%async_computation.22 | async-start | bytes 9732096 | tf_op jit(solution)/shard_map/reduce_scatter | solution.py:329
  451.0 1007.5 %reduce-scatter.29.cloned.1.call-start = ((), (), s32[]{:S(2)}) async-start(), calls=%async_computation.23 | async-start | bytes 9732096 | tf_op jit(solution)/shard_map/reduce_scatter | solution.py:329
  478.1 76.7 %copy-start.84 = (bf16[12,64,128]{2,1,0:T(8,128)(2,1)S(1)}, bf16[12,64,128]{2,1,0:T(8,128)(2,1)}, u32[]{:S(2)}) copy-start(bf16[12,64,128]{2,1,0:T(8,128)(2,1)} %copy-done.83) | copy-start | bytes 589828
  480.5 76.2 %copy-start.88 = (bf16[12,64,128]{2,1,0:T(8,128)(2,1)S(1)}, bf16[12,64,128]{2,1,0:T(8,128)(2,1)}, u32[]{:S(2)}) copy-start(bf16[12,64,128]{2,1,0:T(8,128)(2,1)} %copy-done.87) | copy-start | bytes 589828
  480.5 78.2 %copy-start.86 = (bf16[12,64,128]{2,1,0:T(8,128)(2,1)S(1)}, bf16[12,64,128]{2,1,0:T(8,128)(2,1)}, u32[]{:S(2)}) copy-start(bf16[12,64,128]{2,1,0:T(8,128)(2,1)} %copy-done.85) | copy-start | bytes 589828
  1176.3 282.2 %copy-start.202 = (f32[6,24,768]{2,1,0:T(8,128)}, f32[6,24,768]{2,1,0:T(8,128)S(1)}, u32[]{:S(2)}) copy-start(f32[6,24,768]{2,1,0:T(8,128)S(1)} %bitcast_dynamic-update-slice_fusion) | copy-start | bytes 1327108
  (212 other events, 891.8 us)
Sparse Core Ops, SparseCore 0:
  10.9 75.6 all-gather.6
  89.6 55.5 all-gather.8
  148.1 62.3 all-gather.10
  213.3 61.9 all-gather.12
  349.5 97.9 reduce-scatter.24
  452.7 98.9 reduce-scatter.22
  557.0 98.7 reduce-scatter.10
  661.1 98.6 reduce-scatter.12
  765.1 98.6 reduce-scatter.14
  868.9 98.6 reduce-scatter.16
  972.9 98.6 reduce-scatter.18
  1076.7 98.6 reduce-scatter.20
  1181.9 135.1 reduce-scatter.26
  1323.4 135.0 reduce-scatter.28
where the time goes:
time: 1480 us; the launch traced here: 1470 us
  waiting for transfers between devices  940 us (64%)
  matrix products  222 us (15%)
  blocking collectives  164 us (11%)
  local copies, waits for them, and re-layouts  62.9 us (4%)
  other arithmetic  55.4 us (4%)
  between operations  18.4 us (1%)
    reduce_scatter x10, waiting for transfers between devices, shards(): lax.psum_scatter(tuple(totals), 'fsdp', scatter_dimension=0, tiled=True)  885 us
    unnamed x2, blocking collectives  84.8 us
    dot_general x20, matrix products, matmul(): return jnp.dot(left, right, preferred_element_type=jnp.float32)  64.2 us
    dot_general x20, matrix products, matmul_nt(): lax.dot_general(left, right, (((1,), (1,)), ((), ())), preferred_element_...  52 us
    dot_general x20, matrix products, matmul_tn(): lax.dot_general(left, right, (((0,), (0,)), ((), ())), preferred_element_...  51.2 us
    all_gather x1, waiting for transfers between devices, fetch_forward(): lax.all_gather(fc_out, 'fsdp', axis=0, tiled=True)  50.9 us
    all_gather x1, blocking collectives, fetch_forward(): lax.all_gather(biases, 'fsdp', axis=1, tiled=True)  42.4 us
    all_gather x1, blocking collectives, fetch_forward(): lax.all_gather(gains, 'fsdp', axis=1, tiled=True)  37.2 us
  transfers between devices with their start and end apart: 14, of which 10 were waited for; matrix products, arithmetic and copies ran while one was open for 17% of the time, Pallas kernels for 0%

commit v1 on v0

v1 whole, which is shorter than its diff:
```python
import functools
import math

import jax
import jax.numpy as jnp
from jax import lax
from jax.experimental import pallas as pl
from jax.experimental.pallas import tpu as pltpu
from jax.sharding import PartitionSpec as P

NORM_EPS = 1e-05
LOW = jnp.bfloat16
WIDE = jnp.float32
HEADS = 12
PAIR = 128
HALF_PAIR = 64
SCALE = 0.125


def dot_nn(left, right):
    return lax.dot_general(left, right, (((1,), (0,)), ((), ())), preferred_element_type=WIDE)


def dot_nt(left, right):
    return lax.dot_general(left, right, (((1,), (1,)), ((), ())), preferred_element_type=WIDE)


def dot_tn(left, right):
    return lax.dot_general(left, right, (((0,), (0,)), ((), ())), preferred_element_type=WIDE)


def spec(block, index, once=False):
    if once:
        return pl.BlockSpec(block, index, pipeline_mode=pl.Buffered(1))
    return pl.BlockSpec(block, index)


def run(body, name, grid, operands, in_specs, outs, scratch=(), flops=0, exps=0, limit=40):
    moved = sum(o.size * o.dtype.itemsize for o in operands)
    moved += sum(math.prod(s) * jnp.dtype(d).itemsize for s, d, _ in outs)
    return pl.pallas_call(
        body,
        name=name,
        grid=grid,
        in_specs=in_specs,
        out_specs=[o[2] for o in outs],
        out_shape=[jax.ShapeDtypeStruct(o[0], o[1]) for o in outs],
        scratch_shapes=list(scratch),
        compiler_params=pltpu.CompilerParams(
            dimension_semantics=("arbitrary",) * len(grid), vmem_limit_bytes=limit << 20
        ),
        cost_estimate=pl.CostEstimate(flops=flops, transcendentals=exps, bytes_accessed=moved),
    )(*operands)


def normalised(values):
    center = values - jnp.mean(values, -1, keepdims=True)
    spread = jnp.mean(center * center, -1, keepdims=True)
    scale = lax.rsqrt(spread + NORM_EPS)
    return center * scale, scale


def norm_backward(values, grad, gain):
    unit, scale = normalised(values)
    inner = grad * gain
    mean_inner = jnp.mean(inner, -1, keepdims=True)
    mean_unit = jnp.mean(inner * unit, -1, keepdims=True)
    return scale * (inner - mean_inner - unit * mean_unit), grad * unit


def col_sum(values):
    return jnp.sum(values.astype(WIDE), 0, keepdims=True)


def add_rows(ref, first, rows):
    @pl.when(first)
    def _():
        ref[...] = jnp.zeros_like(ref)

    for place, row in enumerate(rows):
        ref[place : place + 1, :] += row


def masked_squares(values, length_ref, step, per_seq):
    rows = values.shape[0]
    start = (step % per_seq) * rows
    index = start + lax.broadcasted_iota(jnp.int32, (rows, 1), 0)
    inside = index < length_ref[step // per_seq]
    return col_sum(jnp.where(inside, values * values, 0.0))


def qkv_body(x_ref, vec_ref, wq, wk, wv, n_ref, q_ref, k_ref, v_ref):
    unit, _ = normalised(x_ref[...].astype(WIDE))
    norm = (unit * vec_ref[0:1, :] + vec_ref[10:11, :]).astype(LOW)
    n_ref[...] = norm
    query = (dot_nn(norm, wq[0]) + vec_ref[3:4, :]).astype(LOW)
    q_ref[...] = query * jnp.asarray(SCALE, LOW)
    k_ref[...] = dot_nn(norm, wk[0]).astype(LOW)
    v_ref[...] = (dot_nn(norm, wv[0]) + vec_ref[4:5, :]).astype(LOW)


def whole(shape):
    return spec(shape, lambda *_: (0,) * len(shape), once=True)


def qkv(x, vec, self_a, self_b, block):
    rows, width = x.shape
    row = lambda i: (i, 0)
    weight = lambda which: spec((1, width, width), lambda i: (which, 0, 0), once=True)
    return run(
        qkv_body,
        "qkv",
        (rows // block,),
        (x, vec, self_a, self_a, self_b),
        [spec((block, width), row), whole(vec.shape), weight(0), weight(1), weight(0)],
        [((rows, width), LOW, spec((block, width), row))] * 4,
        flops=6 * rows * width * width,
    )


def head_lanes(values, head):
    lane = lax.broadcasted_iota(jnp.int32, (1, PAIR), 1)
    inside = lane < HALF_PAIR if head == 0 else lane >= HALF_PAIR
    return jnp.where(inside, values, jnp.zeros_like(values))


def attend_body(causal, pairs, step_rows, q_ref, k_ref, v_ref, o_ref):
    length = q_ref.shape[0]
    frames = k_ref.shape[0]
    for pair in range(pairs):
        lanes = slice(pair * PAIR, (pair + 1) * PAIR)
        values = v_ref[:, lanes]
        by_head = [head_lanes(values, head) for head in (0, 1)]
        for start in range(0, length, step_rows):
            stop = min(start + step_rows, length)
            seen = stop if causal else frames
            keys = k_ref[0:seen, lanes]
            queries = q_ref[start:stop, lanes]
            total = None
            for head in (0, 1):
                scores = dot_nt(head_lanes(queries, head), keys)
                if causal:
                    shape = scores.shape
                    key_at = lax.broadcasted_iota(jnp.int32, shape, 1)
                    query_at = lax.broadcasted_iota(jnp.int32, shape, 0) + start
                    scores = jnp.where(key_at <= query_at, scores, -1e30)
                top = jnp.max(scores, -1, keepdims=True)
                exps = jnp.exp(scores - top)
                probs = exps * (1.0 / jnp.sum(exps, -1, keepdims=True))
                part = dot_nn(probs.astype(LOW), by_head[head][0:seen])
                total = part if total is None else total + part
            o_ref[start:stop, lanes] = total.astype(LOW)


def attend(q, k, v, batch, causal, pairs=2, step_rows=128):
    rows, width = q.shape
    length, frames = rows // batch, k.shape[0] // batch
    lanes = pairs * PAIR
    at = lambda b, p: (b, p)
    return run(
        functools.partial(attend_body, causal, pairs, step_rows),
        "attend_self" if causal else "attend_cross",
        (batch, width // lanes),
        (q, k, v),
        [spec((length, lanes), at), spec((frames, lanes), at), spec((frames, lanes), at)],
        [((rows, width), LOW, spec((length, lanes), at))],
        flops=4 * rows * frames * width,
        exps=rows * frames * HEADS,
    )[0]


def attend_back_body(causal, pairs, step_rows, q_ref, k_ref, v_ref, g_ref, gq_ref, gk_ref, gv_ref, dk, dv):
    length = q_ref.shape[0]
    frames = k_ref.shape[0]
    for pair in range(pairs):
        lanes = slice(pair * PAIR, (pair + 1) * PAIR)
        for start in range(0, length, step_rows):
            stop = min(start + step_rows, length)
            seen = stop if causal else frames
            keys = k_ref[0:seen, lanes]
            values = v_ref[0:seen, lanes]
            queries = q_ref[start:stop, lanes]
            grads = g_ref[start:stop, lanes]
            grad_q = grad_k = grad_v = None
            for head in (0, 1):
                head_keys = head_lanes(keys, head)
                scores = dot_nt(head_keys, queries)
                if causal:
                    shape = scores.shape
                    key_at = lax.broadcasted_iota(jnp.int32, shape, 0)
                    query_at = lax.broadcasted_iota(jnp.int32, shape, 1) + start
                    scores = jnp.where(key_at <= query_at, scores, -1e30)
                top = jnp.max(scores, 0, keepdims=True)
                exps = jnp.exp(scores - top)
                probs = exps * (1.0 / jnp.sum(exps, 0, keepdims=True))
                grad_probs = dot_nt(head_lanes(values, head), grads)
                weighted = probs * grad_probs
                inner = jnp.sum(weighted, 0, keepdims=True)
                grad_scores = (weighted - probs * inner).astype(LOW)
                part_v = dot_nn(probs.astype(LOW), head_lanes(grads, head))
                part_k = dot_nn(grad_scores, head_lanes(queries, head))
                part_q = dot_tn(grad_scores, head_keys)
                grad_v = part_v if grad_v is None else grad_v + part_v
                grad_k = part_k if grad_k is None else grad_k + part_k
                grad_q = part_q if grad_q is None else grad_q + part_q
            gq_ref[start:stop, lanes] = (grad_q * SCALE).astype(LOW)
            if causal:
                old = 0 if start == 0 else start
                if old:
                    dk[0:old, :] += grad_k[0:old]
                    dv[0:old, :] += grad_v[0:old]
                dk[old:seen, :] = grad_k[old:]
                dv[old:seen, :] = grad_v[old:]
            elif start == 0:
                dk[...] = grad_k
                dv[...] = grad_v
            else:
                dk[...] += grad_k
                dv[...] += grad_v
        gk_ref[:, lanes] = dk[...].astype(LOW)
        gv_ref[:, lanes] = dv[...].astype(LOW)


def attend_back(q, k, v, grad, batch, causal, pairs=2, step_rows=128):
    rows, width = q.shape
    length, frames = rows // batch, k.shape[0] // batch
    lanes = pairs * PAIR
    at = lambda b, p: (b, p)
    long, short = spec((length, lanes), at), spec((frames, lanes), at)
    return run(
        functools.partial(attend_back_body, causal, pairs, step_rows),
        "attend_self_back" if causal else "attend_cross_back",
        (batch, width // lanes),
        (q, k, v, grad),
        [long, short, short, long],
        [((rows, width), LOW, long), (k.shape, LOW, short), (k.shape, LOW, short)],
        [pltpu.VMEM((frames, PAIR), WIDE)] * 2,
        flops=10 * rows * frames * width,
        exps=rows * frames * HEADS,
    )


def mid_body(per_seq, len_ref, a_ref, x_ref, vec_ref, wo, wq, mid_ref, n_ref, q_ref, s_ref):
    step = pl.program_id(0)
    branch = dot_nn(a_ref[...], wo[0]) + vec_ref[5:6, :]
    mid = x_ref[...].astype(WIDE) + branch
    mid_ref[...] = mid
    unit, _ = normalised(mid)
    norm = (unit * vec_ref[1:2, :] + vec_ref[11:12, :]).astype(LOW)
    n_ref[...] = norm
    query = (dot_nn(norm, wq[0]) + vec_ref[6:7, :]).astype(LOW)
    q_ref[...] = query * jnp.asarray(SCALE, LOW)
    add_rows(s_ref, step == 0, [masked_squares(branch, len_ref, step, per_seq)])


def smem():
    return pl.BlockSpec(memory_space=pltpu.SMEM)


def mid_stage(lengths, attended, x, vec, self_b, cross_a, batch, block):
    rows, width = x.shape
    row = lambda i: (i, 0)
    weight = lambda which: spec((1, width, width), lambda i: (which, 0, 0), once=True)
    tile = spec((block, width), row)
    return run(
        functools.partial(mid_body, rows // batch // block),
        "mid_stage",
        (rows // block,),
        (lengths, attended, x, vec, self_b, cross_a),
        [smem(), tile, tile, whole(vec.shape), weight(1), weight(0)],
        [
            ((rows, width), WIDE, tile),
            ((rows, width), LOW, tile),
            ((rows, width), LOW, tile),
            ((8, width), WIDE, spec((8, width), lambda i: (0, 0))),
        ],
        flops=4 * rows * width * width,
    )


def frames_body(f_ref, vec_ref, wk, wv, k_ref, v_ref):
    frames = f_ref[...]
    k_ref[...] = dot_nn(frames, wk[0]).astype(LOW)
    v_ref[...] = (dot_nn(frames, wv[0]) + vec_ref[7:8, :]).astype(LOW)


def frames_stage(frames, vec, cross_b, block):
    rows, width = frames.shape
    tile = spec((block, width), lambda i: (i, 0))
    weight = lambda which: spec((1, width, width), lambda i: (which, 0, 0), once=True)
    return run(
        frames_body,
        "frames_stage",
        (rows // block,),
        (frames, vec, cross_b, cross_b),
        [tile, whole(vec.shape), weight(0), weight(1)],
        [((rows, width), LOW, tile)] * 2,
        flops=4 * rows * width * width,
    )


def late_body(per_seq, len_ref, a_ref, mid_ref, vec_ref, wo, late_ref, n_ref, s_ref):
    step = pl.program_id(0)
    branch = dot_nn(a_ref[...], wo[0]) + vec_ref[8:9, :]
    late = mid_ref[...] + branch
    late_ref[...] = late
    unit, _ = normalised(late)
    n_ref[...] = (unit * vec_ref[2:3, :] + vec_ref[12:13, :]).astype(LOW)
    add_rows(s_ref, step == 0, [masked_squares(branch, len_ref, step, per_seq)])


def late_stage(lengths, attended, mid, vec, cross_a, batch, block):
    rows, width = mid.shape
    tile = spec((block, width), lambda i: (i, 0))
    return run(
        functools.partial(late_body, rows // batch // block),
        "late_stage",
        (rows // block,),
        (lengths, attended, mid, vec, cross_a),
        [smem(), tile, tile, whole(vec.shape), spec((1, width, width), lambda i: (1, 0, 0), once=True)],
        [
            ((rows, width), WIDE, tile),
            ((rows, width), LOW, tile),
            ((8, width), WIDE, spec((8, width), lambda i: (0, 0))),
        ],
        flops=2 * rows * width * width,
    )


def ffn_in_body(n_ref, b_ref, w_ref, h_ref, d_ref):
    pre = dot_nn(n_ref[...], w_ref[0]) + b_ref[0]
    below = 0.5 + 0.5 * lax.erf(pre * (0.5**0.5))
    density = jnp.exp(-0.5 * pre * pre) * (1.0 / math.sqrt(2.0 * math.pi))
    h_ref[...] = (pre * below).astype(LOW)
    d_ref[...] = (below + pre * density).astype(LOW)


def ffn_in(norm, bias, weight, block):
    rows, width = norm.shape
    mats = weight.shape[0]
    tile = spec((block, width), lambda j, i: (i, j))
    return run(
        ffn_in_body,
        "ffn_in",
        (mats, rows // block),
        (norm, bias, weight),
        [
            spec((block, width), lambda j, i: (i, 0)),
            spec((1, 1, width), lambda j, i: (j, 0, 0)),
            spec((1, width, width), lambda j, i: (j, 0, 0)),
        ],
        [((rows, mats * width), LOW, tile)] * 2,
        flops=2 * rows * width * width * mats,
        exps=2 * rows * width * mats,
    )


def ffn_out_body(per_seq, len_ref, ha, hb, late_ref, vec_ref, oa, ob, r_ref, s_ref):
    step = pl.program_id(0)
    parts = [dot_nn(ha[...], w[0]) + dot_nn(hb[...], w[1]) for w in (oa, ob)]
    branch = jnp.concatenate(parts, -1) + vec_ref[9:10, :]
    result = late_ref[...] + branch
    r_ref[...] = result.astype(LOW)
    sums = [masked_squares(v, len_ref, step, per_seq) for v in (result, branch)]
    add_rows(s_ref, step == 0, sums)


def ffn_out(lengths, ha, hb, late, vec, out_a, out_b, batch, block):
    rows, width = late.shape
    inner = ha.shape[1]
    half = out_a.shape[2]
    tile = spec((block, width), lambda i: (i, 0))
    wide = spec((block, inner), lambda i: (i, 0))
    return run(
        functools.partial(ffn_out_body, rows // batch // block),
        "ffn_out",
        (rows // block,),
        (lengths, ha, hb, late, vec, out_a, out_b),
        [smem(), wide, wide, tile, whole(vec.shape), whole((2, inner, half)), whole((2, inner, half))],
        [((rows, width), LOW, tile), ((8, width), WIDE, spec((8, width), lambda i: (0, 0)))],
        flops=8 * rows * inner * half,
    )


def d_out_body(ha, hb, g_ref, da, db, s_ref):
    half = da.shape[2]
    grad = g_ref[...]
    for place, hidden in enumerate((ha, hb)):
        part = dot_tn(hidden[...], grad)
        da[place] = part[:, :half].astype(LOW)
        db[place] = part[:, half:].astype(LOW)
    add_rows(s_ref, pl.program_id(0) == 0, [])

    @pl.when(pl.program_id(0) == 0)
    def _():
        s_ref[0:1, :] = col_sum(grad)


def d_out(ha, hb, grad, block):
    rows, inner = ha.shape
    width = grad.shape[1]
    half = width // 2
    tile = spec((rows, block), lambda j: (0, j))
    return run(
        d_out_body,
        "d_out",
        (inner // block,),
        (ha, hb, grad),
        [tile, tile, whole(grad.shape)],
        [((2, inner, half), LOW, spec((2, block, half), lambda j: (0, j, 0)))] * 2
        + [((8, width), WIDE, spec((8, width), lambda j: (0, 0)))],
        flops=4 * rows * inner * width,
    )


def ffn_back_body(g_ref, d_ref, oa, ob, n_ref, p_ref, dw_ref, s_ref):
    half = oa.shape[2]
    grad = dot_nt(g_ref[:, :half], oa[0]) + dot_nt(g_ref[:, half:], ob[0])
    pre = (grad * d_ref[...].astype(WIDE)).astype(LOW)
    p_ref[...] = pre
    s_ref[0] = col_sum(pre)
    dw_ref[0] = dot_tn(n_ref[...], pre).astype(LOW)


def ffn_back(grad, slope, out_a, out_b, norm, which, width_step):
    rows, inner = slope.shape
    width = grad.shape[1]
    half = out_a.shape[2]
    steps = inner // width_step
    per = width // width_step
    assert per * width_step == width
    weight = spec((1, width_step, half), lambda j: (which, j, 0))
    tile = spec((rows, width_step), lambda j: (0, j))
    return run(
        ffn_back_body,
        "ffn_back",
        (steps,),
        (grad, slope, out_a, out_b, norm),
        [whole(grad.shape), tile, weight, weight, whole(norm.shape)],
        [
            ((rows, inner), LOW, tile),
            ((inner // width, width, width), LOW, spec((1, width, width_step), lambda j: (j // per, 0, j % per))),
            ((steps, 1, width_step), WIDE, spec((1, 1, width_step), lambda j: (j, 0, 0))),
        ],
        flops=4 * rows * inner * width,
    )


def late_back_body(pa, pb, wa, wb, late_ref, og_ref, vec_ref, wo, gl_ref, gc_ref, ga_ref, s_ref):
    width = wa.shape[1]
    grad = None
    for pre, weight in ((pa, wa), (pb, wb)):
        for mat in range(weight.shape[0]):
            part = dot_nt(pre[:, mat * width : (mat + 1) * width], weight[mat])
            grad = part if grad is None else grad + part
    through, for_gain = norm_backward(late_ref[...], grad, vec_ref[2:3, :])
    total = og_ref[...].astype(WIDE) + through
    gl_ref[...] = total
    low = total.astype(LOW)
    gc_ref[...] = low
    ga_ref[...] = dot_nt(low, wo[0]).astype(LOW)
    add_rows(s_ref, pl.program_id(0) == 0, [col_sum(for_gain), col_sum(grad), col_sum(low)])


def late_back(pa, pb, in_a, in_b, late, grad, vec, cross_a, block):
    rows, width = late.shape
    inner = pa.shape[1]
    tile = spec((block, width), lambda i: (i, 0))
    wide = spec((block, inner), lambda i: (i, 0))
    return run(
        late_back_body,
        "late_back",
        (rows // block,),
        (pa, pb, in_a, in_b, late, grad, vec, cross_a),
        [
            wide,
            wide,
            whole(in_a.shape),
            whole(in_b.shape),
            tile,
            tile,
            whole(vec.shape),
            spec((1, width, width), lambda i: (1, 0, 0), once=True),
        ],
        [
            ((rows, width), WIDE, tile),
            ((rows, width), LOW, tile),
            ((rows, width), LOW, tile),
            ((8, width), WIDE, spec((8, width), lambda i: (0, 0))),
        ],
        flops=4 * rows * inner * width + 2 * rows * width * width,
    )


def weights_body(count, *refs):
    out = refs[-1]
    for place in range(count):
        out[place] = dot_tn(refs[2 * place][...], refs[2 * place + 1][...]).astype(LOW)


def weight_grads(pairs, block):
    width = pairs[0][0].shape[1]
    operands, specs = [], []
    for left, right in pairs:
        operands += [left, right]
        specs += [spec((left.shape[0], block), lambda j: (0, j)), whole(right.shape)]
    return run(
        functools.partial(weights_body, len(pairs)),
        "weight_grads",
        (width // block,),
        tuple(operands),
        specs,
        [((len(pairs), width, width), LOW, spec((len(pairs), block, width), lambda j: (0, j, 0)))],
        flops=sum(2 * left.shape[0] * width * width for left, _ in pairs),
    )[0]


def mid_back_body(gq, wq, mid_ref, gl_ref, vec_ref, wo, gm_ref, gs_ref, ga_ref, s_ref):
    query = gq[...]
    grad = dot_nt(query, wq[0])
    through, for_gain = norm_backward(mid_ref[...], grad, vec_ref[1:2, :])
    total = gl_ref[...] + through
    gm_ref[...] = total
    low = total.astype(LOW)
    gs_ref[...] = low
    ga_ref[...] = dot_nt(low, wo[0]).astype(LOW)
    add_rows(
        s_ref,
        pl.program_id(0) == 0,
        [col_sum(for_gain), col_sum(grad), col_sum(low), col_sum(query)],
    )


def mid_back(grad_q, cross_a, mid, grad_late, vec, self_b, block):
    rows, width = mid.shape
    tile = spec((block, width), lambda i: (i, 0))
    weight = lambda which: spec((1, width, width), lambda i: (which, 0, 0), once=True)
    return run(
        mid_back_body,
        "mid_back",
        (rows // block,),
        (grad_q, cross_a, mid, grad_late, vec, self_b),
        [tile, weight(0), tile, tile, whole(vec.shape), weight(1)],
        [
            ((rows, width), WIDE, tile),
            ((rows, width), LOW, tile),
            ((rows, width), LOW, tile),
            ((8, width), WIDE, spec((8, width), lambda i: (0, 0))),
        ],
        flops=4 * rows * width * width,
    )


def frames_back_body(gk, gv, wk, wv, ge_ref, s_ref):
    grad_v = gv[...]
    ge_ref[...] = (dot_nt(gk[...], wk[0]) + dot_nt(grad_v, wv[0])).astype(LOW)
    add_rows(s_ref, pl.program_id(0) == 0, [col_sum(grad_v)])


def frames_back(grad_k, grad_v, cross_b, block):
    rows, width = grad_k.shape
    tile = spec((block, width), lambda i: (i, 0))
    weight = lambda which: spec((1, width, width), lambda i: (which, 0, 0), once=True)
    return run(
        frames_back_body,
        "frames_back",
        (rows // block,),
        (grad_k, grad_v, cross_b, cross_b),
        [tile, tile, weight(0), weight(1)],
        [((rows, width), LOW, tile), ((8, width), WIDE, spec((8, width), lambda i: (0, 0)))],
        flops=4 * rows * width * width,
    )


def in_back_body(gq, gk, gv, wq, wk, wv, x_ref, gm_ref, vec_ref, gi_ref, s_ref):
    query, value = gq[...], gv[...]
    grad = dot_nt(query, wq[0]) + dot_nt(gk[...], wk[0]) + dot_nt(value, wv[0])
    through, for_gain = norm_backward(x_ref[...].astype(WIDE), grad, vec_ref[0:1, :])
    gi_ref[...] = (gm_ref[...] + through).astype(LOW)
    add_rows(
        s_ref,
        pl.program_id(0) == 0,
        [col_sum(for_gain), col_sum(grad), col_sum(query), col_sum(value)],
    )


def in_back(grad_q, grad_k, grad_v, self_a, self_b, x, grad_mid, vec, block):
    rows, width = x.shape
    tile = spec((block, width), lambda i: (i, 0))
    weight = lambda which: spec((1, width, width), lambda i: (which, 0, 0), once=True)
    return run(
        in_back_body,
        "in_back",
        (rows // block,),
        (grad_q, grad_k, grad_v, self_a, self_a, self_b, x, grad_mid, vec),
        [tile, tile, tile, weight(0), weight(1), weight(0), tile, tile, whole(vec.shape)],
        [((rows, width), LOW, tile), ((8, width), WIDE, spec((8, width), lambda i: (0, 0)))],
        flops=6 * rows * width * width,
    )


def layer(vec, ffn_bias, weights, x, frames, lengths, grad, batch):
    self_a, self_b, cross_a, cross_b, in_a, in_b, out_a, out_b = weights
    rows, width = x.shape
    block = rows // batch // 2
    inner = in_a.shape[0] * width
    half = width // 2
    out_a, out_b = (w.reshape(2, inner, half) for w in (out_a, out_b))
    norm_one, query, key, value = qkv(x, vec, self_a, self_b, block)
    attended = attend(query, key, value, batch, True)
    mid, norm_two, cross_q, square_self = mid_stage(lengths, attended, x, vec, self_b, cross_a, batch, block)
    cross_k, cross_v = frames_stage(frames, vec, cross_b, frames.shape[0] // batch)
    cross_attended = attend(cross_q, cross_k, cross_v, batch, False)
    late, norm_three, square_cross = late_stage(lengths, cross_attended, mid, vec, cross_a, batch, block)
    hidden_a, slope_a = ffn_in(norm_three, ffn_bias[: in_a.shape[0]], in_a, block)
    hidden_b, slope_b = ffn_in(norm_three, ffn_bias[in_a.shape[0] :], in_b, block)
    d_out_a, d_out_b, sums_out = d_out(hidden_a, hidden_b, grad, width)
    result, square_rest = ffn_out(lengths, hidden_a, hidden_b, late, vec, out_a, out_b, batch, block)
    pre_a, d_in_a, sums_in_a = ffn_back(grad, slope_a, out_a, out_b, norm_three, 0, width)
    pre_b, d_in_b, sums_in_b = ffn_back(grad, slope_b, out_a, out_b, norm_three, 1, width)
    grad_late, grad_cross, grad_cross_att, sums_late = late_back(
        pre_a, pre_b, in_a, in_b, late, grad, vec, cross_a, block
    )
    grad_cq, grad_ck, grad_cv = attend_back(cross_q, cross_k, cross_v, grad_cross_att, batch, False)
    d_cross_a = weight_grads([(norm_two, grad_cq), (cross_attended, grad_cross)], width // 3)
    d_cross_b = weight_grads([(frames, grad_ck), (frames, grad_cv)], width // 3)
    grad_mid, grad_self, grad_att, sums_mid = mid_back(grad_cq, cross_a, mid, grad_late, vec, self_b, block)
    grad_frames, sums_frames = frames_back(grad_ck, grad_cv, cross_b, frames.shape[0] // batch)
    grad_q, grad_k, grad_v = attend_back(query, key, value, grad_att, batch, True)
    d_self_a = weight_grads([(norm_one, grad_q), (norm_one, grad_k)], width // 3)
    d_self_b = weight_grads([(norm_one, grad_v), (attended, grad_self)], width // 3)
    grad_in, sums_one = in_back(grad_q, grad_k, grad_v, self_a, self_b, x, grad_mid, vec, block)
    squares = jnp.stack([square_rest[0], square_self[0], square_cross[0], square_rest[1]])
    sum_rows = (
        [sums_one[0], sums_mid[0], sums_late[0]]
        + [sums_one[2], sums_one[3], sums_mid[2], sums_mid[3], sums_frames[0], sums_late[2], sums_out[0]]
        + [sums_one[1], sums_mid[1], sums_late[1]]
    )
    sums_ff = jnp.concatenate([sums_in_a, sums_in_b], 0).reshape(-1, width)
    grads = (d_self_a, d_self_b, d_cross_a, d_cross_b, d_in_a, d_in_b, d_out_a, d_out_b)
    return (result, grad_in, grad_frames), grads, jnp.concatenate([jnp.stack(sum_rows), sums_ff]), squares


def bit_orders(count):
    bits = count.bit_length() - 1
    assert 1 << bits == count
    each = (bits - 1) // 3
    x_bits = list(range(1, 1 + each))
    y_bits = list(range(1 + each, 1 + 2 * each))
    z_bits = list(range(1 + 2 * each, bits))
    return ([0] + x_bits + y_bits + z_bits, [0] + y_bits + x_bits + z_bits)


def swap(values, bit, count):
    return lax.ppermute(values, "fsdp", [(i, i ^ (1 << bit)) for i in range(count)])


def own_bit(bit):
    return (lax.axis_index("fsdp") >> bit) & 1


def gather_piece(piece, order, count):
    mats, rows, width = piece.shape
    bits = count.bit_length() - 1
    held = piece.reshape((mats,) + (1,) * bits + (rows, width))
    for bit in reversed(order):
        other = swap(held, bit, count)
        axis = 1 + (bits - 1 - bit)
        first = own_bit(bit) == 0
        held = jnp.where(
            first,
            jnp.concatenate([held, other], axis),
            jnp.concatenate([other, held], axis),
        )
    return held.reshape(mats, count * rows, width)


def scatter_piece(partial, order, count):
    mats, rows, width = partial.shape
    bits = count.bit_length() - 1
    rows = rows // count
    held = partial.reshape((mats,) + (2,) * bits + (rows, width))
    for step, bit in enumerate(order):
        axis = 1 + (bits - 1 - bit)
        mine = own_bit(bit)
        send = lax.dynamic_slice_in_dim(held, 1 - mine, 1, axis)
        keep = lax.dynamic_slice_in_dim(held, mine, 1, axis)
        other = swap(send, bit, count)
        held = keep.astype(jnp.float32) + other.astype(jnp.float32)
        if step < bits - 1:
            held = held.astype(partial.dtype)
    return held.reshape(mats, rows, width)


def sum_all(values, count):
    for bit in range(count.bit_length() - 1):
        values = values + swap(values, bit, count)
    return values


def shards(
    count,
    hidden_in,
    encoder_states,
    lengths,
    out_grad,
    attn_in,
    attn_out,
    fc_in,
    fc_out,
    gains,
    biases,
    ffn_bias,
):
    batch, length, width = hidden_in.shape
    half = width // 2
    order_a, order_b = bit_orders(count)
    share = gains.shape[1]
    small = jnp.concatenate([gains.reshape(-1), biases.reshape(-1), ffn_bias.reshape(-1)])
    small_count = small.shape[0]
    small_rows = -(-small_count // 128)
    small = jnp.pad(small, (0, small_rows * 128 - small_count)).reshape(1, small_rows, 128)
    small = gather_piece(small, order_a, count).reshape(count, small_rows * 128)
    vec = small[:, : 13 * share].reshape(count, 13, share).transpose(1, 0, 2).reshape(13, width)
    vec = jnp.pad(vec.astype(jnp.float32), ((0, 3), (0, 0)))
    ffn_bias_all = small[:, 13 * share : small_count].astype(jnp.float32).reshape(-1)
    ff = ffn_bias_all.shape[0]
    blocks = ff // width
    fc_in_blocks = fc_in.reshape(-1, blocks, width).transpose(1, 0, 2)
    self_a = gather_piece(attn_in[0:2], order_a, count)
    self_b = gather_piece(jnp.stack([attn_in[2], attn_out[0]]), order_b, count)
    cross_a = gather_piece(jnp.stack([attn_in[3], attn_out[1]]), order_a, count)
    cross_b = gather_piece(attn_in[4:6], order_b, count)
    in_a = gather_piece(fc_in_blocks[: blocks // 2], order_a, count)
    in_b = gather_piece(fc_in_blocks[blocks // 2 :], order_b, count)
    out_a = gather_piece(fc_out[None, :, :half], order_a, count)
    out_b = gather_piece(fc_out[None, :, half:], order_b, count)
    valid = jnp.arange(length)[None, :, None] < lengths[:, None, None]
    grad = jnp.where(valid, out_grad, jnp.zeros_like(out_grad))
    results, grads, rows, squares = layer(
        vec,
        ffn_bias_all.reshape(blocks, 1, width),
        (self_a, self_b, cross_a, cross_b, in_a, in_b, out_a, out_b),
        hidden_in.reshape(batch * length, width),
        encoder_states.reshape(-1, width),
        lengths,
        grad.reshape(batch * length, width),
        batch,
    )
    g_self_a, g_self_b, g_cross_a, g_cross_b, g_in_a, g_in_b, g_out_a, g_out_b = grads
    d_out_a = scatter_piece(g_out_a.reshape(1, ff, half), order_a, count)
    d_out_b = scatter_piece(g_out_b.reshape(1, ff, half), order_b, count)
    d_in_a = scatter_piece(g_in_a, order_a, count)
    d_in_b = scatter_piece(g_in_b, order_b, count)
    d_cross_a = scatter_piece(g_cross_a, order_a, count)
    d_cross_b = scatter_piece(g_cross_b, order_b, count)
    d_self_a = scatter_piece(g_self_a, order_a, count)
    d_self_b = scatter_piece(g_self_b, order_b, count)
    stats = jnp.concatenate([jnp.sum(squares, -1), jnp.sum(lengths).astype(jnp.float32)[None]])
    stats = jnp.pad(stats, (0, 123)).reshape(1, 128)
    stats = sum_all(stats, count)[0]
    rms = jnp.sqrt(stats[:4] / (stats[4] * width))
    rows = jnp.pad(rows, ((0, -rows.shape[0] % 8), (0, 0)))
    rows = sum_all(rows, count)
    me = lax.axis_index("fsdp")
    mine = lax.dynamic_slice_in_dim(rows[:13], me * share, share, 1)
    ff_share = ff // count
    mine_ff = lax.dynamic_slice_in_dim(rows[13 : 13 + blocks].reshape(-1), me * ff_share, ff_share)
    return (
        results[0].reshape(hidden_in.shape),
        results[1].reshape(hidden_in.shape),
        results[2].reshape(encoder_states.shape),
        jnp.stack([d_self_a[0], d_self_a[1], d_self_b[0], d_cross_a[0], d_cross_b[0], d_cross_b[1]]),
        jnp.stack([d_self_b[1], d_cross_a[1]]),
        jnp.concatenate([d_in_a, d_in_b]).transpose(1, 0, 2).reshape(-1, ff),
        jnp.concatenate([d_out_a[0], d_out_b[0]], 1),
        mine[:3],
        mine[3:13],
        mine_ff,
        rms,
    )


def solution(mesh):
    placed = (
        P("fsdp", None, None),
        P("fsdp", None, None),
        P("fsdp"),
        P("fsdp", None, None),
        P(None, "fsdp", None),
        P(None, "fsdp", None),
        P("fsdp", None),
        P("fsdp", None),
        P(None, "fsdp"),
        P(None, "fsdp"),
        P("fsdp"),
    )
    return jax.shard_map(
        functools.partial(shards, mesh.shape["fsdp"]),
        mesh=mesh,
        in_specs=placed,
        out_specs=(
            P("fsdp", None, None),
            P("fsdp", None, None),
            P("fsdp", None, None),
            P(None, "fsdp", None),
            P(None, "fsdp", None),
            P("fsdp", None),
            P("fsdp", None),
            P(None, "fsdp"),
            P(None, "fsdp"),
            P("fsdp"),
            P(),
        ),
        check_vma=False,
    )
```

time: 1480 us -> 530 us (0.36)
  waiting for transfers between devices: 940 us -> 192 us
  matrix products: 222 us -> 0 us
  blocking collectives: 164 us -> 0 us
  Pallas kernels: 0 us -> 138 us
  starting transfers between devices: 1.36 us -> 83.4 us
  other arithmetic: 55.4 us -> 24.7 us
    reduce_scatter x10 -> x0, waiting for transfers between devices: 885 us -> none  [shards(): lax.psum_scatter(tuple(totals), 'fsdp', scatter_dimension=0, tiled=True)]
    dot_general x84 -> x0, matrix products: 222 us -> none  [the longest x20 64.2 us: matmul(): return jnp.dot(left, right, preferred_element_type=jnp.float32)]
    ppermute x0 -> x95, waiting for transfers between devices: none -> 192 us  [swap(): lax.ppermute(values, 'fsdp', [(i, i ^ 1 << bit) for i in range(count)])]
    pallas_call x0 -> x22, Pallas kernels: none -> 138 us  [run(): pl.pallas_call(body, name=name, grid=grid, in_specs=in_specs, out_specs=[...]
    unnamed x2 -> x0, blocking collectives: 84.8 us -> none
    ppermute x0 -> x95, starting transfers between devices: none -> 83.4 us  [swap(): lax.ppermute(values, 'fsdp', [(i, i ^ 1 << bit) for i in range(count)])]
    all_gather x2 -> x0, blocking collectives: 79.6 us -> none  [the longest x1 42.4 us: fetch_forward(): lax.all_gather(biases, 'fsdp', axis=1, tiled=True)]
    all_gather x4 -> x0, waiting for transfers between devices: 52.6 us -> none  [the longest x1 50.9 us: fetch_forward(): lax.all_gather(fc_out, 'fsdp', axis=0, tiled=True)]
  transfers between devices with their start and end apart: 14 -> 95, of which waited for: 10 -> 43; matrix products, arithmetic and copies ran while one was open for 17% -> 10% of each run, Pallas kernels for 0% -> 2%
where the time goes in v1:
time: 530 us; the launch traced here: 520 us
  waiting for transfers between devices  192 us (36%)
  Pallas kernels  138 us (26%)
  starting transfers between devices  83.4 us (16%)
  local copies, waits for them, and re-layouts  77 us (15%)
  other arithmetic  24.7 us (5%)
    ppermute x95, waiting for transfers between devices, swap(): lax.ppermute(values, 'fsdp', [(i, i ^ 1 << bit) for i in range(count)])  192 us
    pallas_call x22, Pallas kernels, run(): pl.pallas_call(body, name=name, grid=grid, in_specs=in_specs, out_specs=[...  138 us
    ppermute x95, starting transfers between devices, swap(): lax.ppermute(values, 'fsdp', [(i, i ^ 1 << bit) for i in range(count)])  83.4 us
    unnamed x170, local copies, waits for them, and re-layouts  46.4 us
    convert_element_type x32, other arithmetic, scatter_piece(): held = held.astype(partial.dtype)  12.2 us
  transfers between devices with their start and end apart: 95, of which 43 were waited for; matrix products, arithmetic and copies ran while one was open for 10% of the time, Pallas kernels for 2%

profile of v1, /device:TPU:0, one launch (start us, length us, event | category | flops | bytes accessed | tf_op | source)
XLA Modules:
  0.0 520.2 jit_solution(11164450486425577915)
XLA Ops:
  3.0 4.1 collective-permute-start
  38.3 5.6 %collective-permute-done.35 = bf16[1,1,1,1,1,1,96,384]{7,6,5,4,3,2,1,0:T(8,128)(2,1)S(1)} collective-permute-done((bf16[1,1,1,1,1,1,96,384]{7,6,5,4,3,2,1,0:T(8,128)(2,1)S(1)}, bf16[1,1,1,1,1,1,96,384]{7,6,5,4,3,2,1,0:T(8,128)(2,1)S(1)}, u32[]{:S(2)}, u32[]{:S(2)}) %collective-permute-start.35) | collective-permute-done | bytes 73760 | tf_op jit(solution)/shard_map/ppermute | solution.py:655
  48.9 8.6 %collective-permute-done.41 = bf16[1,2,1,1,1,1,96,384]{7,6,5,4,3,2,1,0:T(8,128)(2,1)S(1)} collective-permute-done((bf16[1,2,1,1,1,1,96,384]{7,6,5,4,3,2,1,0:T(8,128)(2,1)S(1)}, bf16[1,2,1,1,1,1,96,384]{7,6,5,4,3,2,1,0:T(8,128)(2,1)S(1)}, u32[]{:S(2)}, u32[]{:S(2)}) %collective-permute-start.41) | collective-permute-done | bytes 147488 | tf_op jit(solution)/shard_map/ppermute | solution.py:655
  75.9 9.7 %collective-permute-done.7 = bf16[2,2,2,1,1,1,24,768]{7,6,0,1,2,5,4,3:T(8,128)(2,1)S(1)} collective-permute-done((bf16[2,2,2,1,1,1,24,768]{7,6,0,1,2,5,4,3:T(8,128)(2,1)S(1)}, bf16[2,2,2,1,1,1,24,768]{7,6,0,1,2,5,4,3:T(8,128)(2,1)S(1)}, u32[]{:S(2)}, u32[]{:S(2)}) %collective-permute-start.7) | collective-permute-done | bytes 294944 | tf_op jit(solution)/shard_map/ppermute | solution.py:655
  97.2 4.6 collective-permute-done.32
  105.5 15.6 %collective-permute-done.43 = bf16[1,2,2,1,2,1,96,384]{7,6,5,4,3,2,1,0:T(8,128)(2,1)S(1)} collective-permute-done((bf16[1,2,2,1,2,1,96,384]{7,6,5,4,3,2,1,0:T(8,128)(2,1)S(1)}, bf16[1,2,2,1,2,1,96,384]{7,6,5,4,3,2,1,0:T(8,128)(2,1)S(1)}, u32[]{:S(2)}, u32[]{:S(2)}) %collective-permute-start.43) | collective-permute-done | bytes 589856 | tf_op jit(solution)/shard_map/ppermute | solution.py:655
  124.4 15.3 %collective-permute-done.8 = bf16[2,2,2,2,1,1,24,768]{7,6,0,1,2,5,4,3:T(8,128)(2,1)S(1)} collective-permute-done((bf16[2,2,2,2,1,1,24,768]{7,6,0,1,2,5,4,3:T(8,128)(2,1)S(1)}, bf16[2,2,2,2,1,1,24,768]{7,6,0,1,2,5,4,3:T(8,128)(2,1)S(1)}, u32[]{:S(2)}, u32[]{:S(2)}) %collective-permute-start.8) | collective-permute-done | bytes 589856 | tf_op jit(solution)/shard_map/ppermute | solution.py:655
  142.1 4.6 collective-permute-done.18
  147.9 8.0 %collective-permute-done.33 = bf16[2,2,2,1,2,1,24,768]{7,6,2,1,0,3,5,4:T(8,128)(2,1)S(1)} collective-permute-done((bf16[2,2,2,1,2,1,24,768]{7,6,2,1,0,3,5,4:T(8,128)(2,1)S(1)}, bf16[2,2,2,1,2,1,24,768]{7,6,2,1,0,3,5,4:T(8,128)(2,1)S(1)}, u32[]{:S(2)}, u32[]{:S(2)}) %collective-permute-start.33) | collective-permute-done | bytes 589856 | tf_op jit(solution)/shard_map/ppermute | solution.py:655
  173.1 14.6 %attend_self.1.a_ref.refs_2_ = bf16[640,768]{1,0:T(8,128)(2,1)S(1)} custom-call(bf16[640,768]{1,0:T(8,128)(2,1)S(1)} %get-tuple-element.57.q_ref, bf16[640,768]{1,0:T(8,128)(2,1)S(1)} %get-tuple-element.58.k_ref, bf16[640,768]{1,0:T(8,128)(2,1)S(1)} %get-tuple-element.59.v_ref), custom_call_target="tpu_custom_call" | custom-call | flops 629145600 | bytes 3932160 | tf_op jit(solution)/shard_map/attend_self/pallas_call | solution.py:41
  187.8 4.5 mid_stage.1
  193.6 14.2 %attend_cross.1.a_ref.refs_2_ = bf16[640,768]{1,0:T(8,128)(2,1)S(1)} custom-call(bf16[640,768]{1,0:T(8,128)(2,1)S(1)} %get-tuple-element.60.q_ref, bf16[256,768]{1,0:T(8,128)(2,1)S(1)} %get-tuple-element.61.k_ref, bf16[256,768]{1,0:T(8,128)(2,1)S(1)} %get-tuple-element.62.v_ref), custom_call_target="tpu_custom_call" | custom-call | flops 251658240 | bytes 2752512 | tf_op jit(solution)/shard_map/attend_cross/pallas_call | solution.py:41
  212.3 4.1 ffn_in.3
  217.7 4.1 ffn_in.2
  223.1 5.0 d_out.1
  237.0 5.1 ffn_back.3
  249.6 6.3 %ffn_out.1 = (bf16[640,768]{1,0:T(8,128)(2,1)}, f32[8,768]{1,0:T(8,128)S(1)}) custom-call(s32[2]{0:T(128)S(1)} %copy-done.53, bf16[640,1536]{1,0:T(8,128)(2,1)S(1)} %copy-done.67, bf16[640,1536]{1,0:T(8,128)(2,1)S(1)} %copy-done.65, f32[640,768]{1,0:T(8,128)S(1)} %copy-done.43, f32[16,768]{1,0:T(8,128)S(1)} %pad_convert_fusion.vec_ref, ...), custom_call_target="tpu_custom_call" | custom-call | flops 3019898880 | bytes 11673608 | tf_op jit(solution)/shard_map/ffn_out/pallas_call | solution.py:41
  258.6 5.3 %ffn_back.2 = (bf16[640,1536]{1,0:T(8,128)(2,1)S(1)}, bf16[2,768,768]{2,1,0:T(8,128)(2,1)S(1)}, f32[2,1,768]{2,1,0:T(1,128)S(1)}) custom-call(bf16[640,768]{1,0:T(8,128)(2,1)S(1)} %bitcast.362, bf16[640,1536]{1,0:T(8,128)(2,1)S(1)} %copy-done.69, bf16[2,1536,384]{2,1,0:T(8,128)(2,1)S(1)} %bitcast.379, bf16[2,1536,384]{2,1,0:T(8,128)(2,1)S(1)} %bitcast.376, ...), custom_call_target="tpu_custom_call" | custom-call | flops 3019898880 | bytes 12982272 | tf_op jit(solution)/shard_map/ffn_back/pallas_call | solution.py:41
  272.4 13.3 %late_back.1 = (f32[640,768]{1,0:T(8,128)S(1)}, bf16[640,768]{1,0:T(8,128)(2,1)S(1)}, bf16[640,768]{1,0:T(8,128)(2,1)S(1)}, f32[8,768]{1,0:T(8,128)S(1)}) custom-call(bf16[640,1536]{1,0:T(8,128)(2,1)S(1)} %copy-done.48, bf16[640,1536]{1,0:T(8,128)(2,1)S(1)} %copy-done.46, bf16[2,768,768]{2,1,0:T(8,128)(2,1)S(1)} %bitcast.356, ...), custom_call_target="tpu_custom_call" | custom-call | flops 3774873600 | bytes 17965056 | tf_op jit(solution)/shard_map/late_back/pallas_call | solution.py:41
  287.3 13.4 %attend_cross_back.1 = (bf16[640,768]{1,0:T(8,128)(2,1)S(1)}, bf16[256,768]{1,0:T(8,128)(2,1)S(1)}, bf16[256,768]{1,0:T(8,128)(2,1)S(1)}) custom-call(bf16[640,768]{1,0:T(8,128)(2,1)S(1)} %copy-done.23, bf16[256,768]{1,0:T(8,128)(2,1)S(1)} %get-tuple-element.61.k_ref, bf16[256,768]{1,0:T(8,128)(2,1)S(1)} %get-tuple-element.62.v_ref, ...), custom_call_target="tpu_custom_call" | custom-call | flops 629145600 | bytes 4521984 | tf_op jit(solution)/shard_map/attend_cross_back/pallas_call | solution.py:41
  302.6 5.4 %mid_back.1 = (f32[640,768]{1,0:T(8,128)S(1)}, bf16[640,768]{1,0:T(8,128)(2,1)S(1)}, bf16[640,768]{1,0:T(8,128)(2,1)S(1)}, f32[8,768]{1,0:T(8,128)S(1)}) custom-call(bf16[640,768]{1,0:T(8,128)(2,1)S(1)} %get-tuple-element.74.gq.refs_1_, bf16[2,768,768]{2,1,0:T(8,128)(2,1)S(1)} %bitcast.336, f32[640,768]{1,0:T(8,128)S(1)} %copy-done.15, ...), custom_call_target="tpu_custom_call" | custom-call | flops 1509949440 | bytes 13639680 | tf_op jit(solution)/shard_map/mid_back/pallas_call | solution.py:41
  308.1 16.5 %attend_self_back.1 = (bf16[640,768]{1,0:T(8,128)(2,1)S(1)}, bf16[640,768]{1,0:T(8,128)(2,1)S(1)}, bf16[640,768]{1,0:T(8,128)(2,1)S(1)}) custom-call(bf16[640,768]{1,0:T(8,128)(2,1)S(1)} %copy-done.59, bf16[640,768]{1,0:T(8,128)(2,1)S(1)} %copy-done.61, bf16[640,768]{1,0:T(8,128)(2,1)S(1)} %copy-done.63, bf16[640,768]{1,0:T(8,128)(2,1)S(1)} %get-tuple-element.76.g_ref), custom_call_target="tpu_custom_call" | custom-call | flops 1572864000 | bytes 6881280 | tf_op jit(solution)/shard_map/attend_self_back/pallas_call | solution.py:41
  324.6 6.8 %in_back.1 = (bf16[640,768]{1,0:T(8,128)(2,1)}, f32[8,768]{1,0:T(8,128)S(1)}) custom-call(bf16[640,768]{1,0:T(8,128)(2,1)S(1)} %get-tuple-element.77.gq.refs_1_, bf16[640,768]{1,0:T(8,128)(2,1)S(1)} %get-tuple-element.78.gk.refs_3_, bf16[640,768]{1,0:T(8,128)(2,1)S(1)} %get-tuple-element.79.gv.refs_1_, bf16[2,768,768]{2,1,0:T(8,128)(2,1)S(1)} %bitcast.343, ...), custom_call_target="tpu_custom_call" | custom-call | flops 2264924160 | bytes 14032896 | tf_op jit(solution)/shard_map/in_back/pallas_call | solution.py:41
  376.6 4.6 collective-permute-done.89
  406.1 6.0 %collective-permute-done.71 = bf16[2,2,2,1,2,1,24,768]{7,6,5,4,3,2,1,0:T(8,128)(2,1)S(1)} collective-permute-done((bf16[2,2,2,1,2,1,24,768]{7,6,5,4,3,2,1,0:T(8,128)(2,1)S(1)}, bf16[2,2,2,1,2,1,24,768]{7,6,5,4,3,2,1,0:T(8,128)(2,1)S(1)}, u32[]{:S(2)}, u32[]{:S(2)}) %collective-permute-start.71) | collective-permute-done | bytes 589856 | tf_op jit(solution)/shard_map/ppermute | solution.py:655
  412.8 11.9 %collective-permute-done.81 = bf16[1,2,2,1,2,1,96,384]{7,6,5,4,3,2,1,0:T(8,128)(2,1)S(1)} collective-permute-done((bf16[1,2,2,1,2,1,96,384]{7,6,5,4,3,2,1,0:T(8,128)(2,1)S(1)}, bf16[1,2,2,1,2,1,96,384]{7,6,5,4,3,2,1,0:T(8,128)(2,1)S(1)}, u32[]{:S(2)}, u32[]{:S(2)}) %collective-permute-start.81) | collective-permute-done | bytes 589856 | tf_op jit(solution)/shard_map/ppermute | solution.py:655
  428.3 11.5 %collective-permute-done.46 = bf16[2,2,2,2,1,1,24,768]{7,6,5,4,3,2,1,0:T(8,128)(2,1)S(1)} collective-permute-done((bf16[2,2,2,2,1,1,24,768]{7,6,5,4,3,2,1,0:T(8,128)(2,1)S(1)}, bf16[2,2,2,2,1,1,24,768]{7,6,5,4,3,2,1,0:T(8,128)(2,1)S(1)}, u32[]{:S(2)}, u32[]{:S(2)}) %collective-permute-start.46) | collective-permute-done | bytes 589856 | tf_op jit(solution)/shard_map/ppermute | solution.py:655
  442.3 10.1 %collective-permute-done.66 = bf16[2,2,2,2,1,1,24,768]{7,6,0,5,4,3,2,1:T(8,128)(2,1)S(1)} collective-permute-done((bf16[2,2,2,2,1,1,24,768]{7,6,0,5,4,3,2,1:T(8,128)(2,1)S(1)}, bf16[2,2,2,2,1,1,24,768]{7,6,0,5,4,3,2,1:T(8,128)(2,1)S(1)}, u32[]{:S(2)}, u32[]{:S(2)}) %collective-permute-start.66) | collective-permute-done | bytes 589856 | tf_op jit(solution)/shard_map/ppermute | solution.py:655
  486.6 5.8 %collective-permute-done.53 = bf16[2,2,1,1,1,1,24,768]{7,6,5,4,3,2,1,0:T(8,128)(2,1)S(1)} collective-permute-done((bf16[2,2,1,1,1,1,24,768]{7,6,5,4,3,2,1,0:T(8,128)(2,1)S(1)}, bf16[2,2,1,1,1,1,24,768]{7,6,5,4,3,2,1,0:T(8,128)(2,1)S(1)}, u32[]{:S(2)}, u32[]{:S(2)}) %collective-permute-start.53) | collective-permute-done | bytes 147488 | tf_op jit(solution)/shard_map/ppermute | solution.py:655
  498.8 5.8 %collective-permute-done.59 = bf16[2,1,1,1,1,1,24,768]{7,6,5,4,3,2,1,0:T(8,128)(2,1)S(1)} collective-permute-done((bf16[2,1,1,1,1,1,24,768]{7,6,5,4,3,2,1,0:T(8,128)(2,1)S(1)}, bf16[2,1,1,1,1,1,24,768]{7,6,5,4,3,2,1,0:T(8,128)(2,1)S(1)}, u32[]{:S(2)}, u32[]{:S(2)}) %collective-permute-start.59) | collective-permute-done | bytes 73760 | tf_op jit(solution)/shard_map/ppermute | solution.py:655
  507.7 4.5 collective-permute-done.54
  512.3 5.1 collective-permute-done.64
  (577 shorter events, 255.5 us)
Async XLA Ops:
  8.7 25.1 %collective-permute-start.15 = (bf16[2,1,1,1,1,1,24,768]{7,6,0,5,4,3,2,1:T(8,128)(2,1)S(1)}, bf16[2,1,1,1,1,1,24,768]{7,6,0,5,4,3,2,1:T(8,128)(2,1)S(1)}, u32[]{:S(2)}, u32[]{:S(2)}) collective-permute-start(bf16[2,1,1,1,1,1,24,768]{7,6,0,5,4,3,2,1:T(8,128)(2,1)S(1)} %get-tuple-element.155), channel_id=1, source_target_pairs={{0,16},{1,17},{2,18},{3,19},{4,20},{5,21},{6,22},{7,23},{8,24},{9,... | collective-permute-start | bytes 221192 | tf_op jit(solution)/shard_map/ppermute | solution.py:655
  8.8 24.9 %collective-permute-start.10 = (bf16[2,1,1,1,1,1,24,768]{7,6,0,5,4,3,2,1:T(8,128)(2,1)S(1)}, bf16[2,1,1,1,1,1,24,768]{7,6,0,5,4,3,2,1:T(8,128)(2,1)S(1)}, u32[]{:S(2)}, u32[]{:S(2)}) collective-permute-start(bf16[2,1,1,1,1,1,24,768]{7,6,0,5,4,3,2,1:T(8,128)(2,1)S(1)} %get-tuple-element.160), channel_id=1, source_target_pairs={{0,16},{1,17},{2,18},{3,19},{4,20},{5,21},{6,22},{7,23},{8,24},{9,... | collective-permute-start | bytes 221192 | tf_op jit(solution)/shard_map/ppermute | solution.py:655
  12.7 24.1 %collective-permute-start.25 = (bf16[2,1,1,1,1,1,24,768]{7,6,0,5,4,3,2,1:T(8,128)(2,1)S(1)}, bf16[2,1,1,1,1,1,24,768]{7,6,0,5,4,3,2,1:T(8,128)(2,1)S(1)}, u32[]{:S(2)}, u32[]{:S(2)}) collective-permute-start(bf16[2,1,1,1,1,1,24,768]{7,6,0,5,4,3,2,1:T(8,128)(2,1)S(1)} %get-tuple-element.141), channel_id=1, source_target_pairs={{0,16},{1,17},{2,18},{3,19},{4,20},{5,21},{6,22},{7,23},{8,24},{9,... | collective-permute-start | bytes 221192 | tf_op jit(solution)/shard_map/ppermute | solution.py:655
  36.8 34.2 %collective-permute-start.31 = (bf16[2,2,1,1,1,1,24,768]{7,6,1,0,5,4,3,2:T(8,128)(2,1)S(1)}, bf16[2,2,1,1,1,1,24,768]{7,6,1,0,5,4,3,2:T(8,128)(2,1)S(1)}, u32[]{:S(2)}, u32[]{:S(2)}) collective-permute-start(bf16[2,2,1,1,1,1,24,768]{7,6,1,0,5,4,3,2:T(8,128)(2,1)S(1)} %copy.245), channel_id=1, source_target_pairs={{0,8},{1,9},{2,10},{3,11},{4,12},{5,13},{6,14},{7,15},{8,0},{9,1},... | collective-permute-start | bytes 442376 | tf_op jit(solution)/shard_map/ppermute | solution.py:655
  43.9 20.6 %collective-permute-start.26 = (bf16[2,2,1,1,1,1,24,768]{7,6,0,5,4,3,2,1:T(8,128)(2,1)S(1)}, bf16[2,2,1,1,1,1,24,768]{7,6,0,5,4,3,2,1:T(8,128)(2,1)S(1)}, u32[]{:S(2)}, u32[]{:S(2)}) collective-permute-start(bf16[2,2,1,1,1,1,24,768]{7,6,0,5,4,3,2,1:T(8,128)(2,1)S(1)} %bitcast_select_fusion.3), channel_id=1, source_target_pairs={{0,8},{1,9},{2,10},{3,11},{4,12},{5,13},{6,14},{7,15},{8,0},{9,1},... | collective-permute-start | bytes 442376 | tf_op jit(solution)/shard_map/ppermute | solution.py:655
  43.9 29.3 %collective-permute-start.11 = (bf16[2,2,1,1,1,1,24,768]{7,6,0,1,2,5,4,3:T(8,128)(2,1)S(1)}, bf16[2,2,1,1,1,1,24,768]{7,6,0,1,2,5,4,3:T(8,128)(2,1)S(1)}, u32[]{:S(2)}, u32[]{:S(2)}) collective-permute-start(bf16[2,2,1,1,1,1,24,768]{7,6,0,1,2,5,4,3:T(8,128)(2,1)S(1)} %fusion.11), channel_id=1, source_target_pairs={{0,8},{1,9},{2,10},{3,11},{4,12},{5,13},{6,14},{7,15},{8,0},{9,1},... | collective-permute-start | bytes 442376 | tf_op jit(solution)/shard_map/ppermute | solution.py:655
  69.4 18.5 %collective-permute-start.27 = (bf16[2,2,2,1,1,1,24,768]{7,6,0,5,4,3,2,1:T(8,128)(2,1)S(1)}, bf16[2,2,2,1,1,1,24,768]{7,6,0,5,4,3,2,1:T(8,128)(2,1)S(1)}, u32[]{:S(2)}, u32[]{:S(2)}) collective-permute-start(bf16[2,2,2,1,1,1,24,768]{7,6,0,5,4,3,2,1:T(8,128)(2,1)S(1)} %maximum_select_fusion.37), channel_id=1, source_target_pairs={{0,4},{1,5},{2,6},{3,7},{4,0},{5,1},{6,2},{7,3},{8,12},{9,13},{10,... | collective-permute-start | bytes 884744 | tf_op jit(solution)/shard_map/ppermute | solution.py:655
  73.3 18.7 %collective-permute-start.37 = (bf16[1,2,2,1,1,1,96,384]{7,6,2,1,4,5,3,0:T(8,128)(2,1)S(1)}, bf16[1,2,2,1,1,1,96,384]{7,6,2,1,4,5,3,0:T(8,128)(2,1)S(1)}, u32[]{:S(2)}, u32[]{:S(2)}) collective-permute-start(bf16[1,2,2,1,1,1,96,384]{7,6,2,1,4,5,3,0:T(8,128)(2,1)S(1)} %copy.255), channel_id=1, source_target_pairs={{0,4},{1,5},{2,6},{3,7},{4,0},{5,1},{6,2},{7,3},{8,12},{9,13},{10,... | collective-permute-start | bytes 884744 | tf_op jit(solution)/shard_map/ppermute | solution.py:655
  75.2 28.4 %collective-permute-start.17 = (bf16[2,2,2,1,1,1,24,768]{7,6,0,1,5,4,3,2:T(8,128)(2,1)S(1)}, bf16[2,2,2,1,1,1,24,768]{7,6,0,1,5,4,3,2:T(8,128)(2,1)S(1)}, u32[]{:S(2)}, u32[]{:S(2)}) collective-permute-start(bf16[2,2,2,1,1,1,24,768]{7,6,0,1,5,4,3,2:T(8,128)(2,1)S(1)} %bitcast_select_fusion.1), channel_id=1, source_target_pairs={{0,4},{1,5},{2,6},{3,7},{4,0},{5,1},{6,2},{7,3},{8,12},{9,13},{10,... | collective-permute-start | bytes 884744 | tf_op jit(solution)/shard_map/ppermute | solution.py:655
  88.0 34.9 %collective-permute-start.23 = (bf16[2,2,2,1,2,1,24,768]{7,6,0,1,5,4,3,2:T(8,128)(2,1)S(1)}, bf16[2,2,2,1,2,1,24,768]{7,6,0,1,5,4,3,2:T(8,128)(2,1)S(1)}, u32[]{:S(2)}, u32[]{:S(2)}) collective-permute-start(bf16[2,2,2,1,2,1,24,768]{7,6,0,1,5,4,3,2:T(8,128)(2,1)S(1)} %maximum_select_fusion.23), channel_id=1, source_target_pairs={{0,4},{1,5},{2,6},{3,7},{4,0},{5,1},{6,2},{7,3},{8,12},{9,13},{10,... | collective-permute-start | bytes 1769480 | tf_op jit(solution)/shard_map/ppermute | solution.py:655
  91.9 48.1 %collective-permute-start.28 = (bf16[2,2,2,2,1,1,24,768]{7,6,0,5,4,3,2,1:T(8,128)(2,1)S(1)}, bf16[2,2,2,2,1,1,24,768]{7,6,0,5,4,3,2,1:T(8,128)(2,1)S(1)}, u32[]{:S(2)}, u32[]{:S(2)}) collective-permute-start(bf16[2,2,2,2,1,1,24,768]{7,6,0,5,4,3,2,1:T(8,128)(2,1)S(1)} %maximum_select_fusion.25), channel_id=1, source_target_pairs={{0,2},{1,3},{2,0},{3,1},{4,6},{5,7},{6,4},{7,5},{8,10},{9,11},{10,... | collective-permute-start | bytes 1769480 | tf_op jit(solution)/shard_map/ppermute | solution.py:655
  95.5 46.1 %collective-permute-start.38 = (bf16[1,2,2,2,1,1,96,384]{7,6,2,1,4,5,3,0:T(8,128)(2,1)S(1)}, bf16[1,2,2,2,1,1,96,384]{7,6,2,1,4,5,3,0:T(8,128)(2,1)S(1)}, u32[]{:S(2)}, u32[]{:S(2)}) collective-permute-start(bf16[1,2,2,2,1,1,96,384]{7,6,2,1,4,5,3,0:T(8,128)(2,1)S(1)} %maximum_select_fusion.29), channel_id=1, source_target_pairs={{0,2},{1,3},{2,0},{3,1},{4,6},{5,7},{6,4},{7,5},{8,10},{9,11},{10,... | collective-permute-start | bytes 1769480 | tf_op jit(solution)/shard_map/ppermute | solution.py:655
  101.8 37.9 %collective-permute-start.8 = (bf16[2,2,2,2,1,1,24,768]{7,6,0,1,2,5,4,3:T(8,128)(2,1)S(1)}, bf16[2,2,2,2,1,1,24,768]{7,6,0,1,2,5,4,3:T(8,128)(2,1)S(1)}, u32[]{:S(2)}, u32[]{:S(2)}) collective-permute-start(bf16[2,2,2,2,1,1,24,768]{7,6,0,1,2,5,4,3:T(8,128)(2,1)S(1)} %maximum_select_fusion.17), channel_id=1, source_target_pairs={{0,2},{1,3},{2,0},{3,1},{4,6},{5,7},{6,4},{7,5},{8,10},{9,11},{10,... | collective-permute-start | bytes 1769480 | tf_op jit(solution)/shard_map/ppermute | solution.py:655
  121.1 25.6 %collective-permute-start.18 = (bf16[2,2,2,2,1,1,24,768]{7,6,0,1,5,4,3,2:T(8,128)(2,1)S(1)}, bf16[2,2,2,2,1,1,24,768]{7,6,0,1,5,4,3,2:T(8,128)(2,1)S(1)}, u32[]{:S(2)}, u32[]{:S(2)}) collective-permute-start(bf16[2,2,2,2,1,1,24,768]{7,6,0,1,5,4,3,2:T(8,128)(2,1)S(1)} %maximum_select_fusion.21), channel_id=1, source_target_pairs={{0,2},{1,3},{2,0},{3,1},{4,6},{5,7},{6,4},{7,5},{8,10},{9,11},{10,... | collective-permute-start | bytes 1769480 | tf_op jit(solution)/shard_map/ppermute | solution.py:655
  122.9 24.1 %collective-permute-start.13 = (bf16[2,2,2,1,2,1,24,768]{7,6,0,1,2,5,4,3:T(8,128)(2,1)S(1)}, bf16[2,2,2,1,2,1,24,768]{7,6,0,1,2,5,4,3:T(8,128)(2,1)S(1)}, u32[]{:S(2)}, u32[]{:S(2)}) collective-permute-start(bf16[2,2,2,1,2,1,24,768]{7,6,0,1,2,5,4,3:T(8,128)(2,1)S(1)} %maximum_select_fusion.19), channel_id=1, source_target_pairs={{0,4},{1,5},{2,6},{3,7},{4,0},{5,1},{6,2},{7,3},{8,12},{9,13},{10,... | collective-permute-start | bytes 1769480 | tf_op jit(solution)/shard_map/ppermute | solution.py:655
  334.0 52.6 %collective-permute-start.70 = (bf16[2,2,2,2,2,1,24,768]{7,6,5,4,3,2,1,0:T(8,128)(2,1)}, bf16[2,2,2,2,2,1,24,768]{7,6,5,4,3,2,1,0:T(8,128)(2,1)}, u32[]{:S(2)}, u32[]{:S(2)}) collective-permute-start(bf16[2,2,2,2,2,1,24,768]{7,6,5,4,3,2,1,0:T(8,128)(2,1)} %constant_dynamic-slice_fusion.15), channel_id=1, source_target_pairs={{0,1},{1,0},{2,3},{3,2},{4,5},{5,4},{6,7},{7,6},{8,9},{9,8},{10,11... | collective-permute-start | bytes 3538952 | tf_op jit(solution)/shard_map/ppermute | solution.py:655
  350.1 39.1 %collective-permute-start.80 = (bf16[1,2,2,2,2,1,96,384]{7,6,5,4,3,2,1,0:T(8,128)(2,1)}, bf16[1,2,2,2,2,1,96,384]{7,6,5,4,3,2,1,0:T(8,128)(2,1)}, u32[]{:S(2)}, u32[]{:S(2)}) collective-permute-start(bf16[1,2,2,2,2,1,96,384]{7,6,5,4,3,2,1,0:T(8,128)(2,1)} %constant_dynamic-slice_fusion.5), channel_id=1, source_target_pairs={{0,1},{1,0},{2,3},{3,2},{4,5},{5,4},{6,7},{7,6},{8,9},{9,8},{10,11... | collective-permute-start | bytes 3538952 | tf_op jit(solution)/shard_map/ppermute | solution.py:655
  366.5 25.8 %collective-permute-start.75 = (bf16[1,2,2,2,2,1,96,384]{7,6,5,4,3,2,1,0:T(8,128)(2,1)}, bf16[1,2,2,2,2,1,96,384]{7,6,5,4,3,2,1,0:T(8,128)(2,1)}, u32[]{:S(2)}, u32[]{:S(2)}) collective-permute-start(bf16[1,2,2,2,2,1,96,384]{7,6,5,4,3,2,1,0:T(8,128)(2,1)} %constant_dynamic-slice_fusion.10), channel_id=1, source_target_pairs={{0,1},{1,0},{2,3},{3,2},{4,5},{5,4},{6,7},{7,6},{8,9},{9,8},{10,11... | collective-permute-start | bytes 3538952 | tf_op jit(solution)/shard_map/ppermute | solution.py:655
  373.1 22.7 %collective-permute-start.55 = (bf16[2,2,2,2,2,1,24,768]{7,6,5,4,3,2,1,0:T(8,128)(2,1)}, bf16[2,2,2,2,2,1,24,768]{7,6,5,4,3,2,1,0:T(8,128)(2,1)}, u32[]{:S(2)}, u32[]{:S(2)}) collective-permute-start(bf16[2,2,2,2,2,1,24,768]{7,6,5,4,3,2,1,0:T(8,128)(2,1)} %constant_dynamic-slice_fusion.31), channel_id=1, source_target_pairs={{0,1},{1,0},{2,3},{3,2},{4,5},{5,4},{6,7},{7,6},{8,9},{9,8},{10,11... | collective-permute-start | bytes 3538952 | tf_op jit(solution)/shard_map/ppermute | solution.py:655
  398.2 27.2 %collective-permute-start.76 = (bf16[1,2,2,2,1,1,96,384]{7,6,5,4,3,2,1,0:T(8,128)(2,1)S(1)}, bf16[1,2,2,2,1,1,96,384]{7,6,5,4,3,2,1,0:T(8,128)(2,1)S(1)}, u32[]{:S(2)}, u32[]{:S(2)}) collective-permute-start(bf16[1,2,2,2,1,1,96,384]{7,6,5,4,3,2,1,0:T(8,128)(2,1)S(1)} %constant_dynamic-slice_fusion.9), channel_id=1, source_target_pairs={{0,2},{1,3},{2,0},{3,1},{4,6},{5,7},{6,4},{7,5},{8,10},{9,11},{10,... | collective-permute-start | bytes 1769480 | tf_op jit(solution)/shard_map/ppermute | solution.py:655
  400.9 23.8 %collective-permute-start.81 = (bf16[1,2,2,1,2,1,96,384]{7,6,5,4,3,2,1,0:T(8,128)(2,1)S(1)}, bf16[1,2,2,1,2,1,96,384]{7,6,5,4,3,2,1,0:T(8,128)(2,1)S(1)}, u32[]{:S(2)}, u32[]{:S(2)}) collective-permute-start(bf16[1,2,2,1,2,1,96,384]{7,6,5,4,3,2,1,0:T(8,128)(2,1)S(1)} %constant_dynamic-slice_fusion.4), channel_id=1, source_target_pairs={{0,4},{1,5},{2,6},{3,7},{4,0},{5,1},{6,2},{7,3},{8,12},{9,13},{10,... | collective-permute-start | bytes 1769480 | tf_op jit(solution)/shard_map/ppermute | solution.py:655
  402.5 24.7 %collective-permute-start.56 = (bf16[2,2,2,2,1,1,24,768]{7,6,5,4,3,2,1,0:T(8,128)(2,1)S(1)}, bf16[2,2,2,2,1,1,24,768]{7,6,5,4,3,2,1,0:T(8,128)(2,1)S(1)}, u32[]{:S(2)}, u32[]{:S(2)}) collective-permute-start(bf16[2,2,2,2,1,1,24,768]{7,6,5,4,3,2,1,0:T(8,128)(2,1)S(1)} %constant_dynamic-slice_fusion.30), channel_id=1, source_target_pairs={{0,2},{1,3},{2,0},{3,1},{4,6},{5,7},{6,4},{7,5},{8,10},{9,11},{10,... | collective-permute-start | bytes 1769480 | tf_op jit(solution)/shard_map/ppermute | solution.py:655
  404.4 35.3 %collective-permute-start.46 = (bf16[2,2,2,2,1,1,24,768]{7,6,5,4,3,2,1,0:T(8,128)(2,1)S(1)}, bf16[2,2,2,2,1,1,24,768]{7,6,5,4,3,2,1,0:T(8,128)(2,1)S(1)}, u32[]{:S(2)}, u32[]{:S(2)}) collective-permute-start(bf16[2,2,2,2,1,1,24,768]{7,6,5,4,3,2,1,0:T(8,128)(2,1)S(1)} %constant_dynamic-slice_fusion.40), channel_id=1, source_target_pairs={{0,2},{1,3},{2,0},{3,1},{4,6},{5,7},{6,4},{7,5},{8,10},{9,11},{10,... | collective-permute-start | bytes 1769480 | tf_op jit(solution)/shard_map/ppermute | solution.py:655
  412.1 29.4 %collective-permute-start.51 = (bf16[2,2,2,1,2,1,24,768]{7,6,5,4,3,2,1,0:T(8,128)(2,1)S(1)}, bf16[2,2,2,1,2,1,24,768]{7,6,5,4,3,2,1,0:T(8,128)(2,1)S(1)}, u32[]{:S(2)}, u32[]{:S(2)}) collective-permute-start(bf16[2,2,2,1,2,1,24,768]{7,6,5,4,3,2,1,0:T(8,128)(2,1)S(1)} %constant_dynamic-slice_fusion.35), channel_id=1, source_target_pairs={{0,4},{1,5},{2,6},{3,7},{4,0},{5,1},{6,2},{7,3},{8,12},{9,13},{10,... | collective-permute-start | bytes 1769480 | tf_op jit(solution)/shard_map/ppermute | solution.py:655
  424.7 27.7 %collective-permute-start.66 = (bf16[2,2,2,2,1,1,24,768]{7,6,0,5,4,3,2,1:T(8,128)(2,1)S(1)}, bf16[2,2,2,2,1,1,24,768]{7,6,0,5,4,3,2,1:T(8,128)(2,1)S(1)}, u32[]{:S(2)}, u32[]{:S(2)}) collective-permute-start(bf16[2,2,2,2,1,1,24,768]{7,6,0,5,4,3,2,1:T(8,128)(2,1)S(1)} %constant_dynamic-slice_fusion.19), channel_id=1, source_target_pairs={{0,2},{1,3},{2,0},{3,1},{4,6},{5,7},{6,4},{7,5},{8,10},{9,11},{10,... | collective-permute-start | bytes 1769480 | tf_op jit(solution)/shard_map/ppermute | solution.py:655
  425.4 28.7 %collective-permute-start.61 = (bf16[2,2,2,1,2,1,24,768]{7,6,5,4,3,2,1,0:T(8,128)(2,1)S(1)}, bf16[2,2,2,1,2,1,24,768]{7,6,5,4,3,2,1,0:T(8,128)(2,1)S(1)}, u32[]{:S(2)}, u32[]{:S(2)}) collective-permute-start(bf16[2,2,2,1,2,1,24,768]{7,6,5,4,3,2,1,0:T(8,128)(2,1)S(1)} %constant_dynamic-slice_fusion.25), channel_id=1, source_target_pairs={{0,4},{1,5},{2,6},{3,7},{4,0},{5,1},{6,2},{7,3},{8,12},{9,13},{10,... | collective-permute-start | bytes 1769480 | tf_op jit(solution)/shard_map/ppermute | solution.py:655
  427.1 31.6 %collective-permute-start.72 = (bf16[2,2,2,1,1,1,24,768]{7,6,5,4,3,2,1,0:T(8,128)(2,1)S(1)}, bf16[2,2,2,1,1,1,24,768]{7,6,5,4,3,2,1,0:T(8,128)(2,1)S(1)}, u32[]{:S(2)}, u32[]{:S(2)}) collective-permute-start(bf16[2,2,2,1,1,1,24,768]{7,6,5,4,3,2,1,0:T(8,128)(2,1)S(1)} %constant_dynamic-slice_fusion.13), channel_id=1, source_target_pairs={{0,2},{1,3},{2,0},{3,1},{4,6},{5,7},{6,4},{7,5},{8,10},{9,11},{10,... | collective-permute-start | bytes 884744 | tf_op jit(solution)/shard_map/ppermute | solution.py:655
  439.8 20.0 %collective-permute-start.77 = (bf16[1,2,2,1,1,1,96,384]{7,6,5,4,3,2,1,0:T(8,128)(2,1)S(1)}, bf16[1,2,2,1,1,1,96,384]{7,6,5,4,3,2,1,0:T(8,128)(2,1)S(1)}, u32[]{:S(2)}, u32[]{:S(2)}) collective-permute-start(bf16[1,2,2,1,1,1,96,384]{7,6,5,4,3,2,1,0:T(8,128)(2,1)S(1)} %constant_dynamic-slice_fusion.8), channel_id=1, source_target_pairs={{0,4},{1,5},{2,6},{3,7},{4,0},{5,1},{6,2},{7,3},{8,12},{9,13},{10,... | collective-permute-start | bytes 884744 | tf_op jit(solution)/shard_map/ppermute | solution.py:655
  441.5 23.5 %collective-permute-start.82 = (bf16[1,2,2,1,1,1,96,384]{7,6,5,4,3,2,1,0:T(8,128)(2,1)S(1)}, bf16[1,2,2,1,1,1,96,384]{7,6,5,4,3,2,1,0:T(8,128)(2,1)S(1)}, u32[]{:S(2)}, u32[]{:S(2)}) collective-permute-start(bf16[1,2,2,1,1,1,96,384]{7,6,5,4,3,2,1,0:T(8,128)(2,1)S(1)} %constant_dynamic-slice_fusion.3), channel_id=1, source_target_pairs={{0,2},{1,3},{2,0},{3,1},{4,6},{5,7},{6,4},{7,5},{8,10},{9,11},{10,... | collective-permute-start | bytes 884744 | tf_op jit(solution)/shard_map/ppermute | solution.py:655
  482.2 30.0 %collective-permute-start.74 = (bf16[2,1,1,1,1,1,24,768]{7,6,5,4,3,2,1,0:T(8,128)(2,1)S(1)}, bf16[2,1,1,1,1,1,24,768]{7,6,5,4,3,2,1,0:T(8,128)(2,1)S(1)}, u32[]{:S(2)}, u32[]{:S(2)}) collective-permute-start(bf16[2,1,1,1,1,1,24,768]{7,6,5,4,3,2,1,0:T(8,128)(2,1)S(1)} %constant_dynamic-slice_fusion.11), channel_id=1, source_target_pairs={{0,16},{1,17},{2,18},{3,19},{4,20},{5,21},{6,22},{7,23},{8,24},{9,... | collective-permute-start | bytes 221192 | tf_op jit(solution)/shard_map/ppermute | solution.py:655
  486.2 31.3 %collective-permute-start.79 = (bf16[1,1,1,1,1,1,96,384]{7,6,5,4,3,2,1,0:T(8,128)(2,1)S(1)}, bf16[1,1,1,1,1,1,96,384]{7,6,5,4,3,2,1,0:T(8,128)(2,1)S(1)}, u32[]{:S(2)}, u32[]{:S(2)}) collective-permute-start(bf16[1,1,1,1,1,1,96,384]{7,6,5,4,3,2,1,0:T(8,128)(2,1)S(1)} %constant_dynamic-slice_fusion.6), channel_id=1, source_target_pairs={{0,16},{1,17},{2,18},{3,19},{4,20},{5,21},{6,22},{7,23},{8,24},{9,... | collective-permute-start | bytes 221192 | tf_op jit(solution)/shard_map/ppermute | solution.py:655
  492.4 26.0 %collective-permute-start.84 = (bf16[1,1,1,1,1,1,96,384]{7,6,5,4,3,2,1,0:T(8,128)(2,1)S(1)}, bf16[1,1,1,1,1,1,96,384]{7,6,5,4,3,2,1,0:T(8,128)(2,1)S(1)}, u32[]{:S(2)}, u32[]{:S(2)}) collective-permute-start(bf16[1,1,1,1,1,1,96,384]{7,6,5,4,3,2,1,0:T(8,128)(2,1)S(1)} %constant_dynamic-slice_fusion.1), channel_id=1, source_target_pairs={{0,16},{1,17},{2,18},{3,19},{4,20},{5,21},{6,22},{7,23},{8,24},{9,... | collective-permute-start | bytes 221192 | tf_op jit(solution)/shard_map/ppermute | solution.py:655
  (144 other events, 1162.5 us)

commit v2 on v1

--- a/solution.py
+++ b/solution.py
@@ -240,16 +240,13 @@
     )
 
 
-def mid_body(per_seq, len_ref, a_ref, x_ref, vec_ref, wo, wq, mid_ref, n_ref, q_ref, s_ref):
+def mid_body(per_seq, len_ref, a_ref, x_ref, vec_ref, wo, mid_ref, n_ref, s_ref):
     step = pl.program_id(0)
     branch = dot_nn(a_ref[...], wo[0]) + vec_ref[5:6, :]
     mid = x_ref[...].astype(WIDE) + branch
     mid_ref[...] = mid
     unit, _ = normalised(mid)
-    norm = (unit * vec_ref[1:2, :] + vec_ref[11:12, :]).astype(LOW)
-    n_ref[...] = norm
-    query = (dot_nn(norm, wq[0]) + vec_ref[6:7, :]).astype(LOW)
-    q_ref[...] = query * jnp.asarray(SCALE, LOW)
+    n_ref[...] = (unit * vec_ref[1:2, :] + vec_ref[11:12, :]).astype(LOW)
     add_rows(s_ref, step == 0, [masked_squares(branch, len_ref, step, per_seq)])
 
 
@@ -257,45 +254,47 @@
     return pl.BlockSpec(memory_space=pltpu.SMEM)
 
 
-def mid_stage(lengths, attended, x, vec, self_b, cross_a, batch, block):
+def mid_stage(lengths, attended, x, vec, self_b, batch, block):
     rows, width = x.shape
-    row = lambda i: (i, 0)
-    weight = lambda which: spec((1, width, width), lambda i: (which, 0, 0), once=True)
-    tile = spec((block, width), row)
+    weight = spec((1, width, width), lambda i: (1, 0, 0), once=True)
+    tile = spec((block, width), lambda i: (i, 0))
     return run(
         functools.partial(mid_body, rows // batch // block),
         "mid_stage",
         (rows // block,),
-        (lengths, attended, x, vec, self_b, cross_a),
-        [smem(), tile, tile, whole(vec.shape), weight(1), weight(0)],
+        (lengths, attended, x, vec, self_b),
+        [smem(), tile, tile, whole(vec.shape), weight],
         [
             ((rows, width), WIDE, tile),
             ((rows, width), LOW, tile),
-            ((rows, width), LOW, tile),
             ((8, width), WIDE, spec((8, width), lambda i: (0, 0))),
         ],
-        flops=4 * rows * width * width,
-    )
-
-
-def frames_body(f_ref, vec_ref, wk, wv, k_ref, v_ref):
+        flops=2 * rows * width * width,
+    )
+
+
+def cross_body(n_ref, f_ref, vec_ref, wq, wk, wv, q_ref, k_ref, v_ref):
+    query = (dot_nn(n_ref[...], wq[0]) + vec_ref[6:7, :]).astype(LOW)
+    q_ref[...] = query * jnp.asarray(SCALE, LOW)
     frames = f_ref[...]
     k_ref[...] = dot_nn(frames, wk[0]).astype(LOW)
     v_ref[...] = (dot_nn(frames, wv[0]) + vec_ref[7:8, :]).astype(LOW)
 
 
-def frames_stage(frames, vec, cross_b, block):
-    rows, width = frames.shape
-    tile = spec((block, width), lambda i: (i, 0))
+def cross_stage(norm, frames, vec, cross_a, cross_b, batch):
+    width = norm.shape[1]
+    rows, frame_rows = norm.shape[0], frames.shape[0]
+    long = spec((rows // batch, width), lambda i: (i, 0))
+    short = spec((frame_rows // batch, width), lambda i: (i, 0))
     weight = lambda which: spec((1, width, width), lambda i: (which, 0, 0), once=True)
     return run(
-        frames_body,
-        "frames_stage",
-        (rows // block,),
-        (frames, vec, cross_b, cross_b),
-        [tile, whole(vec.shape), weight(0), weight(1)],
-        [((rows, width), LOW, tile)] * 2,
-        flops=4 * rows * width * width,
+        cross_body,
+        "cross_stage",
+        (batch,),
+        (norm, frames, vec, cross_a, cross_b, cross_b),
+        [long, short, whole(vec.shape), weight(0), weight(0), weight(1)],
+        [((rows, width), LOW, long), ((frame_rows, width), LOW, short), ((frame_rows, width), LOW, short)],
+        flops=(2 * rows + 4 * frame_rows) * width * width,
     )
 
 
@@ -357,8 +356,11 @@
 
 def ffn_out_body(per_seq, len_ref, ha, hb, late_ref, vec_ref, oa, ob, r_ref, s_ref):
     step = pl.program_id(0)
-    parts = [dot_nn(ha[...], w[0]) + dot_nn(hb[...], w[1]) for w in (oa, ob)]
-    branch = jnp.concatenate(parts, -1) + vec_ref[9:10, :]
+    width = oa.shape[2]
+    branch = vec_ref[9:10, :]
+    for hidden, weight in ((ha, oa), (hb, ob)):
+        for mat in range(weight.shape[0]):
+            branch = branch + dot_nn(hidden[:, mat * width : (mat + 1) * width], weight[mat])
     result = late_ref[...] + branch
     r_ref[...] = result.astype(LOW)
     sums = [masked_squares(v, len_ref, step, per_seq) for v in (result, branch)]
@@ -368,7 +370,6 @@
 def ffn_out(lengths, ha, hb, late, vec, out_a, out_b, batch, block):
     rows, width = late.shape
     inner = ha.shape[1]
-    half = out_a.shape[2]
     tile = spec((block, width), lambda i: (i, 0))
     wide = spec((block, inner), lambda i: (i, 0))
     return run(
@@ -376,19 +377,15 @@
         "ffn_out",
         (rows // block,),
         (lengths, ha, hb, late, vec, out_a, out_b),
-        [smem(), wide, wide, tile, whole(vec.shape), whole((2, inner, half)), whole((2, inner, half))],
+        [smem(), wide, wide, tile, whole(vec.shape), whole(out_a.shape), whole(out_b.shape)],
         [((rows, width), LOW, tile), ((8, width), WIDE, spec((8, width), lambda i: (0, 0)))],
-        flops=8 * rows * inner * half,
-    )
-
-
-def d_out_body(ha, hb, g_ref, da, db, s_ref):
-    half = da.shape[2]
+        flops=4 * rows * inner * width,
+    )
+
+
+def d_out_body(hidden, g_ref, dw_ref, s_ref):
     grad = g_ref[...]
-    for place, hidden in enumerate((ha, hb)):
-        part = dot_tn(hidden[...], grad)
-        da[place] = part[:, :half].astype(LOW)
-        db[place] = part[:, half:].astype(LOW)
+    dw_ref[0] = dot_tn(hidden[...], grad).astype(LOW)
     add_rows(s_ref, pl.program_id(0) == 0, [])
 
     @pl.when(pl.program_id(0) == 0)
@@ -396,51 +393,48 @@
         s_ref[0:1, :] = col_sum(grad)
 
 
-def d_out(ha, hb, grad, block):
-    rows, inner = ha.shape
+def d_out(hidden, grad):
+    rows, inner = hidden.shape
     width = grad.shape[1]
-    half = width // 2
-    tile = spec((rows, block), lambda j: (0, j))
+    mats = inner // width
     return run(
         d_out_body,
         "d_out",
-        (inner // block,),
-        (ha, hb, grad),
-        [tile, tile, whole(grad.shape)],
-        [((2, inner, half), LOW, spec((2, block, half), lambda j: (0, j, 0)))] * 2
-        + [((8, width), WIDE, spec((8, width), lambda j: (0, 0)))],
-        flops=4 * rows * inner * width,
-    )
-
-
-def ffn_back_body(g_ref, d_ref, oa, ob, n_ref, p_ref, dw_ref, s_ref):
-    half = oa.shape[2]
-    grad = dot_nt(g_ref[:, :half], oa[0]) + dot_nt(g_ref[:, half:], ob[0])
+        (mats,),
+        (hidden, grad),
+        [spec((rows, width), lambda j: (0, j)), whole(grad.shape)],
+        [
+            ((mats, width, width), LOW, spec((1, width, width), lambda j: (j, 0, 0))),
+            ((8, width), WIDE, spec((8, width), lambda j: (0, 0))),
+        ],
+        flops=2 * rows * inner * width,
+    )
+
+
+def ffn_back_body(g_ref, d_ref, o_ref, n_ref, p_ref, dw_ref, s_ref):
+    grad = dot_nt(g_ref[...], o_ref[0])
     pre = (grad * d_ref[...].astype(WIDE)).astype(LOW)
     p_ref[...] = pre
     s_ref[0] = col_sum(pre)
     dw_ref[0] = dot_tn(n_ref[...], pre).astype(LOW)
 
 
-def ffn_back(grad, slope, out_a, out_b, norm, which, width_step):
+def ffn_back(grad, slope, weight, norm):
     rows, inner = slope.shape
     width = grad.shape[1]
-    half = out_a.shape[2]
-    steps = inner // width_step
-    per = width // width_step
-    assert per * width_step == width
-    weight = spec((1, width_step, half), lambda j: (which, j, 0))
-    tile = spec((rows, width_step), lambda j: (0, j))
+    mats = inner // width
+    mat = spec((1, width, width), lambda j: (j, 0, 0))
+    tile = spec((rows, width), lambda j: (0, j))
     return run(
         ffn_back_body,
         "ffn_back",
-        (steps,),
-        (grad, slope, out_a, out_b, norm),
-        [whole(grad.shape), tile, weight, weight, whole(norm.shape)],
+        (mats,),
+        (grad, slope, weight, norm),
+        [whole(grad.shape), tile, mat, whole(norm.shape)],
         [
             ((rows, inner), LOW, tile),
-            ((inner // width, width, width), LOW, spec((1, width, width_step), lambda j: (j // per, 0, j % per))),
-            ((steps, 1, width_step), WIDE, spec((1, 1, width_step), lambda j: (j, 0, 0))),
+            ((mats, width, width), LOW, mat),
+            ((mats, 1, width), WIDE, spec((1, 1, width), lambda j: (j, 0, 0))),
         ],
         flops=4 * rows * inner * width,
     )
@@ -599,56 +593,31 @@
     )
 
 
-def layer(vec, ffn_bias, weights, x, frames, lengths, grad, batch):
-    self_a, self_b, cross_a, cross_b, in_a, in_b, out_a, out_b = weights
-    rows, width = x.shape
-    block = rows // batch // 2
-    inner = in_a.shape[0] * width
-    half = width // 2
-    out_a, out_b = (w.reshape(2, inner, half) for w in (out_a, out_b))
-    norm_one, query, key, value = qkv(x, vec, self_a, self_b, block)
-    attended = attend(query, key, value, batch, True)
-    mid, norm_two, cross_q, square_self = mid_stage(lengths, attended, x, vec, self_b, cross_a, batch, block)
-    cross_k, cross_v = frames_stage(frames, vec, cross_b, frames.shape[0] // batch)
-    cross_attended = attend(cross_q, cross_k, cross_v, batch, False)
-    late, norm_three, square_cross = late_stage(lengths, cross_attended, mid, vec, cross_a, batch, block)
-    hidden_a, slope_a = ffn_in(norm_three, ffn_bias[: in_a.shape[0]], in_a, block)
-    hidden_b, slope_b = ffn_in(norm_three, ffn_bias[in_a.shape[0] :], in_b, block)
-    d_out_a, d_out_b, sums_out = d_out(hidden_a, hidden_b, grad, width)
-    result, square_rest = ffn_out(lengths, hidden_a, hidden_b, late, vec, out_a, out_b, batch, block)
-    pre_a, d_in_a, sums_in_a = ffn_back(grad, slope_a, out_a, out_b, norm_three, 0, width)
-    pre_b, d_in_b, sums_in_b = ffn_back(grad, slope_b, out_a, out_b, norm_three, 1, width)
-    grad_late, grad_cross, grad_cross_att, sums_late = late_back(
-        pre_a, pre_b, in_a, in_b, late, grad, vec, cross_a, block
-    )
-    grad_cq, grad_ck, grad_cv = attend_back(cross_q, cross_k, cross_v, grad_cross_att, batch, False)
-    d_cross_a = weight_grads([(norm_two, grad_cq), (cross_attended, grad_cross)], width // 3)
-    d_cross_b = weight_grads([(frames, grad_ck), (frames, grad_cv)], width // 3)
-    grad_mid, grad_self, grad_att, sums_mid = mid_back(grad_cq, cross_a, mid, grad_late, vec, self_b, block)
-    grad_frames, sums_frames = frames_back(grad_ck, grad_cv, cross_b, frames.shape[0] // batch)
-    grad_q, grad_k, grad_v = attend_back(query, key, value, grad_att, batch, True)
-    d_self_a = weight_grads([(norm_one, grad_q), (norm_one, grad_k)], width // 3)
-    d_self_b = weight_grads([(norm_one, grad_v), (attended, grad_self)], width // 3)
-    grad_in, sums_one = in_back(grad_q, grad_k, grad_v, self_a, self_b, x, grad_mid, vec, block)
-    squares = jnp.stack([square_rest[0], square_self[0], square_cross[0], square_rest[1]])
-    sum_rows = (
-        [sums_one[0], sums_mid[0], sums_late[0]]
-        + [sums_one[2], sums_one[3], sums_mid[2], sums_mid[3], sums_frames[0], sums_late[2], sums_out[0]]
-        + [sums_one[1], sums_mid[1], sums_late[1]]
-    )
-    sums_ff = jnp.concatenate([sums_in_a, sums_in_b], 0).reshape(-1, width)
-    grads = (d_self_a, d_self_b, d_cross_a, d_cross_b, d_in_a, d_in_b, d_out_a, d_out_b)
-    return (result, grad_in, grad_frames), grads, jnp.concatenate([jnp.stack(sum_rows), sums_ff]), squares
-
-
-def bit_orders(count):
+def axis_bits(count):
     bits = count.bit_length() - 1
     assert 1 << bits == count
     each = (bits - 1) // 3
     x_bits = list(range(1, 1 + each))
     y_bits = list(range(1 + each, 1 + 2 * each))
     z_bits = list(range(1 + 2 * each, bits))
-    return ([0] + x_bits + y_bits + z_bits, [0] + y_bits + x_bits + z_bits)
+    return x_bits, y_bits, z_bits
+
+
+def gather_stages(count, parts):
+    x_bits, y_bits, z_bits = (list(reversed(b)) for b in axis_bits(count))
+    if parts == 1:
+        return [[(b,) for b in bits] for bits in (z_bits[:1], z_bits[1:], y_bits, x_bits, [0])]
+    return [
+        [(z_bits[0],)],
+        [(b,) for b in z_bits[1:]],
+        list(zip(y_bits, x_bits)),
+        list(zip(x_bits, y_bits)),
+        [(0, 0)],
+    ]
+
+
+def scatter_stages(count, parts):
+    return [list(reversed(stage)) for stage in reversed(gather_stages(count, parts))]
 
 
 def swap(values, bit, count):
@@ -659,42 +628,120 @@
     return (lax.axis_index("fsdp") >> bit) & 1
 
 
-def gather_piece(piece, order, count):
-    mats, rows, width = piece.shape
-    bits = count.bit_length() - 1
-    held = piece.reshape((mats,) + (1,) * bits + (rows, width))
-    for bit in reversed(order):
-        other = swap(held, bit, count)
-        axis = 1 + (bits - 1 - bit)
-        first = own_bit(bit) == 0
-        held = jnp.where(
-            first,
-            jnp.concatenate([held, other], axis),
-            jnp.concatenate([other, held], axis),
-        )
-    return held.reshape(mats, count * rows, width)
-
-
-def scatter_piece(partial, order, count):
-    mats, rows, width = partial.shape
-    bits = count.bit_length() - 1
-    rows = rows // count
-    held = partial.reshape((mats,) + (2,) * bits + (rows, width))
-    for step, bit in enumerate(order):
-        axis = 1 + (bits - 1 - bit)
-        mine = own_bit(bit)
-        send = lax.dynamic_slice_in_dim(held, 1 - mine, 1, axis)
-        keep = lax.dynamic_slice_in_dim(held, mine, 1, axis)
-        other = swap(send, bit, count)
-        held = keep.astype(jnp.float32) + other.astype(jnp.float32)
-        if step < bits - 1:
-            held = held.astype(partial.dtype)
-    return held.reshape(mats, rows, width)
-
-
-def sum_all(values, count):
-    for bit in range(count.bit_length() - 1):
-        values = values + swap(values, bit, count)
+def halves(parts):
+    if len(parts) == 2:
+        return parts
+    middle = parts[0].shape[0] // 2
+    return [parts[0][:middle], parts[0][middle:]]
+
+
+class Gather:
+    def __init__(self, piece, count, parts=2):
+        self.count = count
+        self.bits = count.bit_length() - 1
+        mats, rows, width = piece.shape
+        self.shape = (rows, width)
+        self.parts = [piece.reshape((mats,) + (1,) * self.bits + (rows, width))]
+        self.stages = gather_stages(count, parts)
+        self.flight = None
+
+    def axis(self, bit):
+        return self.bits - bit
+
+    def land(self):
+        if self.flight is not None:
+            parts = []
+            for held, (bit, other) in zip(self.parts, self.flight):
+                axis = self.axis(bit)
+                parts.append(
+                    jnp.where(
+                        own_bit(bit) == 0,
+                        jnp.concatenate([held, other], axis),
+                        jnp.concatenate([other, held], axis),
+                    )
+                )
+            self.parts = parts
+            self.flight = None
+
+    def ready(self):
+        self.land()
+        if len(self.stages[0][0]) == 2:
+            self.parts = halves(self.parts)
+        return self.parts
+
+    def launch(self, parts):
+        self.parts = parts
+        for place, step in enumerate(self.stages.pop(0)):
+            if place:
+                self.land()
+            self.flight = [(bit, swap(part, bit, self.count)) for bit, part in zip(step, self.parts)]
+
+    def result(self):
+        self.land()
+        rows, width = self.shape
+        return [part.reshape(part.shape[0], self.count * rows, width) for part in self.parts]
+
+
+class Scatter:
+    def __init__(self, parts, count):
+        self.count = count
+        self.bits = count.bit_length() - 1
+        self.pairs = []
+        for part in parts:
+            mats, rows, width = part.shape
+            self.shape = (rows // count, width)
+            self.pairs.append((part.reshape((mats,) + (2,) * self.bits + (rows // count, width)), None))
+        self.stages = scatter_stages(count, len(parts))
+        self.kind = parts[0].dtype
+
+    def pick(self, pair, bit, side):
+        axis = self.bits - bit
+        values = [
+            lax.dynamic_slice_in_dim(v, side, 1, axis) for v in pair if v is not None
+        ]
+        if len(values) == 1:
+            return values[0]
+        return (values[0].astype(jnp.float32) + values[1].astype(jnp.float32)).astype(self.kind)
+
+    def prepare(self):
+        step = self.stages[0][0]
+        if len(step) == 1 and len(self.pairs) == 2:
+            self.pairs = [
+                (jnp.concatenate([self.total(p, self.kind) for p in self.pairs]), None)
+            ]
+        return [self.pick(pair, bit, 1 - own_bit(bit)) for bit, pair in zip(step, self.pairs)]
+
+    def ready(self):
+        return self.prepare()
+
+    def total(self, pair, kind):
+        if pair[1] is None:
+            return pair[0]
+        return (pair[0].astype(jnp.float32) + pair[1].astype(jnp.float32)).astype(kind)
+
+    def launch(self, sends):
+        steps = self.stages.pop(0)
+        for place, step in enumerate(steps):
+            if place:
+                self.stages.insert(0, [step])
+                sends = self.prepare()
+                self.stages.pop(0)
+            flight = [swap(v, bit, self.count) for bit, v in zip(step, sends)]
+            self.pairs = [
+                (self.pick(pair, bit, own_bit(bit)), other)
+                for bit, pair, other in zip(step, self.pairs, flight)
+            ]
+
+    def result(self):
+        total = jnp.concatenate([self.total(p, jnp.float32) for p in self.pairs])
+        return total.astype(jnp.float32).reshape((total.shape[0],) + self.shape)
+
+
+def tick(chains, values=()):
+    ready = [chain.ready() for chain in chains]
+    ready, values = lax.optimization_barrier((ready, values))
+    for chain, parts in zip(chains, ready):
+        chain.launch(parts)
     return values
 
 
@@ -713,70 +760,134 @@
     ffn_bias,
 ):
     batch, length, width = hidden_in.shape
-    half = width // 2
-    order_a, order_b = bit_orders(count)
+    rows = batch * length
+    block = length // 2
+    frame_rows = encoder_states.shape[1]
     share = gains.shape[1]
-    small = jnp.concatenate([gains.reshape(-1), biases.reshape(-1), ffn_bias.reshape(-1)])
+    ff_share = ffn_bias.shape[0]
+    mats = ff_share // share
+    middle = mats // 2
+
+    small = jnp.concatenate([gains.reshape(-1), biases.reshape(-1), ffn_bias])
     small_count = small.shape[0]
-    small_rows = -(-small_count // 128)
-    small = jnp.pad(small, (0, small_rows * 128 - small_count)).reshape(1, small_rows, 128)
-    small = gather_piece(small, order_a, count).reshape(count, small_rows * 128)
+    small_rows = -(-(small_count + 5) // 128)
+    small_size = small_rows * 128
+    small = jnp.pad(small, (0, small_size - small_count)).reshape(1, small_rows, 128)
+    fc_in_mats = fc_in.reshape(share, count, mats, share).transpose(2, 0, 1, 3).reshape(mats, share, width)
+    fc_out_mats = fc_out.reshape(mats, share, width)
+    g_small = Gather(small, count, 1)
+    g_self = Gather(jnp.concatenate([attn_in[0:3], attn_out[0:1]]), count)
+    g_cross = Gather(jnp.concatenate([attn_in[3:4], attn_out[1:2], attn_in[4:6]]), count)
+    g_in = Gather(fc_in_mats, count)
+    g_out = Gather(fc_out_mats, count)
+
+    x = hidden_in.reshape(rows, width)
+    frames = encoder_states.reshape(-1, width)
+    valid = jnp.arange(length)[None, :, None] < lengths[:, None, None]
+    grad = jnp.where(valid, out_grad, jnp.zeros_like(out_grad)).reshape(rows, width)
+
+    tick([g_self, g_small])
+    tick([g_self, g_small])
+    tick([g_self, g_small, g_cross])
+    tick([g_self, g_small, g_cross, g_in])
+    tick([g_self, g_small, g_cross, g_in])
+    small = g_small.result()[0].astype(jnp.float32).reshape(count, small_size)
     vec = small[:, : 13 * share].reshape(count, 13, share).transpose(1, 0, 2).reshape(13, width)
-    vec = jnp.pad(vec.astype(jnp.float32), ((0, 3), (0, 0)))
-    ffn_bias_all = small[:, 13 * share : small_count].astype(jnp.float32).reshape(-1)
-    ff = ffn_bias_all.shape[0]
-    blocks = ff // width
-    fc_in_blocks = fc_in.reshape(-1, blocks, width).transpose(1, 0, 2)
-    self_a = gather_piece(attn_in[0:2], order_a, count)
-    self_b = gather_piece(jnp.stack([attn_in[2], attn_out[0]]), order_b, count)
-    cross_a = gather_piece(jnp.stack([attn_in[3], attn_out[1]]), order_a, count)
-    cross_b = gather_piece(attn_in[4:6], order_b, count)
-    in_a = gather_piece(fc_in_blocks[: blocks // 2], order_a, count)
-    in_b = gather_piece(fc_in_blocks[blocks // 2 :], order_b, count)
-    out_a = gather_piece(fc_out[None, :, :half], order_a, count)
-    out_b = gather_piece(fc_out[None, :, half:], order_b, count)
-    valid = jnp.arange(length)[None, :, None] < lengths[:, None, None]
-    grad = jnp.where(valid, out_grad, jnp.zeros_like(out_grad))
-    results, grads, rows, squares = layer(
-        vec,
-        ffn_bias_all.reshape(blocks, 1, width),
-        (self_a, self_b, cross_a, cross_b, in_a, in_b, out_a, out_b),
-        hidden_in.reshape(batch * length, width),
-        encoder_states.reshape(-1, width),
-        lengths,
-        grad.reshape(batch * length, width),
-        batch,
-    )
-    g_self_a, g_self_b, g_cross_a, g_cross_b, g_in_a, g_in_b, g_out_a, g_out_b = grads
-    d_out_a = scatter_piece(g_out_a.reshape(1, ff, half), order_a, count)
-    d_out_b = scatter_piece(g_out_b.reshape(1, ff, half), order_b, count)
-    d_in_a = scatter_piece(g_in_a, order_a, count)
-    d_in_b = scatter_piece(g_in_b, order_b, count)
-    d_cross_a = scatter_piece(g_cross_a, order_a, count)
-    d_cross_b = scatter_piece(g_cross_b, order_b, count)
-    d_self_a = scatter_piece(g_self_a, order_a, count)
-    d_self_b = scatter_piece(g_self_b, order_b, count)
-    stats = jnp.concatenate([jnp.sum(squares, -1), jnp.sum(lengths).astype(jnp.float32)[None]])
-    stats = jnp.pad(stats, (0, 123)).reshape(1, 128)
-    stats = sum_all(stats, count)[0]
+    vec = jnp.pad(vec, ((0, 3), (0, 0)))
+    bias = small[:, 13 * share : small_count].reshape(count, mats, share)
+    bias = bias.transpose(1, 0, 2).reshape(mats, 1, width)
+    self_a, self_b = g_self.result()
+    norm_one, query, key, value = qkv(x, vec, self_a, self_b, block)
+    query, key, value = tick([g_cross, g_in, g_out], (query, key, value))
+    attended = attend(query, key, value, batch, True)
+    mid, norm_two, square_self = mid_stage(lengths, attended, x, vec, self_b, batch, block)
+    norm_two = tick([g_cross, g_in, g_out], norm_two)
+    cross_a, cross_b = g_cross.result()
+    cross_q, cross_k, cross_v = cross_stage(norm_two, frames, vec, cross_a, cross_b, batch)
+    cross_attended = attend(cross_q, cross_k, cross_v, batch, False)
+    cross_attended = tick([g_in, g_out], cross_attended)
+    late, norm_three, square_cross = late_stage(lengths, cross_attended, mid, vec, cross_a, batch, block)
+    in_a, in_b = g_in.result()
+    hidden_a, slope_a = ffn_in(norm_three, bias[:middle], in_a, block)
+    hidden_b, slope_b = ffn_in(norm_three, bias[middle:], in_b, block)
+    hidden_a, hidden_b = tick([g_out], (hidden_a, hidden_b))
+    d_out_a, sums_out = d_out(hidden_a, grad)
+    d_out_b, _ = d_out(hidden_b, grad)
+    s_out = Scatter([d_out_a, d_out_b], count)
+    grad = tick([g_out, s_out], grad)
+    out_a, out_b = g_out.result()
+    pre_a, d_in_a, sums_in_a = ffn_back(grad, slope_a, out_a, norm_three)
+    hidden_a, hidden_b, grad = tick([s_out], (hidden_a, hidden_b, grad))
+    pre_b, d_in_b, sums_in_b = ffn_back(grad, slope_b, out_b, norm_three)
+    result, square_rest = ffn_out(lengths, hidden_a, hidden_b, late, vec, out_a, out_b, batch, block)
+    s_in = Scatter([d_in_a, d_in_b], count)
+    pre_a, pre_b = tick([s_in], (pre_a, pre_b))
+    grad_late, grad_cross, grad_cross_att, sums_late = late_back(
+        pre_a, pre_b, in_a, in_b, late, grad, vec, cross_a, block
+    )
+    grad_cross_att = tick([s_in, s_out], grad_cross_att)
+    grad_cq, grad_ck, grad_cv = attend_back(
+        cross_q, cross_k, cross_v, grad_cross_att, batch, False
+    )
+    d_cross_a = weight_grads([(norm_two, grad_cq), (cross_attended, grad_cross)], width // 3)
+    d_cross_b = weight_grads([(frames, grad_ck), (frames, grad_cv)], width // 3)
+    s_cross = Scatter([d_cross_a, d_cross_b], count)
+    grad_cq = tick([s_cross, s_in, s_out], grad_cq)
+    grad_mid, grad_self, grad_att, sums_mid = mid_back(
+        grad_cq, cross_a, mid, grad_late, vec, self_b, block
+    )
+    grad_att = tick([s_cross, s_in, s_out], grad_att)
+    grad_q, grad_k, grad_v = attend_back(query, key, value, grad_att, batch, True)
+    grad_q, grad_k, grad_v = tick([s_cross, s_in], (grad_q, grad_k, grad_v))
+    d_self_a = weight_grads([(norm_one, grad_q), (norm_one, grad_k)], width // 3)
+    d_self_b = weight_grads([(norm_one, grad_v), (attended, grad_self)], width // 3)
+    s_self = Scatter([d_self_a, d_self_b], count)
+    grad_q, grad_k, grad_v = tick([s_self, s_cross], (grad_q, grad_k, grad_v))
+    grad_in, sums_one = in_back(grad_q, grad_k, grad_v, self_a, self_b, x, grad_mid, vec, block)
+    grad_ck, grad_cv = tick([s_self, s_cross], (grad_ck, grad_cv))
+    grad_frames, sums_frames = frames_back(grad_ck, grad_cv, cross_b, frame_rows)
+
+    sum_rows = jnp.stack(
+        [sums_one[0], sums_mid[0], sums_late[0]]
+        + [sums_one[2], sums_one[3], sums_mid[2], sums_mid[3], sums_frames[0], sums_late[2], sums_out[0]]
+        + [sums_one[1], sums_mid[1], sums_late[1]]
+    )
+    squares = jnp.stack([square_rest[0], square_self[0], square_cross[0], square_rest[1]])
+    stats = jnp.concatenate([jnp.sum(squares, -1), jnp.sum(lengths).astype(WIDE)[None]])
+    sums_ff = jnp.concatenate([sums_in_a, sums_in_b]).reshape(mats, count, share)
+    sums = jnp.concatenate(
+        [
+            sum_rows.reshape(13, count, share).transpose(1, 0, 2).reshape(count, 13 * share),
+            sums_ff.transpose(1, 0, 2).reshape(count, ff_share),
+            jnp.broadcast_to(stats[None], (count, 5)),
+        ],
+        1,
+    )
+    sums = jnp.pad(sums, ((0, 0), (0, small_size - sums.shape[1])))
+    s_small = Scatter([sums.reshape(1, count * small_rows, 128)], count)
+    tick([s_self, s_small])
+    tick([s_self, s_small])
+    tick([s_self, s_small])
+    tick([s_small])
+    tick([s_small])
+    d_out_all = s_out.result()
+    d_in_all = s_in.result()
+    d_cross = s_cross.result()
+    d_self = s_self.result()
+    small = s_small.result().reshape(-1)
+    stats = small[small_count : small_count + 5]
     rms = jnp.sqrt(stats[:4] / (stats[4] * width))
-    rows = jnp.pad(rows, ((0, -rows.shape[0] % 8), (0, 0)))
-    rows = sum_all(rows, count)
-    me = lax.axis_index("fsdp")
-    mine = lax.dynamic_slice_in_dim(rows[:13], me * share, share, 1)
-    ff_share = ff // count
-    mine_ff = lax.dynamic_slice_in_dim(rows[13 : 13 + blocks].reshape(-1), me * ff_share, ff_share)
     return (
-        results[0].reshape(hidden_in.shape),
-        results[1].reshape(hidden_in.shape),
-        results[2].reshape(encoder_states.shape),
-        jnp.stack([d_self_a[0], d_self_a[1], d_self_b[0], d_cross_a[0], d_cross_b[0], d_cross_b[1]]),
-        jnp.stack([d_self_b[1], d_cross_a[1]]),
-        jnp.concatenate([d_in_a, d_in_b]).transpose(1, 0, 2).reshape(-1, ff),
-        jnp.concatenate([d_out_a[0], d_out_b[0]], 1),
-        mine[:3],
-        mine[3:13],
-        mine_ff,
+        result.reshape(hidden_in.shape),
+        grad_in.reshape(hidden_in.shape),
+        grad_frames.reshape(encoder_states.shape),
+        jnp.concatenate([d_self[:3], d_cross[:1], d_cross[2:]]),
+        jnp.concatenate([d_self[3:], d_cross[1:2]]),
+        d_in_all.reshape(mats, share, count, share).transpose(1, 2, 0, 3).reshape(share, -1),
+        d_out_all.reshape(ff_share, width),
+        small[: 3 * share].reshape(3, share),
+        small[3 * share : 13 * share].reshape(10, share),
+        small[13 * share : small_count],
         rms,
     )
 

time: 530 us -> 465 us (0.88)
  waiting for transfers between devices: 192 us -> 93.3 us
  other arithmetic: 24.7 us -> 74.5 us
  starting transfers between devices: 83.4 us -> 67.9 us
    ppermute x95 -> x74, waiting for transfers between devices: 192 us -> 93.3 us  [swap(): lax.ppermute(values, 'fsdp', [(i, i ^ 1 << bit) for i in range(count)])]
    select_n x46 -> x37, other arithmetic: 7.01 us -> 34.4 us  [the longest x36 33.3 us: land(): jnp.where(own_bit(bit) == 0, jnp.concatenate([held, other], axis), jnp.co...]
    convert_element_type x33 -> x29, other arithmetic: 12.3 us -> 31.2 us  [the longest x20 27.2 us: pick(): (values[0].astype(jnp.float32) + values[1].astype(jnp.float32)).astype(se...]
    ppermute x95 -> x74, starting transfers between devices: 83.4 us -> 67.9 us  [swap(): lax.ppermute(values, 'fsdp', [(i, i ^ 1 << bit) for i in range(count)])]
    unnamed x170 -> x263, local copies, waits for them, and re-layouts: 46.4 us -> 49.1 us
    dynamic_slice x41 -> x10, local copies, waits for them, and re-layouts: 11.5 us -> 9.4 us  [pick(): lax.dynamic_slice_in_dim(v, side, 1, axis)]
    pallas_call x22 -> x23, Pallas kernels: 138 us -> 137 us  [run(): pl.pallas_call(body, name=name, grid=grid, in_specs=in_specs, out_specs=[...]
  transfers between devices with their start and end apart: 95 -> 74, of which waited for: 43 -> 24; matrix products, arithmetic and copies ran while one was open for 10% -> 17% of each run, Pallas kernels for 2% -> 19%
where the time goes in v2:
time: 465 us; the launch traced here: 458 us
  Pallas kernels  137 us (29%)
  waiting for transfers between devices  93.3 us (20%)
  local copies, waits for them, and re-layouts  81.4 us (18%)
  other arithmetic  74.5 us (16%)
  starting transfers between devices  67.9 us (15%)
    pallas_call x23, Pallas kernels, run(): pl.pallas_call(body, name=name, grid=grid, in_specs=in_specs, out_specs=[...  137 us
    ppermute x74, waiting for transfers between devices, swap(): lax.ppermute(values, 'fsdp', [(i, i ^ 1 << bit) for i in range(count)])  93.3 us
    ppermute x74, starting transfers between devices, swap(): lax.ppermute(values, 'fsdp', [(i, i ^ 1 << bit) for i in range(count)])  67.9 us
    unnamed x263, local copies, waits for them, and re-layouts  49.1 us
    select_n x36, other arithmetic, land(): jnp.where(own_bit(bit) == 0, jnp.concatenate([held, other], axis), jnp.co...  33.3 us
    convert_element_type x20, other arithmetic, pick(): (values[0].astype(jnp.float32) + values[1].astype(jnp.float32)).astype(se...  27.2 us
    dynamic_slice x10, local copies, waits for them, and re-layouts, pick(): lax.dynamic_slice_in_dim(v, side, 1, axis)  9.4 us
  transfers between devices with their start and end apart: 74, of which 24 were waited for; matrix products, arithmetic and copies ran while one was open for 17% of the time, Pallas kernels for 19%

profile of v2, /device:TPU:0, one launch (start us, length us, event | category | flops | bytes accessed | tf_op | source)
XLA Modules:
  0.0 458.4 jit_solution(6176532118091538629)
XLA Ops:
  4.7 4.1 collective-permute-start
  8.8 7.0 %collective-permute-done.1 = bf16[1,1,1,1,1,1,4,128]{7,6,5,4,3,2,1,0:T(4,128)(2,1)S(1)} collective-permute-done((bf16[1,1,1,1,1,1,4,128]{7,6,5,4,3,2,1,0:T(4,128)(2,1)S(1)}, bf16[1,1,1,1,1,1,4,128]{7,6,5,4,3,2,1,0:T(4,128)(2,1)S(1)}, u32[]{:S(2)}, u32[]{:S(2)}) %collective-permute-start.1) | collective-permute-done | bytes 1056 | tf_op jit(solution)/shard_map/ppermute | solution.py:624
  18.0 6.1 %collective-permute-done.3 = bf16[1,2,1,1,1,1,4,128]{7,6,5,4,3,2,1,0:T(4,128)(2,1)S(1)} collective-permute-done((bf16[1,2,1,1,1,1,4,128]{7,6,5,4,3,2,1,0:T(4,128)(2,1)S(1)}, bf16[1,2,1,1,1,1,4,128]{7,6,5,4,3,2,1,0:T(4,128)(2,1)S(1)}, u32[]{:S(2)}, u32[]{:S(2)}) %collective-permute-start.3) | collective-permute-done | bytes 2080 | tf_op jit(solution)/shard_map/ppermute | solution.py:624
  35.4 4.2 collective-permute-done.5
  49.7 5.8 %collective-permute-done.8 = bf16[2,2,2,2,1,1,24,768]{7,6,0,5,4,3,2,1:T(8,128)(2,1)S(1)} collective-permute-done((bf16[2,2,2,2,1,1,24,768]{7,6,0,5,4,3,2,1:T(8,128)(2,1)S(1)}, bf16[2,2,2,2,1,1,24,768]{7,6,0,5,4,3,2,1:T(8,128)(2,1)S(1)}, u32[]{:S(2)}, u32[]{:S(2)}) %collective-permute-start.8) | collective-permute-done | bytes 589856 | tf_op jit(solution)/shard_map/ppermute | solution.py:624
  62.7 3.7 collective-permute-done.13
  67.4 3.4 collective-permute-done.15
  74.3 3.6 maximum_select_fusion.1
  79.1 4.3 qkv.1
  89.6 14.6 %attend_self.1.a_ref.refs_2_ = bf16[640,768]{1,0:T(8,128)(2,1)S(1)} custom-call(bf16[640,768]{1,0:T(8,128)(2,1)S(1)} %get-tuple-element.180.q_ref, bf16[640,768]{1,0:T(8,128)(2,1)S(1)} %get-tuple-element.181.k_ref, bf16[640,768]{1,0:T(8,128)(2,1)S(1)} %get-tuple-element.182.v_ref), custom_call_target="tpu_custom_call" | custom-call | flops 629145600 | bytes 3932160 | tf_op jit(solution)/shard_map/attend_self/pallas_call | solution.py:41
  113.7 5.5 %collective-permute-done.26 = bf16[4,2,1,1,1,1,24,768]{7,6,0,5,4,3,2,1:T(8,128)(2,1)S(1)} collective-permute-done((bf16[4,2,1,1,1,1,24,768]{7,6,0,5,4,3,2,1:T(8,128)(2,1)S(1)}, bf16[4,2,1,1,1,1,24,768]{7,6,0,5,4,3,2,1:T(8,128)(2,1)S(1)}, u32[]{:S(2)}, u32[]{:S(2)}) %collective-permute-start.26) | collective-permute-done | bytes 294944 | tf_op jit(solution)/shard_map/ppermute | solution.py:624
  120.2 6.3 %collective-permute-done.24 = bf16[2,2,2,2,1,1,24,768]{7,6,0,5,4,3,2,1:T(8,128)(2,1)S(1)} collective-permute-done((bf16[2,2,2,2,1,1,24,768]{7,6,0,5,4,3,2,1:T(8,128)(2,1)S(1)}, bf16[2,2,2,2,1,1,24,768]{7,6,0,5,4,3,2,1:T(8,128)(2,1)S(1)}, u32[]{:S(2)}, u32[]{:S(2)}) %collective-permute-start.24) | collective-permute-done | bytes 589856 | tf_op jit(solution)/shard_map/ppermute | solution.py:624
  132.6 14.2 %attend_cross.1.a_ref.refs_2_ = bf16[640,768]{1,0:T(8,128)(2,1)S(1)} custom-call(bf16[640,768]{1,0:T(8,128)(2,1)S(1)} %get-tuple-element.190.q_ref, bf16[256,768]{1,0:T(8,128)(2,1)S(1)} %get-tuple-element.191.k_ref, bf16[256,768]{1,0:T(8,128)(2,1)S(1)} %get-tuple-element.192.v_ref), custom_call_target="tpu_custom_call" | custom-call | flops 251658240 | bytes 2752512 | tf_op jit(solution)/shard_map/attend_cross/pallas_call | solution.py:41
  166.9 3.6 maximum_select_fusion.5
  170.8 4.1 ffn_in.3
  176.2 4.1 ffn_in.2
  190.7 3.4 d_out.3
  213.8 3.6 maximum_select_fusion.7
  220.4 4.2 ffn_back.3
  229.3 4.2 ffn_back.2
  247.8 13.4 %late_back.1 = (f32[640,768]{1,0:T(8,128)S(1)}, bf16[640,768]{1,0:T(8,128)(2,1)S(1)}, bf16[640,768]{1,0:T(8,128)(2,1)S(1)}, f32[8,768]{1,0:T(8,128)S(1)}) custom-call(bf16[640,1536]{1,0:T(8,128)(2,1)S(1)} %copy-done.65, bf16[640,1536]{1,0:T(8,128)(2,1)S(1)} %copy-done.63, bf16[2,768,768]{2,1,0:T(8,128)(2,1)S(1)} %bitcast.89, bf16[2,768,768]{2,1,0:T(8,128)(2,1)} %bitcast.91, ...), custom_call_target="tpu_custom_call" | custom-call | flops 3774873600 | bytes 17965056 | tf_op jit(solution)/shard_map/late_back/pallas_call | solution.py:41
  265.6 13.6 %attend_cross_back.1 = (bf16[640,768]{1,0:T(8,128)(2,1)S(1)}, bf16[256,768]{1,0:T(8,128)(2,1)S(1)}, bf16[256,768]{1,0:T(8,128)(2,1)S(1)}) custom-call(bf16[640,768]{1,0:T(8,128)(2,1)S(1)} %copy-done.40, bf16[256,768]{1,0:T(8,128)(2,1)S(1)} %copy-done.67, bf16[256,768]{1,0:T(8,128)(2,1)S(1)} %copy-done.69, bf16[640,768]{1,0:T(8,128)(2,1)S(1)} %get-tuple-element.232.g_ref), custom_call_target="tpu_custom_call" | custom-call | flops 629145600 | bytes 4521984 | tf_op jit(solution)/shard_map/attend_cross_back/pallas_call | solution.py:41
  291.5 9.4 %collective-permute-done.43 = bf16[2,2,2,2,1,1,24,768]{7,6,0,5,4,3,2,1:T(8,128)(2,1)S(1)} collective-permute-done((bf16[2,2,2,2,1,1,24,768]{7,6,0,5,4,3,2,1:T(8,128)(2,1)S(1)}, bf16[2,2,2,2,1,1,24,768]{7,6,0,5,4,3,2,1:T(8,128)(2,1)S(1)}, u32[]{:S(2)}, u32[]{:S(2)}) %collective-permute-start.43) | collective-permute-done | bytes 589856 | tf_op jit(solution)/shard_map/ppermute | solution.py:624
  314.1 5.4 %mid_back.1 = (f32[640,768]{1,0:T(8,128)S(1)}, bf16[640,768]{1,0:T(8,128)(2,1)S(1)}, bf16[640,768]{1,0:T(8,128)(2,1)S(1)}, f32[8,768]{1,0:T(8,128)S(1)}) custom-call(bf16[640,768]{1,0:T(8,128)(2,1)S(1)} %copy-done.34, bf16[2,768,768]{2,1,0:T(8,128)(2,1)S(1)} %bitcast.71, f32[640,768]{1,0:T(8,128)S(1)} %copy-done.24, f32[640,768]{1,0:T(8,128)S(1)} %copy-done.58, ...), custom_call_target="tpu_custom_call" | custom-call | flops 1509949440 | bytes 13639680 | tf_op jit(solution)/shard_map/mid_back/pallas_call | solution.py:41
  330.0 16.5 %attend_self_back.1 = (bf16[640,768]{1,0:T(8,128)(2,1)S(1)}, bf16[640,768]{1,0:T(8,128)(2,1)S(1)}, bf16[640,768]{1,0:T(8,128)(2,1)S(1)}) custom-call(bf16[640,768]{1,0:T(8,128)(2,1)S(1)} %copy-done.78, bf16[640,768]{1,0:T(8,128)(2,1)S(1)} %copy-done.80, bf16[640,768]{1,0:T(8,128)(2,1)S(1)} %copy-done.82, bf16[640,768]{1,0:T(8,128)(2,1)S(1)} %get-tuple-element.252.g_ref), custom_call_target="tpu_custom_call" | custom-call | flops 1572864000 | bytes 6881280 | tf_op jit(solution)/shard_map/attend_self_back/pallas_call | solution.py:41
  368.9 5.3 %ffn_out.1 = (bf16[640,768]{1,0:T(8,128)(2,1)}, f32[8,768]{1,0:T(8,128)S(1)}) custom-call(s32[2]{0:T(128)S(1)} %copy-done.74, bf16[640,1536]{1,0:T(8,128)(2,1)S(1)} %copy-done.88, bf16[640,1536]{1,0:T(8,128)(2,1)S(1)} %copy-done.85, f32[640,768]{1,0:T(8,128)S(1)} %copy-done.61, f32[16,768]{1,0:T(8,128)S(1)} %pad.13.vec_ref, ...), custom_call_target="tpu_custom_call" | custom-call | flops 3019898880 | bytes 11673608 | tf_op jit(solution)/shard_map/ffn_out/pallas_call | solution.py:41
  377.1 7.1 %in_back.1 = (bf16[640,768]{1,0:T(8,128)(2,1)}, f32[8,768]{1,0:T(8,128)S(1)}) custom-call(bf16[640,768]{1,0:T(8,128)(2,1)S(1)} %copy-done.28, bf16[640,768]{1,0:T(8,128)(2,1)S(1)} %copy-done.30, bf16[640,768]{1,0:T(8,128)(2,1)S(1)} %copy-done.32, bf16[2,768,768]{2,1,0:T(8,128)(2,1)S(1)} %bitcast.78, bf16[2,768,768]{2,1,0:T(8,128)(2,1)S(1)} %bitcast.79, ...), custom_call_target="tpu_custom_call" | custom-call | flops 2264924160 | bytes 14032896 | tf_op jit(solution)/shard_map/in_back/pallas_call | solution.py:41
  398.7 9.2 %collective-permute-done.60 = bf16[2,2,2,2,1,1,24,768]{7,6,5,4,3,2,1,0:T(8,128)(2,1)} collective-permute-done((bf16[2,2,2,2,1,1,24,768]{7,6,5,4,3,2,1,0:T(8,128)(2,1)}, bf16[2,2,2,2,1,1,24,768]{7,6,5,4,3,2,1,0:T(8,128)(2,1)}, u32[]{:S(2)}, u32[]{:S(2)}) %collective-permute-start.60) | collective-permute-done | bytes 589856 | tf_op jit(solution)/shard_map/ppermute | solution.py:624
  414.0 5.5 %collective-permute-done.62 = bf16[2,2,2,1,1,1,24,768]{7,6,5,4,3,2,1,0:T(8,128)(2,1)S(1)} collective-permute-done((bf16[2,2,2,1,1,1,24,768]{7,6,5,4,3,2,1,0:T(8,128)(2,1)S(1)}, bf16[2,2,2,1,1,1,24,768]{7,6,5,4,3,2,1,0:T(8,128)(2,1)S(1)}, u32[]{:S(2)}, u32[]{:S(2)}) %collective-permute-start.62) | collective-permute-done | bytes 294944 | tf_op jit(solution)/shard_map/ppermute | solution.py:624
  429.9 4.0 reshape.1696
  437.5 4.8 %collective-permute-done.68 = bf16[4,1,1,1,1,1,24,768]{7,6,5,4,3,2,1,0:T(8,128)(2,1)S(1)} collective-permute-done((bf16[4,1,1,1,1,1,24,768]{7,6,5,4,3,2,1,0:T(8,128)(2,1)S(1)}, bf16[4,1,1,1,1,1,24,768]{7,6,5,4,3,2,1,0:T(8,128)(2,1)S(1)}, u32[]{:S(2)}, u32[]{:S(2)}) %collective-permute-start.68) | collective-permute-done | bytes 147488 | tf_op jit(solution)/shard_map/ppermute | solution.py:624
  442.4 3.6 collective-permute-done.72
  (571 shorter events, 246.2 us)
Async XLA Ops:
  57.0 15.0 %collective-permute-start.17 = (bf16[2,2,2,2,2,1,24,768]{7,6,0,5,4,3,2,1:T(8,128)(2,1)S(1)}, bf16[2,2,2,2,2,1,24,768]{7,6,0,5,4,3,2,1:T(8,128)(2,1)}, u32[]{:S(2)}, u32[]{:S(2)}) collective-permute-start(bf16[2,2,2,2,2,1,24,768]{7,6,0,5,4,3,2,1:T(8,128)(2,1)S(1)} %maximum_select_fusion.8), channel_id=1, source_target_pairs={{0,1},{1,0},{2,3},{3,2},{4,5},{5,4},{6,7},{7,6},{8,9},{9,8},{10,11... | collective-permute-start | bytes 3538952 | tf_op jit(solution)/shard_map/ppermute | solution.py:624
  57.0 17.3 %collective-permute-start.18 = (bf16[2,2,2,2,2,1,24,768]{7,6,0,5,4,3,2,1:T(8,128)(2,1)}, bf16[2,2,2,2,2,1,24,768]{7,6,0,5,4,3,2,1:T(8,128)(2,1)}, u32[]{:S(2)}, u32[]{:S(2)}) collective-permute-start(bf16[2,2,2,2,2,1,24,768]{7,6,0,5,4,3,2,1:T(8,128)(2,1)} %maximum_select_fusion.9), channel_id=1, source_target_pairs={{0,1},{1,0},{2,3},{3,2},{4,5},{5,4},{6,7},{7,6},{8,9},{9,8},{10,11... | collective-permute-start | bytes 3538952 | tf_op jit(solution)/shard_map/ppermute | solution.py:624
  83.4 26.1 %collective-permute-start.19 = (bf16[2,2,2,2,1,1,24,768]{7,6,0,5,4,3,2,1:T(8,128)(2,1)S(1)}, bf16[2,2,2,2,1,1,24,768]{7,6,0,5,4,3,2,1:T(8,128)(2,1)S(1)}, u32[]{:S(2)}, u32[]{:S(2)}) collective-permute-start(bf16[2,2,2,2,1,1,24,768]{7,6,0,5,4,3,2,1:T(8,128)(2,1)S(1)} %maximum_select_fusion.20), channel_id=1, source_target_pairs={{0,2},{1,3},{2,0},{3,1},{4,6},{5,7},{6,4},{7,5},{8,10},{9,11},{10,... | collective-permute-start | bytes 1769480 | tf_op jit(solution)/shard_map/ppermute | solution.py:624
  84.8 23.5 %collective-permute-start.21 = (bf16[2,2,2,1,1,1,24,768]{7,6,0,5,4,3,2,1:T(8,128)(2,1)S(1)}, bf16[2,2,2,1,1,1,24,768]{7,6,0,5,4,3,2,1:T(8,128)(2,1)S(1)}, u32[]{:S(2)}, u32[]{:S(2)}) collective-permute-start(bf16[2,2,2,1,1,1,24,768]{7,6,0,5,4,3,2,1:T(8,128)(2,1)S(1)} %get-tuple-element.177), channel_id=1, source_target_pairs={{0,4},{1,5},{2,6},{3,7},{4,0},{5,1},{6,2},{7,3},{8,12},{9,13},{10,... | collective-permute-start | bytes 884744 | tf_op jit(solution)/shard_map/ppermute | solution.py:624
  86.0 22.2 %collective-permute-start.23 = (bf16[4,1,1,1,1,1,24,768]{7,6,0,5,4,3,2,1:T(8,128)(2,1)S(1)}, bf16[4,1,1,1,1,1,24,768]{7,6,0,5,4,3,2,1:T(8,128)(2,1)S(1)}, u32[]{:S(2)}, u32[]{:S(2)}) collective-permute-start(bf16[4,1,1,1,1,1,24,768]{7,6,0,5,4,3,2,1:T(8,128)(2,1)S(1)} %bitcast.126), channel_id=1, source_target_pairs={{0,16},{1,17},{2,18},{3,19},{4,20},{5,21},{6,22},{7,23},{8,24},{9,... | collective-permute-start | bytes 442376 | tf_op jit(solution)/shard_map/ppermute | solution.py:624
  88.4 20.0 %collective-permute-start.22 = (bf16[2,2,2,1,1,1,24,768]{7,6,0,5,4,3,2,1:T(8,128)(2,1)S(1)}, bf16[2,2,2,1,1,1,24,768]{7,6,0,5,4,3,2,1:T(8,128)(2,1)S(1)}, u32[]{:S(2)}, u32[]{:S(2)}) collective-permute-start(bf16[2,2,2,1,1,1,24,768]{7,6,0,5,4,3,2,1:T(8,128)(2,1)S(1)} %get-tuple-element.178), channel_id=1, source_target_pairs={{0,2},{1,3},{2,0},{3,1},{4,6},{5,7},{6,4},{7,5},{8,10},{9,11},{10,... | collective-permute-start | bytes 884744 | tf_op jit(solution)/shard_map/ppermute | solution.py:624
  89.1 20.5 %collective-permute-start.20 = (bf16[2,2,2,1,2,1,24,768]{7,6,0,5,4,3,2,1:T(8,128)(2,1)S(1)}, bf16[2,2,2,1,2,1,24,768]{7,6,0,5,4,3,2,1:T(8,128)(2,1)S(1)}, u32[]{:S(2)}, u32[]{:S(2)}) collective-permute-start(bf16[2,2,2,1,2,1,24,768]{7,6,0,5,4,3,2,1:T(8,128)(2,1)S(1)} %maximum_select_fusion.21), channel_id=1, source_target_pairs={{0,4},{1,5},{2,6},{3,7},{4,0},{5,1},{6,2},{7,3},{8,12},{9,13},{10,... | collective-permute-start | bytes 1769480 | tf_op jit(solution)/shard_map/ppermute | solution.py:624
  109.8 19.0 %collective-permute-start.27 = (bf16[2,2,2,2,2,1,24,768]{7,6,0,5,4,3,2,1:T(8,128)(2,1)S(1)}, bf16[2,2,2,2,2,1,24,768]{7,6,0,5,4,3,2,1:T(8,128)(2,1)S(1)}, u32[]{:S(2)}, u32[]{:S(2)}) collective-permute-start(bf16[2,2,2,2,2,1,24,768]{7,6,0,5,4,3,2,1:T(8,128)(2,1)S(1)} %maximum_select_fusion.10), channel_id=1, source_target_pairs={{0,1},{1,0},{2,3},{3,2},{4,5},{5,4},{6,7},{7,6},{8,9},{9,8},{10,11... | collective-permute-start | bytes 3538952 | tf_op jit(solution)/shard_map/ppermute | solution.py:624
  110.7 18.5 %collective-permute-start.28 = (bf16[2,2,2,2,2,1,24,768]{7,6,0,5,4,3,2,1:T(8,128)(2,1)S(1)}, bf16[2,2,2,2,2,1,24,768]{7,6,0,5,4,3,2,1:T(8,128)(2,1)S(1)}, u32[]{:S(2)}, u32[]{:S(2)}) collective-permute-start(bf16[2,2,2,2,2,1,24,768]{7,6,0,5,4,3,2,1:T(8,128)(2,1)S(1)} %maximum_select_fusion.11), channel_id=1, source_target_pairs={{0,1},{1,0},{2,3},{3,2},{4,5},{5,4},{6,7},{7,6},{8,9},{9,8},{10,11... | collective-permute-start | bytes 3538952 | tf_op jit(solution)/shard_map/ppermute | solution.py:624
  110.9 15.6 %collective-permute-start.24 = (bf16[2,2,2,2,1,1,24,768]{7,6,0,5,4,3,2,1:T(8,128)(2,1)S(1)}, bf16[2,2,2,2,1,1,24,768]{7,6,0,5,4,3,2,1:T(8,128)(2,1)S(1)}, u32[]{:S(2)}, u32[]{:S(2)}) collective-permute-start(bf16[2,2,2,2,1,1,24,768]{7,6,0,5,4,3,2,1:T(8,128)(2,1)S(1)} %maximum_select_fusion.23), channel_id=1, source_target_pairs={{0,2},{1,3},{2,0},{3,1},{4,6},{5,7},{6,4},{7,5},{8,10},{9,11},{10,... | collective-permute-start | bytes 1769480 | tf_op jit(solution)/shard_map/ppermute | solution.py:624
  112.2 15.4 %collective-permute-start.25 = (bf16[2,2,2,1,2,1,24,768]{7,6,0,5,4,3,2,1:T(8,128)(2,1)S(1)}, bf16[2,2,2,1,2,1,24,768]{7,6,0,5,4,3,2,1:T(8,128)(2,1)S(1)}, u32[]{:S(2)}, u32[]{:S(2)}) collective-permute-start(bf16[2,2,2,1,2,1,24,768]{7,6,0,5,4,3,2,1:T(8,128)(2,1)S(1)} %maximum_select_fusion.24), channel_id=1, source_target_pairs={{0,4},{1,5},{2,6},{3,7},{4,0},{5,1},{6,2},{7,3},{8,12},{9,13},{10,... | collective-permute-start | bytes 1769480 | tf_op jit(solution)/shard_map/ppermute | solution.py:624
  147.8 16.0 %collective-permute-start.31 = (bf16[2,2,2,2,2,1,24,768]{7,6,0,5,4,3,2,1:T(8,128)(2,1)}, bf16[2,2,2,2,2,1,24,768]{7,6,0,5,4,3,2,1:T(8,128)(2,1)}, u32[]{:S(2)}, u32[]{:S(2)}) collective-permute-start(bf16[2,2,2,2,2,1,24,768]{7,6,0,5,4,3,2,1:T(8,128)(2,1)} %maximum_select_fusion.12), channel_id=1, source_target_pairs={{0,1},{1,0},{2,3},{3,2},{4,5},{5,4},{6,7},{7,6},{8,9},{9,8},{10,11... | collective-permute-start | bytes 3538952 | tf_op jit(solution)/shard_map/ppermute | solution.py:624
  147.8 19.1 %collective-permute-start.32 = (bf16[2,2,2,2,2,1,24,768]{7,6,0,5,4,3,2,1:T(8,128)(2,1)}, bf16[2,2,2,2,2,1,24,768]{7,6,0,5,4,3,2,1:T(8,128)(2,1)}, u32[]{:S(2)}, u32[]{:S(2)}) collective-permute-start(bf16[2,2,2,2,2,1,24,768]{7,6,0,5,4,3,2,1:T(8,128)(2,1)} %maximum_select_fusion.13), channel_id=1, source_target_pairs={{0,1},{1,0},{2,3},{3,2},{4,5},{5,4},{6,7},{7,6},{8,9},{9,8},{10,11... | collective-permute-start | bytes 3538952 | tf_op jit(solution)/shard_map/ppermute | solution.py:624
  182.8 15.0 %collective-permute-start.33 = (bf16[2,2,2,2,1,1,24,768]{7,6,0,5,4,3,2,1:T(8,128)(2,1)}, bf16[2,2,2,2,1,1,24,768]{7,6,0,5,4,3,2,1:T(8,128)(2,1)}, u32[]{:S(2)}, u32[]{:S(2)}) collective-permute-start(bf16[2,2,2,2,1,1,24,768]{7,6,0,5,4,3,2,1:T(8,128)(2,1)} %maximum_select_fusion.26), channel_id=1, source_target_pairs={{0,2},{1,3},{2,0},{3,1},{4,6},{5,7},{6,4},{7,5},{8,10},{9,11},{10,... | collective-permute-start | bytes 1769480 | tf_op jit(solution)/shard_map/ppermute | solution.py:624
  184.7 16.2 %collective-permute-start.34 = (bf16[2,2,2,1,2,1,24,768]{7,6,0,5,4,3,2,1:T(8,128)(2,1)}, bf16[2,2,2,1,2,1,24,768]{7,6,0,5,4,3,2,1:T(8,128)(2,1)S(1)}, u32[]{:S(2)}, u32[]{:S(2)}) collective-permute-start(bf16[2,2,2,1,2,1,24,768]{7,6,0,5,4,3,2,1:T(8,128)(2,1)} %maximum_select_fusion.27), channel_id=1, source_target_pairs={{0,4},{1,5},{2,6},{3,7},{4,0},{5,1},{6,2},{7,3},{8,12},{9,13},{10,... | collective-permute-start | bytes 1769480 | tf_op jit(solution)/shard_map/ppermute | solution.py:624
  237.2 24.3 %collective-permute-start.39 = (bf16[2,2,2,2,2,1,24,768]{7,6,0,5,4,3,2,1:T(8,128)(2,1)}, bf16[2,2,2,2,2,1,24,768]{7,6,0,5,4,3,2,1:T(8,128)(2,1)}, u32[]{:S(2)}, u32[]{:S(2)}) collective-permute-start(bf16[2,2,2,2,2,1,24,768]{7,6,0,5,4,3,2,1:T(8,128)(2,1)} %copy.109), channel_id=1, source_target_pairs={{0,1},{1,0},{2,3},{3,2},{4,5},{5,4},{6,7},{7,6},{8,9},{9,8},{10,11... | collective-permute-start | bytes 3538952 | tf_op jit(solution)/shard_map/ppermute | solution.py:624
  237.4 26.1 %collective-permute-start.40 = (bf16[2,2,2,2,2,1,24,768]{7,6,0,5,4,3,2,1:T(8,128)(2,1)}, bf16[2,2,2,2,2,1,24,768]{7,6,0,5,4,3,2,1:T(8,128)(2,1)}, u32[]{:S(2)}, u32[]{:S(2)}) collective-permute-start(bf16[2,2,2,2,2,1,24,768]{7,6,0,5,4,3,2,1:T(8,128)(2,1)} %copy.110), channel_id=1, source_target_pairs={{0,1},{1,0},{2,3},{3,2},{4,5},{5,4},{6,7},{7,6},{8,9},{9,8},{10,11... | collective-permute-start | bytes 3538952 | tf_op jit(solution)/shard_map/ppermute | solution.py:624
  237.7 23.5 %collective-permute-start.41 = (bf16[2,2,2,2,1,1,24,768]{7,6,5,4,3,2,1,0:T(8,128)(2,1)}, bf16[2,2,2,2,1,1,24,768]{7,6,5,4,3,2,1,0:T(8,128)(2,1)S(1)}, u32[]{:S(2)}, u32[]{:S(2)}) collective-permute-start(bf16[2,2,2,2,1,1,24,768]{7,6,5,4,3,2,1,0:T(8,128)(2,1)} %get-tuple-element.227), channel_id=1, source_target_pairs={{0,2},{1,3},{2,0},{3,1},{4,6},{5,7},{6,4},{7,5},{8,10},{9,11},{10,... | collective-permute-start | bytes 1769480 | tf_op jit(solution)/shard_map/ppermute | solution.py:624
  238.5 22.9 %collective-permute-start.42 = (bf16[2,2,2,1,2,1,24,768]{7,6,5,4,3,2,1,0:T(8,128)(2,1)}, bf16[2,2,2,1,2,1,24,768]{7,6,5,4,3,2,1,0:T(8,128)(2,1)S(1)}, u32[]{:S(2)}, u32[]{:S(2)}) collective-permute-start(bf16[2,2,2,1,2,1,24,768]{7,6,5,4,3,2,1,0:T(8,128)(2,1)} %get-tuple-element.228), channel_id=1, source_target_pairs={{0,4},{1,5},{2,6},{3,7},{4,0},{5,1},{6,2},{7,3},{8,12},{9,13},{10,... | collective-permute-start | bytes 1769480 | tf_op jit(solution)/shard_map/ppermute | solution.py:624
  281.4 19.6 %collective-permute-start.43 = (bf16[2,2,2,2,1,1,24,768]{7,6,0,5,4,3,2,1:T(8,128)(2,1)S(1)}, bf16[2,2,2,2,1,1,24,768]{7,6,0,5,4,3,2,1:T(8,128)(2,1)S(1)}, u32[]{:S(2)}, u32[]{:S(2)}) collective-permute-start(bf16[2,2,2,2,1,1,24,768]{7,6,0,5,4,3,2,1:T(8,128)(2,1)S(1)} %get-tuple-element.237), channel_id=1, source_target_pairs={{0,2},{1,3},{2,0},{3,1},{4,6},{5,7},{6,4},{7,5},{8,10},{9,11},{10,... | collective-permute-start | bytes 1769480 | tf_op jit(solution)/shard_map/ppermute | solution.py:624
  282.1 19.8 %collective-permute-start.44 = (bf16[2,2,2,1,2,1,24,768]{7,6,0,5,4,3,2,1:T(8,128)(2,1)S(1)}, bf16[2,2,2,1,2,1,24,768]{7,6,0,5,4,3,2,1:T(8,128)(2,1)S(1)}, u32[]{:S(2)}, u32[]{:S(2)}) collective-permute-start(bf16[2,2,2,1,2,1,24,768]{7,6,0,5,4,3,2,1:T(8,128)(2,1)S(1)} %get-tuple-element.238), channel_id=1, source_target_pairs={{0,4},{1,5},{2,6},{3,7},{4,0},{5,1},{6,2},{7,3},{8,12},{9,13},{10,... | collective-permute-start | bytes 1769480 | tf_op jit(solution)/shard_map/ppermute | solution.py:624
  302.8 20.3 %collective-permute-start.47 = (bf16[2,2,2,2,2,1,24,768]{7,6,5,4,3,2,1,0:T(8,128)(2,1)}, bf16[2,2,2,2,2,1,24,768]{7,6,5,4,3,2,1,0:T(8,128)(2,1)}, u32[]{:S(2)}, u32[]{:S(2)}) collective-permute-start(bf16[2,2,2,2,2,1,24,768]{7,6,5,4,3,2,1,0:T(8,128)(2,1)} %constant_dynamic-slice_fusion.20), channel_id=1, source_target_pairs={{0,1},{1,0},{2,3},{3,2},{4,5},{5,4},{6,7},{7,6},{8,9},{9,8},{10,11... | collective-permute-start | bytes 3538952 | tf_op jit(solution)/shard_map/ppermute | solution.py:624
  302.8 22.4 %collective-permute-start.48 = (bf16[2,2,2,2,2,1,24,768]{7,6,5,4,3,2,1,0:T(8,128)(2,1)}, bf16[2,2,2,2,2,1,24,768]{7,6,5,4,3,2,1,0:T(8,128)(2,1)}, u32[]{:S(2)}, u32[]{:S(2)}) collective-permute-start(bf16[2,2,2,2,2,1,24,768]{7,6,5,4,3,2,1,0:T(8,128)(2,1)} %constant_dynamic-slice_fusion.19), channel_id=1, source_target_pairs={{0,1},{1,0},{2,3},{3,2},{4,5},{5,4},{6,7},{7,6},{8,9},{9,8},{10,11... | collective-permute-start | bytes 3538952 | tf_op jit(solution)/shard_map/ppermute | solution.py:624
  303.3 16.2 %collective-permute-start.51 = (bf16[4,2,1,1,1,1,24,768]{7,6,5,4,3,2,1,0:T(8,128)(2,1)}, bf16[4,2,1,1,1,1,24,768]{7,6,5,4,3,2,1,0:T(8,128)(2,1)}, u32[]{:S(2)}, u32[]{:S(2)}) collective-permute-start(bf16[4,2,1,1,1,1,24,768]{7,6,5,4,3,2,1,0:T(8,128)(2,1)} %fusion.3), channel_id=1, source_target_pairs={{0,8},{1,9},{2,10},{3,11},{4,12},{5,13},{6,14},{7,15},{8,0},{9,1},... | collective-permute-start | bytes 884744 | tf_op jit(solution)/shard_map/ppermute | solution.py:624
  304.5 17.1 %collective-permute-start.49 = (bf16[2,2,2,1,1,1,24,768]{7,6,0,5,4,3,2,1:T(8,128)(2,1)}, bf16[2,2,2,1,1,1,24,768]{7,6,0,5,4,3,2,1:T(8,128)(2,1)}, u32[]{:S(2)}, u32[]{:S(2)}) collective-permute-start(bf16[2,2,2,1,1,1,24,768]{7,6,0,5,4,3,2,1:T(8,128)(2,1)} %add_convert_fusion.37), channel_id=1, source_target_pairs={{0,4},{1,5},{2,6},{3,7},{4,0},{5,1},{6,2},{7,3},{8,12},{9,13},{10,... | collective-permute-start | bytes 884744 | tf_op jit(solution)/shard_map/ppermute | solution.py:624
  305.7 17.2 %collective-permute-start.50 = (bf16[2,2,2,1,1,1,24,768]{7,6,0,5,4,3,2,1:T(8,128)(2,1)}, bf16[2,2,2,1,1,1,24,768]{7,6,0,5,4,3,2,1:T(8,128)(2,1)S(1)}, u32[]{:S(2)}, u32[]{:S(2)}) collective-permute-start(bf16[2,2,2,1,1,1,24,768]{7,6,0,5,4,3,2,1:T(8,128)(2,1)} %add_convert_fusion.36), channel_id=1, source_target_pairs={{0,2},{1,3},{2,0},{3,1},{4,6},{5,7},{6,4},{7,5},{8,10},{9,11},{10,... | collective-permute-start | bytes 884744 | tf_op jit(solution)/shard_map/ppermute | solution.py:624
  327.0 20.3 %collective-permute-start.52 = (bf16[2,2,2,2,1,1,24,768]{7,6,5,4,3,2,1,0:T(8,128)(2,1)S(1)}, bf16[2,2,2,2,1,1,24,768]{7,6,5,4,3,2,1,0:T(8,128)(2,1)S(1)}, u32[]{:S(2)}, u32[]{:S(2)}) collective-permute-start(bf16[2,2,2,2,1,1,24,768]{7,6,5,4,3,2,1,0:T(8,128)(2,1)S(1)} %get-tuple-element.249), channel_id=1, source_target_pairs={{0,2},{1,3},{2,0},{3,1},{4,6},{5,7},{6,4},{7,5},{8,10},{9,11},{10,... | collective-permute-start | bytes 1769480 | tf_op jit(solution)/shard_map/ppermute | solution.py:624
  328.4 19.0 %collective-permute-start.53 = (bf16[2,2,2,1,2,1,24,768]{7,6,5,4,3,2,1,0:T(8,128)(2,1)S(1)}, bf16[2,2,2,1,2,1,24,768]{7,6,5,4,3,2,1,0:T(8,128)(2,1)S(1)}, u32[]{:S(2)}, u32[]{:S(2)}) collective-permute-start(bf16[2,2,2,1,2,1,24,768]{7,6,5,4,3,2,1,0:T(8,128)(2,1)S(1)} %get-tuple-element.250), channel_id=1, source_target_pairs={{0,4},{1,5},{2,6},{3,7},{4,0},{5,1},{6,2},{7,3},{8,12},{9,13},{10,... | collective-permute-start | bytes 1769480 | tf_op jit(solution)/shard_map/ppermute | solution.py:624
  329.2 17.4 %collective-permute-start.54 = (bf16[4,2,1,1,1,1,24,768]{7,6,0,5,4,3,2,1:T(8,128)(2,1)S(1)}, bf16[4,2,1,1,1,1,24,768]{7,6,0,5,4,3,2,1:T(8,128)(2,1)S(1)}, u32[]{:S(2)}, u32[]{:S(2)}) collective-permute-start(bf16[4,2,1,1,1,1,24,768]{7,6,0,5,4,3,2,1:T(8,128)(2,1)S(1)} %fusion.2), channel_id=1, source_target_pairs={{0,8},{1,9},{2,10},{3,11},{4,12},{5,13},{6,14},{7,15},{8,0},{9,1},... | collective-permute-start | bytes 884744 | tf_op jit(solution)/shard_map/ppermute | solution.py:624
  358.4 29.4 %collective-permute-start.57 = (bf16[2,2,2,2,2,1,24,768]{7,6,5,4,3,2,1,0:T(8,128)(2,1)}, bf16[2,2,2,2,2,1,24,768]{7,6,5,4,3,2,1,0:T(8,128)(2,1)}, u32[]{:S(2)}, u32[]{:S(2)}) collective-permute-start(bf16[2,2,2,2,2,1,24,768]{7,6,5,4,3,2,1,0:T(8,128)(2,1)} %get-tuple-element.267), channel_id=1, source_target_pairs={{0,1},{1,0},{2,3},{3,2},{4,5},{5,4},{6,7},{7,6},{8,9},{9,8},{10,11... | collective-permute-start | bytes 3538952 | tf_op jit(solution)/shard_map/ppermute | solution.py:624
  360.1 30.5 %collective-permute-start.58 = (bf16[2,2,2,2,2,1,24,768]{7,6,5,4,3,2,1,0:T(8,128)(2,1)}, bf16[2,2,2,2,2,1,24,768]{7,6,5,4,3,2,1,0:T(8,128)(2,1)}, u32[]{:S(2)}, u32[]{:S(2)}) collective-permute-start(bf16[2,2,2,2,2,1,24,768]{7,6,5,4,3,2,1,0:T(8,128)(2,1)} %get-tuple-element.268), channel_id=1, source_target_pairs={{0,1},{1,0},{2,3},{3,2},{4,5},{5,4},{6,7},{7,6},{8,9},{9,8},{10,11... | collective-permute-start | bytes 3538952 | tf_op jit(solution)/shard_map/ppermute | solution.py:624
  376.3 35.2 %collective-permute-start.70 = (bf16[4,1,1,1,1,1,24,768]{7,6,5,4,3,2,1,0:T(8,128)(2,1)}, bf16[4,1,1,1,1,1,24,768]{7,6,5,4,3,2,1,0:T(8,128)(2,1)S(1)}, u32[]{:S(2)}, u32[]{:S(2)}) collective-permute-start(bf16[4,1,1,1,1,1,24,768]{7,6,5,4,3,2,1,0:T(8,128)(2,1)} %add_convert_fusion.47), channel_id=1, source_target_pairs={{0,16},{1,17},{2,18},{3,19},{4,20},{5,21},{6,22},{7,23},{8,24},{9,... | collective-permute-start | bytes 442376 | tf_op jit(solution)/shard_map/ppermute | solution.py:624
  (175 other events, 1273.9 us)

commit v3 on v2

--- a/solution.py
+++ b/solution.py
@@ -35,7 +35,7 @@
     return pl.BlockSpec(block, index)
 
 
-def run(body, name, grid, operands, in_specs, outs, scratch=(), flops=0, exps=0, limit=40):
+def run(body, name, grid, operands, in_specs, outs, scratch=(), flops=0, exps=0, limit=20):
     moved = sum(o.size * o.dtype.itemsize for o in operands)
     moved += sum(math.prod(s) * jnp.dtype(d).itemsize for s, d, _ in outs)
     return pl.pallas_call(
@@ -124,41 +124,70 @@
     return jnp.where(inside, values, jnp.zeros_like(values))
 
 
-def attend_body(causal, pairs, step_rows, q_ref, k_ref, v_ref, o_ref):
-    length = q_ref.shape[0]
-    frames = k_ref.shape[0]
+def attend_cross_body(pairs, q_ref, k_ref, v_ref, o_ref):
     for pair in range(pairs):
         lanes = slice(pair * PAIR, (pair + 1) * PAIR)
-        values = v_ref[:, lanes]
-        by_head = [head_lanes(values, head) for head in (0, 1)]
-        for start in range(0, length, step_rows):
+        values, keys, queries = v_ref[:, lanes], k_ref[:, lanes], q_ref[:, lanes]
+        total = None
+        for head in (0, 1):
+            scores = dot_nt(head_lanes(queries, head), keys)
+            exps = jnp.exp(scores - jnp.max(scores, -1, keepdims=True))
+            probs = exps * (1.0 / jnp.sum(exps, -1, keepdims=True))
+            part = dot_nn(probs.astype(LOW), head_lanes(values, head))
+            total = part if total is None else total + part
+        o_ref[:, lanes] = total.astype(LOW)
+
+
+def attend_body(pairs, step_rows, q_ref, k_ref, v_ref, o_ref):
+    length = q_ref.shape[0]
+    starts = list(range(0, length, step_rows))
+    for pair in range(pairs):
+        lanes = slice(pair * PAIR, (pair + 1) * PAIR)
+        turned = v_ref[:, lanes].T
+        keys = [head_lanes(k_ref[:, lanes], head) for head in (0, 1)]
+        work = []
+        for start in starts:
             stop = min(start + step_rows, length)
-            seen = stop if causal else frames
-            keys = k_ref[0:seen, lanes]
             queries = q_ref[start:stop, lanes]
-            total = None
+            cuts = ([(0, start)] if start else []) + [(start, stop)]
             for head in (0, 1):
-                scores = dot_nt(head_lanes(queries, head), keys)
-                if causal:
-                    shape = scores.shape
-                    key_at = lax.broadcasted_iota(jnp.int32, shape, 1)
-                    query_at = lax.broadcasted_iota(jnp.int32, shape, 0) + start
-                    scores = jnp.where(key_at <= query_at, scores, -1e30)
-                top = jnp.max(scores, -1, keepdims=True)
-                exps = jnp.exp(scores - top)
-                probs = exps * (1.0 / jnp.sum(exps, -1, keepdims=True))
-                part = dot_nn(probs.astype(LOW), by_head[head][0:seen])
-                total = part if total is None else total + part
-            o_ref[start:stop, lanes] = total.astype(LOW)
-
-
-def attend(q, k, v, batch, causal, pairs=2, step_rows=128):
+                parts = []
+                for low, high in cuts:
+                    scores = dot_nt(keys[head][low:high], queries)
+                    if low == start:
+                        key_at = lax.broadcasted_iota(jnp.int32, scores.shape, 0)
+                        query_at = lax.broadcasted_iota(jnp.int32, scores.shape, 1)
+                        scores = jnp.where(key_at <= query_at, scores, -1e30)
+                    parts.append(scores)
+                work.append((start, stop, head, cuts, parts))
+        tops = []
+        for start, stop, head, cuts, parts in work:
+            top = jnp.max(parts[0], 0, keepdims=True)
+            for scores in parts[1:]:
+                top = jnp.maximum(top, jnp.max(scores, 0, keepdims=True))
+            tops.append(top)
+        exps = [[jnp.exp(s - top) for s in item[4]] for item, top in zip(work, tops)]
+        totals = [sum(jnp.sum(e, 0, keepdims=True) for e in group) for group in exps]
+        outs = []
+        for (start, stop, head, cuts, _), group, total in zip(work, exps, totals):
+            out = None
+            for (low, high), e in zip(cuts, group):
+                part = dot_nn(turned[head * HALF_PAIR : (head + 1) * HALF_PAIR, low:high], e.astype(LOW))
+                out = part if out is None else out + part
+            outs.append(out * (1.0 / total))
+        for place, start in enumerate(starts):
+            stop = min(start + step_rows, length)
+            both = jnp.concatenate(outs[2 * place : 2 * place + 2], 0)
+            o_ref[start:stop, lanes] = both.T.astype(LOW)
+
+
+def attend(q, k, v, batch, causal, pairs=6, step_rows=128):
     rows, width = q.shape
     length, frames = rows // batch, k.shape[0] // batch
     lanes = pairs * PAIR
     at = lambda b, p: (b, p)
     return run(
-        functools.partial(attend_body, causal, pairs, step_rows),
+        functools.partial(attend_body, pairs, step_rows) if causal else functools.partial(attend_cross_body, pairs),
         "attend_self" if causal else "attend_cross",
         (batch, width // lanes),
         (q, k, v),
@@ -172,63 +201,70 @@
 def attend_back_body(causal, pairs, step_rows, q_ref, k_ref, v_ref, g_ref, gq_ref, gk_ref, gv_ref, dk, dv):
     length = q_ref.shape[0]
     frames = k_ref.shape[0]
+    starts = list(range(0, length, step_rows))
     for pair in range(pairs):
         lanes = slice(pair * PAIR, (pair + 1) * PAIR)
-        for start in range(0, length, step_rows):
+        keys = [head_lanes(k_ref[:, lanes], head) for head in (0, 1)]
+        values = [head_lanes(v_ref[:, lanes], head) for head in (0, 1)]
+        work = []
+        for start in starts:
             stop = min(start + step_rows, length)
-            seen = stop if causal else frames
-            keys = k_ref[0:seen, lanes]
-            values = v_ref[0:seen, lanes]
-            queries = q_ref[start:stop, lanes]
-            grads = g_ref[start:stop, lanes]
-            grad_q = grad_k = grad_v = None
+            cuts = ([(0, start)] if start else []) + [(start, stop)] if causal else [(0, frames)]
             for head in (0, 1):
-                head_keys = head_lanes(keys, head)
-                scores = dot_nt(head_keys, queries)
-                if causal:
-                    shape = scores.shape
-                    key_at = lax.broadcasted_iota(jnp.int32, shape, 0)
-                    query_at = lax.broadcasted_iota(jnp.int32, shape, 1) + start
-                    scores = jnp.where(key_at <= query_at, scores, -1e30)
-                top = jnp.max(scores, 0, keepdims=True)
-                exps = jnp.exp(scores - top)
-                probs = exps * (1.0 / jnp.sum(exps, 0, keepdims=True))
-                grad_probs = dot_nt(head_lanes(values, head), grads)
-                weighted = probs * grad_probs
-                inner = jnp.sum(weighted, 0, keepdims=True)
-                grad_scores = (weighted - probs * inner).astype(LOW)
-                part_v = dot_nn(probs.astype(LOW), head_lanes(grads, head))
-                part_k = dot_nn(grad_scores, head_lanes(queries, head))
-                part_q = dot_tn(grad_scores, head_keys)
-                grad_v = part_v if grad_v is None else grad_v + part_v
-                grad_k = part_k if grad_k is None else grad_k + part_k
-                grad_q = part_q if grad_q is None else grad_q + part_q
-            gq_ref[start:stop, lanes] = (grad_q * SCALE).astype(LOW)
-            if causal:
-                old = 0 if start == 0 else start
-                if old:
-                    dk[0:old, :] += grad_k[0:old]
-                    dv[0:old, :] += grad_v[0:old]
-                dk[old:seen, :] = grad_k[old:]
-                dv[old:seen, :] = grad_v[old:]
-            elif start == 0:
-                dk[...] = grad_k
-                dv[...] = grad_v
-            else:
-                dk[...] += grad_k
-                dv[...] += grad_v
+                queries, grads = q_ref[start:stop, lanes], g_ref[start:stop, lanes]
+                parts = []
+                for low, high in cuts:
+                    scores = dot_nt(keys[head][low:high], queries)
+                    if causal and low == start:
+                        key_at = lax.broadcasted_iota(jnp.int32, scores.shape, 0)
+                        query_at = lax.broadcasted_iota(jnp.int32, scores.shape, 1)
+                        scores = jnp.where(key_at <= query_at, scores, -1e30)
+                    parts.append(scores)
+                grad_parts = [dot_nt(values[head][low:high], grads) for low, high in cuts]
+                work.append((start, stop, head, cuts, parts, grad_parts))
+        probs = []
+        for item in work:
+            parts = item[4]
+            top = jnp.max(parts[0], 0, keepdims=True)
+            for scores in parts[1:]:
+                top = jnp.maximum(top, jnp.max(scores, 0, keepdims=True))
+            exps = [jnp.exp(scores - top) for scores in parts]
+            total = 1.0 / sum(jnp.sum(e, 0, keepdims=True) for e in exps)
+            probs.append([e * total for e in exps])
+        scores = []
+        for item, group in zip(work, probs):
+            weighted = [p * g for p, g in zip(group, item[5])]
+            inner = sum(jnp.sum(w, 0, keepdims=True) for w in weighted)
+            scores.append([(w - p * inner).astype(LOW) for w, p in zip(weighted, group)])
+        grad_q = {}
+        for (start, stop, head, cuts, _, _), group, low_scores in zip(work, probs, scores):
+            queries = head_lanes(q_ref[start:stop, lanes], head)
+            grads = head_lanes(g_ref[start:stop, lanes], head)
+            for (low, high), p, s in zip(cuts, group, low_scores):
+                part_v = dot_nn(p.astype(LOW), grads)
+                part_k = dot_nn(s, queries)
+                part_q = dot_tn(s, keys[head][low:high])
+                grad_q[start] = part_q if start not in grad_q else grad_q[start] + part_q
+                if head == 0 and (low == start or not causal and start == 0):
+                    dv[low:high, :] = part_v
+                    dk[low:high, :] = part_k
+                else:
+                    dv[low:high, :] += part_v
+                    dk[low:high, :] += part_k
+        for start, total in grad_q.items():
+            gq_ref[start : start + total.shape[0], lanes] = (total * SCALE).astype(LOW)
         gk_ref[:, lanes] = dk[...].astype(LOW)
         gv_ref[:, lanes] = dv[...].astype(LOW)
 
 
-def attend_back(q, k, v, grad, batch, causal, pairs=2, step_rows=128):
+def attend_back(q, k, v, grad, batch, causal, pairs=6):
     rows, width = q.shape
     length, frames = rows // batch, k.shape[0] // batch
     lanes = pairs * PAIR
     at = lambda b, p: (b, p)
     long, short = spec((length, lanes), at), spec((frames, lanes), at)
     return run(
-        functools.partial(attend_back_body, causal, pairs, step_rows),
+        functools.partial(attend_back_body, causal, pairs, 128 if causal else length),
         "attend_self_back" if causal else "attend_cross_back",
         (batch, width // lanes),
         (q, k, v, grad),
@@ -326,127 +362,106 @@
     )
 
 
-def ffn_in_body(n_ref, b_ref, w_ref, h_ref, d_ref):
-    pre = dot_nn(n_ref[...], w_ref[0]) + b_ref[0]
-    below = 0.5 + 0.5 * lax.erf(pre * (0.5**0.5))
-    density = jnp.exp(-0.5 * pre * pre) * (1.0 / math.sqrt(2.0 * math.pi))
-    h_ref[...] = (pre * below).astype(LOW)
-    d_ref[...] = (below + pre * density).astype(LOW)
-
-
-def ffn_in(norm, bias, weight, block):
+def ffn_body(first, last, batch, block, len_ref, n_ref, g_ref, b_ref, wi_ref, wo_ref, *refs):
+    refs = list(refs)
+    before = [] if first else [refs.pop(0), refs.pop(0)]
+    late_ref, vec_ref = (refs.pop(0), refs.pop(0)) if last else (None, None)
+    gn_ref, di_ref, do_ref, sf_ref, f_ref = refs[:5]
+    rest = refs[5:]
+    s_ref = rest.pop(0) if last else None
+    hidden_ref, pre_ref = rest[:2]
+    acc_ref = rest[2] if last else f_ref
+    step = pl.program_id(0)
+    rows = n_ref.shape[0]
+
+    @pl.when(step == 0)
+    def _():
+        if first:
+            acc_ref[...] = jnp.zeros_like(acc_ref)
+            gn_ref[...] = jnp.zeros_like(gn_ref)
+        else:
+            acc_ref[...] = before[0][...]
+            gn_ref[...] = before[1][...]
+
+    def chunk(place, carry):
+        at = pl.ds(pl.multiple_of(place * block, block), block)
+        pre = dot_nn(n_ref[at, :], wi_ref[0]) + b_ref[0]
+        below = 0.5 + 0.5 * lax.erf(pre * (0.5**0.5))
+        density = jnp.exp(-0.5 * pre * pre) * (1.0 / math.sqrt(2.0 * math.pi))
+        hidden = (pre * below).astype(LOW)
+        hidden_ref[at, :] = hidden
+        acc_ref[at, :] += dot_nn(hidden, wo_ref[0])
+        grad = dot_nt(g_ref[at, :], wo_ref[0])
+        grad = (grad * (below + pre * density)).astype(LOW)
+        pre_ref[at, :] = grad
+        gn_ref[at, :] += dot_nt(grad, wi_ref[0])
+        return carry
+
+    lax.fori_loop(0, rows // block, chunk, 0)
+    sf_ref[0] = col_sum(pre_ref[...])
+    di_ref[0] = dot_tn(n_ref[...], pre_ref[...]).astype(LOW)
+    do_ref[0] = dot_tn(hidden_ref[...], g_ref[...]).astype(LOW)
+    if last:
+        @pl.when(step == pl.num_programs(0) - 1)
+        def _():
+            s_ref[...] = jnp.zeros_like(s_ref)
+
+            def finish(place, carry):
+                at = pl.ds(pl.multiple_of(place * block, block), block)
+                branch = acc_ref[at, :] + vec_ref[9:10, :]
+                result = late_ref[at, :] + branch
+                f_ref[at, :] = result.astype(LOW)
+                per_seq = rows // batch // block
+                s_ref[0:1, :] += masked_squares(result, len_ref, place, per_seq)
+                s_ref[1:2, :] += masked_squares(branch, len_ref, place, per_seq)
+                s_ref[2:3, :] += col_sum(g_ref[at, :])
+                return carry
+
+            lax.fori_loop(0, rows // block, finish, 0)
+
+
+def ffn_stage(lengths, norm, grad, bias, w_in, w_out, before, late, vec, batch, block):
     rows, width = norm.shape
-    mats = weight.shape[0]
-    tile = spec((block, width), lambda j, i: (i, j))
-    return run(
-        ffn_in_body,
-        "ffn_in",
-        (mats, rows // block),
-        (norm, bias, weight),
-        [
-            spec((block, width), lambda j, i: (i, 0)),
-            spec((1, 1, width), lambda j, i: (j, 0, 0)),
-            spec((1, width, width), lambda j, i: (j, 0, 0)),
-        ],
-        [((rows, mats * width), LOW, tile)] * 2,
-        flops=2 * rows * width * width * mats,
+    mats = w_in.shape[0]
+    first, last = before is None, late is not None
+    mat = spec((1, width, width), lambda j: (j, 0, 0))
+    line = spec((1, 1, width), lambda j: (j, 0, 0))
+    operands = [lengths, norm, grad, bias, w_in, w_out]
+    specs = [smem(), whole(norm.shape), whole(grad.shape), line, mat, mat]
+    if not first:
+        operands += list(before)
+        specs += [whole((rows, width))] * 2
+    if last:
+        operands += [late, vec]
+        specs += [whole((rows, width)), whole(vec.shape)]
+    fixed = whole((rows, width))
+    outs = [
+        ((rows, width), WIDE, fixed),
+        ((mats, width, width), LOW, mat),
+        ((mats, width, width), LOW, mat),
+        ((mats, 1, width), WIDE, line),
+        ((rows, width), LOW if last else WIDE, fixed),
+    ]
+    scratch = [pltpu.VMEM((rows, width), LOW)] * 2
+    if last:
+        outs.append(((8, width), WIDE, whole((8, width))))
+        scratch.append(pltpu.VMEM((rows, width), WIDE))
+    return run(
+        functools.partial(ffn_body, first, last, batch, block),
+        "ffn_stage",
+        (mats,),
+        tuple(operands),
+        specs,
+        outs,
+        scratch,
+        flops=12 * rows * width * width * mats,
         exps=2 * rows * width * mats,
-    )
-
-
-def ffn_out_body(per_seq, len_ref, ha, hb, late_ref, vec_ref, oa, ob, r_ref, s_ref):
-    step = pl.program_id(0)
-    width = oa.shape[2]
-    branch = vec_ref[9:10, :]
-    for hidden, weight in ((ha, oa), (hb, ob)):
-        for mat in range(weight.shape[0]):
-            branch = branch + dot_nn(hidden[:, mat * width : (mat + 1) * width], weight[mat])
-    result = late_ref[...] + branch
-    r_ref[...] = result.astype(LOW)
-    sums = [masked_squares(v, len_ref, step, per_seq) for v in (result, branch)]
-    add_rows(s_ref, step == 0, sums)
-
-
-def ffn_out(lengths, ha, hb, late, vec, out_a, out_b, batch, block):
-    rows, width = late.shape
-    inner = ha.shape[1]
-    tile = spec((block, width), lambda i: (i, 0))
-    wide = spec((block, inner), lambda i: (i, 0))
-    return run(
-        functools.partial(ffn_out_body, rows // batch // block),
-        "ffn_out",
-        (rows // block,),
-        (lengths, ha, hb, late, vec, out_a, out_b),
-        [smem(), wide, wide, tile, whole(vec.shape), whole(out_a.shape), whole(out_b.shape)],
-        [((rows, width), LOW, tile), ((8, width), WIDE, spec((8, width), lambda i: (0, 0)))],
-        flops=4 * rows * inner * width,
-    )
-
-
-def d_out_body(hidden, g_ref, dw_ref, s_ref):
-    grad = g_ref[...]
-    dw_ref[0] = dot_tn(hidden[...], grad).astype(LOW)
-    add_rows(s_ref, pl.program_id(0) == 0, [])
-
-    @pl.when(pl.program_id(0) == 0)
-    def _():
-        s_ref[0:1, :] = col_sum(grad)
-
-
-def d_out(hidden, grad):
-    rows, inner = hidden.shape
-    width = grad.shape[1]
-    mats = inner // width
-    return run(
-        d_out_body,
-        "d_out",
-        (mats,),
-        (hidden, grad),
-        [spec((rows, width), lambda j: (0, j)), whole(grad.shape)],
-        [
-            ((mats, width, width), LOW, spec((1, width, width), lambda j: (j, 0, 0))),
-            ((8, width), WIDE, spec((8, width), lambda j: (0, 0))),
-        ],
-        flops=2 * rows * inner * width,
-    )
-
-
-def ffn_back_body(g_ref, d_ref, o_ref, n_ref, p_ref, dw_ref, s_ref):
-    grad = dot_nt(g_ref[...], o_ref[0])
-    pre = (grad * d_ref[...].astype(WIDE)).astype(LOW)
-    p_ref[...] = pre
-    s_ref[0] = col_sum(pre)
-    dw_ref[0] = dot_tn(n_ref[...], pre).astype(LOW)
-
-
-def ffn_back(grad, slope, weight, norm):
-    rows, inner = slope.shape
-    width = grad.shape[1]
-    mats = inner // width
-    mat = spec((1, width, width), lambda j: (j, 0, 0))
-    tile = spec((rows, width), lambda j: (0, j))
-    return run(
-        ffn_back_body,
-        "ffn_back",
-        (mats,),
-        (grad, slope, weight, norm),
-        [whole(grad.shape), tile, mat, whole(norm.shape)],
-        [
-            ((rows, inner), LOW, tile),
-            ((mats, width, width), LOW, mat),
-            ((mats, 1, width), WIDE, spec((1, 1, width), lambda j: (j, 0, 0))),
-        ],
-        flops=4 * rows * inner * width,
-    )
-
-
-def late_back_body(pa, pb, wa, wb, late_ref, og_ref, vec_ref, wo, gl_ref, gc_ref, ga_ref, s_ref):
-    width = wa.shape[1]
-    grad = None
-    for pre, weight in ((pa, wa), (pb, wb)):
-        for mat in range(weight.shape[0]):
-            part = dot_nt(pre[:, mat * width : (mat + 1) * width], weight[mat])
-            grad = part if grad is None else grad + part
+        limit=44,
+    )
+
+
+def late_back_body(gn_ref, late_ref, og_ref, vec_ref, wo, gl_ref, gc_ref, ga_ref, s_ref):
+    grad = gn_ref[...]
     through, for_gain = norm_backward(late_ref[...], grad, vec_ref[2:3, :])
     total = og_ref[...].astype(WIDE) + through
     gl_ref[...] = total
@@ -456,21 +471,16 @@
     add_rows(s_ref, pl.program_id(0) == 0, [col_sum(for_gain), col_sum(grad), col_sum(low)])
 
 
-def late_back(pa, pb, in_a, in_b, late, grad, vec, cross_a, block):
+def late_back(grad_norm, late, grad, vec, cross_a, block):
     rows, width = late.shape
-    inner = pa.shape[1]
     tile = spec((block, width), lambda i: (i, 0))
-    wide = spec((block, inner), lambda i: (i, 0))
     return run(
         late_back_body,
         "late_back",
         (rows // block,),
-        (pa, pb, in_a, in_b, late, grad, vec, cross_a),
+        (grad_norm, late, grad, vec, cross_a),
         [
-            wide,
-            wide,
-            whole(in_a.shape),
-            whole(in_b.shape),
+            tile,
             tile,
             tile,
             whole(vec.shape),
@@ -482,7 +492,7 @@
             ((rows, width), LOW, tile),
             ((8, width), WIDE, spec((8, width), lambda i: (0, 0))),
         ],
-        flops=4 * rows * inner * width + 2 * rows * width * width,
+        flops=2 * rows * width * width,
     )
 
 
@@ -766,7 +776,6 @@
     share = gains.shape[1]
     ff_share = ffn_bias.shape[0]
     mats = ff_share // share
-    middle = mats // 2
 
     small = jnp.concatenate([gains.reshape(-1), biases.reshape(-1), ffn_bias])
     small_count = small.shape[0]
@@ -778,8 +787,7 @@
     g_small = Gather(small, count, 1)
     g_self = Gather(jnp.concatenate([attn_in[0:3], attn_out[0:1]]), count)
     g_cross = Gather(jnp.concatenate([attn_in[3:4], attn_out[1:2], attn_in[4:6]]), count)
-    g_in = Gather(fc_in_mats, count)
-    g_out = Gather(fc_out_mats, count)
+    g_ffn = Gather(jnp.concatenate([fc_in_mats, fc_out_mats]), count)
 
     x = hidden_in.reshape(rows, width)
     frames = encoder_states.reshape(-1, width)
@@ -789,8 +797,8 @@
     tick([g_self, g_small])
     tick([g_self, g_small])
     tick([g_self, g_small, g_cross])
-    tick([g_self, g_small, g_cross, g_in])
-    tick([g_self, g_small, g_cross, g_in])
+    tick([g_self, g_small, g_cross, g_ffn])
+    tick([g_self, g_small, g_cross, g_ffn])
     small = g_small.result()[0].astype(jnp.float32).reshape(count, small_size)
     vec = small[:, : 13 * share].reshape(count, 13, share).transpose(1, 0, 2).reshape(13, width)
     vec = jnp.pad(vec, ((0, 3), (0, 0)))
@@ -798,63 +806,53 @@
     bias = bias.transpose(1, 0, 2).reshape(mats, 1, width)
     self_a, self_b = g_self.result()
     norm_one, query, key, value = qkv(x, vec, self_a, self_b, block)
-    query, key, value = tick([g_cross, g_in, g_out], (query, key, value))
+    query, key, value = tick([g_cross, g_ffn], (query, key, value))
     attended = attend(query, key, value, batch, True)
     mid, norm_two, square_self = mid_stage(lengths, attended, x, vec, self_b, batch, block)
-    norm_two = tick([g_cross, g_in, g_out], norm_two)
+    norm_two = tick([g_cross, g_ffn], norm_two)
     cross_a, cross_b = g_cross.result()
     cross_q, cross_k, cross_v = cross_stage(norm_two, frames, vec, cross_a, cross_b, batch)
     cross_attended = attend(cross_q, cross_k, cross_v, batch, False)
-    cross_attended = tick([g_in, g_out], cross_attended)
     late, norm_three, square_cross = late_stage(lengths, cross_attended, mid, vec, cross_a, batch, block)
-    in_a, in_b = g_in.result()
-    hidden_a, slope_a = ffn_in(norm_three, bias[:middle], in_a, block)
-    hidden_b, slope_b = ffn_in(norm_three, bias[middle:], in_b, block)
-    hidden_a, hidden_b = tick([g_out], (hidden_a, hidden_b))
-    d_out_a, sums_out = d_out(hidden_a, grad)
-    d_out_b, _ = d_out(hidden_b, grad)
-    s_out = Scatter([d_out_a, d_out_b], count)
-    grad = tick([g_out, s_out], grad)
-    out_a, out_b = g_out.result()
-    pre_a, d_in_a, sums_in_a = ffn_back(grad, slope_a, out_a, norm_three)
-    hidden_a, hidden_b, grad = tick([s_out], (hidden_a, hidden_b, grad))
-    pre_b, d_in_b, sums_in_b = ffn_back(grad, slope_b, out_b, norm_three)
-    result, square_rest = ffn_out(lengths, hidden_a, hidden_b, late, vec, out_a, out_b, batch, block)
-    s_in = Scatter([d_in_a, d_in_b], count)
-    pre_a, pre_b = tick([s_in], (pre_a, pre_b))
+    norm_three = tick([g_ffn], norm_three)
+    w_in, w_out = g_ffn.result()
+    grad_norm, d_in, d_out, sums_ff, result, square_rest = ffn_stage(
+        lengths, norm_three, grad, bias, w_in, w_out, None, late, vec, batch, block
+    )
+    s_ffn = Scatter([d_in, d_out], count)
+    grad_norm = tick([s_ffn], grad_norm)
     grad_late, grad_cross, grad_cross_att, sums_late = late_back(
-        pre_a, pre_b, in_a, in_b, late, grad, vec, cross_a, block
-    )
-    grad_cross_att = tick([s_in, s_out], grad_cross_att)
+        grad_norm, late, grad, vec, cross_a, block
+    )
+    grad_cross_att = tick([s_ffn], grad_cross_att)
     grad_cq, grad_ck, grad_cv = attend_back(
         cross_q, cross_k, cross_v, grad_cross_att, batch, False
     )
     d_cross_a = weight_grads([(norm_two, grad_cq), (cross_attended, grad_cross)], width // 3)
     d_cross_b = weight_grads([(frames, grad_ck), (frames, grad_cv)], width // 3)
     s_cross = Scatter([d_cross_a, d_cross_b], count)
-    grad_cq = tick([s_cross, s_in, s_out], grad_cq)
+    grad_cq = tick([s_cross], grad_cq)
     grad_mid, grad_self, grad_att, sums_mid = mid_back(
         grad_cq, cross_a, mid, grad_late, vec, self_b, block
     )
-    grad_att = tick([s_cross, s_in, s_out], grad_att)
+    grad_att = tick([s_cross, s_ffn], grad_att)
     grad_q, grad_k, grad_v = attend_back(query, key, value, grad_att, batch, True)
-    grad_q, grad_k, grad_v = tick([s_cross, s_in], (grad_q, grad_k, grad_v))
     d_self_a = weight_grads([(norm_one, grad_q), (norm_one, grad_k)], width // 3)
     d_self_b = weight_grads([(norm_one, grad_v), (attended, grad_self)], width // 3)
     s_self = Scatter([d_self_a, d_self_b], count)
-    grad_q, grad_k, grad_v = tick([s_self, s_cross], (grad_q, grad_k, grad_v))
+    grad_q, grad_k, grad_v = tick([s_self, s_cross, s_ffn], (grad_q, grad_k, grad_v))
     grad_in, sums_one = in_back(grad_q, grad_k, grad_v, self_a, self_b, x, grad_mid, vec, block)
-    grad_ck, grad_cv = tick([s_self, s_cross], (grad_ck, grad_cv))
+    grad_ck, grad_cv = tick([s_self, s_cross, s_ffn], (grad_ck, grad_cv))
     grad_frames, sums_frames = frames_back(grad_ck, grad_cv, cross_b, frame_rows)
 
     sum_rows = jnp.stack(
         [sums_one[0], sums_mid[0], sums_late[0]]
-        + [sums_one[2], sums_one[3], sums_mid[2], sums_mid[3], sums_frames[0], sums_late[2], sums_out[0]]
+        + [sums_one[2], sums_one[3], sums_mid[2], sums_mid[3], sums_frames[0], sums_late[2], square_rest[2]]
         + [sums_one[1], sums_mid[1], sums_late[1]]
     )
     squares = jnp.stack([square_rest[0], square_self[0], square_cross[0], square_rest[1]])
     stats = jnp.concatenate([jnp.sum(squares, -1), jnp.sum(lengths).astype(WIDE)[None]])
-    sums_ff = jnp.concatenate([sums_in_a, sums_in_b]).reshape(mats, count, share)
+    sums_ff = sums_ff.reshape(mats, count, share)
     sums = jnp.concatenate(
         [
             sum_rows.reshape(13, count, share).transpose(1, 0, 2).reshape(count, 13 * share),
@@ -865,13 +863,13 @@
     )
     sums = jnp.pad(sums, ((0, 0), (0, small_size - sums.shape[1])))
     s_small = Scatter([sums.reshape(1, count * small_rows, 128)], count)
-    tick([s_self, s_small])
+    tick([s_self, s_cross, s_small])
     tick([s_self, s_small])
     tick([s_self, s_small])
     tick([s_small])
     tick([s_small])
-    d_out_all = s_out.result()
-    d_in_all = s_in.result()
+    d_ffn = s_ffn.result()
+    d_in_all, d_out_all = d_ffn[:mats], d_ffn[mats:]
     d_cross = s_cross.result()
     d_self = s_self.result()
     small = s_small.result().reshape(-1)

time: 465 us -> 401 us (0.86)
  Pallas kernels: 137 us -> 100 us
  starting transfers between devices: 67.9 us -> 51.6 us
  waiting for transfers between devices: 93.3 us -> 108 us
  other arithmetic: 74.5 us -> 61.5 us
  local copies, waits for them, and re-layouts: 81.4 us -> 69.3 us
    pallas_call x23 -> x17, Pallas kernels: 137 us -> 100 us  [run(): pl.pallas_call(body, name=name, grid=grid, in_specs=in_specs, out_specs=[...]
    unnamed x263 -> x191, local copies, waits for them, and re-layouts: 49.1 us -> 28.6 us
    ppermute x74 -> x58, starting transfers between devices: 67.9 us -> 51.6 us  [swap(): lax.ppermute(values, 'fsdp', [(i, i ^ 1 << bit) for i in range(count)])]
    ppermute x74 -> x58, waiting for transfers between devices: 93.3 us -> 108 us  [swap(): lax.ppermute(values, 'fsdp', [(i, i ^ 1 << bit) for i in range(count)])]
    select_n x36 -> x28, other arithmetic: 33.3 us -> 22.8 us  [land(): jnp.where(own_bit(bit) == 0, jnp.concatenate([held, other], axis), jnp.co...]
    convert_element_type x20 -> x15, other arithmetic: 27.2 us -> 23.6 us  [pick(): (values[0].astype(jnp.float32) + values[1].astype(jnp.float32)).astype(se...]
    dynamic_slice x10 -> x8, local copies, waits for them, and re-layouts: 9.4 us -> 8.95 us  [pick(): lax.dynamic_slice_in_dim(v, side, 1, axis)]
  transfers between devices with their start and end apart: 74 -> 58, of which waited for: 24 -> 28; matrix products, arithmetic and copies ran while one was open for 17% -> 17% of each run, Pallas kernels for 19% -> 13%
where the time goes in v3:
time: 401 us; the launch traced here: 394 us
  waiting for transfers between devices  108 us (27%)
  Pallas kernels  100 us (25%)
  local copies, waits for them, and re-layouts  69.3 us (17%)
  other arithmetic  61.5 us (15%)
  starting transfers between devices  51.6 us (13%)
    ppermute x58, waiting for transfers between devices, swap(): lax.ppermute(values, 'fsdp', [(i, i ^ 1 << bit) for i in range(count)])  108 us
    pallas_call x17, Pallas kernels, run(): pl.pallas_call(body, name=name, grid=grid, in_specs=in_specs, out_specs=[...  100 us
    ppermute x58, starting transfers between devices, swap(): lax.ppermute(values, 'fsdp', [(i, i ^ 1 << bit) for i in range(count)])  51.6 us
    unnamed x191, local copies, waits for them, and re-layouts  28.6 us
    convert_element_type x15, other arithmetic, pick(): (values[0].astype(jnp.float32) + values[1].astype(jnp.float32)).astype(se...  23.6 us
    select_n x28, other arithmetic, land(): jnp.where(own_bit(bit) == 0, jnp.concatenate([held, other], axis), jnp.co...  22.8 us
    dynamic_slice x8, local copies, waits for them, and re-layouts, pick(): lax.dynamic_slice_in_dim(v, side, 1, axis)  8.95 us
  transfers between devices with their start and end apart: 58, of which 28 were waited for; matrix products, arithmetic and copies ran while one was open for 17% of the time, Pallas kernels for 13%

profile of v3, /device:TPU:0, one launch (start us, length us, event | category | flops | bytes accessed | tf_op | source)
XLA Modules:
  0.0 394.4 jit_solution(684863750923576646)
XLA Ops:
  4.7 4.1 %collective-permute-start = (bf16[4,1,1,1,1,1,24,768]{7,6,0,5,4,3,2,1:T(8,128)(2,1)S(1)}, bf16[4,1,1,1,1,1,24,768]{7,6,0,5,4,3,2,1:T(8,128)(2,1)S(1)}, u32[]{:S(2)}, u32[]{:S(2)}) collective-permute-start(bf16[4,1,1,1,1,1,24,768]{7,6,0,5,4,3,2,1:T(8,128)(2,1)S(1)} %maximum_bitcast_fusion.1), channel_id=1, source_target_pairs={{0,16},{1,17},{2,18},{3,19},{4,20},{5,21},{6,22},{7,23},{8,24},{9,... | collective-permute-start | bytes 442376 | tf_op jit(solution)/shard_map/ppermute | solution.py:634
  8.9 7.0 %collective-permute-done.1 = bf16[1,1,1,1,1,1,4,128]{7,6,5,4,3,2,1,0:T(4,128)(2,1)S(1)} collective-permute-done((bf16[1,1,1,1,1,1,4,128]{7,6,5,4,3,2,1,0:T(4,128)(2,1)S(1)}, bf16[1,1,1,1,1,1,4,128]{7,6,5,4,3,2,1,0:T(4,128)(2,1)S(1)}, u32[]{:S(2)}, u32[]{:S(2)}) %collective-permute-start.1) | collective-permute-done | bytes 1056 | tf_op jit(solution)/shard_map/ppermute | solution.py:634
  20.7 3.5 collective-permute-done.3
  25.7 3.3 collective-permute-start.7
  31.2 4.2 %collective-permute-done.7 = bf16[4,1,1,1,1,1,24,768]{7,6,0,5,4,3,2,1:T(8,128)(2,1)S(1)} collective-permute-done((bf16[4,1,1,1,1,1,24,768]{7,6,0,5,4,3,2,1:T(8,128)(2,1)S(1)}, bf16[4,1,1,1,1,1,24,768]{7,6,0,5,4,3,2,1:T(8,128)(2,1)S(1)}, u32[]{:S(2)}, u32[]{:S(2)}) %collective-permute-start.7) | collective-permute-done | bytes 147488 | tf_op jit(solution)/shard_map/ppermute | solution.py:634
  43.4 6.5 %collective-permute-done.11 = bf16[4,2,1,1,1,1,24,768]{7,6,0,5,4,3,2,1:T(8,128)(2,1)S(1)} collective-permute-done((bf16[4,2,1,1,1,1,24,768]{7,6,0,5,4,3,2,1:T(8,128)(2,1)S(1)}, bf16[4,2,1,1,1,1,24,768]{7,6,0,5,4,3,2,1:T(8,128)(2,1)S(1)}, u32[]{:S(2)}, u32[]{:S(2)}) %collective-permute-start.11) | collective-permute-done | bytes 294944 | tf_op jit(solution)/shard_map/ppermute | solution.py:634
  57.3 3.2 collective-permute-done.16
  79.4 4.0 %qkv.1 = (bf16[640,768]{1,0:T(8,128)(2,1)S(1)}, bf16[640,768]{1,0:T(8,128)(2,1)S(1)}, bf16[640,768]{1,0:T(8,128)(2,1)S(1)}, bf16[640,768]{1,0:T(8,128)(2,1)S(1)}) custom-call(bf16[640,768]{1,0:T(8,128)(2,1)S(1)} %bitcast.88, f32[16,768]{1,0:T(8,128)S(1)} %pad.13.vec_ref.refs_1_, bf16[2,768,768]{2,1,0:T(8,128)(2,1)S(1)} %bitcast.74, ...), custom_call_target="tpu_custom_call" | custom-call | flops 2264924160 | bytes 12042240 | tf_op jit(solution)/shard_map/qkv/pallas_call | solution.py:41
  87.5 5.4 %attend_self.1.a_ref.refs_2_ = bf16[640,768]{1,0:T(8,128)(2,1)S(1)} custom-call(bf16[640,768]{1,0:T(8,128)(2,1)S(1)} %get-tuple-element.144.q_ref, bf16[640,768]{1,0:T(8,128)(2,1)S(1)} %get-tuple-element.145.k_ref, bf16[640,768]{1,0:T(8,128)(2,1)S(1)} %get-tuple-element.146.v_ref), custom_call_target="tpu_custom_call" | custom-call | flops 629145600 | bytes 3932160 | tf_op jit(solution)/shard_map/attend_self/pallas_call | solution.py:41
  93.0 3.0 mid_stage.1
  96.0 3.6 collective-permute-done.19
  101.3 10.8 %collective-permute-done.21 = bf16[4,2,2,1,1,1,24,768]{7,6,0,5,4,3,2,1:T(8,128)(2,1)S(1)} collective-permute-done((bf16[4,2,2,1,1,1,24,768]{7,6,0,5,4,3,2,1:T(8,128)(2,1)S(1)}, bf16[4,2,2,1,1,1,24,768]{7,6,0,5,4,3,2,1:T(8,128)(2,1)S(1)}, u32[]{:S(2)}, u32[]{:S(2)}) %collective-permute-start.21) | collective-permute-done | bytes 589856 | tf_op jit(solution)/shard_map/ppermute | solution.py:634
  120.0 3.2 attend_cross.1.a_ref.refs_2_
  123.3 3.0 late_stage.1
  128.5 12.4 %collective-permute-done.23 = bf16[4,2,2,2,1,1,24,768]{7,6,0,5,4,3,2,1:T(8,128)(2,1)S(1)} collective-permute-done((bf16[4,2,2,2,1,1,24,768]{7,6,0,5,4,3,2,1:T(8,128)(2,1)S(1)}, bf16[4,2,2,2,1,1,24,768]{7,6,0,5,4,3,2,1:T(8,128)(2,1)S(1)}, u32[]{:S(2)}, u32[]{:S(2)}) %collective-permute-start.23) | collective-permute-done | bytes 1179680 | tf_op jit(solution)/shard_map/ppermute | solution.py:634
  149.8 4.8 %maximum_select_fusion = bf16[4,2,2,2,2,2,24,768]{7,6,0,5,4,3,2,1:T(8,128)(2,1)S(1)} fusion(bf16[4,2,2,2,2,1,24,768]{7,6,0,5,4,3,2,1:T(8,128)(2,1)} %collective-permute-done.27, bf16[4,2,2,2,2,1,24,768]{7,6,0,5,4,3,2,1:T(8,128)(2,1)} %maximum_select_fusion.4, pred[]{:T(512)S(6)} %eq.14), kind=kLoop, calls=%fused_computation | loop fusion | flops 7077888 | bytes 9437185 | tf_op jit(solution)/shard_map/jit(_where)/select_n | solution.py:667
  157.3 4.5 %maximum_select_fusion.1 = bf16[4,2,2,2,2,2,24,768]{7,6,0,5,4,3,2,1:T(8,128)(2,1)S(1)} fusion(bf16[4,2,2,2,2,1,24,768]{7,6,0,5,4,3,2,1:T(8,128)(2,1)} %collective-permute-done.28, bf16[4,2,2,2,2,1,24,768]{7,6,0,5,4,3,2,1:T(8,128)(2,1)} %maximum_select_fusion.5, pred[]{:T(512)S(6)} %eq.14), kind=kLoop, calls=%fused_computation.1 | loop fusion | flops 7077888 | bytes 9437185 | tf_op jit(solution)/shard_map/jit(_where)/select_n | solution.py:667
  165.2 36.1 %ffn_stage.1 = (f32[640,768]{1,0:T(8,128)S(1)}, bf16[4,768,768]{2,1,0:T(8,128)(2,1)}, bf16[4,768,768]{2,1,0:T(8,128)(2,1)}, f32[4,1,768]{2,1,0:T(1,128)S(1)}, bf...) custom-call(s32[2]{0:T(128)S(1)} %copy-done.56, bf16[640,768]{1,0:T(8,128)(2,1)S(1)} %copy-done.58, ...), custom_call_target="tpu_custom_call" | custom-call | flops 18119393280 | bytes 25853960 | tf_op jit(solution)/shard_map/ffn_stage/pallas_call | solution.py:41
  213.8 3.6 late_back.1
  220.6 3.7 add_convert_fusion.1
  224.4 3.8 add_convert_fusion
  228.2 5.4 %attend_cross_back.1 = (bf16[640,768]{1,0:T(8,128)(2,1)S(1)}, bf16[256,768]{1,0:T(8,128)(2,1)S(1)}, bf16[256,768]{1,0:T(8,128)(2,1)S(1)}) custom-call(bf16[640,768]{1,0:T(8,128)(2,1)S(1)} %copy-done.36, bf16[256,768]{1,0:T(8,128)(2,1)S(1)} %copy-done.49, bf16[256,768]{1,0:T(8,128)(2,1)S(1)} %copy-done.51, bf16[640,768]{1,0:T(8,128)(2,1)S(1)} %get-tuple-element.171.g_ref), custom_call_target="tpu_custom_call" | custom-call | flops 629145600 | bytes 4521984 | tf_op jit(solution)/shard_map/attend_cross_back/pallas_call | solution.py:41
  250.4 5.6 %mid_back.1 = (f32[640,768]{1,0:T(8,128)S(1)}, bf16[640,768]{1,0:T(8,128)(2,1)S(1)}, bf16[640,768]{1,0:T(8,128)(2,1)S(1)}, f32[8,768]{1,0:T(8,128)S(1)}) custom-call(bf16[640,768]{1,0:T(8,128)(2,1)S(1)} %copy-done.30, bf16[2,768,768]{2,1,0:T(8,128)(2,1)S(1)} %bitcast.65, f32[640,768]{1,0:T(8,128)S(1)} %copy-done.18, f32[640,768]{1,0:T(8,128)S(1)} %copy-done.42, ...), custom_call_target="tpu_custom_call" | custom-call | flops 1509949440 | bytes 13639680 | tf_op jit(solution)/shard_map/mid_back/pallas_call | solution.py:41
  256.1 10.3 %collective-permute-done.33 = bf16[4,2,2,2,1,1,24,768]{7,6,0,5,4,3,2,1:T(8,128)(2,1)} collective-permute-done((bf16[4,2,2,2,1,1,24,768]{7,6,0,5,4,3,2,1:T(8,128)(2,1)}, bf16[4,2,2,2,1,1,24,768]{7,6,0,5,4,3,2,1:T(8,128)(2,1)}, u32[]{:S(2)}, u32[]{:S(2)}) %collective-permute-start.33) | collective-permute-done | bytes 1179680 | tf_op jit(solution)/shard_map/ppermute | solution.py:634
  274.2 10.0 %attend_self_back.1 = (bf16[640,768]{1,0:T(8,128)(2,1)S(1)}, bf16[640,768]{1,0:T(8,128)(2,1)S(1)}, bf16[640,768]{1,0:T(8,128)(2,1)S(1)}) custom-call(bf16[640,768]{1,0:T(8,128)(2,1)S(1)} %copy-done.60, bf16[640,768]{1,0:T(8,128)(2,1)S(1)} %copy-done.62, bf16[640,768]{1,0:T(8,128)(2,1)S(1)} %copy-done.64, bf16[640,768]{1,0:T(8,128)(2,1)S(1)} %get-tuple-element.183.g_ref), custom_call_target="tpu_custom_call" | custom-call | flops 1572864000 | bytes 6881280 | tf_op jit(solution)/shard_map/attend_self_back/pallas_call | solution.py:41
  297.2 3.0 collective-permute-done.38
  314.4 6.9 %in_back.1 = (bf16[640,768]{1,0:T(8,128)(2,1)}, f32[8,768]{1,0:T(8,128)S(1)}) custom-call(bf16[640,768]{1,0:T(8,128)(2,1)S(1)} %copy-done.22, bf16[640,768]{1,0:T(8,128)(2,1)S(1)} %copy-done.24, bf16[640,768]{1,0:T(8,128)(2,1)S(1)} %copy-done.26, bf16[2,768,768]{2,1,0:T(8,128)(2,1)S(1)} %bitcast.76, bf16[2,768,768]{2,1,0:T(8,128)(2,1)S(1)} %bitcast.77, ...), custom_call_target="tpu_custom_call" | custom-call | flops 2264924160 | bytes 14032896 | tf_op jit(solution)/shard_map/in_back/pallas_call | solution.py:41
  336.4 10.3 %collective-permute-done.46 = bf16[4,2,1,1,1,1,24,768]{7,6,5,4,3,2,1,0:T(8,128)(2,1)S(1)} collective-permute-done((bf16[4,2,1,1,1,1,24,768]{7,6,5,4,3,2,1,0:T(8,128)(2,1)}, bf16[4,2,1,1,1,1,24,768]{7,6,5,4,3,2,1,0:T(8,128)(2,1)S(1)}, u32[]{:S(2)}, u32[]{:S(2)}) %collective-permute-start.46) | collective-permute-done | bytes 294944 | tf_op jit(solution)/shard_map/ppermute | solution.py:634
  352.3 6.8 %collective-permute-done.47 = bf16[2,2,2,1,1,1,24,768]{7,6,5,4,3,2,1,0:T(8,128)(2,1)S(1)} collective-permute-done((bf16[2,2,2,1,1,1,24,768]{7,6,5,4,3,2,1,0:T(8,128)(2,1)S(1)}, bf16[2,2,2,1,1,1,24,768]{7,6,5,4,3,2,1,0:T(8,128)(2,1)S(1)}, u32[]{:S(2)}, u32[]{:S(2)}) %collective-permute-start.47) | collective-permute-done | bytes 294944 | tf_op jit(solution)/shard_map/ppermute | solution.py:634
  368.6 4.2 %collective-permute-start.53 = (bf16[4,1,1,1,1,1,24,768]{7,6,5,4,3,2,1,0:T(8,128)(2,1)S(1)}, bf16[4,1,1,1,1,1,24,768]{7,6,5,4,3,2,1,0:T(8,128)(2,1)S(1)}, u32[]{:S(2)}, u32[]{:S(2)}) collective-permute-start(bf16[4,1,1,1,1,1,24,768]{7,6,5,4,3,2,1,0:T(8,128)(2,1)S(1)} %copy-done.94), channel_id=1, source_target_pairs={{0,16},{1,17},{2,18},{3,19},{4,20},{5,21},{6,22},{7,23},{8,24},{9,... | collective-permute-start | bytes 442376 | tf_op jit(solution)/shard_map/ppermute | solution.py:634
  374.7 4.3 %collective-permute-done.53 = bf16[4,1,1,1,1,1,24,768]{7,6,5,4,3,2,1,0:T(8,128)(2,1)S(1)} collective-permute-done((bf16[4,1,1,1,1,1,24,768]{7,6,5,4,3,2,1,0:T(8,128)(2,1)S(1)}, bf16[4,1,1,1,1,1,24,768]{7,6,5,4,3,2,1,0:T(8,128)(2,1)S(1)}, u32[]{:S(2)}, u32[]{:S(2)}) %collective-permute-start.53) | collective-permute-done | bytes 147488 | tf_op jit(solution)/shard_map/ppermute | solution.py:634
  379.2 3.6 collective-permute-done.56
  (437 shorter events, 186.4 us)
Async XLA Ops:
  37.2 12.8 %collective-permute-start.11 = (bf16[4,2,1,1,1,1,24,768]{7,6,0,5,4,3,2,1:T(8,128)(2,1)S(1)}, bf16[4,2,1,1,1,1,24,768]{7,6,0,5,4,3,2,1:T(8,128)(2,1)S(1)}, u32[]{:S(2)}, u32[]{:S(2)}) collective-permute-start(bf16[4,2,1,1,1,1,24,768]{7,6,0,5,4,3,2,1:T(8,128)(2,1)S(1)} %maximum_select_fusion.23), channel_id=1, source_target_pairs={{0,8},{1,9},{2,10},{3,11},{4,12},{5,13},{6,14},{7,15},{8,0},{9,1},... | collective-permute-start | bytes 884744 | tf_op jit(solution)/shard_map/ppermute | solution.py:634
  38.7 14.1 %collective-permute-start.12 = (bf16[8,1,1,1,1,1,24,768]{7,6,0,5,4,3,2,1:T(8,128)(2,1)S(1)}, bf16[8,1,1,1,1,1,24,768]{7,6,0,5,4,3,2,1:T(8,128)(2,1)S(1)}, u32[]{:S(2)}, u32[]{:S(2)}) collective-permute-start(bf16[8,1,1,1,1,1,24,768]{7,6,0,5,4,3,2,1:T(8,128)(2,1)S(1)} %maximum_bitcast_fusion), channel_id=1, source_target_pairs={{0,16},{1,17},{2,18},{3,19},{4,20},{5,21},{6,22},{7,23},{8,24},{9,... | collective-permute-start | bytes 884744 | tf_op jit(solution)/shard_map/ppermute | solution.py:634
  41.2 14.3 %collective-permute-start.8 = (bf16[2,2,2,2,1,1,24,768]{7,6,0,5,4,3,2,1:T(8,128)(2,1)S(1)}, bf16[2,2,2,2,1,1,24,768]{7,6,0,5,4,3,2,1:T(8,128)(2,1)S(1)}, u32[]{:S(2)}, u32[]{:S(2)}) collective-permute-start(bf16[2,2,2,2,1,1,24,768]{7,6,0,5,4,3,2,1:T(8,128)(2,1)S(1)} %maximum_select_fusion.16), channel_id=1, source_target_pairs={{0,2},{1,3},{2,0},{3,1},{4,6},{5,7},{6,4},{7,5},{8,10},{9,11},{10,... | collective-permute-start | bytes 1769480 | tf_op jit(solution)/shard_map/ppermute | solution.py:634
  41.7 13.9 %collective-permute-start.9 = (bf16[2,2,2,1,2,1,24,768]{7,6,0,5,4,3,2,1:T(8,128)(2,1)S(1)}, bf16[2,2,2,1,2,1,24,768]{7,6,0,5,4,3,2,1:T(8,128)(2,1)S(1)}, u32[]{:S(2)}, u32[]{:S(2)}) collective-permute-start(bf16[2,2,2,1,2,1,24,768]{7,6,0,5,4,3,2,1:T(8,128)(2,1)S(1)} %maximum_select_fusion.17), channel_id=1, source_target_pairs={{0,4},{1,5},{2,6},{3,7},{4,0},{5,1},{6,2},{7,3},{8,12},{9,13},{10,... | collective-permute-start | bytes 1769480 | tf_op jit(solution)/shard_map/ppermute | solution.py:634
  55.8 17.4 %collective-permute-start.17 = (bf16[2,2,2,2,2,1,24,768]{7,6,0,5,4,3,2,1:T(8,128)(2,1)S(1)}, bf16[2,2,2,2,2,1,24,768]{7,6,0,5,4,3,2,1:T(8,128)(2,1)}, u32[]{:S(2)}, u32[]{:S(2)}) collective-permute-start(bf16[2,2,2,2,2,1,24,768]{7,6,0,5,4,3,2,1:T(8,128)(2,1)S(1)} %maximum_select_fusion.8), channel_id=1, source_target_pairs={{0,1},{1,0},{2,3},{3,2},{4,5},{5,4},{6,7},{7,6},{8,9},{9,8},{10,11... | collective-permute-start | bytes 3538952 | tf_op jit(solution)/shard_map/ppermute | solution.py:634
  55.8 15.8 %collective-permute-start.15 = (bf16[8,2,1,1,1,1,24,768]{7,6,0,5,4,3,2,1:T(8,128)(2,1)S(1)}, bf16[8,2,1,1,1,1,24,768]{7,6,0,5,4,3,2,1:T(8,128)(2,1)}, u32[]{:S(2)}, u32[]{:S(2)}) collective-permute-start(bf16[8,2,1,1,1,1,24,768]{7,6,0,5,4,3,2,1:T(8,128)(2,1)S(1)} %maximum_select_fusion.19), channel_id=1, source_target_pairs={{0,8},{1,9},{2,10},{3,11},{4,12},{5,13},{6,14},{7,15},{8,0},{9,1},... | collective-permute-start | bytes 1769480 | tf_op jit(solution)/shard_map/ppermute | solution.py:634
  56.8 18.6 %collective-permute-start.18 = (bf16[2,2,2,2,2,1,24,768]{7,6,0,5,4,3,2,1:T(8,128)(2,1)S(1)}, bf16[2,2,2,2,2,1,24,768]{7,6,0,5,4,3,2,1:T(8,128)(2,1)}, u32[]{:S(2)}, u32[]{:S(2)}) collective-permute-start(bf16[2,2,2,2,2,1,24,768]{7,6,0,5,4,3,2,1:T(8,128)(2,1)S(1)} %maximum_select_fusion.9), channel_id=1, source_target_pairs={{0,1},{1,0},{2,3},{3,2},{4,5},{5,4},{6,7},{7,6},{8,9},{9,8},{10,11... | collective-permute-start | bytes 3538952 | tf_op jit(solution)/shard_map/ppermute | solution.py:634
  83.4 16.3 %collective-permute-start.19 = (bf16[2,2,2,2,1,1,24,768]{7,6,0,5,4,3,2,1:T(8,128)(2,1)S(1)}, bf16[2,2,2,2,1,1,24,768]{7,6,0,5,4,3,2,1:T(8,128)(2,1)S(1)}, u32[]{:S(2)}, u32[]{:S(2)}) collective-permute-start(bf16[2,2,2,2,1,1,24,768]{7,6,0,5,4,3,2,1:T(8,128)(2,1)S(1)} %maximum_select_fusion.20), channel_id=1, source_target_pairs={{0,2},{1,3},{2,0},{3,1},{4,6},{5,7},{6,4},{7,5},{8,10},{9,11},{10,... | collective-permute-start | bytes 1769480 | tf_op jit(solution)/shard_map/ppermute | solution.py:634
  85.0 16.2 %collective-permute-start.20 = (bf16[2,2,2,1,2,1,24,768]{7,6,0,5,4,3,2,1:T(8,128)(2,1)S(1)}, bf16[2,2,2,1,2,1,24,768]{7,6,0,5,4,3,2,1:T(8,128)(2,1)S(1)}, u32[]{:S(2)}, u32[]{:S(2)}) collective-permute-start(bf16[2,2,2,1,2,1,24,768]{7,6,0,5,4,3,2,1:T(8,128)(2,1)S(1)} %maximum_select_fusion.21), channel_id=1, source_target_pairs={{0,4},{1,5},{2,6},{3,7},{4,0},{5,1},{6,2},{7,3},{8,12},{9,13},{10,... | collective-permute-start | bytes 1769480 | tf_op jit(solution)/shard_map/ppermute | solution.py:634
  85.5 26.7 %collective-permute-start.21 = (bf16[4,2,2,1,1,1,24,768]{7,6,0,5,4,3,2,1:T(8,128)(2,1)S(1)}, bf16[4,2,2,1,1,1,24,768]{7,6,0,5,4,3,2,1:T(8,128)(2,1)S(1)}, u32[]{:S(2)}, u32[]{:S(2)}) collective-permute-start(bf16[4,2,2,1,1,1,24,768]{7,6,0,5,4,3,2,1:T(8,128)(2,1)S(1)} %get-tuple-element.142), channel_id=1, source_target_pairs={{0,4},{1,5},{2,6},{3,7},{4,0},{5,1},{6,2},{7,3},{8,12},{9,13},{10,... | collective-permute-start | bytes 1769480 | tf_op jit(solution)/shard_map/ppermute | solution.py:634
  87.0 25.3 %collective-permute-start.22 = (bf16[4,2,2,1,1,1,24,768]{7,6,0,5,4,3,2,1:T(8,128)(2,1)S(1)}, bf16[4,2,2,1,1,1,24,768]{7,6,0,5,4,3,2,1:T(8,128)(2,1)S(1)}, u32[]{:S(2)}, u32[]{:S(2)}) collective-permute-start(bf16[4,2,2,1,1,1,24,768]{7,6,0,5,4,3,2,1:T(8,128)(2,1)S(1)} %get-tuple-element.143), channel_id=1, source_target_pairs={{0,2},{1,3},{2,0},{3,1},{4,6},{5,7},{6,4},{7,5},{8,10},{9,11},{10,... | collective-permute-start | bytes 1769480 | tf_op jit(solution)/shard_map/ppermute | solution.py:634
  112.9 28.0 %collective-permute-start.23 = (bf16[4,2,2,2,1,1,24,768]{7,6,0,5,4,3,2,1:T(8,128)(2,1)S(1)}, bf16[4,2,2,2,1,1,24,768]{7,6,0,5,4,3,2,1:T(8,128)(2,1)S(1)}, u32[]{:S(2)}, u32[]{:S(2)}) collective-permute-start(bf16[4,2,2,2,1,1,24,768]{7,6,0,5,4,3,2,1:T(8,128)(2,1)S(1)} %maximum_select_fusion.13), channel_id=1, source_target_pairs={{0,2},{1,3},{2,0},{3,1},{4,6},{5,7},{6,4},{7,5},{8,10},{9,11},{10,... | collective-permute-start | bytes 3538952 | tf_op jit(solution)/shard_map/ppermute | solution.py:634
  113.5 29.1 %collective-permute-start.24 = (bf16[4,2,2,1,2,1,24,768]{7,6,0,5,4,3,2,1:T(8,128)(2,1)S(1)}, bf16[4,2,2,1,2,1,24,768]{7,6,0,5,4,3,2,1:T(8,128)(2,1)S(1)}, u32[]{:S(2)}, u32[]{:S(2)}) collective-permute-start(bf16[4,2,2,1,2,1,24,768]{7,6,0,5,4,3,2,1:T(8,128)(2,1)S(1)} %maximum_select_fusion.14), channel_id=1, source_target_pairs={{0,4},{1,5},{2,6},{3,7},{4,0},{5,1},{6,2},{7,3},{8,12},{9,13},{10,... | collective-permute-start | bytes 3538952 | tf_op jit(solution)/shard_map/ppermute | solution.py:634
  144.3 13.0 %collective-permute-start.28 = (bf16[4,2,2,2,2,1,24,768]{7,6,0,5,4,3,2,1:T(8,128)(2,1)}, bf16[4,2,2,2,2,1,24,768]{7,6,0,5,4,3,2,1:T(8,128)(2,1)}, u32[]{:S(2)}, u32[]{:S(2)}) collective-permute-start(bf16[4,2,2,2,2,1,24,768]{7,6,0,5,4,3,2,1:T(8,128)(2,1)} %maximum_select_fusion.5), channel_id=1, source_target_pairs={{0,1},{1,0},{2,3},{3,2},{4,5},{5,4},{6,7},{7,6},{8,9},{9,8},{10,11... | collective-permute-start | bytes 7077896 | tf_op jit(solution)/shard_map/ppermute | solution.py:634
  209.0 15.4 %collective-permute-start.30 = (bf16[4,2,2,2,2,1,24,768]{7,6,0,5,4,3,2,1:T(8,128)(2,1)}, bf16[4,2,2,2,2,1,24,768]{7,6,0,5,4,3,2,1:T(8,128)(2,1)}, u32[]{:S(2)}, u32[]{:S(2)}) collective-permute-start(bf16[4,2,2,2,2,1,24,768]{7,6,0,5,4,3,2,1:T(8,128)(2,1)} %copy.94), channel_id=1, source_target_pairs={{0,1},{1,0},{2,3},{3,2},{4,5},{5,4},{6,7},{7,6},{8,9},{9,8},{10,11... | collective-permute-start | bytes 7077896 | tf_op jit(solution)/shard_map/ppermute | solution.py:634
  238.2 28.2 %collective-permute-start.33 = (bf16[4,2,2,2,1,1,24,768]{7,6,0,5,4,3,2,1:T(8,128)(2,1)}, bf16[4,2,2,2,1,1,24,768]{7,6,0,5,4,3,2,1:T(8,128)(2,1)}, u32[]{:S(2)}, u32[]{:S(2)}) collective-permute-start(bf16[4,2,2,2,1,1,24,768]{7,6,0,5,4,3,2,1:T(8,128)(2,1)} %get-tuple-element.178), channel_id=1, source_target_pairs={{0,2},{1,3},{2,0},{3,1},{4,6},{5,7},{6,4},{7,5},{8,10},{9,11},{10,... | collective-permute-start | bytes 3538952 | tf_op jit(solution)/shard_map/ppermute | solution.py:634
  242.0 25.7 %collective-permute-start.31 = (bf16[2,2,2,2,2,1,24,768]{7,6,5,4,3,2,1,0:T(8,128)(2,1)}, bf16[2,2,2,2,2,1,24,768]{7,6,5,4,3,2,1,0:T(8,128)(2,1)}, u32[]{:S(2)}, u32[]{:S(2)}) collective-permute-start(bf16[2,2,2,2,2,1,24,768]{7,6,5,4,3,2,1,0:T(8,128)(2,1)} %constant_dynamic-slice_fusion.21), channel_id=1, source_target_pairs={{0,1},{1,0},{2,3},{3,2},{4,5},{5,4},{6,7},{7,6},{8,9},{9,8},{10,11... | collective-permute-start | bytes 3538952 | tf_op jit(solution)/shard_map/ppermute | solution.py:634
  242.0 27.5 %collective-permute-start.32 = (bf16[2,2,2,2,2,1,24,768]{7,6,5,4,3,2,1,0:T(8,128)(2,1)}, bf16[2,2,2,2,2,1,24,768]{7,6,5,4,3,2,1,0:T(8,128)(2,1)}, u32[]{:S(2)}, u32[]{:S(2)}) collective-permute-start(bf16[2,2,2,2,2,1,24,768]{7,6,5,4,3,2,1,0:T(8,128)(2,1)} %constant_dynamic-slice_fusion.20), channel_id=1, source_target_pairs={{0,1},{1,0},{2,3},{3,2},{4,5},{5,4},{6,7},{7,6},{8,9},{9,8},{10,11... | collective-permute-start | bytes 3538952 | tf_op jit(solution)/shard_map/ppermute | solution.py:634
  242.5 29.1 %collective-permute-start.34 = (bf16[4,2,2,1,2,1,24,768]{7,6,0,5,4,3,2,1:T(8,128)(2,1)}, bf16[4,2,2,1,2,1,24,768]{7,6,0,5,4,3,2,1:T(8,128)(2,1)}, u32[]{:S(2)}, u32[]{:S(2)}) collective-permute-start(bf16[4,2,2,1,2,1,24,768]{7,6,0,5,4,3,2,1:T(8,128)(2,1)} %get-tuple-element.179), channel_id=1, source_target_pairs={{0,4},{1,5},{2,6},{3,7},{4,0},{5,1},{6,2},{7,3},{8,12},{9,13},{10,... | collective-permute-start | bytes 3538952 | tf_op jit(solution)/shard_map/ppermute | solution.py:634
  273.1 21.9 %collective-permute-start.35 = (bf16[2,2,2,2,1,1,24,768]{7,6,5,4,3,2,1,0:T(8,128)(2,1)S(1)}, bf16[2,2,2,2,1,1,24,768]{7,6,5,4,3,2,1,0:T(8,128)(2,1)S(1)}, u32[]{:S(2)}, u32[]{:S(2)}) collective-permute-start(bf16[2,2,2,2,1,1,24,768]{7,6,5,4,3,2,1,0:T(8,128)(2,1)S(1)} %get-tuple-element.188), channel_id=1, source_target_pairs={{0,2},{1,3},{2,0},{3,1},{4,6},{5,7},{6,4},{7,5},{8,10},{9,11},{10,... | collective-permute-start | bytes 1769480 | tf_op jit(solution)/shard_map/ppermute | solution.py:634
  273.7 22.2 %collective-permute-start.37 = (bf16[4,2,2,1,1,1,24,768]{7,6,0,5,4,3,2,1:T(8,128)(2,1)S(1)}, bf16[4,2,2,1,1,1,24,768]{7,6,0,5,4,3,2,1:T(8,128)(2,1)S(1)}, u32[]{:S(2)}, u32[]{:S(2)}) collective-permute-start(bf16[4,2,2,1,1,1,24,768]{7,6,0,5,4,3,2,1:T(8,128)(2,1)S(1)} %add_convert_fusion.15), channel_id=1, source_target_pairs={{0,4},{1,5},{2,6},{3,7},{4,0},{5,1},{6,2},{7,3},{8,12},{9,13},{10,... | collective-permute-start | bytes 1769480 | tf_op jit(solution)/shard_map/ppermute | solution.py:634
  284.3 18.2 %collective-permute-start.36 = (bf16[2,2,2,1,2,1,24,768]{7,6,5,4,3,2,1,0:T(8,128)(2,1)S(1)}, bf16[2,2,2,1,2,1,24,768]{7,6,5,4,3,2,1,0:T(8,128)(2,1)S(1)}, u32[]{:S(2)}, u32[]{:S(2)}) collective-permute-start(bf16[2,2,2,1,2,1,24,768]{7,6,5,4,3,2,1,0:T(8,128)(2,1)S(1)} %get-tuple-element.189), channel_id=1, source_target_pairs={{0,4},{1,5},{2,6},{3,7},{4,0},{5,1},{6,2},{7,3},{8,12},{9,13},{10,... | collective-permute-start | bytes 1769480 | tf_op jit(solution)/shard_map/ppermute | solution.py:634
  285.9 14.3 %collective-permute-start.38 = (bf16[4,2,2,1,1,1,24,768]{7,6,0,5,4,3,2,1:T(8,128)(2,1)S(1)}, bf16[4,2,2,1,1,1,24,768]{7,6,0,5,4,3,2,1:T(8,128)(2,1)S(1)}, u32[]{:S(2)}, u32[]{:S(2)}) collective-permute-start(bf16[4,2,2,1,1,1,24,768]{7,6,0,5,4,3,2,1:T(8,128)(2,1)S(1)} %add_convert_fusion.14), channel_id=1, source_target_pairs={{0,2},{1,3},{2,0},{3,1},{4,6},{5,7},{6,4},{7,5},{8,10},{9,11},{10,... | collective-permute-start | bytes 1769480 | tf_op jit(solution)/shard_map/ppermute | solution.py:634
  303.4 20.8 %collective-permute-start.39 = (bf16[2,2,2,2,2,1,24,768]{7,6,5,4,3,2,1,0:T(8,128)(2,1)}, bf16[2,2,2,2,2,1,24,768]{7,6,5,4,3,2,1,0:T(8,128)(2,1)}, u32[]{:S(2)}, u32[]{:S(2)}) collective-permute-start(bf16[2,2,2,2,2,1,24,768]{7,6,5,4,3,2,1,0:T(8,128)(2,1)} %get-tuple-element.197), channel_id=1, source_target_pairs={{0,1},{1,0},{2,3},{3,2},{4,5},{5,4},{6,7},{7,6},{8,9},{9,8},{10,11... | collective-permute-start | bytes 3538952 | tf_op jit(solution)/shard_map/ppermute | solution.py:634
  305.2 16.0 %collective-permute-start.41 = (bf16[2,2,2,1,1,1,24,768]{7,6,5,4,3,2,1,0:T(8,128)(2,1)}, bf16[2,2,2,1,1,1,24,768]{7,6,5,4,3,2,1,0:T(8,128)(2,1)S(1)}, u32[]{:S(2)}, u32[]{:S(2)}) collective-permute-start(bf16[2,2,2,1,1,1,24,768]{7,6,5,4,3,2,1,0:T(8,128)(2,1)} %add_convert_fusion.31), channel_id=1, source_target_pairs={{0,4},{1,5},{2,6},{3,7},{4,0},{5,1},{6,2},{7,3},{8,12},{9,13},{10,... | collective-permute-start | bytes 884744 | tf_op jit(solution)/shard_map/ppermute | solution.py:634
  305.8 21.5 %collective-permute-start.40 = (bf16[2,2,2,2,2,1,24,768]{7,6,5,4,3,2,1,0:T(8,128)(2,1)}, bf16[2,2,2,2,2,1,24,768]{7,6,5,4,3,2,1,0:T(8,128)(2,1)S(1)}, u32[]{:S(2)}, u32[]{:S(2)}) collective-permute-start(bf16[2,2,2,2,2,1,24,768]{7,6,5,4,3,2,1,0:T(8,128)(2,1)} %get-tuple-element.198), channel_id=1, source_target_pairs={{0,1},{1,0},{2,3},{3,2},{4,5},{5,4},{6,7},{7,6},{8,9},{9,8},{10,11... | collective-permute-start | bytes 3538952 | tf_op jit(solution)/shard_map/ppermute | solution.py:634
  306.1 15.4 %collective-permute-start.42 = (bf16[2,2,2,1,1,1,24,768]{7,6,5,4,3,2,1,0:T(8,128)(2,1)}, bf16[2,2,2,1,1,1,24,768]{7,6,5,4,3,2,1,0:T(8,128)(2,1)S(1)}, u32[]{:S(2)}, u32[]{:S(2)}) collective-permute-start(bf16[2,2,2,1,1,1,24,768]{7,6,5,4,3,2,1,0:T(8,128)(2,1)} %add_convert_fusion.30), channel_id=1, source_target_pairs={{0,2},{1,3},{2,0},{3,1},{4,6},{5,7},{6,4},{7,5},{8,10},{9,11},{10,... | collective-permute-start | bytes 884744 | tf_op jit(solution)/shard_map/ppermute | solution.py:634
  306.8 16.6 %collective-permute-start.43 = (bf16[8,2,1,1,1,1,24,768]{7,6,0,5,4,3,2,1:T(8,128)(2,1)}, bf16[8,2,1,1,1,1,24,768]{7,6,0,5,4,3,2,1:T(8,128)(2,1)S(1)}, u32[]{:S(2)}, u32[]{:S(2)}) collective-permute-start(bf16[8,2,1,1,1,1,24,768]{7,6,0,5,4,3,2,1:T(8,128)(2,1)} %fusion), channel_id=1, source_target_pairs={{0,8},{1,9},{2,10},{3,11},{4,12},{5,13},{6,14},{7,15},{8,0},{9,1},... | collective-permute-start | bytes 1769480 | tf_op jit(solution)/shard_map/ppermute | solution.py:634
  328.5 18.9 %collective-permute-start.44 = (bf16[2,2,2,2,1,1,24,768]{7,6,5,4,3,2,1,0:T(8,128)(2,1)}, bf16[2,2,2,2,1,1,24,768]{7,6,5,4,3,2,1,0:T(8,128)(2,1)}, u32[]{:S(2)}, u32[]{:S(2)}) collective-permute-start(bf16[2,2,2,2,1,1,24,768]{7,6,5,4,3,2,1,0:T(8,128)(2,1)} %get-tuple-element.205), channel_id=1, source_target_pairs={{0,2},{1,3},{2,0},{3,1},{4,6},{5,7},{6,4},{7,5},{8,10},{9,11},{10,... | collective-permute-start | bytes 1769480 | tf_op jit(solution)/shard_map/ppermute | solution.py:634
  329.9 18.6 %collective-permute-start.45 = (bf16[2,2,2,1,2,1,24,768]{7,6,5,4,3,2,1,0:T(8,128)(2,1)}, bf16[2,2,2,1,2,1,24,768]{7,6,5,4,3,2,1,0:T(8,128)(2,1)}, u32[]{:S(2)}, u32[]{:S(2)}) collective-permute-start(bf16[2,2,2,1,2,1,24,768]{7,6,5,4,3,2,1,0:T(8,128)(2,1)} %get-tuple-element.206), channel_id=1, source_target_pairs={{0,4},{1,5},{2,6},{3,7},{4,0},{5,1},{6,2},{7,3},{8,12},{9,13},{10,... | collective-permute-start | bytes 1769480 | tf_op jit(solution)/shard_map/ppermute | solution.py:634
  334.2 12.5 %collective-permute-start.46 = (bf16[4,2,1,1,1,1,24,768]{7,6,5,4,3,2,1,0:T(8,128)(2,1)}, bf16[4,2,1,1,1,1,24,768]{7,6,5,4,3,2,1,0:T(8,128)(2,1)S(1)}, u32[]{:S(2)}, u32[]{:S(2)}) collective-permute-start(bf16[4,2,1,1,1,1,24,768]{7,6,5,4,3,2,1,0:T(8,128)(2,1)} %fusion.2), channel_id=1, source_target_pairs={{0,8},{1,9},{2,10},{3,11},{4,12},{5,13},{6,14},{7,15},{8,0},{9,1},... | collective-permute-start | bytes 884744 | tf_op jit(solution)/shard_map/ppermute | solution.py:634
  336.1 15.4 %collective-permute-start.54 = (bf16[8,1,1,1,1,1,24,768]{7,6,0,5,4,3,2,1:T(8,128)(2,1)}, bf16[8,1,1,1,1,1,24,768]{7,6,0,5,4,3,2,1:T(8,128)(2,1)S(1)}, u32[]{:S(2)}, u32[]{:S(2)}) collective-permute-start(bf16[8,1,1,1,1,1,24,768]{7,6,0,5,4,3,2,1:T(8,128)(2,1)} %add_convert_fusion.25), channel_id=1, source_target_pairs={{0,16},{1,17},{2,18},{3,19},{4,20},{5,21},{6,22},{7,23},{8,24},{9,... | collective-permute-start | bytes 884744 | tf_op jit(solution)/shard_map/ppermute | solution.py:634
  (123 other events, 762.2 us)

commit v4 on v3

--- a/solution.py
+++ b/solution.py
@@ -638,11 +638,26 @@
     return (lax.axis_index("fsdp") >> bit) & 1
 
 
-def halves(parts):
-    if len(parts) == 2:
-        return parts
-    middle = parts[0].shape[0] // 2
-    return [parts[0][:middle], parts[0][middle:]]
+def weave_body(parts, core_ref, *refs):
+    for part in range(parts):
+        out = refs[2 * parts + part]
+        out[0, :, core_ref[0]] = refs[part][:, 0]
+        out[0, :, 1 - core_ref[0]] = refs[parts + part][:, 0]
+
+
+def weave(held, other, core):
+    groups, mats, rows, width = held[0].shape
+    parts = len(held)
+    half = spec((groups, 1, rows, width), lambda i: (0, i, 0, 0))
+    both = spec((1, groups, 2, rows, width), lambda i: (i, 0, 0, 0, 0))
+    return run(
+        functools.partial(weave_body, parts),
+        "weave",
+        (mats,),
+        (core, *held, *other),
+        [smem()] + [half] * (2 * parts),
+        [((mats, groups, 2, rows, width), held[0].dtype, both)] * parts,
+    )
 
 
 class Gather:
@@ -651,18 +666,15 @@
         self.bits = count.bit_length() - 1
         mats, rows, width = piece.shape
         self.shape = (rows, width)
-        self.parts = [piece.reshape((mats,) + (1,) * self.bits + (rows, width))]
+        self.parts = [piece.reshape((1,) * self.bits + (mats, rows, width))]
         self.stages = gather_stages(count, parts)
         self.flight = None
-
-    def axis(self, bit):
-        return self.bits - bit
 
     def land(self):
         if self.flight is not None:
             parts = []
             for held, (bit, other) in zip(self.parts, self.flight):
-                axis = self.axis(bit)
+                axis = self.bits - 1 - bit
                 parts.append(
                     jnp.where(
                         own_bit(bit) == 0,
@@ -675,8 +687,8 @@
 
     def ready(self):
         self.land()
-        if len(self.stages[0][0]) == 2:
-            self.parts = halves(self.parts)
+        if len(self.stages[0][0]) == 2 and len(self.parts) == 1:
+            self.parts = jnp.split(self.parts[0], 2, self.bits)
         return self.parts
 
     def launch(self, parts):
@@ -687,9 +699,15 @@
             self.flight = [(bit, swap(part, bit, self.count)) for bit, part in zip(step, self.parts)]
 
     def result(self):
-        self.land()
         rows, width = self.shape
-        return [part.reshape(part.shape[0], self.count * rows, width) for part in self.parts]
+        merged = lambda v: v.reshape((self.count // 2,) + v.shape[self.bits :])
+        held = [merged(v) for v in self.parts]
+        other = [merged(v) for _, v in self.flight]
+        if len(held) == 1:
+            self.land()
+            return [self.parts[0].reshape(self.count * rows, width)]
+        done = weave(held, other, own_bit(0).astype(jnp.int32).reshape(1))
+        return [v.reshape(v.shape[0], self.count * rows, width) for v in done]
 
 
 class Scatter:
@@ -831,20 +849,20 @@
     d_cross_a = weight_grads([(norm_two, grad_cq), (cross_attended, grad_cross)], width // 3)
     d_cross_b = weight_grads([(frames, grad_ck), (frames, grad_cv)], width // 3)
     s_cross = Scatter([d_cross_a, d_cross_b], count)
-    grad_cq = tick([s_cross], grad_cq)
+    grad_cq, grad_ck, grad_cv = tick([s_cross], (grad_cq, grad_ck, grad_cv))
     grad_mid, grad_self, grad_att, sums_mid = mid_back(
         grad_cq, cross_a, mid, grad_late, vec, self_b, block
     )
-    grad_att = tick([s_cross, s_ffn], grad_att)
+    grad_frames, sums_frames = frames_back(grad_ck, grad_cv, cross_b, frame_rows)
+    grad_att, grad_frames = tick([s_cross, s_ffn], (grad_att, grad_frames))
     grad_q, grad_k, grad_v = attend_back(query, key, value, grad_att, batch, True)
     d_self_a = weight_grads([(norm_one, grad_q), (norm_one, grad_k)], width // 3)
     d_self_b = weight_grads([(norm_one, grad_v), (attended, grad_self)], width // 3)
     s_self = Scatter([d_self_a, d_self_b], count)
     grad_q, grad_k, grad_v = tick([s_self, s_cross, s_ffn], (grad_q, grad_k, grad_v))
     grad_in, sums_one = in_back(grad_q, grad_k, grad_v, self_a, self_b, x, grad_mid, vec, block)
-    grad_ck, grad_cv = tick([s_self, s_cross, s_ffn], (grad_ck, grad_cv))
-    grad_frames, sums_frames = frames_back(grad_ck, grad_cv, cross_b, frame_rows)
-
+
+    sums_one = tick([s_self, s_cross, s_ffn], sums_one)
     sum_rows = jnp.stack(
         [sums_one[0], sums_mid[0], sums_late[0]]
         + [sums_one[2], sums_one[3], sums_mid[2], sums_mid[3], sums_frames[0], sums_late[2], square_rest[2]]
@@ -863,11 +881,11 @@
     )
     sums = jnp.pad(sums, ((0, 0), (0, small_size - sums.shape[1])))
     s_small = Scatter([sums.reshape(1, count * small_rows, 128)], count)
+    tick([s_small])
+    tick([s_small])
     tick([s_self, s_cross, s_small])
     tick([s_self, s_small])
     tick([s_self, s_small])
-    tick([s_small])
-    tick([s_small])
     d_ffn = s_ffn.result()
     d_in_all, d_out_all = d_ffn[:mats], d_ffn[mats:]
     d_cross = s_cross.result()

time: 401 us -> 388 us (0.968)
  other arithmetic: 61.5 us -> 47.4 us
  Pallas kernels: 100 us -> 108 us
  local copies, waits for them, and re-layouts: 69.3 us -> 64.4 us
    select_n x28 -> x22, other arithmetic: 22.8 us -> 8.36 us  [land(): jnp.where(own_bit(bit) == 0, jnp.concatenate([held, other], axis), jnp.co...]
    pallas_call x17 -> x20, Pallas kernels: 100 us -> 108 us  [run(): pl.pallas_call(body, name=name, grid=grid, in_specs=in_specs, out_specs=[...]
    select_n x6 -> x0, local copies, waits for them, and re-layouts: 6.68 us -> none  [land(): jnp.where(own_bit(bit) == 0, jnp.concatenate([held, other], axis), jnp.co...]
    unnamed x191 -> x197, local copies, waits for them, and re-layouts: 28.6 us -> 30.2 us
  transfers between devices with their start and end apart: 58 -> 58, of which waited for: 28 -> 29; matrix products, arithmetic and copies ran while one was open for 17% -> 15% of each run, Pallas kernels for 13% -> 14%
where the time goes in v4:
time: 388 us; the launch traced here: 381 us
  Pallas kernels  108 us (28%)
  waiting for transfers between devices  106 us (27%)
  local copies, waits for them, and re-layouts  64.4 us (17%)
  starting transfers between devices  52.6 us (14%)
  other arithmetic  47.4 us (12%)
    pallas_call x20, Pallas kernels, run(): pl.pallas_call(body, name=name, grid=grid, in_specs=in_specs, out_specs=[...  108 us
    ppermute x58, waiting for transfers between devices, swap(): lax.ppermute(values, 'fsdp', [(i, i ^ 1 << bit) for i in range(count)])  106 us
    ppermute x58, starting transfers between devices, swap(): lax.ppermute(values, 'fsdp', [(i, i ^ 1 << bit) for i in range(count)])  52.6 us
    unnamed x197, local copies, waits for them, and re-layouts  30.2 us
    convert_element_type x15, other arithmetic, pick(): (values[0].astype(jnp.float32) + values[1].astype(jnp.float32)).astype(se...  24.2 us
    dynamic_slice x8, local copies, waits for them, and re-layouts, pick(): lax.dynamic_slice_in_dim(v, side, 1, axis)  9.02 us
    select_n x22, other arithmetic, land(): jnp.where(own_bit(bit) == 0, jnp.concatenate([held, other], axis), jnp.co...  8.36 us
  transfers between devices with their start and end apart: 58, of which 29 were waited for; matrix products, arithmetic and copies ran while one was open for 15% of the time, Pallas kernels for 14%

profile of v4, /device:TPU:0, one launch (start us, length us, event | category | flops | bytes accessed | tf_op | source)
XLA Modules:
  0.0 381.5 jit_solution(14442749531485388329)
XLA Ops:
  4.7 4.1 %collective-permute-start = (bf16[1,1,1,1,1,4,24,768]{7,6,5,4,3,2,1,0:T(8,128)(2,1)S(1)}, bf16[1,1,1,1,1,4,24,768]{7,6,5,4,3,2,1,0:T(8,128)(2,1)S(1)}, u32[]{:S(2)}, u32[]{:S(2)}) collective-permute-start(bf16[1,1,1,1,1,4,24,768]{7,6,5,4,3,2,1,0:T(8,128)(2,1)S(1)} %maximum_bitcast_fusion.1), channel_id=1, source_target_pairs={{0,16},{1,17},{2,18},{3,19},{4,20},{5,21},{6,22},{7,23},{8,24},{9,... | collective-permute-start | bytes 442376 | tf_op jit(solution)/shard_map/ppermute | solution.py:634
  8.9 7.0 %collective-permute-done.1 = bf16[1,1,1,1,1,1,4,128]{7,6,5,4,3,2,1,0:T(4,128)(2,1)S(1)} collective-permute-done((bf16[1,1,1,1,1,1,4,128]{7,6,5,4,3,2,1,0:T(4,128)(2,1)S(1)}, bf16[1,1,1,1,1,1,4,128]{7,6,5,4,3,2,1,0:T(4,128)(2,1)S(1)}, u32[]{:S(2)}, u32[]{:S(2)}) %collective-permute-start.1) | collective-permute-done | bytes 1056 | tf_op jit(solution)/shard_map/ppermute | solution.py:634
  20.7 3.5 collective-permute-done.3
  25.7 3.3 collective-permute-start.7
  31.2 4.2 %collective-permute-done.7 = bf16[1,1,1,1,1,4,24,768]{7,6,5,4,3,2,1,0:T(8,128)(2,1)S(1)} collective-permute-done((bf16[1,1,1,1,1,4,24,768]{7,6,5,4,3,2,1,0:T(8,128)(2,1)S(1)}, bf16[1,1,1,1,1,4,24,768]{7,6,5,4,3,2,1,0:T(8,128)(2,1)S(1)}, u32[]{:S(2)}, u32[]{:S(2)}) %collective-permute-start.7) | collective-permute-done | bytes 147488 | tf_op jit(solution)/shard_map/ppermute | solution.py:634
  43.4 6.5 %collective-permute-done.11 = bf16[2,1,1,1,1,4,24,768]{7,6,5,4,3,2,1,0:T(8,128)(2,1)S(1)} collective-permute-done((bf16[2,1,1,1,1,4,24,768]{7,6,5,4,3,2,1,0:T(8,128)(2,1)S(1)}, bf16[2,1,1,1,1,4,24,768]{7,6,5,4,3,2,1,0:T(8,128)(2,1)S(1)}, u32[]{:S(2)}, u32[]{:S(2)}) %collective-permute-start.11) | collective-permute-done | bytes 294944 | tf_op jit(solution)/shard_map/ppermute | solution.py:634
  50.0 2.7 collective-permute-done.12
  57.2 3.3 collective-permute-done.16
  75.4 3.8 qkv.1
  83.4 5.3 %attend_self.1.a_ref.refs_2_ = bf16[640,768]{1,0:T(8,128)(2,1)S(1)} custom-call(bf16[640,768]{1,0:T(8,128)(2,1)S(1)} %get-tuple-element.154.q_ref, bf16[640,768]{1,0:T(8,128)(2,1)S(1)} %get-tuple-element.155.k_ref, bf16[640,768]{1,0:T(8,128)(2,1)S(1)} %get-tuple-element.156.v_ref), custom_call_target="tpu_custom_call" | custom-call | flops 629145600 | bytes 3932160 | tf_op jit(solution)/shard_map/attend_self/pallas_call | solution.py:41
  88.8 3.0 mid_stage.1
  91.9 3.7 collective-permute-done.19
  97.1 10.5 %collective-permute-done.21 = bf16[2,2,1,1,1,4,24,768]{7,6,5,4,3,2,1,0:T(8,128)(2,1)S(1)} collective-permute-done((bf16[2,2,1,1,1,4,24,768]{7,6,5,4,3,2,1,0:T(8,128)(2,1)S(1)}, bf16[2,2,1,1,1,4,24,768]{7,6,5,4,3,2,1,0:T(8,128)(2,1)S(1)}, u32[]{:S(2)}, u32[]{:S(2)}) %collective-permute-start.21) | collective-permute-done | bytes 589856 | tf_op jit(solution)/shard_map/ppermute | solution.py:634
  115.3 3.2 attend_cross.1.a_ref.refs_2_
  118.5 3.0 late_stage.1
  123.8 12.6 %collective-permute-done.23 = bf16[2,2,2,1,1,4,24,768]{7,6,5,4,3,2,1,0:T(8,128)(2,1)S(1)} collective-permute-done((bf16[2,2,2,1,1,4,24,768]{7,6,5,4,3,2,1,0:T(8,128)(2,1)S(1)}, bf16[2,2,2,1,1,4,24,768]{7,6,5,4,3,2,1,0:T(8,128)(2,1)S(1)}, u32[]{:S(2)}, u32[]{:S(2)}) %collective-permute-start.23) | collective-permute-done | bytes 1179680 | tf_op jit(solution)/shard_map/ppermute | solution.py:634
  145.3 2.8 collective-permute-done.28
  148.1 5.1 %weave.5 = (bf16[4,16,2,24,768]{4,3,2,1,0:T(8,128)(2,1)S(1)}, bf16[4,16,2,24,768]{4,3,2,1,0:T(8,128)(2,1)S(1)}) custom-call(s32[1]{0:T(128)} %bitcast.9.core_ref, bf16[16,4,24,768]{3,2,1,0:T(8,128)(2,1)} %bitcast.25.refs_0_, bf16[16,4,24,768]{3,2,1,0:T(8,128)(2,1)} %bitcast.26.refs_1_, bf16[16,4,24,768]{3,2,1,0:T(8,128)(2,1)} %bitcast.27.refs_2_, ...), custom_call_target="tpu_custom_call" | custom-call | bytes 18874372 | tf_op jit(solution)/shard_map/weave/pallas_call | solution.py:41
  157.4 35.9 %ffn_stage.1 = (f32[640,768]{1,0:T(8,128)S(1)}, bf16[4,768,768]{2,1,0:T(8,128)(2,1)}, bf16[4,768,768]{2,1,0:T(8,128)(2,1)}, f32[4,1,768]{2,1,0:T(1,128)S(1)}, bf...) custom-call(s32[2]{0:T(128)S(1)} %copy-done.56, bf16[640,768]{1,0:T(8,128)(2,1)S(1)} %copy-done.60, ...), custom_call_target="tpu_custom_call" | custom-call | flops 18119393280 | bytes 25853960 | tf_op jit(solution)/shard_map/ffn_stage/pallas_call | solution.py:41
  205.8 3.7 late_back.1
  212.7 3.7 add_convert_fusion.1
  216.5 3.8 add_convert_fusion
  220.3 5.4 %attend_cross_back.1 = (bf16[640,768]{1,0:T(8,128)(2,1)S(1)}, bf16[256,768]{1,0:T(8,128)(2,1)S(1)}, bf16[256,768]{1,0:T(8,128)(2,1)S(1)}) custom-call(bf16[640,768]{1,0:T(8,128)(2,1)S(1)} %copy-done.36, bf16[256,768]{1,0:T(8,128)(2,1)S(1)} %copy-done.49, bf16[256,768]{1,0:T(8,128)(2,1)S(1)} %copy-done.51, bf16[640,768]{1,0:T(8,128)(2,1)S(1)} %get-tuple-element.185.g_ref), custom_call_target="tpu_custom_call" | custom-call | flops 629145600 | bytes 4521984 | tf_op jit(solution)/shard_map/attend_cross_back/pallas_call | solution.py:41
  225.8 2.7 weight_grads.4
  244.4 5.8 %mid_back.1 = (f32[640,768]{1,0:T(8,128)S(1)}, bf16[640,768]{1,0:T(8,128)(2,1)S(1)}, bf16[640,768]{1,0:T(8,128)(2,1)S(1)}, f32[8,768]{1,0:T(8,128)S(1)}) custom-call(bf16[640,768]{1,0:T(8,128)(2,1)S(1)} %copy-done.30, bf16[2,768,768]{2,1,0:T(8,128)(2,1)S(1)} %bitcast.78, f32[640,768]{1,0:T(8,128)S(1)} %copy-done.18, f32[640,768]{1,0:T(8,128)S(1)} %copy-done.42, ...), custom_call_target="tpu_custom_call" | custom-call | flops 1509949440 | bytes 13639680 | tf_op jit(solution)/shard_map/mid_back/pallas_call | solution.py:41
  250.2 8.5 %collective-permute-done.33 = bf16[4,2,2,2,1,1,24,768]{7,6,0,5,4,3,2,1:T(8,128)(2,1)} collective-permute-done((bf16[4,2,2,2,1,1,24,768]{7,6,0,5,4,3,2,1:T(8,128)(2,1)}, bf16[4,2,2,2,1,1,24,768]{7,6,0,5,4,3,2,1:T(8,128)(2,1)}, u32[]{:S(2)}, u32[]{:S(2)}) %collective-permute-start.33) | collective-permute-done | bytes 1179680 | tf_op jit(solution)/shard_map/ppermute | solution.py:634
  266.4 9.8 %attend_self_back.1 = (bf16[640,768]{1,0:T(8,128)(2,1)S(1)}, bf16[640,768]{1,0:T(8,128)(2,1)S(1)}, bf16[640,768]{1,0:T(8,128)(2,1)S(1)}) custom-call(bf16[640,768]{1,0:T(8,128)(2,1)S(1)} %copy-done.62, bf16[640,768]{1,0:T(8,128)(2,1)S(1)} %copy-done.64, bf16[640,768]{1,0:T(8,128)(2,1)S(1)} %copy-done.66, bf16[640,768]{1,0:T(8,128)(2,1)S(1)} %get-tuple-element.200.g_ref), custom_call_target="tpu_custom_call" | custom-call | flops 1572864000 | bytes 6881280 | tf_op jit(solution)/shard_map/attend_self_back/pallas_call | solution.py:41
  289.2 3.3 collective-permute-done.38
  306.7 7.0 %in_back.1 = (bf16[640,768]{1,0:T(8,128)(2,1)}, f32[8,768]{1,0:T(8,128)S(1)}) custom-call(bf16[640,768]{1,0:T(8,128)(2,1)S(1)} %copy-done.22, bf16[640,768]{1,0:T(8,128)(2,1)S(1)} %copy-done.24, bf16[640,768]{1,0:T(8,128)(2,1)S(1)} %copy-done.26, bf16[2,768,768]{2,1,0:T(8,128)(2,1)S(1)} %bitcast.89, bf16[2,768,768]{2,1,0:T(8,128)(2,1)S(1)} %bitcast.90, ...), custom_call_target="tpu_custom_call" | custom-call | flops 2264924160 | bytes 14032896 | tf_op jit(solution)/shard_map/in_back/pallas_call | solution.py:41
  327.6 12.3 %collective-permute-done.48 = f32[1,2,2,2,1,1,4,128]{7,6,5,4,3,2,1,0:T(4,128)S(1)} collective-permute-done((f32[1,2,2,2,1,1,4,128]{7,6,5,4,3,2,1,0:T(4,128)S(1)}, f32[1,2,2,2,1,1,4,128]{7,6,5,4,3,2,1,0:T(4,128)S(1)}, u32[]{:S(2)}, u32[]{:S(2)}) %collective-permute-start.48) | collective-permute-done | bytes 16416 | tf_op jit(solution)/shard_map/ppermute | solution.py:634
  358.1 4.6 %collective-permute-done.49 = bf16[2,2,2,1,1,1,24,768]{7,6,5,4,3,2,1,0:T(8,128)(2,1)S(1)} collective-permute-done((bf16[2,2,2,1,1,1,24,768]{7,6,5,4,3,2,1,0:T(8,128)(2,1)S(1)}, bf16[2,2,2,1,1,1,24,768]{7,6,5,4,3,2,1,0:T(8,128)(2,1)S(1)}, u32[]{:S(2)}, u32[]{:S(2)}) %collective-permute-start.49) | collective-permute-done | bytes 294944 | tf_op jit(solution)/shard_map/ppermute | solution.py:634
  367.7 3.4 collective-permute-done.52
  (434 shorter events, 180.1 us)
Async XLA Ops:
  37.2 12.8 %collective-permute-start.11 = (bf16[2,1,1,1,1,4,24,768]{7,6,5,4,3,2,1,0:T(8,128)(2,1)S(1)}, bf16[2,1,1,1,1,4,24,768]{7,6,5,4,3,2,1,0:T(8,128)(2,1)S(1)}, u32[]{:S(2)}, u32[]{:S(2)}) collective-permute-start(bf16[2,1,1,1,1,4,24,768]{7,6,5,4,3,2,1,0:T(8,128)(2,1)S(1)} %maximum_select_fusion.17), channel_id=1, source_target_pairs={{0,8},{1,9},{2,10},{3,11},{4,12},{5,13},{6,14},{7,15},{8,0},{9,1},... | collective-permute-start | bytes 884744 | tf_op jit(solution)/shard_map/ppermute | solution.py:634
  38.7 14.1 %collective-permute-start.12 = (bf16[1,1,1,1,1,8,24,768]{7,6,5,4,3,2,1,0:T(8,128)(2,1)S(1)}, bf16[1,1,1,1,1,8,24,768]{7,6,5,4,3,2,1,0:T(8,128)(2,1)S(1)}, u32[]{:S(2)}, u32[]{:S(2)}) collective-permute-start(bf16[1,1,1,1,1,8,24,768]{7,6,5,4,3,2,1,0:T(8,128)(2,1)S(1)} %maximum_bitcast_fusion), channel_id=1, source_target_pairs={{0,16},{1,17},{2,18},{3,19},{4,20},{5,21},{6,22},{7,23},{8,24},{9,... | collective-permute-start | bytes 884744 | tf_op jit(solution)/shard_map/ppermute | solution.py:634
  41.2 14.3 %collective-permute-start.8 = (bf16[2,2,2,1,1,2,24,768]{7,6,5,4,3,2,1,0:T(8,128)(2,1)S(1)}, bf16[2,2,2,1,1,2,24,768]{7,6,5,4,3,2,1,0:T(8,128)(2,1)S(1)}, u32[]{:S(2)}, u32[]{:S(2)}) collective-permute-start(bf16[2,2,2,1,1,2,24,768]{7,6,5,4,3,2,1,0:T(8,128)(2,1)S(1)} %maximum_select_fusion.10), channel_id=1, source_target_pairs={{0,2},{1,3},{2,0},{3,1},{4,6},{5,7},{6,4},{7,5},{8,10},{9,11},{10,... | collective-permute-start | bytes 1769480 | tf_op jit(solution)/shard_map/ppermute | solution.py:634
  41.7 13.9 %collective-permute-start.9 = (bf16[2,2,1,2,1,2,24,768]{7,6,5,4,3,2,1,0:T(8,128)(2,1)S(1)}, bf16[2,2,1,2,1,2,24,768]{7,6,5,4,3,2,1,0:T(8,128)(2,1)S(1)}, u32[]{:S(2)}, u32[]{:S(2)}) collective-permute-start(bf16[2,2,1,2,1,2,24,768]{7,6,5,4,3,2,1,0:T(8,128)(2,1)S(1)} %maximum_select_fusion.11), channel_id=1, source_target_pairs={{0,4},{1,5},{2,6},{3,7},{4,0},{5,1},{6,2},{7,3},{8,12},{9,13},{10,... | collective-permute-start | bytes 1769480 | tf_op jit(solution)/shard_map/ppermute | solution.py:634
  55.8 17.5 %collective-permute-start.17 = (bf16[2,2,2,2,1,2,24,768]{7,6,5,4,3,2,1,0:T(8,128)(2,1)S(1)}, bf16[2,2,2,2,1,2,24,768]{7,6,5,4,3,2,1,0:T(8,128)(2,1)}, u32[]{:S(2)}, u32[]{:S(2)}) collective-permute-start(bf16[2,2,2,2,1,2,24,768]{7,6,5,4,3,2,1,0:T(8,128)(2,1)S(1)} %maximum_select_fusion.2), channel_id=1, source_target_pairs={{0,1},{1,0},{2,3},{3,2},{4,5},{5,4},{6,7},{7,6},{8,9},{9,8},{10,11... | collective-permute-start | bytes 3538952 | tf_op jit(solution)/shard_map/ppermute | solution.py:634
  55.8 17.4 %collective-permute-start.18 = (bf16[2,2,2,2,1,2,24,768]{7,6,5,4,3,2,1,0:T(8,128)(2,1)S(1)}, bf16[2,2,2,2,1,2,24,768]{7,6,5,4,3,2,1,0:T(8,128)(2,1)}, u32[]{:S(2)}, u32[]{:S(2)}) collective-permute-start(bf16[2,2,2,2,1,2,24,768]{7,6,5,4,3,2,1,0:T(8,128)(2,1)S(1)} %maximum_select_fusion.3), channel_id=1, source_target_pairs={{0,1},{1,0},{2,3},{3,2},{4,5},{5,4},{6,7},{7,6},{8,9},{9,8},{10,11... | collective-permute-start | bytes 3538952 | tf_op jit(solution)/shard_map/ppermute | solution.py:634
  56.3 15.4 %collective-permute-start.15 = (bf16[2,1,1,1,1,8,24,768]{7,6,5,4,3,2,1,0:T(8,128)(2,1)S(1)}, bf16[2,1,1,1,1,8,24,768]{7,6,5,4,3,2,1,0:T(8,128)(2,1)}, u32[]{:S(2)}, u32[]{:S(2)}) collective-permute-start(bf16[2,1,1,1,1,8,24,768]{7,6,5,4,3,2,1,0:T(8,128)(2,1)S(1)} %maximum_select_fusion.13), channel_id=1, source_target_pairs={{0,8},{1,9},{2,10},{3,11},{4,12},{5,13},{6,14},{7,15},{8,0},{9,1},... | collective-permute-start | bytes 1769480 | tf_op jit(solution)/shard_map/ppermute | solution.py:634
  79.3 16.3 %collective-permute-start.19 = (bf16[2,2,2,1,1,2,24,768]{7,6,5,4,3,2,1,0:T(8,128)(2,1)S(1)}, bf16[2,2,2,1,1,2,24,768]{7,6,5,4,3,2,1,0:T(8,128)(2,1)S(1)}, u32[]{:S(2)}, u32[]{:S(2)}) collective-permute-start(bf16[2,2,2,1,1,2,24,768]{7,6,5,4,3,2,1,0:T(8,128)(2,1)S(1)} %maximum_select_fusion.14), channel_id=1, source_target_pairs={{0,2},{1,3},{2,0},{3,1},{4,6},{5,7},{6,4},{7,5},{8,10},{9,11},{10,... | collective-permute-start | bytes 1769480 | tf_op jit(solution)/shard_map/ppermute | solution.py:634
  80.8 16.2 %collective-permute-start.20 = (bf16[2,2,1,2,1,2,24,768]{7,6,5,4,3,2,1,0:T(8,128)(2,1)S(1)}, bf16[2,2,1,2,1,2,24,768]{7,6,5,4,3,2,1,0:T(8,128)(2,1)S(1)}, u32[]{:S(2)}, u32[]{:S(2)}) collective-permute-start(bf16[2,2,1,2,1,2,24,768]{7,6,5,4,3,2,1,0:T(8,128)(2,1)S(1)} %maximum_select_fusion.15), channel_id=1, source_target_pairs={{0,4},{1,5},{2,6},{3,7},{4,0},{5,1},{6,2},{7,3},{8,12},{9,13},{10,... | collective-permute-start | bytes 1769480 | tf_op jit(solution)/shard_map/ppermute | solution.py:634
  81.3 26.3 %collective-permute-start.21 = (bf16[2,2,1,1,1,4,24,768]{7,6,5,4,3,2,1,0:T(8,128)(2,1)S(1)}, bf16[2,2,1,1,1,4,24,768]{7,6,5,4,3,2,1,0:T(8,128)(2,1)S(1)}, u32[]{:S(2)}, u32[]{:S(2)}) collective-permute-start(bf16[2,2,1,1,1,4,24,768]{7,6,5,4,3,2,1,0:T(8,128)(2,1)S(1)} %get-tuple-element.152), channel_id=1, source_target_pairs={{0,4},{1,5},{2,6},{3,7},{4,0},{5,1},{6,2},{7,3},{8,12},{9,13},{10,... | collective-permute-start | bytes 1769480 | tf_op jit(solution)/shard_map/ppermute | solution.py:634
  82.9 24.9 %collective-permute-start.22 = (bf16[2,2,1,1,1,4,24,768]{7,6,5,4,3,2,1,0:T(8,128)(2,1)S(1)}, bf16[2,2,1,1,1,4,24,768]{7,6,5,4,3,2,1,0:T(8,128)(2,1)S(1)}, u32[]{:S(2)}, u32[]{:S(2)}) collective-permute-start(bf16[2,2,1,1,1,4,24,768]{7,6,5,4,3,2,1,0:T(8,128)(2,1)S(1)} %get-tuple-element.153), channel_id=1, source_target_pairs={{0,2},{1,3},{2,0},{3,1},{4,6},{5,7},{6,4},{7,5},{8,10},{9,11},{10,... | collective-permute-start | bytes 1769480 | tf_op jit(solution)/shard_map/ppermute | solution.py:634
  108.5 28.0 %collective-permute-start.23 = (bf16[2,2,2,1,1,4,24,768]{7,6,5,4,3,2,1,0:T(8,128)(2,1)S(1)}, bf16[2,2,2,1,1,4,24,768]{7,6,5,4,3,2,1,0:T(8,128)(2,1)S(1)}, u32[]{:S(2)}, u32[]{:S(2)}) collective-permute-start(bf16[2,2,2,1,1,4,24,768]{7,6,5,4,3,2,1,0:T(8,128)(2,1)S(1)} %maximum_select_fusion.7), channel_id=1, source_target_pairs={{0,2},{1,3},{2,0},{3,1},{4,6},{5,7},{6,4},{7,5},{8,10},{9,11},{10,... | collective-permute-start | bytes 3538952 | tf_op jit(solution)/shard_map/ppermute | solution.py:634
  109.0 29.1 %collective-permute-start.24 = (bf16[2,2,1,2,1,4,24,768]{7,6,5,4,3,2,1,0:T(8,128)(2,1)S(1)}, bf16[2,2,1,2,1,4,24,768]{7,6,5,4,3,2,1,0:T(8,128)(2,1)S(1)}, u32[]{:S(2)}, u32[]{:S(2)}) collective-permute-start(bf16[2,2,1,2,1,4,24,768]{7,6,5,4,3,2,1,0:T(8,128)(2,1)S(1)} %maximum_select_fusion.8), channel_id=1, source_target_pairs={{0,4},{1,5},{2,6},{3,7},{4,0},{5,1},{6,2},{7,3},{8,12},{9,13},{10,... | collective-permute-start | bytes 3538952 | tf_op jit(solution)/shard_map/ppermute | solution.py:634
  201.1 15.4 %collective-permute-start.30 = (bf16[4,2,2,2,2,1,24,768]{7,6,0,5,4,3,2,1:T(8,128)(2,1)}, bf16[4,2,2,2,2,1,24,768]{7,6,0,5,4,3,2,1:T(8,128)(2,1)}, u32[]{:S(2)}, u32[]{:S(2)}) collective-permute-start(bf16[4,2,2,2,2,1,24,768]{7,6,0,5,4,3,2,1:T(8,128)(2,1)} %copy.72), channel_id=1, source_target_pairs={{0,1},{1,0},{2,3},{3,2},{4,5},{5,4},{6,7},{7,6},{8,9},{9,8},{10,11... | collective-permute-start | bytes 7077896 | tf_op jit(solution)/shard_map/ppermute | solution.py:634
  230.4 28.3 %collective-permute-start.33 = (bf16[4,2,2,2,1,1,24,768]{7,6,0,5,4,3,2,1:T(8,128)(2,1)}, bf16[4,2,2,2,1,1,24,768]{7,6,0,5,4,3,2,1:T(8,128)(2,1)}, u32[]{:S(2)}, u32[]{:S(2)}) collective-permute-start(bf16[4,2,2,2,1,1,24,768]{7,6,0,5,4,3,2,1:T(8,128)(2,1)} %get-tuple-element.192), channel_id=1, source_target_pairs={{0,2},{1,3},{2,0},{3,1},{4,6},{5,7},{6,4},{7,5},{8,10},{9,11},{10,... | collective-permute-start | bytes 3538952 | tf_op jit(solution)/shard_map/ppermute | solution.py:634
  234.1 25.8 %collective-permute-start.31 = (bf16[2,2,2,2,2,1,24,768]{7,6,5,4,3,2,1,0:T(8,128)(2,1)}, bf16[2,2,2,2,2,1,24,768]{7,6,5,4,3,2,1,0:T(8,128)(2,1)}, u32[]{:S(2)}, u32[]{:S(2)}) collective-permute-start(bf16[2,2,2,2,2,1,24,768]{7,6,5,4,3,2,1,0:T(8,128)(2,1)} %constant_dynamic-slice_fusion.21), channel_id=1, source_target_pairs={{0,1},{1,0},{2,3},{3,2},{4,5},{5,4},{6,7},{7,6},{8,9},{9,8},{10,11... | collective-permute-start | bytes 3538952 | tf_op jit(solution)/shard_map/ppermute | solution.py:634
  234.1 27.6 %collective-permute-start.32 = (bf16[2,2,2,2,2,1,24,768]{7,6,5,4,3,2,1,0:T(8,128)(2,1)}, bf16[2,2,2,2,2,1,24,768]{7,6,5,4,3,2,1,0:T(8,128)(2,1)}, u32[]{:S(2)}, u32[]{:S(2)}) collective-permute-start(bf16[2,2,2,2,2,1,24,768]{7,6,5,4,3,2,1,0:T(8,128)(2,1)} %constant_dynamic-slice_fusion.20), channel_id=1, source_target_pairs={{0,1},{1,0},{2,3},{3,2},{4,5},{5,4},{6,7},{7,6},{8,9},{9,8},{10,11... | collective-permute-start | bytes 3538952 | tf_op jit(solution)/shard_map/ppermute | solution.py:634
  234.6 29.2 %collective-permute-start.34 = (bf16[4,2,2,1,2,1,24,768]{7,6,0,5,4,3,2,1:T(8,128)(2,1)}, bf16[4,2,2,1,2,1,24,768]{7,6,0,5,4,3,2,1:T(8,128)(2,1)}, u32[]{:S(2)}, u32[]{:S(2)}) collective-permute-start(bf16[4,2,2,1,2,1,24,768]{7,6,0,5,4,3,2,1:T(8,128)(2,1)} %get-tuple-element.193), channel_id=1, source_target_pairs={{0,4},{1,5},{2,6},{3,7},{4,0},{5,1},{6,2},{7,3},{8,12},{9,13},{10,... | collective-permute-start | bytes 3538952 | tf_op jit(solution)/shard_map/ppermute | solution.py:634
  265.3 21.7 %collective-permute-start.35 = (bf16[2,2,2,2,1,1,24,768]{7,6,5,4,3,2,1,0:T(8,128)(2,1)S(1)}, bf16[2,2,2,2,1,1,24,768]{7,6,5,4,3,2,1,0:T(8,128)(2,1)S(1)}, u32[]{:S(2)}, u32[]{:S(2)}) collective-permute-start(bf16[2,2,2,2,1,1,24,768]{7,6,5,4,3,2,1,0:T(8,128)(2,1)S(1)} %get-tuple-element.205), channel_id=1, source_target_pairs={{0,2},{1,3},{2,0},{3,1},{4,6},{5,7},{6,4},{7,5},{8,10},{9,11},{10,... | collective-permute-start | bytes 1769480 | tf_op jit(solution)/shard_map/ppermute | solution.py:634
  265.9 22.0 %collective-permute-start.37 = (bf16[4,2,2,1,1,1,24,768]{7,6,0,5,4,3,2,1:T(8,128)(2,1)S(1)}, bf16[4,2,2,1,1,1,24,768]{7,6,0,5,4,3,2,1:T(8,128)(2,1)S(1)}, u32[]{:S(2)}, u32[]{:S(2)}) collective-permute-start(bf16[4,2,2,1,1,1,24,768]{7,6,0,5,4,3,2,1:T(8,128)(2,1)S(1)} %add_convert_fusion.15), channel_id=1, source_target_pairs={{0,4},{1,5},{2,6},{3,7},{4,0},{5,1},{6,2},{7,3},{8,12},{9,13},{10,... | collective-permute-start | bytes 1769480 | tf_op jit(solution)/shard_map/ppermute | solution.py:634
  276.2 18.5 %collective-permute-start.36 = (bf16[2,2,2,1,2,1,24,768]{7,6,5,4,3,2,1,0:T(8,128)(2,1)S(1)}, bf16[2,2,2,1,2,1,24,768]{7,6,5,4,3,2,1,0:T(8,128)(2,1)S(1)}, u32[]{:S(2)}, u32[]{:S(2)}) collective-permute-start(bf16[2,2,2,1,2,1,24,768]{7,6,5,4,3,2,1,0:T(8,128)(2,1)S(1)} %get-tuple-element.206), channel_id=1, source_target_pairs={{0,4},{1,5},{2,6},{3,7},{4,0},{5,1},{6,2},{7,3},{8,12},{9,13},{10,... | collective-permute-start | bytes 1769480 | tf_op jit(solution)/shard_map/ppermute | solution.py:634
  277.8 14.6 %collective-permute-start.38 = (bf16[4,2,2,1,1,1,24,768]{7,6,0,5,4,3,2,1:T(8,128)(2,1)S(1)}, bf16[4,2,2,1,1,1,24,768]{7,6,0,5,4,3,2,1:T(8,128)(2,1)S(1)}, u32[]{:S(2)}, u32[]{:S(2)}) collective-permute-start(bf16[4,2,2,1,1,1,24,768]{7,6,0,5,4,3,2,1:T(8,128)(2,1)S(1)} %add_convert_fusion.14), channel_id=1, source_target_pairs={{0,2},{1,3},{2,0},{3,1},{4,6},{5,7},{6,4},{7,5},{8,10},{9,11},{10,... | collective-permute-start | bytes 1769480 | tf_op jit(solution)/shard_map/ppermute | solution.py:634
  295.7 21.0 %collective-permute-start.39 = (bf16[2,2,2,2,2,1,24,768]{7,6,5,4,3,2,1,0:T(8,128)(2,1)}, bf16[2,2,2,2,2,1,24,768]{7,6,5,4,3,2,1,0:T(8,128)(2,1)}, u32[]{:S(2)}, u32[]{:S(2)}) collective-permute-start(bf16[2,2,2,2,2,1,24,768]{7,6,5,4,3,2,1,0:T(8,128)(2,1)} %get-tuple-element.215), channel_id=1, source_target_pairs={{0,1},{1,0},{2,3},{3,2},{4,5},{5,4},{6,7},{7,6},{8,9},{9,8},{10,11... | collective-permute-start | bytes 3538952 | tf_op jit(solution)/shard_map/ppermute | solution.py:634
  298.1 15.6 %collective-permute-start.41 = (bf16[2,2,2,1,1,1,24,768]{7,6,5,4,3,2,1,0:T(8,128)(2,1)}, bf16[2,2,2,1,1,1,24,768]{7,6,5,4,3,2,1,0:T(8,128)(2,1)S(1)}, u32[]{:S(2)}, u32[]{:S(2)}) collective-permute-start(bf16[2,2,2,1,1,1,24,768]{7,6,5,4,3,2,1,0:T(8,128)(2,1)} %add_convert_fusion.31), channel_id=1, source_target_pairs={{0,4},{1,5},{2,6},{3,7},{4,0},{5,1},{6,2},{7,3},{8,12},{9,13},{10,... | collective-permute-start | bytes 884744 | tf_op jit(solution)/shard_map/ppermute | solution.py:634
  298.7 21.1 %collective-permute-start.40 = (bf16[2,2,2,2,2,1,24,768]{7,6,5,4,3,2,1,0:T(8,128)(2,1)}, bf16[2,2,2,2,2,1,24,768]{7,6,5,4,3,2,1,0:T(8,128)(2,1)S(1)}, u32[]{:S(2)}, u32[]{:S(2)}) collective-permute-start(bf16[2,2,2,2,2,1,24,768]{7,6,5,4,3,2,1,0:T(8,128)(2,1)} %get-tuple-element.216), channel_id=1, source_target_pairs={{0,1},{1,0},{2,3},{3,2},{4,5},{5,4},{6,7},{7,6},{8,9},{9,8},{10,11... | collective-permute-start | bytes 3538952 | tf_op jit(solution)/shard_map/ppermute | solution.py:634
  298.9 15.0 %collective-permute-start.42 = (bf16[2,2,2,1,1,1,24,768]{7,6,5,4,3,2,1,0:T(8,128)(2,1)}, bf16[2,2,2,1,1,1,24,768]{7,6,5,4,3,2,1,0:T(8,128)(2,1)S(1)}, u32[]{:S(2)}, u32[]{:S(2)}) collective-permute-start(bf16[2,2,2,1,1,1,24,768]{7,6,5,4,3,2,1,0:T(8,128)(2,1)} %add_convert_fusion.30), channel_id=1, source_target_pairs={{0,2},{1,3},{2,0},{3,1},{4,6},{5,7},{6,4},{7,5},{8,10},{9,11},{10,... | collective-permute-start | bytes 884744 | tf_op jit(solution)/shard_map/ppermute | solution.py:634
  299.5 16.3 %collective-permute-start.43 = (bf16[8,2,1,1,1,1,24,768]{7,6,0,5,4,3,2,1:T(8,128)(2,1)}, bf16[8,2,1,1,1,1,24,768]{7,6,0,5,4,3,2,1:T(8,128)(2,1)S(1)}, u32[]{:S(2)}, u32[]{:S(2)}) collective-permute-start(bf16[8,2,1,1,1,1,24,768]{7,6,0,5,4,3,2,1:T(8,128)(2,1)} %fusion), channel_id=1, source_target_pairs={{0,8},{1,9},{2,10},{3,11},{4,12},{5,13},{6,14},{7,15},{8,0},{9,1},... | collective-permute-start | bytes 1769480 | tf_op jit(solution)/shard_map/ppermute | solution.py:634
  321.6 18.3 %collective-permute-start.46 = (bf16[4,2,1,1,1,1,24,768]{7,6,5,4,3,2,1,0:T(8,128)(2,1)}, bf16[4,2,1,1,1,1,24,768]{7,6,5,4,3,2,1,0:T(8,128)(2,1)}, u32[]{:S(2)}, u32[]{:S(2)}) collective-permute-start(bf16[4,2,1,1,1,1,24,768]{7,6,5,4,3,2,1,0:T(8,128)(2,1)} %fusion.2), channel_id=1, source_target_pairs={{0,8},{1,9},{2,10},{3,11},{4,12},{5,13},{6,14},{7,15},{8,0},{9,1},... | collective-permute-start | bytes 884744 | tf_op jit(solution)/shard_map/ppermute | solution.py:634
  323.3 18.2 %collective-permute-start.56 = (bf16[8,1,1,1,1,1,24,768]{7,6,0,5,4,3,2,1:T(8,128)(2,1)}, bf16[8,1,1,1,1,1,24,768]{7,6,0,5,4,3,2,1:T(8,128)(2,1)S(1)}, u32[]{:S(2)}, u32[]{:S(2)}) collective-permute-start(bf16[8,1,1,1,1,1,24,768]{7,6,0,5,4,3,2,1:T(8,128)(2,1)} %add_convert_fusion.25), channel_id=1, source_target_pairs={{0,16},{1,17},{2,18},{3,19},{4,20},{5,21},{6,22},{7,23},{8,24},{9,... | collective-permute-start | bytes 884744 | tf_op jit(solution)/shard_map/ppermute | solution.py:634
  323.9 18.7 %collective-permute-start.44 = (bf16[2,2,2,2,1,1,24,768]{7,6,5,4,3,2,1,0:T(8,128)(2,1)}, bf16[2,2,2,2,1,1,24,768]{7,6,5,4,3,2,1,0:T(8,128)(2,1)}, u32[]{:S(2)}, u32[]{:S(2)}) collective-permute-start(bf16[2,2,2,2,1,1,24,768]{7,6,5,4,3,2,1,0:T(8,128)(2,1)} %get-tuple-element.221), channel_id=1, source_target_pairs={{0,2},{1,3},{2,0},{3,1},{4,6},{5,7},{6,4},{7,5},{8,10},{9,11},{10,... | collective-permute-start | bytes 1769480 | tf_op jit(solution)/shard_map/ppermute | solution.py:634
  325.4 14.4 %collective-permute-start.48 = (f32[1,2,2,2,1,1,4,128]{7,6,5,4,3,2,1,0:T(4,128)S(1)}, f32[1,2,2,2,1,1,4,128]{7,6,5,4,3,2,1,0:T(4,128)S(1)}, u32[]{:S(2)}, u32[]{:S(2)}) collective-permute-start(f32[1,2,2,2,1,1,4,128]{7,6,5,4,3,2,1,0:T(4,128)S(1)} %get-tuple-element.268), channel_id=1, source_target_pairs={{0,2},{1,3},{2,0},{3,1},{4,6},{5,7},{6,4},{7,5},{8,10},{9,11},{10,... | collective-permute-start | bytes 49160 | tf_op jit(solution)/shard_map/ppermute | solution.py:634
  326.1 18.3 %collective-permute-start.45 = (bf16[2,2,2,1,2,1,24,768]{7,6,5,4,3,2,1,0:T(8,128)(2,1)}, bf16[2,2,2,1,2,1,24,768]{7,6,5,4,3,2,1,0:T(8,128)(2,1)S(1)}, u32[]{:S(2)}, u32[]{:S(2)}) collective-permute-start(bf16[2,2,2,1,2,1,24,768]{7,6,5,4,3,2,1,0:T(8,128)(2,1)} %get-tuple-element.222), channel_id=1, source_target_pairs={{0,4},{1,5},{2,6},{3,7},{4,0},{5,1},{6,2},{7,3},{8,12},{9,13},{10,... | collective-permute-start | bytes 1769480 | tf_op jit(solution)/shard_map/ppermute | solution.py:634
  (126 other events, 794.9 us)

commit v5 on v4

--- a/solution.py
+++ b/solution.py
@@ -35,7 +35,7 @@
     return pl.BlockSpec(block, index)
 
 
-def run(body, name, grid, operands, in_specs, outs, scratch=(), flops=0, exps=0, limit=20):
+def run(body, name, grid, operands, in_specs, outs, scratch=(), flops=0, exps=0, limit=14):
     moved = sum(o.size * o.dtype.itemsize for o in operands)
     moved += sum(math.prod(s) * jnp.dtype(d).itemsize for s, d, _ in outs)
     return pl.pallas_call(
@@ -362,12 +362,15 @@
     )
 
 
-def ffn_body(first, last, batch, block, len_ref, n_ref, g_ref, b_ref, wi_ref, wo_ref, *refs):
+def ffn_body(first, last, batch, block, split, len_ref, core_ref, n_ref, g_ref, b_ref, wi_ref, wo_ref, *refs):
     refs = list(refs)
     before = [] if first else [refs.pop(0), refs.pop(0)]
     late_ref, vec_ref = (refs.pop(0), refs.pop(0)) if last else (None, None)
-    gn_ref, di_ref, do_ref, sf_ref, f_ref = refs[:5]
-    rest = refs[5:]
+    gn_ref = refs.pop(0)
+    di_refs = [refs.pop(0) for _ in range(split)]
+    do_refs = [refs.pop(0) for _ in range(split)]
+    sf_ref, f_ref = refs[:2]
+    rest = refs[2:]
     s_ref = rest.pop(0) if last else None
     hidden_ref, pre_ref = rest[:2]
     acc_ref = rest[2] if last else f_ref
@@ -399,8 +402,8 @@
 
     lax.fori_loop(0, rows // block, chunk, 0)
     sf_ref[0] = col_sum(pre_ref[...])
-    di_ref[0] = dot_tn(n_ref[...], pre_ref[...]).astype(LOW)
-    do_ref[0] = dot_tn(hidden_ref[...], g_ref[...]).astype(LOW)
+    store_grad(dot_tn(n_ref[...], pre_ref[...]), di_refs, 0, core_ref)
+    store_grad(dot_tn(hidden_ref[...], g_ref[...]), do_refs, 0, core_ref)
     if last:
         @pl.when(step == pl.num_programs(0) - 1)
         def _():
@@ -420,14 +423,14 @@
             lax.fori_loop(0, rows // block, finish, 0)
 
 
-def ffn_stage(lengths, norm, grad, bias, w_in, w_out, before, late, vec, batch, block):
+def ffn_stage(lengths, core, count, norm, grad, bias, w_in, w_out, before, late, vec, batch, block):
     rows, width = norm.shape
     mats = w_in.shape[0]
     first, last = before is None, late is not None
     mat = spec((1, width, width), lambda j: (j, 0, 0))
     line = spec((1, 1, width), lambda j: (j, 0, 0))
-    operands = [lengths, norm, grad, bias, w_in, w_out]
-    specs = [smem(), whole(norm.shape), whole(grad.shape), line, mat, mat]
+    operands = [lengths, core, norm, grad, bias, w_in, w_out]
+    specs = [smem(), smem(), whole(norm.shape), whole(grad.shape), line, mat, mat]
     if not first:
         operands += list(before)
         specs += [whole((rows, width))] * 2
@@ -435,10 +438,11 @@
         operands += [late, vec]
         specs += [whole((rows, width)), whole(vec.shape)]
     fixed = whole((rows, width))
+    grads = grad_outs(mats, width, count, (1, width), lambda j: (j, 0))
     outs = [
         ((rows, width), WIDE, fixed),
-        ((mats, width, width), LOW, mat),
-        ((mats, width, width), LOW, mat),
+        *grads,
+        *grads,
         ((mats, 1, width), WIDE, line),
         ((rows, width), LOW if last else WIDE, fixed),
     ]
@@ -446,8 +450,8 @@
     if last:
         outs.append(((8, width), WIDE, whole((8, width))))
         scratch.append(pltpu.VMEM((rows, width), WIDE))
-    return run(
-        functools.partial(ffn_body, first, last, batch, block),
+    done = run(
+        functools.partial(ffn_body, first, last, batch, block, len(grads)),
         "ffn_stage",
         (mats,),
         tuple(operands),
@@ -456,8 +460,10 @@
         scratch,
         flops=12 * rows * width * width * mats,
         exps=2 * rows * width * mats,
-        limit=44,
-    )
+        limit=30,
+    )
+    split = len(grads)
+    return done[0], done[1 : 1 + split], done[1 + split : 1 + 2 * split], *done[1 + 2 * split :]
 
 
 def late_back_body(gn_ref, late_ref, og_ref, vec_ref, wo, gl_ref, gc_ref, ga_ref, s_ref):
@@ -496,15 +502,41 @@
     )
 
 
-def weights_body(count, *refs):
-    out = refs[-1]
+def store_grad(grad, outs, place, core_ref):
+    if len(outs) == 1:
+        outs[0][place] = grad.astype(LOW)
+        return
+    groups, _, rows, width = outs[0].shape
+    pairs = grad.reshape(groups, 2, rows, width)
+    for core in (0, 1):
+
+        @pl.when(core_ref[0] == core)
+        def _(core=core):
+            outs[0][:, place] = pairs[:, 1 - core].astype(LOW)
+            outs[1][:, place] = pairs[:, core].astype(LOW)
+
+
+def grad_outs(mats, width, count, block, index):
+    rows = width // count
+    if rows % 8 or block[1] % (2 * rows):
+        whole_out = spec(block + (width,), lambda i: index(i) + (0,))
+        return [((mats, width, width), LOW, whole_out)]
+    groups = block[1] // (2 * rows)
+    half = spec((groups, block[0], rows, width), lambda i: index(i)[::-1] + (0, 0))
+    return [((count // 2, mats, rows, width), LOW, half)] * 2
+
+
+def weights_body(count, core_ref, *refs):
+    outs = refs[2 * count :]
     for place in range(count):
-        out[place] = dot_tn(refs[2 * place][...], refs[2 * place + 1][...]).astype(LOW)
-
-
-def weight_grads(pairs, block):
+        grad = dot_tn(refs[2 * place][...], refs[2 * place + 1][...])
+        store_grad(grad, outs, place, core_ref)
+
+
+def weight_grads(pairs, core, count):
     width = pairs[0][0].shape[1]
-    operands, specs = [], []
+    block = width // 2
+    operands, specs = [core], [smem()]
     for left, right in pairs:
         operands += [left, right]
         specs += [spec((left.shape[0], block), lambda j: (0, j)), whole(right.shape)]
@@ -514,9 +546,9 @@
         (width // block,),
         tuple(operands),
         specs,
-        [((len(pairs), width, width), LOW, spec((len(pairs), block, width), lambda j: (0, j, 0)))],
+        grad_outs(len(pairs), width, count, (len(pairs), block), lambda j: (0, j)),
         flops=sum(2 * left.shape[0] * width * width for left, _ in pairs),
-    )[0]
+    )
 
 
 def mid_back_body(gq, wq, mid_ref, gl_ref, vec_ref, wo, gm_ref, gs_ref, ga_ref, s_ref):
@@ -714,55 +746,54 @@
     def __init__(self, parts, count):
         self.count = count
         self.bits = count.bit_length() - 1
-        self.pairs = []
+        self.kind = parts[0][0].dtype
+        self.stages = scatter_stages(count, len(parts))
+        self.sends, self.pairs = [], []
         for part in parts:
-            mats, rows, width = part.shape
-            self.shape = (rows // count, width)
-            self.pairs.append((part.reshape((mats,) + (2,) * self.bits + (rows // count, width)), None))
-        self.stages = scatter_stages(count, len(parts))
-        self.kind = parts[0].dtype
+            if len(part) == 1:
+                mats, rows, width = part[0].shape
+                groups = part[0].reshape(mats, count // 2, 2, rows // count, width)
+                part = [
+                    jnp.swapaxes(lax.dynamic_index_in_dim(groups, side, 2, False), 0, 1)
+                    for side in (1 - own_bit(0), own_bit(0))
+                ]
+            self.shape = part[0].shape[2:]
+            shaped = [v.reshape((2,) * (self.bits - 1) + (1,) + v.shape[1:]) for v in part]
+            self.sends.append(shaped[0])
+            self.pairs.append((shaped[1], None))
 
     def pick(self, pair, bit, side):
-        axis = self.bits - bit
-        values = [
-            lax.dynamic_slice_in_dim(v, side, 1, axis) for v in pair if v is not None
-        ]
-        if len(values) == 1:
-            return values[0]
-        return (values[0].astype(jnp.float32) + values[1].astype(jnp.float32)).astype(self.kind)
-
-    def prepare(self):
+        axis = self.bits - 1 - bit
+        values = [lax.dynamic_slice_in_dim(v, side, 1, axis) for v in pair]
+        return self.total(values, self.kind)
+
+    def total(self, pair, kind):
+        return (pair[0].astype(WIDE) + pair[1].astype(WIDE)).astype(kind)
+
+    def ready(self):
+        if self.sends is not None:
+            return self.sends
         step = self.stages[0][0]
         if len(step) == 1 and len(self.pairs) == 2:
             self.pairs = [
-                (jnp.concatenate([self.total(p, self.kind) for p in self.pairs]), None)
+                tuple(jnp.concatenate([p[i] for p in self.pairs], self.bits) for i in (0, 1))
             ]
         return [self.pick(pair, bit, 1 - own_bit(bit)) for bit, pair in zip(step, self.pairs)]
 
-    def ready(self):
-        return self.prepare()
-
-    def total(self, pair, kind):
-        if pair[1] is None:
-            return pair[0]
-        return (pair[0].astype(jnp.float32) + pair[1].astype(jnp.float32)).astype(kind)
-
     def launch(self, sends):
-        steps = self.stages.pop(0)
-        for place, step in enumerate(steps):
+        for place, step in enumerate(self.stages.pop(0)):
             if place:
-                self.stages.insert(0, [step])
-                sends = self.prepare()
-                self.stages.pop(0)
+                sends = [self.pick(p, b, 1 - own_bit(b)) for b, p in zip(step, self.pairs)]
             flight = [swap(v, bit, self.count) for bit, v in zip(step, sends)]
-            self.pairs = [
-                (self.pick(pair, bit, own_bit(bit)), other)
-                for bit, pair, other in zip(step, self.pairs, flight)
-            ]
+            if self.sends is None:
+                kept = [self.pick(p, bit, own_bit(bit)) for bit, p in zip(step, self.pairs)]
+            else:
+                kept, self.sends = [p[0] for p in self.pairs], None
+            self.pairs = list(zip(kept, flight))
 
     def result(self):
-        total = jnp.concatenate([self.total(p, jnp.float32) for p in self.pairs])
-        return total.astype(jnp.float32).reshape((total.shape[0],) + self.shape)
+        total = jnp.concatenate([self.total(p, WIDE) for p in self.pairs], self.bits)
+        return total.reshape((-1,) + self.shape)
 
 
 def tick(chains, values=()):
@@ -807,6 +838,7 @@
     g_cross = Gather(jnp.concatenate([attn_in[3:4], attn_out[1:2], attn_in[4:6]]), count)
     g_ffn = Gather(jnp.concatenate([fc_in_mats, fc_out_mats]), count)
 
+    core = own_bit(0).astype(jnp.int32).reshape(1)
     x = hidden_in.reshape(rows, width)
     frames = encoder_states.reshape(-1, width)
     valid = jnp.arange(length)[None, :, None] < lengths[:, None, None]
@@ -823,11 +855,13 @@
     bias = small[:, 13 * share : small_count].reshape(count, mats, share)
     bias = bias.transpose(1, 0, 2).reshape(mats, 1, width)
     self_a, self_b = g_self.result()
+    x = tick([g_cross], x)
     norm_one, query, key, value = qkv(x, vec, self_a, self_b, block)
-    query, key, value = tick([g_cross, g_ffn], (query, key, value))
+    query, key, value = tick([g_ffn], (query, key, value))
     attended = attend(query, key, value, batch, True)
     mid, norm_two, square_self = mid_stage(lengths, attended, x, vec, self_b, batch, block)
-    norm_two = tick([g_cross, g_ffn], norm_two)
+    norm_two = tick([g_cross], norm_two)
+    norm_two = tick([g_ffn], norm_two)
     cross_a, cross_b = g_cross.result()
     cross_q, cross_k, cross_v = cross_stage(norm_two, frames, vec, cross_a, cross_b, batch)
     cross_attended = attend(cross_q, cross_k, cross_v, batch, False)
@@ -835,7 +869,7 @@
     norm_three = tick([g_ffn], norm_three)
     w_in, w_out = g_ffn.result()
     grad_norm, d_in, d_out, sums_ff, result, square_rest = ffn_stage(
-        lengths, norm_three, grad, bias, w_in, w_out, None, late, vec, batch, block
+        lengths, core, count, norm_three, grad, bias, w_in, w_out, None, late, vec, batch, block
     )
     s_ffn = Scatter([d_in, d_out], count)
     grad_norm = tick([s_ffn], grad_norm)
@@ -846,8 +880,8 @@
     grad_cq, grad_ck, grad_cv = attend_back(
         cross_q, cross_k, cross_v, grad_cross_att, batch, False
     )
-    d_cross_a = weight_grads([(norm_two, grad_cq), (cross_attended, grad_cross)], width // 3)
-    d_cross_b = weight_grads([(frames, grad_ck), (frames, grad_cv)], width // 3)
+    d_cross_a = weight_grads([(norm_two, grad_cq), (cross_attended, grad_cross)], core, count)
+    d_cross_b = weight_grads([(frames, grad_ck), (frames, grad_cv)], core, count)
     s_cross = Scatter([d_cross_a, d_cross_b], count)
     grad_cq, grad_ck, grad_cv = tick([s_cross], (grad_cq, grad_ck, grad_cv))
     grad_mid, grad_self, grad_att, sums_mid = mid_back(
@@ -856,8 +890,8 @@
     grad_frames, sums_frames = frames_back(grad_ck, grad_cv, cross_b, frame_rows)
     grad_att, grad_frames = tick([s_cross, s_ffn], (grad_att, grad_frames))
     grad_q, grad_k, grad_v = attend_back(query, key, value, grad_att, batch, True)
-    d_self_a = weight_grads([(norm_one, grad_q), (norm_one, grad_k)], width // 3)
-    d_self_b = weight_grads([(norm_one, grad_v), (attended, grad_self)], width // 3)
+    d_self_a = weight_grads([(norm_one, grad_q), (norm_one, grad_k)], core, count)
+    d_self_b = weight_grads([(norm_one, grad_v), (attended, grad_self)], core, count)
     s_self = Scatter([d_self_a, d_self_b], count)
     grad_q, grad_k, grad_v = tick([s_self, s_cross, s_ffn], (grad_q, grad_k, grad_v))
     grad_in, sums_one = in_back(grad_q, grad_k, grad_v, self_a, self_b, x, grad_mid, vec, block)
@@ -880,7 +914,7 @@
         1,
     )
     sums = jnp.pad(sums, ((0, 0), (0, small_size - sums.shape[1])))
-    s_small = Scatter([sums.reshape(1, count * small_rows, 128)], count)
+    s_small = Scatter([[sums.reshape(1, count * small_rows, 128)]], count)
     tick([s_small])
     tick([s_small])
     tick([s_self, s_cross, s_small])

time: 388 us -> 364 us (0.938)
  waiting for transfers between devices: 106 us -> 90.6 us
  local copies, waits for them, and re-layouts: 64.4 us -> 53.5 us
  Pallas kernels: 108 us -> 116 us
  other arithmetic: 47.4 us -> 41.3 us
    ppermute x58, waiting for transfers between devices: 106 us -> 90.6 us  [swap(): lax.ppermute(values, 'fsdp', [(i, i ^ 1 << bit) for i in range(count)])]
    dynamic_slice x8 -> x3, local copies, waits for them, and re-layouts: 9.02 us -> 0.02 us  [__init__(): lax.dynamic_index_in_dim(groups, side, 2, False)]
    pallas_call x20, Pallas kernels: 108 us -> 116 us  [run(): pl.pallas_call(body, name=name, grid=grid, in_specs=in_specs, out_specs=[...]
    unnamed x197 -> x182, local copies, waits for them, and re-layouts: 30.2 us -> 25.9 us
    convert_element_type x21 -> x18, other arithmetic: 28.3 us -> 24.1 us  [total(): return (pair[0].astype(WIDE) + pair[1].astype(WIDE)).astype(kind)]
  transfers between devices with their start and end apart: 58 -> 58, of which waited for: 29 -> 28; matrix products, arithmetic and copies ran while one was open for 15% -> 15% of each run, Pallas kernels for 14% -> 20%
where the time goes in v5:
time: 364 us; the launch traced here: 358 us
  Pallas kernels  116 us (32%)
  waiting for transfers between devices  90.6 us (25%)
  local copies, waits for them, and re-layouts  53.5 us (15%)
  starting transfers between devices  52.8 us (15%)
  other arithmetic  41.3 us (11%)
    pallas_call x20, Pallas kernels, run(): pl.pallas_call(body, name=name, grid=grid, in_specs=in_specs, out_specs=[...  116 us
    ppermute x58, waiting for transfers between devices, swap(): lax.ppermute(values, 'fsdp', [(i, i ^ 1 << bit) for i in range(count)])  90.6 us
    ppermute x58, starting transfers between devices, swap(): lax.ppermute(values, 'fsdp', [(i, i ^ 1 << bit) for i in range(count)])  52.8 us
    unnamed x182, local copies, waits for them, and re-layouts  25.9 us
    convert_element_type x18, other arithmetic, total(): return (pair[0].astype(WIDE) + pair[1].astype(WIDE)).astype(kind)  24.1 us
    select_n x22, other arithmetic, land(): jnp.where(own_bit(bit) == 0, jnp.concatenate([held, other], axis), jnp.co...  8.35 us
  transfers between devices with their start and end apart: 58, of which 28 were waited for; matrix products, arithmetic and copies ran while one was open for 15% of the time, Pallas kernels for 20%

profile of v5, /device:TPU:0, one launch (start us, length us, event | category | flops | bytes accessed | tf_op | source)
XLA Modules:
  0.0 357.5 jit_solution(14701238697962589079)
XLA Ops:
  4.7 4.1 %collective-permute-start = (bf16[1,1,1,1,1,4,24,768]{7,6,5,4,3,2,1,0:T(8,128)(2,1)S(1)}, bf16[1,1,1,1,1,4,24,768]{7,6,5,4,3,2,1,0:T(8,128)(2,1)S(1)}, u32[]{:S(2)}, u32[]{:S(2)}) collective-permute-start(bf16[1,1,1,1,1,4,24,768]{7,6,5,4,3,2,1,0:T(8,128)(2,1)S(1)} %maximum_bitcast_fusion.1), channel_id=1, source_target_pairs={{0,16},{1,17},{2,18},{3,19},{4,20},{5,21},{6,22},{7,23},{8,24},{9,... | collective-permute-start | bytes 442376 | tf_op jit(solution)/shard_map/ppermute | solution.py:666
  8.9 7.0 %collective-permute-done.1 = bf16[1,1,1,1,1,1,4,128]{7,6,5,4,3,2,1,0:T(4,128)(2,1)S(1)} collective-permute-done((bf16[1,1,1,1,1,1,4,128]{7,6,5,4,3,2,1,0:T(4,128)(2,1)S(1)}, bf16[1,1,1,1,1,1,4,128]{7,6,5,4,3,2,1,0:T(4,128)(2,1)S(1)}, u32[]{:S(2)}, u32[]{:S(2)}) %collective-permute-start.1) | collective-permute-done | bytes 1056 | tf_op jit(solution)/shard_map/ppermute | solution.py:666
  20.7 3.5 collective-permute-done.3
  25.7 3.3 collective-permute-start.7
  31.2 4.2 %collective-permute-done.7 = bf16[1,1,1,1,1,4,24,768]{7,6,5,4,3,2,1,0:T(8,128)(2,1)S(1)} collective-permute-done((bf16[1,1,1,1,1,4,24,768]{7,6,5,4,3,2,1,0:T(8,128)(2,1)S(1)}, bf16[1,1,1,1,1,4,24,768]{7,6,5,4,3,2,1,0:T(8,128)(2,1)S(1)}, u32[]{:S(2)}, u32[]{:S(2)}) %collective-permute-start.7) | collective-permute-done | bytes 147488 | tf_op jit(solution)/shard_map/ppermute | solution.py:666
  43.4 6.5 %collective-permute-done.11 = bf16[2,1,1,1,1,4,24,768]{7,6,5,4,3,2,1,0:T(8,128)(2,1)S(1)} collective-permute-done((bf16[2,1,1,1,1,4,24,768]{7,6,5,4,3,2,1,0:T(8,128)(2,1)S(1)}, bf16[2,1,1,1,1,4,24,768]{7,6,5,4,3,2,1,0:T(8,128)(2,1)S(1)}, u32[]{:S(2)}, u32[]{:S(2)}) %collective-permute-start.11) | collective-permute-done | bytes 294944 | tf_op jit(solution)/shard_map/ppermute | solution.py:666
  50.0 2.7 collective-permute-done.12
  57.2 3.3 collective-permute-done.16
  67.0 2.6 collective-permute-done.15
  76.6 3.8 %qkv.1 = (bf16[640,768]{1,0:T(8,128)(2,1)S(1)}, bf16[640,768]{1,0:T(8,128)(2,1)S(1)}, bf16[640,768]{1,0:T(8,128)(2,1)S(1)}, bf16[640,768]{1,0:T(8,128)(2,1)S(1)}) custom-call(bf16[640,768]{1,0:T(8,128)(2,1)S(1)} %bitcast.120, f32[16,768]{1,0:T(8,128)S(1)} %pad.13.vec_ref.refs_1_, bf16[2,768,768]{2,1,0:T(8,128)(2,1)S(1)} %bitcast.110, ...), custom_call_target="tpu_custom_call" | custom-call | flops 2264924160 | bytes 12042240 | tf_op jit(solution)/shard_map/qkv/pallas_call | solution.py:41
  83.4 3.5 collective-permute-done.21
  88.7 5.4 %attend_self.1.a_ref.refs_2_ = bf16[640,768]{1,0:T(8,128)(2,1)S(1)} custom-call(bf16[640,768]{1,0:T(8,128)(2,1)S(1)} %get-tuple-element.167.q_ref, bf16[640,768]{1,0:T(8,128)(2,1)S(1)} %get-tuple-element.168.k_ref, bf16[640,768]{1,0:T(8,128)(2,1)S(1)} %get-tuple-element.169.v_ref), custom_call_target="tpu_custom_call" | custom-call | flops 629145600 | bytes 3932160 | tf_op jit(solution)/shard_map/attend_self/pallas_call | solution.py:41
  94.1 3.0 mid_stage.1
  104.6 3.2 attend_cross.1.a_ref.refs_2_
  107.9 3.0 late_stage.1
  112.2 13.8 %collective-permute-done.23 = bf16[2,2,2,1,1,4,24,768]{7,6,5,4,3,2,1,0:T(8,128)(2,1)S(1)} collective-permute-done((bf16[2,2,2,1,1,4,24,768]{7,6,5,4,3,2,1,0:T(8,128)(2,1)S(1)}, bf16[2,2,2,1,1,4,24,768]{7,6,5,4,3,2,1,0:T(8,128)(2,1)S(1)}, u32[]{:S(2)}, u32[]{:S(2)}) %collective-permute-start.23) | collective-permute-done | bytes 1179680 | tf_op jit(solution)/shard_map/ppermute | solution.py:666
  134.3 3.4 collective-permute-done.28
  137.7 4.9 %weave.5 = (bf16[4,16,2,24,768]{4,3,2,1,0:T(8,128)(2,1)S(1)}, bf16[4,16,2,24,768]{4,3,2,1,0:T(8,128)(2,1)S(1)}) custom-call(s32[1]{0:T(128)} %bitcast.core_ref, bf16[16,4,24,768]{3,2,1,0:T(8,128)(2,1)} %bitcast.25.refs_0_, bf16[16,4,24,768]{3,2,1,0:T(8,128)(2,1)} %bitcast.26.refs_1_, bf16[16,4,24,768]{3,2,1,0:T(8,128)(2,1)} %bitcast.27.refs_2_, ...), custom_call_target="tpu_custom_call" | custom-call | bytes 18874372 | tf_op jit(solution)/shard_map/weave/pallas_call | solution.py:41
  142.5 39.0 %ffn_stage.1 = (f32[640,768]{1,0:T(8,128)S(1)}, bf16[16,4,24,768]{3,2,1,0:T(8,128)(2,1)}, bf16[16,4,24,768]{3,2,1,0:T(8,128)(2,1)S(1)}, bf16[16,4,24,768]{3,2,1,...) custom-call(s32[2]{0:T(128)S(1)} %copy-done.46, ...), custom_call_target="tpu_custom_call" | custom-call | flops 18119393280 | bytes 25853964 | tf_op jit(solution)/shard_map/ffn_stage/pallas_call | solution.py:41
  189.4 3.7 %late_back.1 = (f32[640,768]{1,0:T(8,128)S(1)}, bf16[640,768]{1,0:T(8,128)(2,1)S(1)}, bf16[640,768]{1,0:T(8,128)(2,1)S(1)}, f32[8,768]{1,0:T(8,128)S(1)}) custom-call(f32[640,768]{1,0:T(8,128)S(1)} %copy-done.25, f32[640,768]{1,0:T(8,128)S(1)} %copy-done.23, bf16[640,768]{1,0:T(8,128)(2,1)S(1)} %bitcast.119, f32[16,768]{1,0:T(8,128)S(1)} %pad.13.vec_ref.refs_1_, ...), custom_call_target="tpu_custom_call" | custom-call | flops 754974720 | bytes 11280384 | tf_op jit(solution)/shard_map/late_back/pallas_call | solution.py:41
  199.3 5.4 %attend_cross_back.1 = (bf16[640,768]{1,0:T(8,128)(2,1)S(1)}, bf16[256,768]{1,0:T(8,128)(2,1)S(1)}, bf16[256,768]{1,0:T(8,128)(2,1)S(1)}) custom-call(bf16[640,768]{1,0:T(8,128)(2,1)S(1)} %copy-done.14, bf16[256,768]{1,0:T(8,128)(2,1)S(1)} %copy-done.27, bf16[256,768]{1,0:T(8,128)(2,1)S(1)} %copy-done.29, bf16[640,768]{1,0:T(8,128)(2,1)S(1)} %get-tuple-element.201.g_ref), custom_call_target="tpu_custom_call" | custom-call | flops 629145600 | bytes 4521984 | tf_op jit(solution)/shard_map/attend_cross_back/pallas_call | solution.py:41
  206.7 3.7 %weight_grads.4 = (bf16[16,2,24,768]{3,2,1,0:T(8,128)(2,1)S(1)}, bf16[16,2,24,768]{3,2,1,0:T(8,128)(2,1)S(1)}) custom-call(s32[1]{0:T(128)} %bitcast.core_ref, bf16[640,768]{1,0:T(8,128)(2,1)S(1)} %copy-done.43, bf16[640,768]{1,0:T(8,128)(2,1)S(1)} %get-tuple-element.214.refs_1_.gq, bf16[640,768]{1,0:T(8,128)(2,1)S(1)} %copy-done.12, ...), custom_call_target="tpu_custom_call" | custom-call | flops 1509949440 | bytes 6291460 | tf_op jit(solution)/shard_map/weight_grads/pallas_call | solution.py:41
  214.1 5.6 %mid_back.1 = (f32[640,768]{1,0:T(8,128)S(1)}, bf16[640,768]{1,0:T(8,128)(2,1)S(1)}, bf16[640,768]{1,0:T(8,128)(2,1)S(1)}, f32[8,768]{1,0:T(8,128)S(1)}) custom-call(bf16[640,768]{1,0:T(8,128)(2,1)S(1)} %get-tuple-element.214.refs_1_.gq, bf16[2,768,768]{2,1,0:T(8,128)(2,1)S(1)} %bitcast.101, f32[640,768]{1,0:T(8,128)S(1)} %copy-done.8, ...), custom_call_target="tpu_custom_call" | custom-call | flops 1509949440 | bytes 13639680 | tf_op jit(solution)/shard_map/mid_back/pallas_call | solution.py:41
  219.7 6.5 %collective-permute-done.33 = bf16[2,2,2,1,1,4,24,768]{7,6,5,4,3,2,1,0:T(8,128)(2,1)S(1)} collective-permute-done((bf16[2,2,2,1,1,4,24,768]{7,6,5,4,3,2,1,0:T(8,128)(2,1)S(1)}, bf16[2,2,2,1,1,4,24,768]{7,6,5,4,3,2,1,0:T(8,128)(2,1)S(1)}, u32[]{:S(2)}, u32[]{:S(2)}) %collective-permute-start.33) | collective-permute-done | bytes 1179680 | tf_op jit(solution)/shard_map/ppermute | solution.py:666
  240.1 9.9 %attend_self_back.1 = (bf16[640,768]{1,0:T(8,128)(2,1)S(1)}, bf16[640,768]{1,0:T(8,128)(2,1)S(1)}, bf16[640,768]{1,0:T(8,128)(2,1)S(1)}) custom-call(bf16[640,768]{1,0:T(8,128)(2,1)S(1)} %copy-done.55, bf16[640,768]{1,0:T(8,128)(2,1)S(1)} %copy-done.57, bf16[640,768]{1,0:T(8,128)(2,1)S(1)} %copy-done.59, bf16[640,768]{1,0:T(8,128)(2,1)S(1)} %copy-done.49), custom_call_target="tpu_custom_call" | custom-call | flops 1572864000 | bytes 6881280 | tf_op jit(solution)/shard_map/attend_self_back/pallas_call | solution.py:41
  251.6 4.5 %weight_grads.7 = (bf16[16,2,24,768]{3,2,1,0:T(8,128)(2,1)}, bf16[16,2,24,768]{3,2,1,0:T(8,128)(2,1)S(1)}) custom-call(s32[1]{0:T(128)} %bitcast.core_ref, bf16[640,768]{1,0:T(8,128)(2,1)S(1)} %copy-done.53, bf16[640,768]{1,0:T(8,128)(2,1)S(1)} %get-tuple-element.233.refs_1_.gv, bf16[640,768]{1,0:T(8,128)(2,1)S(1)} %copy-done.35, ...), custom_call_target="tpu_custom_call" | custom-call | flops 1509949440 | bytes 6291460 | tf_op jit(solution)/shard_map/weight_grads/pallas_call | solution.py:41
  257.2 4.5 %weight_grads.6 = (bf16[16,2,24,768]{3,2,1,0:T(8,128)(2,1)}, bf16[16,2,24,768]{3,2,1,0:T(8,128)(2,1)S(1)}) custom-call(s32[1]{0:T(128)} %bitcast.core_ref, bf16[640,768]{1,0:T(8,128)(2,1)S(1)} %copy-done.53, bf16[640,768]{1,0:T(8,128)(2,1)S(1)} %get-tuple-element.231.refs_1_.gq, bf16[640,768]{1,0:T(8,128)(2,1)S(1)} %copy-done.53, ...), custom_call_target="tpu_custom_call" | custom-call | flops 1509949440 | bytes 6291460 | tf_op jit(solution)/shard_map/weight_grads/pallas_call | solution.py:41
  282.6 7.0 %in_back.1 = (bf16[640,768]{1,0:T(8,128)(2,1)}, f32[8,768]{1,0:T(8,128)S(1)}) custom-call(bf16[640,768]{1,0:T(8,128)(2,1)S(1)} %copy-done.37, bf16[640,768]{1,0:T(8,128)(2,1)S(1)} %copy-done.39, bf16[640,768]{1,0:T(8,128)(2,1)S(1)} %copy-done.41, bf16[2,768,768]{2,1,0:T(8,128)(2,1)S(1)} %bitcast.112, bf16[2,768,768]{2,1,0:T(8,128)(2,1)S(1)} %bitcast.113, ...), custom_call_target="tpu_custom_call" | custom-call | flops 2264924160 | bytes 14032896 | tf_op jit(solution)/shard_map/in_back/pallas_call | solution.py:41
  304.3 11.9 %collective-permute-done.48 = f32[2,2,2,1,1,1,4,128]{7,3,2,1,0,6,5,4:T(1,128)} collective-permute-done((f32[2,2,2,1,1,1,4,128]{7,3,2,1,0,6,5,4:T(1,128)}, f32[2,2,2,1,1,1,4,128]{7,3,2,1,0,6,5,4:T(1,128)}, u32[]{:S(2)}, u32[]{:S(2)}) %collective-permute-start.48) | collective-permute-done | bytes 16416 | tf_op jit(solution)/shard_map/ppermute | solution.py:666
  323.4 2.6 collective-permute-start.55
  334.8 4.5 %collective-permute-done.49 = bf16[2,2,1,1,1,2,24,768]{7,6,5,4,3,2,1,0:T(8,128)(2,1)S(1)} collective-permute-done((bf16[2,2,1,1,1,2,24,768]{7,6,5,4,3,2,1,0:T(8,128)(2,1)S(1)}, bf16[2,2,1,1,1,2,24,768]{7,6,5,4,3,2,1,0:T(8,128)(2,1)S(1)}, u32[]{:S(2)}, u32[]{:S(2)}) %collective-permute-start.49) | collective-permute-done | bytes 294944 | tf_op jit(solution)/shard_map/ppermute | solution.py:666
  343.4 3.7 %collective-permute-done.52 = bf16[2,1,1,1,1,4,24,768]{7,6,5,4,3,2,1,0:T(8,128)(2,1)S(1)} collective-permute-done((bf16[2,1,1,1,1,4,24,768]{7,6,5,4,3,2,1,0:T(8,128)(2,1)S(1)}, bf16[2,1,1,1,1,4,24,768]{7,6,5,4,3,2,1,0:T(8,128)(2,1)S(1)}, u32[]{:S(2)}, u32[]{:S(2)}) %collective-permute-start.52) | collective-permute-done | bytes 294944 | tf_op jit(solution)/shard_map/ppermute | solution.py:666
  (409 shorter events, 160.0 us)
Async XLA Ops:
  37.2 12.8 %collective-permute-start.11 = (bf16[2,1,1,1,1,4,24,768]{7,6,5,4,3,2,1,0:T(8,128)(2,1)S(1)}, bf16[2,1,1,1,1,4,24,768]{7,6,5,4,3,2,1,0:T(8,128)(2,1)S(1)}, u32[]{:S(2)}, u32[]{:S(2)}) collective-permute-start(bf16[2,1,1,1,1,4,24,768]{7,6,5,4,3,2,1,0:T(8,128)(2,1)S(1)} %maximum_select_fusion.17), channel_id=1, source_target_pairs={{0,8},{1,9},{2,10},{3,11},{4,12},{5,13},{6,14},{7,15},{8,0},{9,1},... | collective-permute-start | bytes 884744 | tf_op jit(solution)/shard_map/ppermute | solution.py:666
  38.7 14.1 %collective-permute-start.12 = (bf16[1,1,1,1,1,8,24,768]{7,6,5,4,3,2,1,0:T(8,128)(2,1)S(1)}, bf16[1,1,1,1,1,8,24,768]{7,6,5,4,3,2,1,0:T(8,128)(2,1)S(1)}, u32[]{:S(2)}, u32[]{:S(2)}) collective-permute-start(bf16[1,1,1,1,1,8,24,768]{7,6,5,4,3,2,1,0:T(8,128)(2,1)S(1)} %maximum_bitcast_fusion), channel_id=1, source_target_pairs={{0,16},{1,17},{2,18},{3,19},{4,20},{5,21},{6,22},{7,23},{8,24},{9,... | collective-permute-start | bytes 884744 | tf_op jit(solution)/shard_map/ppermute | solution.py:666
  41.2 14.3 %collective-permute-start.8 = (bf16[2,2,2,1,1,2,24,768]{7,6,5,4,3,2,1,0:T(8,128)(2,1)S(1)}, bf16[2,2,2,1,1,2,24,768]{7,6,5,4,3,2,1,0:T(8,128)(2,1)S(1)}, u32[]{:S(2)}, u32[]{:S(2)}) collective-permute-start(bf16[2,2,2,1,1,2,24,768]{7,6,5,4,3,2,1,0:T(8,128)(2,1)S(1)} %maximum_select_fusion.10), channel_id=1, source_target_pairs={{0,2},{1,3},{2,0},{3,1},{4,6},{5,7},{6,4},{7,5},{8,10},{9,11},{10,... | collective-permute-start | bytes 1769480 | tf_op jit(solution)/shard_map/ppermute | solution.py:666
  41.7 13.9 %collective-permute-start.9 = (bf16[2,2,1,2,1,2,24,768]{7,6,5,4,3,2,1,0:T(8,128)(2,1)S(1)}, bf16[2,2,1,2,1,2,24,768]{7,6,5,4,3,2,1,0:T(8,128)(2,1)S(1)}, u32[]{:S(2)}, u32[]{:S(2)}) collective-permute-start(bf16[2,2,1,2,1,2,24,768]{7,6,5,4,3,2,1,0:T(8,128)(2,1)S(1)} %maximum_select_fusion.11), channel_id=1, source_target_pairs={{0,4},{1,5},{2,6},{3,7},{4,0},{5,1},{6,2},{7,3},{8,12},{9,13},{10,... | collective-permute-start | bytes 1769480 | tf_op jit(solution)/shard_map/ppermute | solution.py:666
  55.8 18.6 %collective-permute-start.17 = (bf16[2,2,2,2,1,2,24,768]{7,6,5,4,3,2,1,0:T(8,128)(2,1)S(1)}, bf16[2,2,2,2,1,2,24,768]{7,6,5,4,3,2,1,0:T(8,128)(2,1)}, u32[]{:S(2)}, u32[]{:S(2)}) collective-permute-start(bf16[2,2,2,2,1,2,24,768]{7,6,5,4,3,2,1,0:T(8,128)(2,1)S(1)} %maximum_select_fusion.2), channel_id=1, source_target_pairs={{0,1},{1,0},{2,3},{3,2},{4,5},{5,4},{6,7},{7,6},{8,9},{9,8},{10,11... | collective-permute-start | bytes 3538952 | tf_op jit(solution)/shard_map/ppermute | solution.py:666
  55.8 18.5 %collective-permute-start.18 = (bf16[2,2,2,2,1,2,24,768]{7,6,5,4,3,2,1,0:T(8,128)(2,1)S(1)}, bf16[2,2,2,2,1,2,24,768]{7,6,5,4,3,2,1,0:T(8,128)(2,1)}, u32[]{:S(2)}, u32[]{:S(2)}) collective-permute-start(bf16[2,2,2,2,1,2,24,768]{7,6,5,4,3,2,1,0:T(8,128)(2,1)S(1)} %maximum_select_fusion.3), channel_id=1, source_target_pairs={{0,1},{1,0},{2,3},{3,2},{4,5},{5,4},{6,7},{7,6},{8,9},{9,8},{10,11... | collective-permute-start | bytes 3538952 | tf_op jit(solution)/shard_map/ppermute | solution.py:666
  56.3 16.5 %collective-permute-start.13 = (bf16[2,1,1,1,1,8,24,768]{7,6,5,4,3,2,1,0:T(8,128)(2,1)S(1)}, bf16[2,1,1,1,1,8,24,768]{7,6,5,4,3,2,1,0:T(8,128)(2,1)}, u32[]{:S(2)}, u32[]{:S(2)}) collective-permute-start(bf16[2,1,1,1,1,8,24,768]{7,6,5,4,3,2,1,0:T(8,128)(2,1)S(1)} %maximum_select_fusion.13), channel_id=1, source_target_pairs={{0,8},{1,9},{2,10},{3,11},{4,12},{5,13},{6,14},{7,15},{8,0},{9,1},... | collective-permute-start | bytes 1769480 | tf_op jit(solution)/shard_map/ppermute | solution.py:666
  70.8 16.1 %collective-permute-start.21 = (bf16[2,2,2,1,1,2,24,768]{7,6,5,4,3,2,1,0:T(8,128)(2,1)S(1)}, bf16[2,2,2,1,1,2,24,768]{7,6,5,4,3,2,1,0:T(8,128)(2,1)S(1)}, u32[]{:S(2)}, u32[]{:S(2)}) collective-permute-start(bf16[2,2,2,1,1,2,24,768]{7,6,5,4,3,2,1,0:T(8,128)(2,1)S(1)} %maximum_select_fusion.14), channel_id=1, source_target_pairs={{0,2},{1,3},{2,0},{3,1},{4,6},{5,7},{6,4},{7,5},{8,10},{9,11},{10,... | collective-permute-start | bytes 1769480 | tf_op jit(solution)/shard_map/ppermute | solution.py:666
  72.3 16.2 %collective-permute-start.22 = (bf16[2,2,1,2,1,2,24,768]{7,6,5,4,3,2,1,0:T(8,128)(2,1)S(1)}, bf16[2,2,1,2,1,2,24,768]{7,6,5,4,3,2,1,0:T(8,128)(2,1)S(1)}, u32[]{:S(2)}, u32[]{:S(2)}) collective-permute-start(bf16[2,2,1,2,1,2,24,768]{7,6,5,4,3,2,1,0:T(8,128)(2,1)S(1)} %maximum_select_fusion.15), channel_id=1, source_target_pairs={{0,4},{1,5},{2,6},{3,7},{4,0},{5,1},{6,2},{7,3},{8,12},{9,13},{10,... | collective-permute-start | bytes 1769480 | tf_op jit(solution)/shard_map/ppermute | solution.py:666
  81.3 17.9 %collective-permute-start.19 = (bf16[2,2,1,1,1,4,24,768]{7,6,5,4,3,2,1,0:T(8,128)(2,1)S(1)}, bf16[2,2,1,1,1,4,24,768]{7,6,5,4,3,2,1,0:T(8,128)(2,1)S(1)}, u32[]{:S(2)}, u32[]{:S(2)}) collective-permute-start(bf16[2,2,1,1,1,4,24,768]{7,6,5,4,3,2,1,0:T(8,128)(2,1)S(1)} %get-tuple-element.163), channel_id=1, source_target_pairs={{0,4},{1,5},{2,6},{3,7},{4,0},{5,1},{6,2},{7,3},{8,12},{9,13},{10,... | collective-permute-start | bytes 1769480 | tf_op jit(solution)/shard_map/ppermute | solution.py:666
  82.8 16.5 %collective-permute-start.20 = (bf16[2,2,1,1,1,4,24,768]{7,6,5,4,3,2,1,0:T(8,128)(2,1)S(1)}, bf16[2,2,1,1,1,4,24,768]{7,6,5,4,3,2,1,0:T(8,128)(2,1)S(1)}, u32[]{:S(2)}, u32[]{:S(2)}) collective-permute-start(bf16[2,2,1,1,1,4,24,768]{7,6,5,4,3,2,1,0:T(8,128)(2,1)S(1)} %get-tuple-element.164), channel_id=1, source_target_pairs={{0,2},{1,3},{2,0},{3,1},{4,6},{5,7},{6,4},{7,5},{8,10},{9,11},{10,... | collective-permute-start | bytes 1769480 | tf_op jit(solution)/shard_map/ppermute | solution.py:666
  99.5 26.6 %collective-permute-start.23 = (bf16[2,2,2,1,1,4,24,768]{7,6,5,4,3,2,1,0:T(8,128)(2,1)S(1)}, bf16[2,2,2,1,1,4,24,768]{7,6,5,4,3,2,1,0:T(8,128)(2,1)S(1)}, u32[]{:S(2)}, u32[]{:S(2)}) collective-permute-start(bf16[2,2,2,1,1,4,24,768]{7,6,5,4,3,2,1,0:T(8,128)(2,1)S(1)} %maximum_select_fusion.5), channel_id=1, source_target_pairs={{0,2},{1,3},{2,0},{3,1},{4,6},{5,7},{6,4},{7,5},{8,10},{9,11},{10,... | collective-permute-start | bytes 3538952 | tf_op jit(solution)/shard_map/ppermute | solution.py:666
  100.1 27.6 %collective-permute-start.24 = (bf16[2,2,1,2,1,4,24,768]{7,6,5,4,3,2,1,0:T(8,128)(2,1)S(1)}, bf16[2,2,1,2,1,4,24,768]{7,6,5,4,3,2,1,0:T(8,128)(2,1)S(1)}, u32[]{:S(2)}, u32[]{:S(2)}) collective-permute-start(bf16[2,2,1,2,1,4,24,768]{7,6,5,4,3,2,1,0:T(8,128)(2,1)S(1)} %maximum_select_fusion.6), channel_id=1, source_target_pairs={{0,4},{1,5},{2,6},{3,7},{4,0},{5,1},{6,2},{7,3},{8,12},{9,13},{10,... | collective-permute-start | bytes 3538952 | tf_op jit(solution)/shard_map/ppermute | solution.py:666
  198.2 28.1 %collective-permute-start.33 = (bf16[2,2,2,1,1,4,24,768]{7,6,5,4,3,2,1,0:T(8,128)(2,1)S(1)}, bf16[2,2,2,1,1,4,24,768]{7,6,5,4,3,2,1,0:T(8,128)(2,1)S(1)}, u32[]{:S(2)}, u32[]{:S(2)}) collective-permute-start(bf16[2,2,2,1,1,4,24,768]{7,6,5,4,3,2,1,0:T(8,128)(2,1)S(1)} %get-tuple-element.212), channel_id=1, source_target_pairs={{0,2},{1,3},{2,0},{3,1},{4,6},{5,7},{6,4},{7,5},{8,10},{9,11},{10,... | collective-permute-start | bytes 3538952 | tf_op jit(solution)/shard_map/ppermute | solution.py:666
  198.8 28.8 %collective-permute-start.34 = (bf16[2,2,1,2,1,4,24,768]{7,6,5,4,3,2,1,0:T(8,128)(2,1)S(1)}, bf16[2,2,1,2,1,4,24,768]{7,6,5,4,3,2,1,0:T(8,128)(2,1)S(1)}, u32[]{:S(2)}, u32[]{:S(2)}) collective-permute-start(bf16[2,2,1,2,1,4,24,768]{7,6,5,4,3,2,1,0:T(8,128)(2,1)S(1)} %get-tuple-element.213), channel_id=1, source_target_pairs={{0,4},{1,5},{2,6},{3,7},{4,0},{5,1},{6,2},{7,3},{8,12},{9,13},{10,... | collective-permute-start | bytes 3538952 | tf_op jit(solution)/shard_map/ppermute | solution.py:666
  210.4 18.3 %collective-permute-start.32 = (bf16[2,2,2,2,1,2,24,768]{7,6,5,4,3,2,1,0:T(8,128)(2,1)S(1)}, bf16[2,2,2,2,1,2,24,768]{7,6,5,4,3,2,1,0:T(8,128)(2,1)S(1)}, u32[]{:S(2)}, u32[]{:S(2)}) collective-permute-start(bf16[2,2,2,2,1,2,24,768]{7,6,5,4,3,2,1,0:T(8,128)(2,1)S(1)} %bitcast.137), channel_id=1, source_target_pairs={{0,1},{1,0},{2,3},{3,2},{4,5},{5,4},{6,7},{7,6},{8,9},{9,8},{10,11... | collective-permute-start | bytes 3538952 | tf_op jit(solution)/shard_map/ppermute | solution.py:666
  210.5 19.6 %collective-permute-start.31 = (bf16[2,2,2,2,1,2,24,768]{7,6,5,4,3,2,1,0:T(8,128)(2,1)S(1)}, bf16[2,2,2,2,1,2,24,768]{7,6,5,4,3,2,1,0:T(8,128)(2,1)S(1)}, u32[]{:S(2)}, u32[]{:S(2)}) collective-permute-start(bf16[2,2,2,2,1,2,24,768]{7,6,5,4,3,2,1,0:T(8,128)(2,1)S(1)} %bitcast.136), channel_id=1, source_target_pairs={{0,1},{1,0},{2,3},{3,2},{4,5},{5,4},{6,7},{7,6},{8,9},{9,8},{10,11... | collective-permute-start | bytes 3538952 | tf_op jit(solution)/shard_map/ppermute | solution.py:666
  231.5 30.2 %collective-permute-start.37 = (bf16[2,2,1,1,1,4,24,768]{7,6,5,4,3,2,1,0:T(8,128)(2,1)}, bf16[2,2,1,1,1,4,24,768]{7,6,5,4,3,2,1,0:T(8,128)(2,1)}, u32[]{:S(2)}, u32[]{:S(2)}) collective-permute-start(bf16[2,2,1,1,1,4,24,768]{7,6,5,4,3,2,1,0:T(8,128)(2,1)} %get-tuple-element.229), channel_id=1, source_target_pairs={{0,4},{1,5},{2,6},{3,7},{4,0},{5,1},{6,2},{7,3},{8,12},{9,13},{10,... | collective-permute-start | bytes 1769480 | tf_op jit(solution)/shard_map/ppermute | solution.py:666
  232.0 31.3 %collective-permute-start.35 = (bf16[2,2,2,1,1,2,24,768]{7,6,5,4,3,2,1,0:T(8,128)(2,1)}, bf16[2,2,2,1,1,2,24,768]{7,6,5,4,3,2,1,0:T(8,128)(2,1)}, u32[]{:S(2)}, u32[]{:S(2)}) collective-permute-start(bf16[2,2,2,1,1,2,24,768]{7,6,5,4,3,2,1,0:T(8,128)(2,1)} %get-tuple-element.227), channel_id=1, source_target_pairs={{0,2},{1,3},{2,0},{3,1},{4,6},{5,7},{6,4},{7,5},{8,10},{9,11},{10,... | collective-permute-start | bytes 1769480 | tf_op jit(solution)/shard_map/ppermute | solution.py:666
  235.0 30.5 %collective-permute-start.38 = (bf16[2,2,1,1,1,4,24,768]{7,6,5,4,3,2,1,0:T(8,128)(2,1)S(1)}, bf16[2,2,1,1,1,4,24,768]{7,6,5,4,3,2,1,0:T(8,128)(2,1)S(1)}, u32[]{:S(2)}, u32[]{:S(2)}) collective-permute-start(bf16[2,2,1,1,1,4,24,768]{7,6,5,4,3,2,1,0:T(8,128)(2,1)S(1)} %get-tuple-element.230), channel_id=1, source_target_pairs={{0,2},{1,3},{2,0},{3,1},{4,6},{5,7},{6,4},{7,5},{8,10},{9,11},{10,... | collective-permute-start | bytes 1769480 | tf_op jit(solution)/shard_map/ppermute | solution.py:666
  250.0 16.9 %collective-permute-start.36 = (bf16[2,2,1,2,1,2,24,768]{7,6,5,4,3,2,1,0:T(8,128)(2,1)}, bf16[2,2,1,2,1,2,24,768]{7,6,5,4,3,2,1,0:T(8,128)(2,1)S(1)}, u32[]{:S(2)}, u32[]{:S(2)}) collective-permute-start(bf16[2,2,1,2,1,2,24,768]{7,6,5,4,3,2,1,0:T(8,128)(2,1)} %get-tuple-element.228), channel_id=1, source_target_pairs={{0,4},{1,5},{2,6},{3,7},{4,0},{5,1},{6,2},{7,3},{8,12},{9,13},{10,... | collective-permute-start | bytes 1769480 | tf_op jit(solution)/shard_map/ppermute | solution.py:666
  267.9 23.8 %collective-permute-start.39 = (bf16[2,2,2,2,1,2,24,768]{7,6,5,4,3,2,1,0:T(8,128)(2,1)}, bf16[2,2,2,2,1,2,24,768]{7,6,5,4,3,2,1,0:T(8,128)(2,1)}, u32[]{:S(2)}, u32[]{:S(2)}) collective-permute-start(bf16[2,2,2,2,1,2,24,768]{7,6,5,4,3,2,1,0:T(8,128)(2,1)} %bitcast.58), channel_id=1, source_target_pairs={{0,1},{1,0},{2,3},{3,2},{4,5},{5,4},{6,7},{7,6},{8,9},{9,8},{10,11... | collective-permute-start | bytes 3538952 | tf_op jit(solution)/shard_map/ppermute | solution.py:666
  267.9 26.7 %collective-permute-start.40 = (bf16[2,2,2,2,1,2,24,768]{7,6,5,4,3,2,1,0:T(8,128)(2,1)}, bf16[2,2,2,2,1,2,24,768]{7,6,5,4,3,2,1,0:T(8,128)(2,1)}, u32[]{:S(2)}, u32[]{:S(2)}) collective-permute-start(bf16[2,2,2,2,1,2,24,768]{7,6,5,4,3,2,1,0:T(8,128)(2,1)} %bitcast.62), channel_id=1, source_target_pairs={{0,1},{1,0},{2,3},{3,2},{4,5},{5,4},{6,7},{7,6},{8,9},{9,8},{10,11... | collective-permute-start | bytes 3538952 | tf_op jit(solution)/shard_map/ppermute | solution.py:666
  271.6 18.1 %collective-permute-start.41 = (bf16[2,2,1,1,1,2,24,768]{7,6,5,4,3,2,1,0:T(8,128)(2,1)}, bf16[2,2,1,1,1,2,24,768]{7,6,5,4,3,2,1,0:T(8,128)(2,1)S(1)}, u32[]{:S(2)}, u32[]{:S(2)}) collective-permute-start(bf16[2,2,1,1,1,2,24,768]{7,6,5,4,3,2,1,0:T(8,128)(2,1)} %get-tuple-element.241), channel_id=1, source_target_pairs={{0,4},{1,5},{2,6},{3,7},{4,0},{5,1},{6,2},{7,3},{8,12},{9,13},{10,... | collective-permute-start | bytes 884744 | tf_op jit(solution)/shard_map/ppermute | solution.py:666
  272.1 19.5 %collective-permute-start.43 = (bf16[2,1,1,1,1,8,24,768]{7,6,5,4,3,2,1,0:T(8,128)(2,1)}, bf16[2,1,1,1,1,8,24,768]{7,6,5,4,3,2,1,0:T(8,128)(2,1)S(1)}, u32[]{:S(2)}, u32[]{:S(2)}) collective-permute-start(bf16[2,1,1,1,1,8,24,768]{7,6,5,4,3,2,1,0:T(8,128)(2,1)} %get-tuple-element.243), channel_id=1, source_target_pairs={{0,8},{1,9},{2,10},{3,11},{4,12},{5,13},{6,14},{7,15},{8,0},{9,1},... | collective-permute-start | bytes 1769480 | tf_op jit(solution)/shard_map/ppermute | solution.py:666
  275.3 14.5 %collective-permute-start.42 = (bf16[2,2,1,1,1,2,24,768]{7,6,5,4,3,2,1,0:T(8,128)(2,1)}, bf16[2,2,1,1,1,2,24,768]{7,6,5,4,3,2,1,0:T(8,128)(2,1)S(1)}, u32[]{:S(2)}, u32[]{:S(2)}) collective-permute-start(bf16[2,2,1,1,1,2,24,768]{7,6,5,4,3,2,1,0:T(8,128)(2,1)} %get-tuple-element.242), channel_id=1, source_target_pairs={{0,2},{1,3},{2,0},{3,1},{4,6},{5,7},{6,4},{7,5},{8,10},{9,11},{10,... | collective-permute-start | bytes 884744 | tf_op jit(solution)/shard_map/ppermute | solution.py:666
  297.9 19.6 %collective-permute-start.46 = (bf16[2,1,1,1,1,4,24,768]{7,6,5,4,3,2,1,0:T(8,128)(2,1)}, bf16[2,1,1,1,1,4,24,768]{7,6,5,4,3,2,1,0:T(8,128)(2,1)}, u32[]{:S(2)}, u32[]{:S(2)}) collective-permute-start(bf16[2,1,1,1,1,4,24,768]{7,6,5,4,3,2,1,0:T(8,128)(2,1)} %get-tuple-element.247), channel_id=1, source_target_pairs={{0,8},{1,9},{2,10},{3,11},{4,12},{5,13},{6,14},{7,15},{8,0},{9,1},... | collective-permute-start | bytes 884744 | tf_op jit(solution)/shard_map/ppermute | solution.py:666
  299.5 19.6 %collective-permute-start.56 = (bf16[1,1,1,1,1,8,24,768]{7,6,5,4,3,2,1,0:T(8,128)(2,1)S(1)}, bf16[1,1,1,1,1,8,24,768]{7,6,5,4,3,2,1,0:T(8,128)(2,1)}, u32[]{:S(2)}, u32[]{:S(2)}) collective-permute-start(bf16[1,1,1,1,1,8,24,768]{7,6,5,4,3,2,1,0:T(8,128)(2,1)S(1)} %add_convert_fusion.26), channel_id=1, source_target_pairs={{0,16},{1,17},{2,18},{3,19},{4,20},{5,21},{6,22},{7,23},{8,24},{9,... | collective-permute-start | bytes 884744 | tf_op jit(solution)/shard_map/ppermute | solution.py:666
  300.1 20.1 %collective-permute-start.44 = (bf16[2,2,2,1,1,2,24,768]{7,6,5,4,3,2,1,0:T(8,128)(2,1)}, bf16[2,2,2,1,1,2,24,768]{7,6,5,4,3,2,1,0:T(8,128)(2,1)S(1)}, u32[]{:S(2)}, u32[]{:S(2)}) collective-permute-start(bf16[2,2,2,1,1,2,24,768]{7,6,5,4,3,2,1,0:T(8,128)(2,1)} %get-tuple-element.245), channel_id=1, source_target_pairs={{0,2},{1,3},{2,0},{3,1},{4,6},{5,7},{6,4},{7,5},{8,10},{9,11},{10,... | collective-permute-start | bytes 1769480 | tf_op jit(solution)/shard_map/ppermute | solution.py:666
  302.2 13.9 %collective-permute-start.48 = (f32[2,2,2,1,1,1,4,128]{7,3,2,1,0,6,5,4:T(1,128)}, f32[2,2,2,1,1,1,4,128]{7,3,2,1,0,6,5,4:T(1,128)}, u32[]{:S(2)}, u32[]{:S(2)}) collective-permute-start(f32[2,2,2,1,1,1,4,128]{7,3,2,1,0,6,5,4:T(1,128)} %get-tuple-element.307), channel_id=1, source_target_pairs={{0,2},{1,3},{2,0},{3,1},{4,6},{5,7},{6,4},{7,5},{8,10},{9,11},{10,... | collective-permute-start | bytes 49160 | tf_op jit(solution)/shard_map/ppermute | solution.py:666
  302.8 18.4 %collective-permute-start.45 = (bf16[2,2,1,2,1,2,24,768]{7,6,5,4,3,2,1,0:T(8,128)(2,1)}, bf16[2,2,1,2,1,2,24,768]{7,6,5,4,3,2,1,0:T(8,128)(2,1)S(1)}, u32[]{:S(2)}, u32[]{:S(2)}) collective-permute-start(bf16[2,2,1,2,1,2,24,768]{7,6,5,4,3,2,1,0:T(8,128)(2,1)} %get-tuple-element.246), channel_id=1, source_target_pairs={{0,4},{1,5},{2,6},{3,7},{4,0},{5,1},{6,2},{7,3},{8,12},{9,13},{10,... | collective-permute-start | bytes 1769480 | tf_op jit(solution)/shard_map/ppermute | solution.py:666
  322.1 11.6 %collective-permute-start.51 = (f32[2,2,1,1,1,1,4,128]{7,3,2,1,0,6,5,4:T(1,128)}, f32[2,2,1,1,1,1,4,128]{7,3,2,1,0,6,5,4:T(1,128)S(1)}, u32[]{:S(2)}, u32[]{:S(2)}) collective-permute-start(f32[2,2,1,1,1,1,4,128]{7,3,2,1,0,6,5,4:T(1,128)} %get-tuple-element.258), channel_id=1, source_target_pairs={{0,4},{1,5},{2,6},{3,7},{4,0},{5,1},{6,2},{7,3},{8,12},{9,13},{10,... | collective-permute-start | bytes 24584 | tf_op jit(solution)/shard_map/ppermute | solution.py:666
  (117 other events, 606.1 us)

commit v6 on v5

--- a/solution.py
+++ b/solution.py
@@ -648,7 +648,7 @@
 def gather_stages(count, parts):
     x_bits, y_bits, z_bits = (list(reversed(b)) for b in axis_bits(count))
     if parts == 1:
-        return [[(b,) for b in bits] for bits in (z_bits[:1], z_bits[1:], y_bits, x_bits, [0])]
+        return [[(b,) for b in bits] for bits in (x_bits, y_bits, z_bits[:1], z_bits[1:], [0])]
     return [
         [(z_bits[0],)],
         [(b,) for b in z_bits[1:]],
@@ -893,7 +893,9 @@
     d_self_a = weight_grads([(norm_one, grad_q), (norm_one, grad_k)], core, count)
     d_self_b = weight_grads([(norm_one, grad_v), (attended, grad_self)], core, count)
     s_self = Scatter([d_self_a, d_self_b], count)
-    grad_q, grad_k, grad_v = tick([s_self, s_cross, s_ffn], (grad_q, grad_k, grad_v))
+    grad_q, grad_k, grad_v = tick([s_self], (grad_q, grad_k, grad_v))
+    grad_q, grad_k, grad_v = tick([s_cross, s_ffn], (grad_q, grad_k, grad_v))
+    grad_q, grad_k, grad_v = tick([s_self], (grad_q, grad_k, grad_v))
     grad_in, sums_one = in_back(grad_q, grad_k, grad_v, self_a, self_b, x, grad_mid, vec, block)
 
     sums_one = tick([s_self, s_cross, s_ffn], sums_one)
@@ -917,8 +919,8 @@
     s_small = Scatter([[sums.reshape(1, count * small_rows, 128)]], count)
     tick([s_small])
     tick([s_small])
+    tick([s_small])
     tick([s_self, s_cross, s_small])
-    tick([s_self, s_small])
     tick([s_self, s_small])
     d_ffn = s_ffn.result()
     d_in_all, d_out_all = d_ffn[:mats], d_ffn[mats:]

time: 364 us -> 340 us (0.934)
  local copies, waits for them, and re-layouts: 53.5 us -> 38 us
  waiting for transfers between devices: 90.6 us -> 82.6 us
  starting transfers between devices: 52.8 us -> 58.9 us
  other arithmetic: 41.3 us -> 35.6 us
    unnamed x182 -> x144, local copies, waits for them, and re-layouts: 25.9 us -> 15.8 us
    ppermute x58, waiting for transfers between devices: 90.6 us -> 82.6 us  [swap(): lax.ppermute(values, 'fsdp', [(i, i ^ 1 << bit) for i in range(count)])]
    ppermute x58, starting transfers between devices: 52.8 us -> 58.9 us  [swap(): lax.ppermute(values, 'fsdp', [(i, i ^ 1 << bit) for i in range(count)])]
  transfers between devices with their start and end apart: 58 -> 58, of which waited for: 28 -> 29; matrix products, arithmetic and copies ran while one was open for 15% -> 13% of each run, Pallas kernels for 20% -> 22%
where the time goes in v6:
time: 340 us; the launch traced here: 335 us
  Pallas kernels  116 us (34%)
  waiting for transfers between devices  82.6 us (24%)
  starting transfers between devices  58.9 us (17%)
  local copies, waits for them, and re-layouts  38 us (11%)
  other arithmetic  35.6 us (10%)
  between operations  3.64 us (1%)
    pallas_call x20, Pallas kernels, run(): pl.pallas_call(body, name=name, grid=grid, in_specs=in_specs, out_specs=[...  116 us
    ppermute x58, waiting for transfers between devices, swap(): lax.ppermute(values, 'fsdp', [(i, i ^ 1 << bit) for i in range(count)])  82.6 us
    ppermute x58, starting transfers between devices, swap(): lax.ppermute(values, 'fsdp', [(i, i ^ 1 << bit) for i in range(count)])  58.9 us
    convert_element_type x18, other arithmetic, total(): return (pair[0].astype(WIDE) + pair[1].astype(WIDE)).astype(kind)  21.1 us
    unnamed x144, local copies, waits for them, and re-layouts  15.8 us
    select_n x22, other arithmetic, land(): jnp.where(own_bit(bit) == 0, jnp.concatenate([held, other], axis), jnp.co...  8.33 us
  transfers between devices with their start and end apart: 58, of which 29 were waited for; matrix products, arithmetic and copies ran while one was open for 13% of the time, Pallas kernels for 22%

profile of v6, /device:TPU:0, one launch (start us, length us, event | category | flops | bytes accessed | tf_op | source)
XLA Modules:
  0.0 334.6 jit_solution(5428922047437606673)
XLA Ops:
  4.7 4.1 %collective-permute-start = (bf16[1,1,1,1,1,4,24,768]{7,6,5,4,3,2,1,0:T(8,128)(2,1)S(1)}, bf16[1,1,1,1,1,4,24,768]{7,6,5,4,3,2,1,0:T(8,128)(2,1)S(1)}, u32[]{:S(2)}, u32[]{:S(2)}) collective-permute-start(bf16[1,1,1,1,1,4,24,768]{7,6,5,4,3,2,1,0:T(8,128)(2,1)S(1)} %maximum_bitcast_fusion.1), channel_id=1, source_target_pairs={{0,16},{1,17},{2,18},{3,19},{4,20},{5,21},{6,22},{7,23},{8,24},{9,... | collective-permute-start | bytes 442376 | tf_op jit(solution)/shard_map/ppermute | solution.py:666
  12.4 3.4 %collective-permute-done = bf16[1,1,1,1,1,4,24,768]{7,6,5,4,3,2,1,0:T(8,128)(2,1)S(1)} collective-permute-done((bf16[1,1,1,1,1,4,24,768]{7,6,5,4,3,2,1,0:T(8,128)(2,1)S(1)}, bf16[1,1,1,1,1,4,24,768]{7,6,5,4,3,2,1,0:T(8,128)(2,1)S(1)}, u32[]{:S(2)}, u32[]{:S(2)}) %collective-permute-start) | collective-permute-done | bytes 147488 | tf_op jit(solution)/shard_map/ppermute | solution.py:666
  20.8 3.2 collective-permute-done.2
  24.2 3.2 collective-permute-start.6
  30.6 5.8 %collective-permute-done.7 = bf16[1,1,1,1,1,4,24,768]{7,6,5,4,3,2,1,0:T(8,128)(2,1)S(1)} collective-permute-done((bf16[1,1,1,1,1,4,24,768]{7,6,5,4,3,2,1,0:T(8,128)(2,1)S(1)}, bf16[1,1,1,1,1,4,24,768]{7,6,5,4,3,2,1,0:T(8,128)(2,1)S(1)}, u32[]{:S(2)}, u32[]{:S(2)}) %collective-permute-start.7) | collective-permute-done | bytes 147488 | tf_op jit(solution)/shard_map/ppermute | solution.py:666
  38.4 2.6 collective-permute-start.12
  43.6 7.5 %collective-permute-done.10 = bf16[2,1,2,2,1,1,4,128]{7,6,5,4,3,2,1,0:T(4,128)(2,1)S(1)} collective-permute-done((bf16[2,1,2,2,1,1,4,128]{7,6,5,4,3,2,1,0:T(4,128)(2,1)S(1)}, bf16[2,1,2,2,1,1,4,128]{7,6,5,4,3,2,1,0:T(4,128)(2,1)S(1)}, u32[]{:S(2)}, u32[]{:S(2)}) %collective-permute-start.10) | collective-permute-done | bytes 8224 | tf_op jit(solution)/shard_map/ppermute | solution.py:666
  63.0 2.9 collective-permute-done.14
  75.4 3.8 %qkv.1 = (bf16[640,768]{1,0:T(8,128)(2,1)S(1)}, bf16[640,768]{1,0:T(8,128)(2,1)S(1)}, bf16[640,768]{1,0:T(8,128)(2,1)S(1)}, bf16[640,768]{1,0:T(8,128)(2,1)S(1)}) custom-call(bf16[640,768]{1,0:T(8,128)(2,1)S(1)} %bitcast.120, f32[16,768]{1,0:T(8,128)S(1)} %pad.13.vec_ref.refs_1_, bf16[2,768,768]{2,1,0:T(8,128)(2,1)S(1)} %bitcast.110, ...), custom_call_target="tpu_custom_call" | custom-call | flops 2264924160 | bytes 12042240 | tf_op jit(solution)/shard_map/qkv/pallas_call | solution.py:41
  82.7 3.6 %collective-permute-done.21 = bf16[2,2,2,1,1,2,24,768]{7,6,5,4,3,2,1,0:T(8,128)(2,1)S(1)} collective-permute-done((bf16[2,2,2,1,1,2,24,768]{7,6,5,4,3,2,1,0:T(8,128)(2,1)S(1)}, bf16[2,2,2,1,1,2,24,768]{7,6,5,4,3,2,1,0:T(8,128)(2,1)S(1)}, u32[]{:S(2)}, u32[]{:S(2)}) %collective-permute-start.21) | collective-permute-done | bytes 589856 | tf_op jit(solution)/shard_map/ppermute | solution.py:666
  87.0 5.4 %attend_self.1.a_ref.refs_2_ = bf16[640,768]{1,0:T(8,128)(2,1)S(1)} custom-call(bf16[640,768]{1,0:T(8,128)(2,1)S(1)} %get-tuple-element.172.q_ref, bf16[640,768]{1,0:T(8,128)(2,1)S(1)} %get-tuple-element.173.k_ref, bf16[640,768]{1,0:T(8,128)(2,1)S(1)} %get-tuple-element.174.v_ref), custom_call_target="tpu_custom_call" | custom-call | flops 629145600 | bytes 3932160 | tf_op jit(solution)/shard_map/attend_self/pallas_call | solution.py:41
  92.4 3.0 mid_stage.1
  103.2 3.2 attend_cross.1.a_ref.refs_2_
  106.5 3.0 late_stage.1
  110.8 13.5 %collective-permute-done.23 = bf16[2,2,2,1,1,4,24,768]{7,6,5,4,3,2,1,0:T(8,128)(2,1)S(1)} collective-permute-done((bf16[2,2,2,1,1,4,24,768]{7,6,5,4,3,2,1,0:T(8,128)(2,1)S(1)}, bf16[2,2,2,1,1,4,24,768]{7,6,5,4,3,2,1,0:T(8,128)(2,1)S(1)}, u32[]{:S(2)}, u32[]{:S(2)}) %collective-permute-start.23) | collective-permute-done | bytes 1179680 | tf_op jit(solution)/shard_map/ppermute | solution.py:666
  132.6 3.4 %collective-permute-done.28 = bf16[2,2,2,2,1,4,24,768]{7,6,5,4,3,2,1,0:T(8,128)(2,1)} collective-permute-done((bf16[2,2,2,2,1,4,24,768]{7,6,5,4,3,2,1,0:T(8,128)(2,1)}, bf16[2,2,2,2,1,4,24,768]{7,6,5,4,3,2,1,0:T(8,128)(2,1)}, u32[]{:S(2)}, u32[]{:S(2)}) %collective-permute-start.28) | collective-permute-done | bytes 2359328 | tf_op jit(solution)/shard_map/ppermute | solution.py:666
  136.0 4.9 %weave.5 = (bf16[4,16,2,24,768]{4,3,2,1,0:T(8,128)(2,1)S(1)}, bf16[4,16,2,24,768]{4,3,2,1,0:T(8,128)(2,1)S(1)}) custom-call(s32[1]{0:T(128)} %bitcast.core_ref, bf16[16,4,24,768]{3,2,1,0:T(8,128)(2,1)} %bitcast.25.refs_0_, bf16[16,4,24,768]{3,2,1,0:T(8,128)(2,1)} %bitcast.26.refs_1_, bf16[16,4,24,768]{3,2,1,0:T(8,128)(2,1)} %bitcast.27.refs_2_, ...), custom_call_target="tpu_custom_call" | custom-call | bytes 18874372 | tf_op jit(solution)/shard_map/weave/pallas_call | solution.py:41
  140.9 39.0 %ffn_stage.1 = (f32[640,768]{1,0:T(8,128)S(1)}, bf16[16,4,24,768]{3,2,1,0:T(8,128)(2,1)}, bf16[16,4,24,768]{3,2,1,0:T(8,128)(2,1)S(1)}, bf16[16,4,24,768]{3,2,1,...) custom-call(s32[2]{0:T(128)S(1)} %copy-done.42, ...), custom_call_target="tpu_custom_call" | custom-call | flops 18119393280 | bytes 25853964 | tf_op jit(solution)/shard_map/ffn_stage/pallas_call | solution.py:41
  187.6 3.7 %late_back.1 = (f32[640,768]{1,0:T(8,128)S(1)}, bf16[640,768]{1,0:T(8,128)(2,1)S(1)}, bf16[640,768]{1,0:T(8,128)(2,1)S(1)}, f32[8,768]{1,0:T(8,128)S(1)}) custom-call(f32[640,768]{1,0:T(8,128)S(1)} %copy-done.25, f32[640,768]{1,0:T(8,128)S(1)} %copy-done.23, bf16[640,768]{1,0:T(8,128)(2,1)S(1)} %bitcast.119, f32[16,768]{1,0:T(8,128)S(1)} %pad.13.vec_ref.refs_1_, ...), custom_call_target="tpu_custom_call" | custom-call | flops 754974720 | bytes 11280384 | tf_op jit(solution)/shard_map/late_back/pallas_call | solution.py:41
  199.1 5.4 %attend_cross_back.1 = (bf16[640,768]{1,0:T(8,128)(2,1)S(1)}, bf16[256,768]{1,0:T(8,128)(2,1)S(1)}, bf16[256,768]{1,0:T(8,128)(2,1)S(1)}) custom-call(bf16[640,768]{1,0:T(8,128)(2,1)S(1)} %copy-done.14, bf16[256,768]{1,0:T(8,128)(2,1)S(1)} %copy-done.27, bf16[256,768]{1,0:T(8,128)(2,1)S(1)} %copy-done.29, bf16[640,768]{1,0:T(8,128)(2,1)S(1)} %get-tuple-element.206.g_ref), custom_call_target="tpu_custom_call" | custom-call | flops 629145600 | bytes 4521984 | tf_op jit(solution)/shard_map/attend_cross_back/pallas_call | solution.py:41
  206.5 3.7 %weight_grads.4 = (bf16[16,2,24,768]{3,2,1,0:T(8,128)(2,1)S(1)}, bf16[16,2,24,768]{3,2,1,0:T(8,128)(2,1)S(1)}) custom-call(s32[1]{0:T(128)} %bitcast.core_ref, bf16[640,768]{1,0:T(8,128)(2,1)S(1)} %copy-done.39, bf16[640,768]{1,0:T(8,128)(2,1)S(1)} %get-tuple-element.219.refs_1_.gq, bf16[640,768]{1,0:T(8,128)(2,1)S(1)} %copy-done.12, ...), custom_call_target="tpu_custom_call" | custom-call | flops 1509949440 | bytes 6291460 | tf_op jit(solution)/shard_map/weight_grads/pallas_call | solution.py:41
  214.0 5.6 %mid_back.1 = (f32[640,768]{1,0:T(8,128)S(1)}, bf16[640,768]{1,0:T(8,128)(2,1)S(1)}, bf16[640,768]{1,0:T(8,128)(2,1)S(1)}, f32[8,768]{1,0:T(8,128)S(1)}) custom-call(bf16[640,768]{1,0:T(8,128)(2,1)S(1)} %get-tuple-element.219.refs_1_.gq, bf16[2,768,768]{2,1,0:T(8,128)(2,1)S(1)} %bitcast.101, f32[640,768]{1,0:T(8,128)S(1)} %copy-done.8, ...), custom_call_target="tpu_custom_call" | custom-call | flops 1509949440 | bytes 13639680 | tf_op jit(solution)/shard_map/mid_back/pallas_call | solution.py:41
  220.5 4.0 %collective-permute-done.33 = bf16[2,2,2,1,1,4,24,768]{7,6,5,4,3,2,1,0:T(8,128)(2,1)S(1)} collective-permute-done((bf16[2,2,2,1,1,4,24,768]{7,6,5,4,3,2,1,0:T(8,128)(2,1)S(1)}, bf16[2,2,2,1,1,4,24,768]{7,6,5,4,3,2,1,0:T(8,128)(2,1)S(1)}, u32[]{:S(2)}, u32[]{:S(2)}) %collective-permute-start.33) | collective-permute-done | bytes 1179680 | tf_op jit(solution)/shard_map/ppermute | solution.py:666
  237.6 10.0 %attend_self_back.1 = (bf16[640,768]{1,0:T(8,128)(2,1)S(1)}, bf16[640,768]{1,0:T(8,128)(2,1)S(1)}, bf16[640,768]{1,0:T(8,128)(2,1)S(1)}) custom-call(bf16[640,768]{1,0:T(8,128)(2,1)S(1)} %copy-done.53, bf16[640,768]{1,0:T(8,128)(2,1)S(1)} %copy-done.55, bf16[640,768]{1,0:T(8,128)(2,1)S(1)} %copy-done.57, bf16[640,768]{1,0:T(8,128)(2,1)S(1)} %copy-done.47), custom_call_target="tpu_custom_call" | custom-call | flops 1572864000 | bytes 6881280 | tf_op jit(solution)/shard_map/attend_self_back/pallas_call | solution.py:41
  247.6 4.5 %weight_grads.7 = (bf16[16,2,24,768]{3,2,1,0:T(8,128)(2,1)}, bf16[16,2,24,768]{3,2,1,0:T(8,128)(2,1)S(1)}) custom-call(s32[1]{0:T(128)} %bitcast.core_ref, bf16[640,768]{1,0:T(8,128)(2,1)S(1)} %copy-done.51, bf16[640,768]{1,0:T(8,128)(2,1)S(1)} %get-tuple-element.248.refs_1_.gv, bf16[640,768]{1,0:T(8,128)(2,1)S(1)} %copy-done.31, bf16[640,768]{1,0:T(8,128)(2,1)S(1)} %copy-done.45), custom_call_target="tpu_custom_call" | custom-call | flops 1509949440 | bytes 6291460 | tf_op jit(solution)/shard_map/weight_grads/pallas_call | solution.py:41
  252.2 4.7 %weight_grads.6 = (bf16[16,2,24,768]{3,2,1,0:T(8,128)(2,1)}, bf16[16,2,24,768]{3,2,1,0:T(8,128)(2,1)S(1)}) custom-call(s32[1]{0:T(128)} %bitcast.core_ref, bf16[640,768]{1,0:T(8,128)(2,1)S(1)} %copy-done.51, bf16[640,768]{1,0:T(8,128)(2,1)S(1)} %get-tuple-element.246.refs_1_.gq, bf16[640,768]{1,0:T(8,128)(2,1)S(1)} %copy-done.51, ...), custom_call_target="tpu_custom_call" | custom-call | flops 1509949440 | bytes 6291460 | tf_op jit(solution)/shard_map/weight_grads/pallas_call | solution.py:41
  274.9 6.9 %in_back.1 = (bf16[640,768]{1,0:T(8,128)(2,1)}, f32[8,768]{1,0:T(8,128)S(1)}) custom-call(bf16[640,768]{1,0:T(8,128)(2,1)S(1)} %copy-done.33, bf16[640,768]{1,0:T(8,128)(2,1)S(1)} %copy-done.35, bf16[640,768]{1,0:T(8,128)(2,1)S(1)} %copy-done.37, bf16[2,768,768]{2,1,0:T(8,128)(2,1)S(1)} %bitcast.112, bf16[2,768,768]{2,1,0:T(8,128)(2,1)S(1)} %bitcast.113, ...), custom_call_target="tpu_custom_call" | custom-call | flops 2264924160 | bytes 14032896 | tf_op jit(solution)/shard_map/in_back/pallas_call | solution.py:41
  281.9 4.5 %collective-permute-done.41 = bf16[2,2,2,1,1,2,24,768]{7,6,5,4,3,2,1,0:T(8,128)(2,1)S(1)} collective-permute-done((bf16[2,2,2,1,1,2,24,768]{7,6,5,4,3,2,1,0:T(8,128)(2,1)S(1)}, bf16[2,2,2,1,1,2,24,768]{7,6,5,4,3,2,1,0:T(8,128)(2,1)S(1)}, u32[]{:S(2)}, u32[]{:S(2)}) %collective-permute-start.41) | collective-permute-done | bytes 589856 | tf_op jit(solution)/shard_map/ppermute | solution.py:666
  299.3 2.5 collective-permute-done.48
  307.7 8.7 %collective-permute-done.56 = bf16[1,1,1,1,1,8,24,768]{7,6,5,4,3,2,1,0:T(8,128)(2,1)S(1)} collective-permute-done((bf16[1,1,1,1,1,8,24,768]{7,6,5,4,3,2,1,0:T(8,128)(2,1)S(1)}, bf16[1,1,1,1,1,8,24,768]{7,6,5,4,3,2,1,0:T(8,128)(2,1)S(1)}, u32[]{:S(2)}, u32[]{:S(2)}) %collective-permute-start.56) | collective-permute-done | bytes 294944 | tf_op jit(solution)/shard_map/ppermute | solution.py:666
  319.7 2.5 reshape.1462
  325.0 2.9 collective-permute-done.57
  (371 shorter events, 145.7 us)
Async XLA Ops:
  4.7 11.1 %collective-permute-start = (bf16[1,1,1,1,1,4,24,768]{7,6,5,4,3,2,1,0:T(8,128)(2,1)S(1)}, bf16[1,1,1,1,1,4,24,768]{7,6,5,4,3,2,1,0:T(8,128)(2,1)S(1)}, u32[]{:S(2)}, u32[]{:S(2)}) collective-permute-start(bf16[1,1,1,1,1,4,24,768]{7,6,5,4,3,2,1,0:T(8,128)(2,1)S(1)} %maximum_bitcast_fusion.1), channel_id=1, source_target_pairs={{0,16},{1,17},{2,18},{3,19},{4,20},{5,21},{6,22},{7,23},{8,24},{9,... | collective-permute-start | bytes 442376 | tf_op jit(solution)/shard_map/ppermute | solution.py:666
  36.9 14.2 %collective-permute-start.11 = (bf16[2,1,1,1,1,4,24,768]{7,6,5,4,3,2,1,0:T(8,128)(2,1)S(1)}, bf16[2,1,1,1,1,4,24,768]{7,6,5,4,3,2,1,0:T(8,128)(2,1)S(1)}, u32[]{:S(2)}, u32[]{:S(2)}) collective-permute-start(bf16[2,1,1,1,1,4,24,768]{7,6,5,4,3,2,1,0:T(8,128)(2,1)S(1)} %maximum_select_fusion.17), channel_id=1, source_target_pairs={{0,8},{1,9},{2,10},{3,11},{4,12},{5,13},{6,14},{7,15},{8,0},{9,1},... | collective-permute-start | bytes 884744 | tf_op jit(solution)/shard_map/ppermute | solution.py:666
  38.4 13.7 %collective-permute-start.12 = (bf16[1,1,1,1,1,8,24,768]{7,6,5,4,3,2,1,0:T(8,128)(2,1)S(1)}, bf16[1,1,1,1,1,8,24,768]{7,6,5,4,3,2,1,0:T(8,128)(2,1)S(1)}, u32[]{:S(2)}, u32[]{:S(2)}) collective-permute-start(bf16[1,1,1,1,1,8,24,768]{7,6,5,4,3,2,1,0:T(8,128)(2,1)S(1)} %maximum_bitcast_fusion), channel_id=1, source_target_pairs={{0,16},{1,17},{2,18},{3,19},{4,20},{5,21},{6,22},{7,23},{8,24},{9,... | collective-permute-start | bytes 884744 | tf_op jit(solution)/shard_map/ppermute | solution.py:666
  41.6 12.1 %collective-permute-start.8 = (bf16[2,2,2,1,1,2,24,768]{7,6,5,4,3,2,1,0:T(8,128)(2,1)S(1)}, bf16[2,2,2,1,1,2,24,768]{7,6,5,4,3,2,1,0:T(8,128)(2,1)S(1)}, u32[]{:S(2)}, u32[]{:S(2)}) collective-permute-start(bf16[2,2,2,1,1,2,24,768]{7,6,5,4,3,2,1,0:T(8,128)(2,1)S(1)} %maximum_select_fusion.10), channel_id=1, source_target_pairs={{0,2},{1,3},{2,0},{3,1},{4,6},{5,7},{6,4},{7,5},{8,10},{9,11},{10,... | collective-permute-start | bytes 1769480 | tf_op jit(solution)/shard_map/ppermute | solution.py:666
  43.1 11.9 %collective-permute-start.9 = (bf16[2,2,1,2,1,2,24,768]{7,6,5,4,3,2,1,0:T(8,128)(2,1)S(1)}, bf16[2,2,1,2,1,2,24,768]{7,6,5,4,3,2,1,0:T(8,128)(2,1)S(1)}, u32[]{:S(2)}, u32[]{:S(2)}) collective-permute-start(bf16[2,2,1,2,1,2,24,768]{7,6,5,4,3,2,1,0:T(8,128)(2,1)S(1)} %maximum_select_fusion.11), channel_id=1, source_target_pairs={{0,4},{1,5},{2,6},{3,7},{4,0},{5,1},{6,2},{7,3},{8,12},{9,13},{10,... | collective-permute-start | bytes 1769480 | tf_op jit(solution)/shard_map/ppermute | solution.py:666
  55.0 18.2 %collective-permute-start.17 = (bf16[2,2,2,2,1,2,24,768]{7,6,5,4,3,2,1,0:T(8,128)(2,1)S(1)}, bf16[2,2,2,2,1,2,24,768]{7,6,5,4,3,2,1,0:T(8,128)(2,1)}, u32[]{:S(2)}, u32[]{:S(2)}) collective-permute-start(bf16[2,2,2,2,1,2,24,768]{7,6,5,4,3,2,1,0:T(8,128)(2,1)S(1)} %maximum_select_fusion.2), channel_id=1, source_target_pairs={{0,1},{1,0},{2,3},{3,2},{4,5},{5,4},{6,7},{7,6},{8,9},{9,8},{10,11... | collective-permute-start | bytes 3538952 | tf_op jit(solution)/shard_map/ppermute | solution.py:666
  55.1 18.1 %collective-permute-start.18 = (bf16[2,2,2,2,1,2,24,768]{7,6,5,4,3,2,1,0:T(8,128)(2,1)S(1)}, bf16[2,2,2,2,1,2,24,768]{7,6,5,4,3,2,1,0:T(8,128)(2,1)}, u32[]{:S(2)}, u32[]{:S(2)}) collective-permute-start(bf16[2,2,2,2,1,2,24,768]{7,6,5,4,3,2,1,0:T(8,128)(2,1)S(1)} %maximum_select_fusion.3), channel_id=1, source_target_pairs={{0,1},{1,0},{2,3},{3,2},{4,5},{5,4},{6,7},{7,6},{8,9},{9,8},{10,11... | collective-permute-start | bytes 3538952 | tf_op jit(solution)/shard_map/ppermute | solution.py:666
  55.6 16.1 %collective-permute-start.13 = (bf16[2,1,1,1,1,8,24,768]{7,6,5,4,3,2,1,0:T(8,128)(2,1)S(1)}, bf16[2,1,1,1,1,8,24,768]{7,6,5,4,3,2,1,0:T(8,128)(2,1)}, u32[]{:S(2)}, u32[]{:S(2)}) collective-permute-start(bf16[2,1,1,1,1,8,24,768]{7,6,5,4,3,2,1,0:T(8,128)(2,1)S(1)} %maximum_select_fusion.13), channel_id=1, source_target_pairs={{0,8},{1,9},{2,10},{3,11},{4,12},{5,13},{6,14},{7,15},{8,0},{9,1},... | collective-permute-start | bytes 1769480 | tf_op jit(solution)/shard_map/ppermute | solution.py:666
  70.0 16.3 %collective-permute-start.21 = (bf16[2,2,2,1,1,2,24,768]{7,6,5,4,3,2,1,0:T(8,128)(2,1)S(1)}, bf16[2,2,2,1,1,2,24,768]{7,6,5,4,3,2,1,0:T(8,128)(2,1)S(1)}, u32[]{:S(2)}, u32[]{:S(2)}) collective-permute-start(bf16[2,2,2,1,1,2,24,768]{7,6,5,4,3,2,1,0:T(8,128)(2,1)S(1)} %maximum_select_fusion.14), channel_id=1, source_target_pairs={{0,2},{1,3},{2,0},{3,1},{4,6},{5,7},{6,4},{7,5},{8,10},{9,11},{10,... | collective-permute-start | bytes 1769480 | tf_op jit(solution)/shard_map/ppermute | solution.py:666
  70.6 16.2 %collective-permute-start.22 = (bf16[2,2,1,2,1,2,24,768]{7,6,5,4,3,2,1,0:T(8,128)(2,1)S(1)}, bf16[2,2,1,2,1,2,24,768]{7,6,5,4,3,2,1,0:T(8,128)(2,1)S(1)}, u32[]{:S(2)}, u32[]{:S(2)}) collective-permute-start(bf16[2,2,1,2,1,2,24,768]{7,6,5,4,3,2,1,0:T(8,128)(2,1)S(1)} %maximum_select_fusion.15), channel_id=1, source_target_pairs={{0,4},{1,5},{2,6},{3,7},{4,0},{5,1},{6,2},{7,3},{8,12},{9,13},{10,... | collective-permute-start | bytes 1769480 | tf_op jit(solution)/shard_map/ppermute | solution.py:666
  80.2 17.3 %collective-permute-start.19 = (bf16[2,2,1,1,1,4,24,768]{7,6,5,4,3,2,1,0:T(8,128)(2,1)S(1)}, bf16[2,2,1,1,1,4,24,768]{7,6,5,4,3,2,1,0:T(8,128)(2,1)S(1)}, u32[]{:S(2)}, u32[]{:S(2)}) collective-permute-start(bf16[2,2,1,1,1,4,24,768]{7,6,5,4,3,2,1,0:T(8,128)(2,1)S(1)} %get-tuple-element.168), channel_id=1, source_target_pairs={{0,4},{1,5},{2,6},{3,7},{4,0},{5,1},{6,2},{7,3},{8,12},{9,13},{10,... | collective-permute-start | bytes 1769480 | tf_op jit(solution)/shard_map/ppermute | solution.py:666
  81.2 16.5 %collective-permute-start.20 = (bf16[2,2,1,1,1,4,24,768]{7,6,5,4,3,2,1,0:T(8,128)(2,1)S(1)}, bf16[2,2,1,1,1,4,24,768]{7,6,5,4,3,2,1,0:T(8,128)(2,1)S(1)}, u32[]{:S(2)}, u32[]{:S(2)}) collective-permute-start(bf16[2,2,1,1,1,4,24,768]{7,6,5,4,3,2,1,0:T(8,128)(2,1)S(1)} %get-tuple-element.169), channel_id=1, source_target_pairs={{0,2},{1,3},{2,0},{3,1},{4,6},{5,7},{6,4},{7,5},{8,10},{9,11},{10,... | collective-permute-start | bytes 1769480 | tf_op jit(solution)/shard_map/ppermute | solution.py:666
  97.8 26.6 %collective-permute-start.23 = (bf16[2,2,2,1,1,4,24,768]{7,6,5,4,3,2,1,0:T(8,128)(2,1)S(1)}, bf16[2,2,2,1,1,4,24,768]{7,6,5,4,3,2,1,0:T(8,128)(2,1)S(1)}, u32[]{:S(2)}, u32[]{:S(2)}) collective-permute-start(bf16[2,2,2,1,1,4,24,768]{7,6,5,4,3,2,1,0:T(8,128)(2,1)S(1)} %maximum_select_fusion.5), channel_id=1, source_target_pairs={{0,2},{1,3},{2,0},{3,1},{4,6},{5,7},{6,4},{7,5},{8,10},{9,11},{10,... | collective-permute-start | bytes 3538952 | tf_op jit(solution)/shard_map/ppermute | solution.py:666
  99.3 26.6 %collective-permute-start.24 = (bf16[2,2,1,2,1,4,24,768]{7,6,5,4,3,2,1,0:T(8,128)(2,1)S(1)}, bf16[2,2,1,2,1,4,24,768]{7,6,5,4,3,2,1,0:T(8,128)(2,1)S(1)}, u32[]{:S(2)}, u32[]{:S(2)}) collective-permute-start(bf16[2,2,1,2,1,4,24,768]{7,6,5,4,3,2,1,0:T(8,128)(2,1)S(1)} %maximum_select_fusion.6), channel_id=1, source_target_pairs={{0,4},{1,5},{2,6},{3,7},{4,0},{5,1},{6,2},{7,3},{8,12},{9,13},{10,... | collective-permute-start | bytes 3538952 | tf_op jit(solution)/shard_map/ppermute | solution.py:666
  196.4 28.1 %collective-permute-start.33 = (bf16[2,2,2,1,1,4,24,768]{7,6,5,4,3,2,1,0:T(8,128)(2,1)S(1)}, bf16[2,2,2,1,1,4,24,768]{7,6,5,4,3,2,1,0:T(8,128)(2,1)S(1)}, u32[]{:S(2)}, u32[]{:S(2)}) collective-permute-start(bf16[2,2,2,1,1,4,24,768]{7,6,5,4,3,2,1,0:T(8,128)(2,1)S(1)} %get-tuple-element.217), channel_id=1, source_target_pairs={{0,2},{1,3},{2,0},{3,1},{4,6},{5,7},{6,4},{7,5},{8,10},{9,11},{10,... | collective-permute-start | bytes 3538952 | tf_op jit(solution)/shard_map/ppermute | solution.py:666
  198.0 27.8 %collective-permute-start.34 = (bf16[2,2,1,2,1,4,24,768]{7,6,5,4,3,2,1,0:T(8,128)(2,1)S(1)}, bf16[2,2,1,2,1,4,24,768]{7,6,5,4,3,2,1,0:T(8,128)(2,1)S(1)}, u32[]{:S(2)}, u32[]{:S(2)}) collective-permute-start(bf16[2,2,1,2,1,4,24,768]{7,6,5,4,3,2,1,0:T(8,128)(2,1)S(1)} %get-tuple-element.218), channel_id=1, source_target_pairs={{0,4},{1,5},{2,6},{3,7},{4,0},{5,1},{6,2},{7,3},{8,12},{9,13},{10,... | collective-permute-start | bytes 3538952 | tf_op jit(solution)/shard_map/ppermute | solution.py:666
  210.2 16.9 %collective-permute-start.32 = (bf16[2,2,2,2,1,2,24,768]{7,6,5,4,3,2,1,0:T(8,128)(2,1)S(1)}, bf16[2,2,2,2,1,2,24,768]{7,6,5,4,3,2,1,0:T(8,128)(2,1)S(1)}, u32[]{:S(2)}, u32[]{:S(2)}) collective-permute-start(bf16[2,2,2,2,1,2,24,768]{7,6,5,4,3,2,1,0:T(8,128)(2,1)S(1)} %bitcast.137), channel_id=1, source_target_pairs={{0,1},{1,0},{2,3},{3,2},{4,5},{5,4},{6,7},{7,6},{8,9},{9,8},{10,11... | collective-permute-start | bytes 3538952 | tf_op jit(solution)/shard_map/ppermute | solution.py:666
  210.3 18.2 %collective-permute-start.31 = (bf16[2,2,2,2,1,2,24,768]{7,6,5,4,3,2,1,0:T(8,128)(2,1)S(1)}, bf16[2,2,2,2,1,2,24,768]{7,6,5,4,3,2,1,0:T(8,128)(2,1)S(1)}, u32[]{:S(2)}, u32[]{:S(2)}) collective-permute-start(bf16[2,2,2,2,1,2,24,768]{7,6,5,4,3,2,1,0:T(8,128)(2,1)S(1)} %bitcast.136), channel_id=1, source_target_pairs={{0,1},{1,0},{2,3},{3,2},{4,5},{5,4},{6,7},{7,6},{8,9},{9,8},{10,11... | collective-permute-start | bytes 3538952 | tf_op jit(solution)/shard_map/ppermute | solution.py:666
  229.7 27.2 %collective-permute-start.39 = (bf16[2,2,1,1,1,4,24,768]{7,6,5,4,3,2,1,0:T(8,128)(2,1)}, bf16[2,2,1,1,1,4,24,768]{7,6,5,4,3,2,1,0:T(8,128)(2,1)}, u32[]{:S(2)}, u32[]{:S(2)}) collective-permute-start(bf16[2,2,1,1,1,4,24,768]{7,6,5,4,3,2,1,0:T(8,128)(2,1)} %get-tuple-element.238), channel_id=1, source_target_pairs={{0,4},{1,5},{2,6},{3,7},{4,0},{5,1},{6,2},{7,3},{8,12},{9,13},{10,... | collective-permute-start | bytes 1769480 | tf_op jit(solution)/shard_map/ppermute | solution.py:666
  232.1 27.0 %collective-permute-start.37 = (bf16[2,2,2,1,1,2,24,768]{7,6,5,4,3,2,1,0:T(8,128)(2,1)}, bf16[2,2,2,1,1,2,24,768]{7,6,5,4,3,2,1,0:T(8,128)(2,1)}, u32[]{:S(2)}, u32[]{:S(2)}) collective-permute-start(bf16[2,2,2,1,1,2,24,768]{7,6,5,4,3,2,1,0:T(8,128)(2,1)} %get-tuple-element.236), channel_id=1, source_target_pairs={{0,2},{1,3},{2,0},{3,1},{4,6},{5,7},{6,4},{7,5},{8,10},{9,11},{10,... | collective-permute-start | bytes 1769480 | tf_op jit(solution)/shard_map/ppermute | solution.py:666
  233.7 26.7 %collective-permute-start.38 = (bf16[2,2,1,2,1,2,24,768]{7,6,5,4,3,2,1,0:T(8,128)(2,1)}, bf16[2,2,1,2,1,2,24,768]{7,6,5,4,3,2,1,0:T(8,128)(2,1)}, u32[]{:S(2)}, u32[]{:S(2)}) collective-permute-start(bf16[2,2,1,2,1,2,24,768]{7,6,5,4,3,2,1,0:T(8,128)(2,1)} %get-tuple-element.237), channel_id=1, source_target_pairs={{0,4},{1,5},{2,6},{3,7},{4,0},{5,1},{6,2},{7,3},{8,12},{9,13},{10,... | collective-permute-start | bytes 1769480 | tf_op jit(solution)/shard_map/ppermute | solution.py:666
  234.6 27.1 %collective-permute-start.40 = (bf16[2,2,1,1,1,4,24,768]{7,6,5,4,3,2,1,0:T(8,128)(2,1)}, bf16[2,2,1,1,1,4,24,768]{7,6,5,4,3,2,1,0:T(8,128)(2,1)}, u32[]{:S(2)}, u32[]{:S(2)}) collective-permute-start(bf16[2,2,1,1,1,4,24,768]{7,6,5,4,3,2,1,0:T(8,128)(2,1)} %get-tuple-element.239), channel_id=1, source_target_pairs={{0,2},{1,3},{2,0},{3,1},{4,6},{5,7},{6,4},{7,5},{8,10},{9,11},{10,... | collective-permute-start | bytes 1769480 | tf_op jit(solution)/shard_map/ppermute | solution.py:666
  256.8 11.4 %collective-permute-start.36 = (bf16[2,2,2,2,1,2,24,768]{7,6,5,4,3,2,1,0:T(8,128)(2,1)}, bf16[2,2,2,2,1,2,24,768]{7,6,5,4,3,2,1,0:T(8,128)(2,1)}, u32[]{:S(2)}, u32[]{:S(2)}) collective-permute-start(bf16[2,2,2,2,1,2,24,768]{7,6,5,4,3,2,1,0:T(8,128)(2,1)} %bitcast.57), channel_id=1, source_target_pairs={{0,1},{1,0},{2,3},{3,2},{4,5},{5,4},{6,7},{7,6},{8,9},{9,8},{10,11... | collective-permute-start | bytes 3538952 | tf_op jit(solution)/shard_map/ppermute | solution.py:666
  256.9 13.0 %collective-permute-start.35 = (bf16[2,2,2,2,1,2,24,768]{7,6,5,4,3,2,1,0:T(8,128)(2,1)}, bf16[2,2,2,2,1,2,24,768]{7,6,5,4,3,2,1,0:T(8,128)(2,1)}, u32[]{:S(2)}, u32[]{:S(2)}) collective-permute-start(bf16[2,2,2,2,1,2,24,768]{7,6,5,4,3,2,1,0:T(8,128)(2,1)} %bitcast.54), channel_id=1, source_target_pairs={{0,1},{1,0},{2,3},{3,2},{4,5},{5,4},{6,7},{7,6},{8,9},{9,8},{10,11... | collective-permute-start | bytes 3538952 | tf_op jit(solution)/shard_map/ppermute | solution.py:666
  266.6 15.3 %collective-permute-start.45 = (bf16[2,1,1,1,1,8,24,768]{7,6,5,4,3,2,1,0:T(8,128)(2,1)S(1)}, bf16[2,1,1,1,1,8,24,768]{7,6,5,4,3,2,1,0:T(8,128)(2,1)S(1)}, u32[]{:S(2)}, u32[]{:S(2)}) collective-permute-start(bf16[2,1,1,1,1,8,24,768]{7,6,5,4,3,2,1,0:T(8,128)(2,1)S(1)} %get-tuple-element.256), channel_id=1, source_target_pairs={{0,8},{1,9},{2,10},{3,11},{4,12},{5,13},{6,14},{7,15},{8,0},{9,1},... | collective-permute-start | bytes 1769480 | tf_op jit(solution)/shard_map/ppermute | solution.py:666
  271.7 14.7 %collective-permute-start.41 = (bf16[2,2,2,1,1,2,24,768]{7,6,5,4,3,2,1,0:T(8,128)(2,1)S(1)}, bf16[2,2,2,1,1,2,24,768]{7,6,5,4,3,2,1,0:T(8,128)(2,1)S(1)}, u32[]{:S(2)}, u32[]{:S(2)}) collective-permute-start(bf16[2,2,2,1,1,2,24,768]{7,6,5,4,3,2,1,0:T(8,128)(2,1)S(1)} %get-tuple-element.252), channel_id=1, source_target_pairs={{0,2},{1,3},{2,0},{3,1},{4,6},{5,7},{6,4},{7,5},{8,10},{9,11},{10,... | collective-permute-start | bytes 1769480 | tf_op jit(solution)/shard_map/ppermute | solution.py:666
  272.3 15.0 %collective-permute-start.42 = (bf16[2,2,1,2,1,2,24,768]{7,6,5,4,3,2,1,0:T(8,128)(2,1)S(1)}, bf16[2,2,1,2,1,2,24,768]{7,6,5,4,3,2,1,0:T(8,128)(2,1)S(1)}, u32[]{:S(2)}, u32[]{:S(2)}) collective-permute-start(bf16[2,2,1,2,1,2,24,768]{7,6,5,4,3,2,1,0:T(8,128)(2,1)S(1)} %get-tuple-element.253), channel_id=1, source_target_pairs={{0,4},{1,5},{2,6},{3,7},{4,0},{5,1},{6,2},{7,3},{8,12},{9,13},{10,... | collective-permute-start | bytes 1769480 | tf_op jit(solution)/shard_map/ppermute | solution.py:666
  288.2 11.1 %collective-permute-start.46 = (bf16[2,2,1,1,1,2,24,768]{7,6,5,4,3,2,1,0:T(8,128)(2,1)}, bf16[2,2,1,1,1,2,24,768]{7,6,5,4,3,2,1,0:T(8,128)(2,1)S(1)}, u32[]{:S(2)}, u32[]{:S(2)}) collective-permute-start(bf16[2,2,1,1,1,2,24,768]{7,6,5,4,3,2,1,0:T(8,128)(2,1)} %get-tuple-element.258), channel_id=1, source_target_pairs={{0,4},{1,5},{2,6},{3,7},{4,0},{5,1},{6,2},{7,3},{8,12},{9,13},{10,... | collective-permute-start | bytes 884744 | tf_op jit(solution)/shard_map/ppermute | solution.py:666
  296.8 19.6 %collective-permute-start.56 = (bf16[1,1,1,1,1,8,24,768]{7,6,5,4,3,2,1,0:T(8,128)(2,1)S(1)}, bf16[1,1,1,1,1,8,24,768]{7,6,5,4,3,2,1,0:T(8,128)(2,1)S(1)}, u32[]{:S(2)}, u32[]{:S(2)}) collective-permute-start(bf16[1,1,1,1,1,8,24,768]{7,6,5,4,3,2,1,0:T(8,128)(2,1)S(1)} %add_convert_fusion.22), channel_id=1, source_target_pairs={{0,16},{1,17},{2,18},{3,19},{4,20},{5,21},{6,22},{7,23},{8,24},{9,... | collective-permute-start | bytes 884744 | tf_op jit(solution)/shard_map/ppermute | solution.py:666
  304.1 18.1 %collective-permute-start.53 = (f32[1,1,1,2,1,1,4,128]{7,3,2,1,0,6,5,4:T(2,128)S(1)}, f32[1,1,1,2,1,1,4,128]{7,3,2,1,0,6,5,4:T(2,128)S(1)}, u32[]{:S(2)}, u32[]{:S(2)}) collective-permute-start(f32[1,1,1,2,1,1,4,128]{7,3,2,1,0,6,5,4:T(2,128)S(1)} %get-tuple-element.270), channel_id=1, source_target_pairs={{0,4},{1,5},{2,6},{3,7},{4,0},{5,1},{6,2},{7,3},{8,12},{9,13},{10,... | collective-permute-start | bytes 12296 | tf_op jit(solution)/shard_map/ppermute | solution.py:666
  305.0 17.2 %collective-permute-start.55 = (bf16[1,1,1,1,1,4,24,768]{7,6,5,4,3,2,1,0:T(8,128)(2,1)}, bf16[1,1,1,1,1,4,24,768]{7,6,5,4,3,2,1,0:T(8,128)(2,1)}, u32[]{:S(2)}, u32[]{:S(2)}) collective-permute-start(bf16[1,1,1,1,1,4,24,768]{7,6,5,4,3,2,1,0:T(8,128)(2,1)} %add_convert_fusion.35), channel_id=1, source_target_pairs={{0,16},{1,17},{2,18},{3,19},{4,20},{5,21},{6,22},{7,23},{8,24},{9,... | collective-permute-start | bytes 442376 | tf_op jit(solution)/shard_map/ppermute | solution.py:666
  306.1 17.2 %collective-permute-start.52 = (bf16[2,1,1,1,1,4,24,768]{7,6,5,4,3,2,1,0:T(8,128)(2,1)}, bf16[2,1,1,1,1,4,24,768]{7,6,5,4,3,2,1,0:T(8,128)(2,1)}, u32[]{:S(2)}, u32[]{:S(2)}) collective-permute-start(bf16[2,1,1,1,1,4,24,768]{7,6,5,4,3,2,1,0:T(8,128)(2,1)} %get-tuple-element.269), channel_id=1, source_target_pairs={{0,8},{1,9},{2,10},{3,11},{4,12},{5,13},{6,14},{7,15},{8,0},{9,1},... | collective-permute-start | bytes 884744 | tf_op jit(solution)/shard_map/ppermute | solution.py:666
  (98 other events, 569.3 us)

commit v7 on v6

--- a/solution.py
+++ b/solution.py
@@ -35,7 +35,7 @@
     return pl.BlockSpec(block, index)
 
 
-def run(body, name, grid, operands, in_specs, outs, scratch=(), flops=0, exps=0, limit=14):
+def run(body, name, grid, operands, in_specs, outs, scratch=(), flops=0, exps=0, limit=14, far=()):
     moved = sum(o.size * o.dtype.itemsize for o in operands)
     moved += sum(math.prod(s) * jnp.dtype(d).itemsize for s, d, _ in outs)
     return pl.pallas_call(
@@ -44,13 +44,20 @@
         grid=grid,
         in_specs=in_specs,
         out_specs=[o[2] for o in outs],
-        out_shape=[jax.ShapeDtypeStruct(o[0], o[1]) for o in outs],
+        out_shape=[
+            pltpu.HBM(o[0], o[1]) if i in far else jax.ShapeDtypeStruct(o[0], o[1])
+            for i, o in enumerate(outs)
+        ],
         scratch_shapes=list(scratch),
         compiler_params=pltpu.CompilerParams(
             dimension_semantics=("arbitrary",) * len(grid), vmem_limit_bytes=limit << 20
         ),
         cost_estimate=pl.CostEstimate(flops=flops, transcendentals=exps, bytes_accessed=moved),
     )(*operands)
+
+
+def in_hbm(values):
+    return pltpu.with_memory_space_constraint(values, pltpu.HBM)
 
 
 def normalised(values):
@@ -359,6 +366,7 @@
             ((8, width), WIDE, spec((8, width), lambda i: (0, 0))),
         ],
         flops=2 * rows * width * width,
+        far=(0,),
     )
 
 
@@ -461,6 +469,7 @@
         flops=12 * rows * width * width * mats,
         exps=2 * rows * width * mats,
         limit=30,
+        far=(0, 2, 4),
     )
     split = len(grads)
     return done[0], done[1 : 1 + split], done[1 + split : 1 + 2 * split], *done[1 + 2 * split :]
@@ -484,7 +493,7 @@
         late_back_body,
         "late_back",
         (rows // block,),
-        (grad_norm, late, grad, vec, cross_a),
+        (in_hbm(grad_norm), in_hbm(late), grad, vec, cross_a),
         [
             tile,
             tile,

time: 340 us -> 336 us (0.988)
  local copies, waits for them, and re-layouts: 38 us -> 29.4 us
    unnamed x144 -> x132, local copies, waits for them, and re-layouts: 15.8 us -> 7.26 us
    pallas_call x20, Pallas kernels: 116 us -> 119 us  [run(): pl.pallas_call(body, name=name, grid=grid, in_specs=in_specs, out_specs=[...]
  transfers between devices with their start and end apart: 58 -> 58, of which waited for: 29 -> 29; matrix products, arithmetic and copies ran while one was open for 13% -> 14% of each run, Pallas kernels for 22% -> 23%
where the time goes in v7:
time: 336 us; the launch traced here: 330 us
  Pallas kernels  119 us (35%)
  waiting for transfers between devices  82.9 us (25%)
  starting transfers between devices  59 us (18%)
  other arithmetic  35.7 us (11%)
  local copies, waits for them, and re-layouts  29.4 us (9%)
  between operations  3.62 us (1%)
    pallas_call x20, Pallas kernels, run(): pl.pallas_call(body, name=name, grid=grid, in_specs=in_specs, out_specs=[...  119 us
    ppermute x58, waiting for transfers between devices, swap(): lax.ppermute(values, 'fsdp', [(i, i ^ 1 << bit) for i in range(count)])  82.9 us
    ppermute x58, starting transfers between devices, swap(): lax.ppermute(values, 'fsdp', [(i, i ^ 1 << bit) for i in range(count)])  59 us
    convert_element_type x18, other arithmetic, total(): return (pair[0].astype(WIDE) + pair[1].astype(WIDE)).astype(kind)  21.1 us
    select_n x22, other arithmetic, land(): jnp.where(own_bit(bit) == 0, jnp.concatenate([held, other], axis), jnp.co...  8.39 us
    unnamed x132, local copies, waits for them, and re-layouts  7.26 us
  transfers between devices with their start and end apart: 58, of which 29 were waited for; matrix products, arithmetic and copies ran while one was open for 14% of the time, Pallas kernels for 23%

profile of v7, /device:TPU:0, one launch (start us, length us, event | category | flops | bytes accessed | tf_op | source)
XLA Modules:
  0.0 330.0 jit_solution(763926894959924167)
XLA Ops:
  4.7 4.1 %collective-permute-start = (bf16[1,1,1,1,1,4,24,768]{7,6,5,4,3,2,1,0:T(8,128)(2,1)S(1)}, bf16[1,1,1,1,1,4,24,768]{7,6,5,4,3,2,1,0:T(8,128)(2,1)S(1)}, u32[]{:S(2)}, u32[]{:S(2)}) collective-permute-start(bf16[1,1,1,1,1,4,24,768]{7,6,5,4,3,2,1,0:T(8,128)(2,1)S(1)} %maximum_bitcast_fusion.1), channel_id=1, source_target_pairs={{0,16},{1,17},{2,18},{3,19},{4,20},{5,21},{6,22},{7,23},{8,24},{9,... | collective-permute-start | bytes 442376 | tf_op jit(solution)/shard_map/ppermute | solution.py:675
  12.4 3.4 %collective-permute-done = bf16[1,1,1,1,1,4,24,768]{7,6,5,4,3,2,1,0:T(8,128)(2,1)S(1)} collective-permute-done((bf16[1,1,1,1,1,4,24,768]{7,6,5,4,3,2,1,0:T(8,128)(2,1)S(1)}, bf16[1,1,1,1,1,4,24,768]{7,6,5,4,3,2,1,0:T(8,128)(2,1)S(1)}, u32[]{:S(2)}, u32[]{:S(2)}) %collective-permute-start) | collective-permute-done | bytes 147488 | tf_op jit(solution)/shard_map/ppermute | solution.py:675
  20.8 3.2 collective-permute-done.2
  24.2 3.2 collective-permute-start.6
  30.6 5.8 %collective-permute-done.7 = bf16[1,1,1,1,1,4,24,768]{7,6,5,4,3,2,1,0:T(8,128)(2,1)S(1)} collective-permute-done((bf16[1,1,1,1,1,4,24,768]{7,6,5,4,3,2,1,0:T(8,128)(2,1)S(1)}, bf16[1,1,1,1,1,4,24,768]{7,6,5,4,3,2,1,0:T(8,128)(2,1)S(1)}, u32[]{:S(2)}, u32[]{:S(2)}) %collective-permute-start.7) | collective-permute-done | bytes 147488 | tf_op jit(solution)/shard_map/ppermute | solution.py:675
  38.4 2.6 collective-permute-start.12
  43.6 7.5 %collective-permute-done.10 = bf16[2,1,2,2,1,1,4,128]{7,6,5,4,3,2,1,0:T(4,128)(2,1)S(1)} collective-permute-done((bf16[2,1,2,2,1,1,4,128]{7,6,5,4,3,2,1,0:T(4,128)(2,1)S(1)}, bf16[2,1,2,2,1,1,4,128]{7,6,5,4,3,2,1,0:T(4,128)(2,1)S(1)}, u32[]{:S(2)}, u32[]{:S(2)}) %collective-permute-start.10) | collective-permute-done | bytes 8224 | tf_op jit(solution)/shard_map/ppermute | solution.py:675
  63.0 2.9 collective-permute-done.14
  75.4 3.8 %qkv.1 = (bf16[640,768]{1,0:T(8,128)(2,1)S(1)}, bf16[640,768]{1,0:T(8,128)(2,1)S(1)}, bf16[640,768]{1,0:T(8,128)(2,1)S(1)}, bf16[640,768]{1,0:T(8,128)(2,1)S(1)}) custom-call(bf16[640,768]{1,0:T(8,128)(2,1)S(1)} %bitcast.120, f32[16,768]{1,0:T(8,128)S(1)} %pad.13.vec_ref.refs_1_, bf16[2,768,768]{2,1,0:T(8,128)(2,1)S(1)} %bitcast.110, ...), custom_call_target="tpu_custom_call" | custom-call | flops 2264924160 | bytes 12042240 | tf_op jit(solution)/shard_map/qkv/pallas_call | solution.py:41
  82.7 3.6 %collective-permute-done.21 = bf16[2,2,2,1,1,2,24,768]{7,6,5,4,3,2,1,0:T(8,128)(2,1)S(1)} collective-permute-done((bf16[2,2,2,1,1,2,24,768]{7,6,5,4,3,2,1,0:T(8,128)(2,1)S(1)}, bf16[2,2,2,1,1,2,24,768]{7,6,5,4,3,2,1,0:T(8,128)(2,1)S(1)}, u32[]{:S(2)}, u32[]{:S(2)}) %collective-permute-start.21) | collective-permute-done | bytes 589856 | tf_op jit(solution)/shard_map/ppermute | solution.py:675
  87.0 5.4 %attend_self.1.a_ref.refs_2_ = bf16[640,768]{1,0:T(8,128)(2,1)S(1)} custom-call(bf16[640,768]{1,0:T(8,128)(2,1)S(1)} %get-tuple-element.172.q_ref, bf16[640,768]{1,0:T(8,128)(2,1)S(1)} %get-tuple-element.173.k_ref, bf16[640,768]{1,0:T(8,128)(2,1)S(1)} %get-tuple-element.174.v_ref), custom_call_target="tpu_custom_call" | custom-call | flops 629145600 | bytes 3932160 | tf_op jit(solution)/shard_map/attend_self/pallas_call | solution.py:41
  92.4 3.0 mid_stage.1
  103.2 3.2 attend_cross.1.a_ref.refs_2_
  106.5 4.0 %late_stage.1 = (f32[640,768]{1,0:T(8,128)}, bf16[640,768]{1,0:T(8,128)(2,1)S(1)}, f32[8,768]{1,0:T(8,128)S(1)}) custom-call(s32[2]{0:T(128)S(1)} %copy-done.34, bf16[640,768]{1,0:T(8,128)(2,1)S(1)} %attend_cross.1.a_ref.refs_2_, f32[640,768]{1,0:T(8,128)S(1)} %get-tuple-element.187.mid_ref, f32[16,768]{1,0:T(8,128)S(1)} %pad.13.vec_ref.refs_1_, ...), custom_call_target="tpu_custom_call" | custom-call | flops 754974720 | bytes 8331272 | tf_op jit(solution)/shard_map/late_stage/pallas_call | solution.py:41
  110.5 13.8 %collective-permute-done.23 = bf16[2,2,2,1,1,4,24,768]{7,6,5,4,3,2,1,0:T(8,128)(2,1)S(1)} collective-permute-done((bf16[2,2,2,1,1,4,24,768]{7,6,5,4,3,2,1,0:T(8,128)(2,1)S(1)}, bf16[2,2,2,1,1,4,24,768]{7,6,5,4,3,2,1,0:T(8,128)(2,1)S(1)}, u32[]{:S(2)}, u32[]{:S(2)}) %collective-permute-start.23) | collective-permute-done | bytes 1179680 | tf_op jit(solution)/shard_map/ppermute | solution.py:675
  132.7 3.4 %collective-permute-done.28 = bf16[2,2,2,2,1,4,24,768]{7,6,5,4,3,2,1,0:T(8,128)(2,1)} collective-permute-done((bf16[2,2,2,2,1,4,24,768]{7,6,5,4,3,2,1,0:T(8,128)(2,1)}, bf16[2,2,2,2,1,4,24,768]{7,6,5,4,3,2,1,0:T(8,128)(2,1)}, u32[]{:S(2)}, u32[]{:S(2)}) %collective-permute-start.28) | collective-permute-done | bytes 2359328 | tf_op jit(solution)/shard_map/ppermute | solution.py:675
  136.0 4.9 %weave.5 = (bf16[4,16,2,24,768]{4,3,2,1,0:T(8,128)(2,1)S(1)}, bf16[4,16,2,24,768]{4,3,2,1,0:T(8,128)(2,1)S(1)}) custom-call(s32[1]{0:T(128)} %bitcast.core_ref, bf16[16,4,24,768]{3,2,1,0:T(8,128)(2,1)} %bitcast.25.refs_0_, bf16[16,4,24,768]{3,2,1,0:T(8,128)(2,1)} %bitcast.26.refs_1_, bf16[16,4,24,768]{3,2,1,0:T(8,128)(2,1)} %bitcast.27.refs_2_, ...), custom_call_target="tpu_custom_call" | custom-call | bytes 18874372 | tf_op jit(solution)/shard_map/weave/pallas_call | solution.py:41
  140.9 39.8 %ffn_stage.1 = (f32[640,768]{1,0:T(8,128)}, bf16[16,4,24,768]{3,2,1,0:T(8,128)(2,1)}, bf16[16,4,24,768]{3,2,1,0:T(8,128)(2,1)}, bf16[16,4,24,768]{3,2,1,0:T(8,12...) custom-call(s32[2]{0:T(128)S(1)} %copy-done.34, ...), custom_call_target="tpu_custom_call" | custom-call | flops 18119393280 | bytes 25853964 | tf_op jit(solution)/shard_map/ffn_stage/pallas_call | solution.py:41
  181.4 5.4 %late_back.1 = (f32[640,768]{1,0:T(8,128)S(1)}, bf16[640,768]{1,0:T(8,128)(2,1)S(1)}, bf16[640,768]{1,0:T(8,128)(2,1)S(1)}, f32[8,768]{1,0:T(8,128)S(1)}) custom-call(f32[640,768]{1,0:T(8,128)} %get-tuple-element.204.gn_ref, f32[640,768]{1,0:T(8,128)} %get-tuple-element.194.refs_0_.late_ref, bf16[640,768]{1,0:T(8,128)(2,1)S(1)} %bitcast.119, ...), custom_call_target="tpu_custom_call" | custom-call | flops 754974720 | bytes 11280384 | tf_op jit(solution)/shard_map/late_back/pallas_call | solution.py:41
  194.4 5.4 %attend_cross_back.1 = (bf16[640,768]{1,0:T(8,128)(2,1)S(1)}, bf16[256,768]{1,0:T(8,128)(2,1)S(1)}, bf16[256,768]{1,0:T(8,128)(2,1)S(1)}) custom-call(bf16[640,768]{1,0:T(8,128)(2,1)S(1)} %copy-done.14, bf16[256,768]{1,0:T(8,128)(2,1)S(1)} %copy-done.19, bf16[256,768]{1,0:T(8,128)(2,1)S(1)} %copy-done.21, bf16[640,768]{1,0:T(8,128)(2,1)S(1)} %get-tuple-element.206.g_ref), custom_call_target="tpu_custom_call" | custom-call | flops 629145600 | bytes 4521984 | tf_op jit(solution)/shard_map/attend_cross_back/pallas_call | solution.py:41
  201.9 3.7 %weight_grads.4 = (bf16[16,2,24,768]{3,2,1,0:T(8,128)(2,1)S(1)}, bf16[16,2,24,768]{3,2,1,0:T(8,128)(2,1)S(1)}) custom-call(s32[1]{0:T(128)} %bitcast.core_ref, bf16[640,768]{1,0:T(8,128)(2,1)S(1)} %copy-done.31, bf16[640,768]{1,0:T(8,128)(2,1)S(1)} %get-tuple-element.219.refs_1_.gq, bf16[640,768]{1,0:T(8,128)(2,1)S(1)} %copy-done.12, ...), custom_call_target="tpu_custom_call" | custom-call | flops 1509949440 | bytes 6291460 | tf_op jit(solution)/shard_map/weight_grads/pallas_call | solution.py:41
  209.3 5.6 %mid_back.1 = (f32[640,768]{1,0:T(8,128)S(1)}, bf16[640,768]{1,0:T(8,128)(2,1)S(1)}, bf16[640,768]{1,0:T(8,128)(2,1)S(1)}, f32[8,768]{1,0:T(8,128)S(1)}) custom-call(bf16[640,768]{1,0:T(8,128)(2,1)S(1)} %get-tuple-element.219.refs_1_.gq, bf16[2,768,768]{2,1,0:T(8,128)(2,1)S(1)} %bitcast.101, f32[640,768]{1,0:T(8,128)S(1)} %copy-done.8, ...), custom_call_target="tpu_custom_call" | custom-call | flops 1509949440 | bytes 13639680 | tf_op jit(solution)/shard_map/mid_back/pallas_call | solution.py:41
  215.8 4.0 %collective-permute-done.33 = bf16[2,2,2,1,1,4,24,768]{7,6,5,4,3,2,1,0:T(8,128)(2,1)S(1)} collective-permute-done((bf16[2,2,2,1,1,4,24,768]{7,6,5,4,3,2,1,0:T(8,128)(2,1)S(1)}, bf16[2,2,2,1,1,4,24,768]{7,6,5,4,3,2,1,0:T(8,128)(2,1)S(1)}, u32[]{:S(2)}, u32[]{:S(2)}) %collective-permute-start.33) | collective-permute-done | bytes 1179680 | tf_op jit(solution)/shard_map/ppermute | solution.py:675
  232.9 10.0 %attend_self_back.1 = (bf16[640,768]{1,0:T(8,128)(2,1)S(1)}, bf16[640,768]{1,0:T(8,128)(2,1)S(1)}, bf16[640,768]{1,0:T(8,128)(2,1)S(1)}) custom-call(bf16[640,768]{1,0:T(8,128)(2,1)S(1)} %copy-done.45, bf16[640,768]{1,0:T(8,128)(2,1)S(1)} %copy-done.47, bf16[640,768]{1,0:T(8,128)(2,1)S(1)} %copy-done.49, bf16[640,768]{1,0:T(8,128)(2,1)S(1)} %copy-done.39), custom_call_target="tpu_custom_call" | custom-call | flops 1572864000 | bytes 6881280 | tf_op jit(solution)/shard_map/attend_self_back/pallas_call | solution.py:41
  243.0 4.5 %weight_grads.7 = (bf16[16,2,24,768]{3,2,1,0:T(8,128)(2,1)}, bf16[16,2,24,768]{3,2,1,0:T(8,128)(2,1)S(1)}) custom-call(s32[1]{0:T(128)} %bitcast.core_ref, bf16[640,768]{1,0:T(8,128)(2,1)S(1)} %copy-done.43, bf16[640,768]{1,0:T(8,128)(2,1)S(1)} %get-tuple-element.248.refs_1_.gv, bf16[640,768]{1,0:T(8,128)(2,1)S(1)} %copy-done.23, bf16[640,768]{1,0:T(8,128)(2,1)S(1)} %copy-done.37), custom_call_target="tpu_custom_call" | custom-call | flops 1509949440 | bytes 6291460 | tf_op jit(solution)/shard_map/weight_grads/pallas_call | solution.py:41
  247.5 4.7 %weight_grads.6 = (bf16[16,2,24,768]{3,2,1,0:T(8,128)(2,1)}, bf16[16,2,24,768]{3,2,1,0:T(8,128)(2,1)S(1)}) custom-call(s32[1]{0:T(128)} %bitcast.core_ref, bf16[640,768]{1,0:T(8,128)(2,1)S(1)} %copy-done.43, bf16[640,768]{1,0:T(8,128)(2,1)S(1)} %get-tuple-element.246.refs_1_.gq, bf16[640,768]{1,0:T(8,128)(2,1)S(1)} %copy-done.43, ...), custom_call_target="tpu_custom_call" | custom-call | flops 1509949440 | bytes 6291460 | tf_op jit(solution)/shard_map/weight_grads/pallas_call | solution.py:41
  270.2 6.9 %in_back.1 = (bf16[640,768]{1,0:T(8,128)(2,1)}, f32[8,768]{1,0:T(8,128)S(1)}) custom-call(bf16[640,768]{1,0:T(8,128)(2,1)S(1)} %copy-done.25, bf16[640,768]{1,0:T(8,128)(2,1)S(1)} %copy-done.27, bf16[640,768]{1,0:T(8,128)(2,1)S(1)} %copy-done.29, bf16[2,768,768]{2,1,0:T(8,128)(2,1)S(1)} %bitcast.112, bf16[2,768,768]{2,1,0:T(8,128)(2,1)S(1)} %bitcast.113, ...), custom_call_target="tpu_custom_call" | custom-call | flops 2264924160 | bytes 14032896 | tf_op jit(solution)/shard_map/in_back/pallas_call | solution.py:41
  277.2 4.5 %collective-permute-done.41 = bf16[2,2,2,1,1,2,24,768]{7,6,5,4,3,2,1,0:T(8,128)(2,1)S(1)} collective-permute-done((bf16[2,2,2,1,1,2,24,768]{7,6,5,4,3,2,1,0:T(8,128)(2,1)S(1)}, bf16[2,2,2,1,1,2,24,768]{7,6,5,4,3,2,1,0:T(8,128)(2,1)S(1)}, u32[]{:S(2)}, u32[]{:S(2)}) %collective-permute-start.41) | collective-permute-done | bytes 589856 | tf_op jit(solution)/shard_map/ppermute | solution.py:675
  294.7 2.5 collective-permute-done.48
  303.1 8.6 %collective-permute-done.56 = bf16[1,1,1,1,1,8,24,768]{7,6,5,4,3,2,1,0:T(8,128)(2,1)S(1)} collective-permute-done((bf16[1,1,1,1,1,8,24,768]{7,6,5,4,3,2,1,0:T(8,128)(2,1)S(1)}, bf16[1,1,1,1,1,8,24,768]{7,6,5,4,3,2,1,0:T(8,128)(2,1)S(1)}, u32[]{:S(2)}, u32[]{:S(2)}) %collective-permute-start.56) | collective-permute-done | bytes 294944 | tf_op jit(solution)/shard_map/ppermute | solution.py:675
  315.0 2.5 reshape.1462
  320.4 2.9 collective-permute-done.57
  (359 shorter events, 137.4 us)
Async XLA Ops:
  4.7 11.1 %collective-permute-start = (bf16[1,1,1,1,1,4,24,768]{7,6,5,4,3,2,1,0:T(8,128)(2,1)S(1)}, bf16[1,1,1,1,1,4,24,768]{7,6,5,4,3,2,1,0:T(8,128)(2,1)S(1)}, u32[]{:S(2)}, u32[]{:S(2)}) collective-permute-start(bf16[1,1,1,1,1,4,24,768]{7,6,5,4,3,2,1,0:T(8,128)(2,1)S(1)} %maximum_bitcast_fusion.1), channel_id=1, source_target_pairs={{0,16},{1,17},{2,18},{3,19},{4,20},{5,21},{6,22},{7,23},{8,24},{9,... | collective-permute-start | bytes 442376 | tf_op jit(solution)/shard_map/ppermute | solution.py:675
  36.9 14.2 %collective-permute-start.11 = (bf16[2,1,1,1,1,4,24,768]{7,6,5,4,3,2,1,0:T(8,128)(2,1)S(1)}, bf16[2,1,1,1,1,4,24,768]{7,6,5,4,3,2,1,0:T(8,128)(2,1)S(1)}, u32[]{:S(2)}, u32[]{:S(2)}) collective-permute-start(bf16[2,1,1,1,1,4,24,768]{7,6,5,4,3,2,1,0:T(8,128)(2,1)S(1)} %maximum_select_fusion.17), channel_id=1, source_target_pairs={{0,8},{1,9},{2,10},{3,11},{4,12},{5,13},{6,14},{7,15},{8,0},{9,1},... | collective-permute-start | bytes 884744 | tf_op jit(solution)/shard_map/ppermute | solution.py:675
  38.4 13.7 %collective-permute-start.12 = (bf16[1,1,1,1,1,8,24,768]{7,6,5,4,3,2,1,0:T(8,128)(2,1)S(1)}, bf16[1,1,1,1,1,8,24,768]{7,6,5,4,3,2,1,0:T(8,128)(2,1)S(1)}, u32[]{:S(2)}, u32[]{:S(2)}) collective-permute-start(bf16[1,1,1,1,1,8,24,768]{7,6,5,4,3,2,1,0:T(8,128)(2,1)S(1)} %maximum_bitcast_fusion), channel_id=1, source_target_pairs={{0,16},{1,17},{2,18},{3,19},{4,20},{5,21},{6,22},{7,23},{8,24},{9,... | collective-permute-start | bytes 884744 | tf_op jit(solution)/shard_map/ppermute | solution.py:675
  41.6 12.1 %collective-permute-start.8 = (bf16[2,2,2,1,1,2,24,768]{7,6,5,4,3,2,1,0:T(8,128)(2,1)S(1)}, bf16[2,2,2,1,1,2,24,768]{7,6,5,4,3,2,1,0:T(8,128)(2,1)S(1)}, u32[]{:S(2)}, u32[]{:S(2)}) collective-permute-start(bf16[2,2,2,1,1,2,24,768]{7,6,5,4,3,2,1,0:T(8,128)(2,1)S(1)} %maximum_select_fusion.10), channel_id=1, source_target_pairs={{0,2},{1,3},{2,0},{3,1},{4,6},{5,7},{6,4},{7,5},{8,10},{9,11},{10,... | collective-permute-start | bytes 1769480 | tf_op jit(solution)/shard_map/ppermute | solution.py:675
  43.1 11.9 %collective-permute-start.9 = (bf16[2,2,1,2,1,2,24,768]{7,6,5,4,3,2,1,0:T(8,128)(2,1)S(1)}, bf16[2,2,1,2,1,2,24,768]{7,6,5,4,3,2,1,0:T(8,128)(2,1)S(1)}, u32[]{:S(2)}, u32[]{:S(2)}) collective-permute-start(bf16[2,2,1,2,1,2,24,768]{7,6,5,4,3,2,1,0:T(8,128)(2,1)S(1)} %maximum_select_fusion.11), channel_id=1, source_target_pairs={{0,4},{1,5},{2,6},{3,7},{4,0},{5,1},{6,2},{7,3},{8,12},{9,13},{10,... | collective-permute-start | bytes 1769480 | tf_op jit(solution)/shard_map/ppermute | solution.py:675
  55.0 18.2 %collective-permute-start.17 = (bf16[2,2,2,2,1,2,24,768]{7,6,5,4,3,2,1,0:T(8,128)(2,1)S(1)}, bf16[2,2,2,2,1,2,24,768]{7,6,5,4,3,2,1,0:T(8,128)(2,1)}, u32[]{:S(2)}, u32[]{:S(2)}) collective-permute-start(bf16[2,2,2,2,1,2,24,768]{7,6,5,4,3,2,1,0:T(8,128)(2,1)S(1)} %maximum_select_fusion.2), channel_id=1, source_target_pairs={{0,1},{1,0},{2,3},{3,2},{4,5},{5,4},{6,7},{7,6},{8,9},{9,8},{10,11... | collective-permute-start | bytes 3538952 | tf_op jit(solution)/shard_map/ppermute | solution.py:675
  55.1 18.2 %collective-permute-start.18 = (bf16[2,2,2,2,1,2,24,768]{7,6,5,4,3,2,1,0:T(8,128)(2,1)S(1)}, bf16[2,2,2,2,1,2,24,768]{7,6,5,4,3,2,1,0:T(8,128)(2,1)}, u32[]{:S(2)}, u32[]{:S(2)}) collective-permute-start(bf16[2,2,2,2,1,2,24,768]{7,6,5,4,3,2,1,0:T(8,128)(2,1)S(1)} %maximum_select_fusion.3), channel_id=1, source_target_pairs={{0,1},{1,0},{2,3},{3,2},{4,5},{5,4},{6,7},{7,6},{8,9},{9,8},{10,11... | collective-permute-start | bytes 3538952 | tf_op jit(solution)/shard_map/ppermute | solution.py:675
  55.6 16.1 %collective-permute-start.13 = (bf16[2,1,1,1,1,8,24,768]{7,6,5,4,3,2,1,0:T(8,128)(2,1)S(1)}, bf16[2,1,1,1,1,8,24,768]{7,6,5,4,3,2,1,0:T(8,128)(2,1)}, u32[]{:S(2)}, u32[]{:S(2)}) collective-permute-start(bf16[2,1,1,1,1,8,24,768]{7,6,5,4,3,2,1,0:T(8,128)(2,1)S(1)} %maximum_select_fusion.13), channel_id=1, source_target_pairs={{0,8},{1,9},{2,10},{3,11},{4,12},{5,13},{6,14},{7,15},{8,0},{9,1},... | collective-permute-start | bytes 1769480 | tf_op jit(solution)/shard_map/ppermute | solution.py:675
  70.1 16.3 %collective-permute-start.21 = (bf16[2,2,2,1,1,2,24,768]{7,6,5,4,3,2,1,0:T(8,128)(2,1)S(1)}, bf16[2,2,2,1,1,2,24,768]{7,6,5,4,3,2,1,0:T(8,128)(2,1)S(1)}, u32[]{:S(2)}, u32[]{:S(2)}) collective-permute-start(bf16[2,2,2,1,1,2,24,768]{7,6,5,4,3,2,1,0:T(8,128)(2,1)S(1)} %maximum_select_fusion.14), channel_id=1, source_target_pairs={{0,2},{1,3},{2,0},{3,1},{4,6},{5,7},{6,4},{7,5},{8,10},{9,11},{10,... | collective-permute-start | bytes 1769480 | tf_op jit(solution)/shard_map/ppermute | solution.py:675
  70.7 16.2 %collective-permute-start.22 = (bf16[2,2,1,2,1,2,24,768]{7,6,5,4,3,2,1,0:T(8,128)(2,1)S(1)}, bf16[2,2,1,2,1,2,24,768]{7,6,5,4,3,2,1,0:T(8,128)(2,1)S(1)}, u32[]{:S(2)}, u32[]{:S(2)}) collective-permute-start(bf16[2,2,1,2,1,2,24,768]{7,6,5,4,3,2,1,0:T(8,128)(2,1)S(1)} %maximum_select_fusion.15), channel_id=1, source_target_pairs={{0,4},{1,5},{2,6},{3,7},{4,0},{5,1},{6,2},{7,3},{8,12},{9,13},{10,... | collective-permute-start | bytes 1769480 | tf_op jit(solution)/shard_map/ppermute | solution.py:675
  80.3 17.3 %collective-permute-start.19 = (bf16[2,2,1,1,1,4,24,768]{7,6,5,4,3,2,1,0:T(8,128)(2,1)S(1)}, bf16[2,2,1,1,1,4,24,768]{7,6,5,4,3,2,1,0:T(8,128)(2,1)S(1)}, u32[]{:S(2)}, u32[]{:S(2)}) collective-permute-start(bf16[2,2,1,1,1,4,24,768]{7,6,5,4,3,2,1,0:T(8,128)(2,1)S(1)} %get-tuple-element.168), channel_id=1, source_target_pairs={{0,4},{1,5},{2,6},{3,7},{4,0},{5,1},{6,2},{7,3},{8,12},{9,13},{10,... | collective-permute-start | bytes 1769480 | tf_op jit(solution)/shard_map/ppermute | solution.py:675
  81.2 16.4 %collective-permute-start.20 = (bf16[2,2,1,1,1,4,24,768]{7,6,5,4,3,2,1,0:T(8,128)(2,1)S(1)}, bf16[2,2,1,1,1,4,24,768]{7,6,5,4,3,2,1,0:T(8,128)(2,1)S(1)}, u32[]{:S(2)}, u32[]{:S(2)}) collective-permute-start(bf16[2,2,1,1,1,4,24,768]{7,6,5,4,3,2,1,0:T(8,128)(2,1)S(1)} %get-tuple-element.169), channel_id=1, source_target_pairs={{0,2},{1,3},{2,0},{3,1},{4,6},{5,7},{6,4},{7,5},{8,10},{9,11},{10,... | collective-permute-start | bytes 1769480 | tf_op jit(solution)/shard_map/ppermute | solution.py:675
  97.8 26.6 %collective-permute-start.23 = (bf16[2,2,2,1,1,4,24,768]{7,6,5,4,3,2,1,0:T(8,128)(2,1)S(1)}, bf16[2,2,2,1,1,4,24,768]{7,6,5,4,3,2,1,0:T(8,128)(2,1)S(1)}, u32[]{:S(2)}, u32[]{:S(2)}) collective-permute-start(bf16[2,2,2,1,1,4,24,768]{7,6,5,4,3,2,1,0:T(8,128)(2,1)S(1)} %maximum_select_fusion.5), channel_id=1, source_target_pairs={{0,2},{1,3},{2,0},{3,1},{4,6},{5,7},{6,4},{7,5},{8,10},{9,11},{10,... | collective-permute-start | bytes 3538952 | tf_op jit(solution)/shard_map/ppermute | solution.py:675
  99.3 26.6 %collective-permute-start.24 = (bf16[2,2,1,2,1,4,24,768]{7,6,5,4,3,2,1,0:T(8,128)(2,1)S(1)}, bf16[2,2,1,2,1,4,24,768]{7,6,5,4,3,2,1,0:T(8,128)(2,1)S(1)}, u32[]{:S(2)}, u32[]{:S(2)}) collective-permute-start(bf16[2,2,1,2,1,4,24,768]{7,6,5,4,3,2,1,0:T(8,128)(2,1)S(1)} %maximum_select_fusion.6), channel_id=1, source_target_pairs={{0,4},{1,5},{2,6},{3,7},{4,0},{5,1},{6,2},{7,3},{8,12},{9,13},{10,... | collective-permute-start | bytes 3538952 | tf_op jit(solution)/shard_map/ppermute | solution.py:675
  191.8 28.1 %collective-permute-start.33 = (bf16[2,2,2,1,1,4,24,768]{7,6,5,4,3,2,1,0:T(8,128)(2,1)S(1)}, bf16[2,2,2,1,1,4,24,768]{7,6,5,4,3,2,1,0:T(8,128)(2,1)S(1)}, u32[]{:S(2)}, u32[]{:S(2)}) collective-permute-start(bf16[2,2,2,1,1,4,24,768]{7,6,5,4,3,2,1,0:T(8,128)(2,1)S(1)} %get-tuple-element.217), channel_id=1, source_target_pairs={{0,2},{1,3},{2,0},{3,1},{4,6},{5,7},{6,4},{7,5},{8,10},{9,11},{10,... | collective-permute-start | bytes 3538952 | tf_op jit(solution)/shard_map/ppermute | solution.py:675
  193.4 27.8 %collective-permute-start.34 = (bf16[2,2,1,2,1,4,24,768]{7,6,5,4,3,2,1,0:T(8,128)(2,1)S(1)}, bf16[2,2,1,2,1,4,24,768]{7,6,5,4,3,2,1,0:T(8,128)(2,1)S(1)}, u32[]{:S(2)}, u32[]{:S(2)}) collective-permute-start(bf16[2,2,1,2,1,4,24,768]{7,6,5,4,3,2,1,0:T(8,128)(2,1)S(1)} %get-tuple-element.218), channel_id=1, source_target_pairs={{0,4},{1,5},{2,6},{3,7},{4,0},{5,1},{6,2},{7,3},{8,12},{9,13},{10,... | collective-permute-start | bytes 3538952 | tf_op jit(solution)/shard_map/ppermute | solution.py:675
  205.6 16.9 %collective-permute-start.32 = (bf16[2,2,2,2,1,2,24,768]{7,6,5,4,3,2,1,0:T(8,128)(2,1)S(1)}, bf16[2,2,2,2,1,2,24,768]{7,6,5,4,3,2,1,0:T(8,128)(2,1)S(1)}, u32[]{:S(2)}, u32[]{:S(2)}) collective-permute-start(bf16[2,2,2,2,1,2,24,768]{7,6,5,4,3,2,1,0:T(8,128)(2,1)S(1)} %bitcast.135), channel_id=1, source_target_pairs={{0,1},{1,0},{2,3},{3,2},{4,5},{5,4},{6,7},{7,6},{8,9},{9,8},{10,11... | collective-permute-start | bytes 3538952 | tf_op jit(solution)/shard_map/ppermute | solution.py:675
  205.7 18.2 %collective-permute-start.31 = (bf16[2,2,2,2,1,2,24,768]{7,6,5,4,3,2,1,0:T(8,128)(2,1)S(1)}, bf16[2,2,2,2,1,2,24,768]{7,6,5,4,3,2,1,0:T(8,128)(2,1)S(1)}, u32[]{:S(2)}, u32[]{:S(2)}) collective-permute-start(bf16[2,2,2,2,1,2,24,768]{7,6,5,4,3,2,1,0:T(8,128)(2,1)S(1)} %bitcast.134), channel_id=1, source_target_pairs={{0,1},{1,0},{2,3},{3,2},{4,5},{5,4},{6,7},{7,6},{8,9},{9,8},{10,11... | collective-permute-start | bytes 3538952 | tf_op jit(solution)/shard_map/ppermute | solution.py:675
  225.1 27.2 %collective-permute-start.39 = (bf16[2,2,1,1,1,4,24,768]{7,6,5,4,3,2,1,0:T(8,128)(2,1)}, bf16[2,2,1,1,1,4,24,768]{7,6,5,4,3,2,1,0:T(8,128)(2,1)}, u32[]{:S(2)}, u32[]{:S(2)}) collective-permute-start(bf16[2,2,1,1,1,4,24,768]{7,6,5,4,3,2,1,0:T(8,128)(2,1)} %get-tuple-element.238), channel_id=1, source_target_pairs={{0,4},{1,5},{2,6},{3,7},{4,0},{5,1},{6,2},{7,3},{8,12},{9,13},{10,... | collective-permute-start | bytes 1769480 | tf_op jit(solution)/shard_map/ppermute | solution.py:675
  227.5 26.9 %collective-permute-start.37 = (bf16[2,2,2,1,1,2,24,768]{7,6,5,4,3,2,1,0:T(8,128)(2,1)}, bf16[2,2,2,1,1,2,24,768]{7,6,5,4,3,2,1,0:T(8,128)(2,1)}, u32[]{:S(2)}, u32[]{:S(2)}) collective-permute-start(bf16[2,2,2,1,1,2,24,768]{7,6,5,4,3,2,1,0:T(8,128)(2,1)} %get-tuple-element.236), channel_id=1, source_target_pairs={{0,2},{1,3},{2,0},{3,1},{4,6},{5,7},{6,4},{7,5},{8,10},{9,11},{10,... | collective-permute-start | bytes 1769480 | tf_op jit(solution)/shard_map/ppermute | solution.py:675
  229.0 26.7 %collective-permute-start.38 = (bf16[2,2,1,2,1,2,24,768]{7,6,5,4,3,2,1,0:T(8,128)(2,1)}, bf16[2,2,1,2,1,2,24,768]{7,6,5,4,3,2,1,0:T(8,128)(2,1)}, u32[]{:S(2)}, u32[]{:S(2)}) collective-permute-start(bf16[2,2,1,2,1,2,24,768]{7,6,5,4,3,2,1,0:T(8,128)(2,1)} %get-tuple-element.237), channel_id=1, source_target_pairs={{0,4},{1,5},{2,6},{3,7},{4,0},{5,1},{6,2},{7,3},{8,12},{9,13},{10,... | collective-permute-start | bytes 1769480 | tf_op jit(solution)/shard_map/ppermute | solution.py:675
  230.0 27.1 %collective-permute-start.40 = (bf16[2,2,1,1,1,4,24,768]{7,6,5,4,3,2,1,0:T(8,128)(2,1)}, bf16[2,2,1,1,1,4,24,768]{7,6,5,4,3,2,1,0:T(8,128)(2,1)}, u32[]{:S(2)}, u32[]{:S(2)}) collective-permute-start(bf16[2,2,1,1,1,4,24,768]{7,6,5,4,3,2,1,0:T(8,128)(2,1)} %get-tuple-element.239), channel_id=1, source_target_pairs={{0,2},{1,3},{2,0},{3,1},{4,6},{5,7},{6,4},{7,5},{8,10},{9,11},{10,... | collective-permute-start | bytes 1769480 | tf_op jit(solution)/shard_map/ppermute | solution.py:675
  252.2 11.4 %collective-permute-start.36 = (bf16[2,2,2,2,1,2,24,768]{7,6,5,4,3,2,1,0:T(8,128)(2,1)}, bf16[2,2,2,2,1,2,24,768]{7,6,5,4,3,2,1,0:T(8,128)(2,1)}, u32[]{:S(2)}, u32[]{:S(2)}) collective-permute-start(bf16[2,2,2,2,1,2,24,768]{7,6,5,4,3,2,1,0:T(8,128)(2,1)} %bitcast.57), channel_id=1, source_target_pairs={{0,1},{1,0},{2,3},{3,2},{4,5},{5,4},{6,7},{7,6},{8,9},{9,8},{10,11... | collective-permute-start | bytes 3538952 | tf_op jit(solution)/shard_map/ppermute | solution.py:675
  252.3 13.0 %collective-permute-start.35 = (bf16[2,2,2,2,1,2,24,768]{7,6,5,4,3,2,1,0:T(8,128)(2,1)}, bf16[2,2,2,2,1,2,24,768]{7,6,5,4,3,2,1,0:T(8,128)(2,1)}, u32[]{:S(2)}, u32[]{:S(2)}) collective-permute-start(bf16[2,2,2,2,1,2,24,768]{7,6,5,4,3,2,1,0:T(8,128)(2,1)} %bitcast.54), channel_id=1, source_target_pairs={{0,1},{1,0},{2,3},{3,2},{4,5},{5,4},{6,7},{7,6},{8,9},{9,8},{10,11... | collective-permute-start | bytes 3538952 | tf_op jit(solution)/shard_map/ppermute | solution.py:675
  261.9 15.3 %collective-permute-start.45 = (bf16[2,1,1,1,1,8,24,768]{7,6,5,4,3,2,1,0:T(8,128)(2,1)S(1)}, bf16[2,1,1,1,1,8,24,768]{7,6,5,4,3,2,1,0:T(8,128)(2,1)S(1)}, u32[]{:S(2)}, u32[]{:S(2)}) collective-permute-start(bf16[2,1,1,1,1,8,24,768]{7,6,5,4,3,2,1,0:T(8,128)(2,1)S(1)} %get-tuple-element.256), channel_id=1, source_target_pairs={{0,8},{1,9},{2,10},{3,11},{4,12},{5,13},{6,14},{7,15},{8,0},{9,1},... | collective-permute-start | bytes 1769480 | tf_op jit(solution)/shard_map/ppermute | solution.py:675
  267.0 14.7 %collective-permute-start.41 = (bf16[2,2,2,1,1,2,24,768]{7,6,5,4,3,2,1,0:T(8,128)(2,1)S(1)}, bf16[2,2,2,1,1,2,24,768]{7,6,5,4,3,2,1,0:T(8,128)(2,1)S(1)}, u32[]{:S(2)}, u32[]{:S(2)}) collective-permute-start(bf16[2,2,2,1,1,2,24,768]{7,6,5,4,3,2,1,0:T(8,128)(2,1)S(1)} %get-tuple-element.252), channel_id=1, source_target_pairs={{0,2},{1,3},{2,0},{3,1},{4,6},{5,7},{6,4},{7,5},{8,10},{9,11},{10,... | collective-permute-start | bytes 1769480 | tf_op jit(solution)/shard_map/ppermute | solution.py:675
  267.7 15.0 %collective-permute-start.42 = (bf16[2,2,1,2,1,2,24,768]{7,6,5,4,3,2,1,0:T(8,128)(2,1)S(1)}, bf16[2,2,1,2,1,2,24,768]{7,6,5,4,3,2,1,0:T(8,128)(2,1)S(1)}, u32[]{:S(2)}, u32[]{:S(2)}) collective-permute-start(bf16[2,2,1,2,1,2,24,768]{7,6,5,4,3,2,1,0:T(8,128)(2,1)S(1)} %get-tuple-element.253), channel_id=1, source_target_pairs={{0,4},{1,5},{2,6},{3,7},{4,0},{5,1},{6,2},{7,3},{8,12},{9,13},{10,... | collective-permute-start | bytes 1769480 | tf_op jit(solution)/shard_map/ppermute | solution.py:675
  283.6 11.1 %collective-permute-start.46 = (bf16[2,2,1,1,1,2,24,768]{7,6,5,4,3,2,1,0:T(8,128)(2,1)}, bf16[2,2,1,1,1,2,24,768]{7,6,5,4,3,2,1,0:T(8,128)(2,1)S(1)}, u32[]{:S(2)}, u32[]{:S(2)}) collective-permute-start(bf16[2,2,1,1,1,2,24,768]{7,6,5,4,3,2,1,0:T(8,128)(2,1)} %get-tuple-element.258), channel_id=1, source_target_pairs={{0,4},{1,5},{2,6},{3,7},{4,0},{5,1},{6,2},{7,3},{8,12},{9,13},{10,... | collective-permute-start | bytes 884744 | tf_op jit(solution)/shard_map/ppermute | solution.py:675
  292.2 19.6 %collective-permute-start.56 = (bf16[1,1,1,1,1,8,24,768]{7,6,5,4,3,2,1,0:T(8,128)(2,1)S(1)}, bf16[1,1,1,1,1,8,24,768]{7,6,5,4,3,2,1,0:T(8,128)(2,1)S(1)}, u32[]{:S(2)}, u32[]{:S(2)}) collective-permute-start(bf16[1,1,1,1,1,8,24,768]{7,6,5,4,3,2,1,0:T(8,128)(2,1)S(1)} %add_convert_fusion.22), channel_id=1, source_target_pairs={{0,16},{1,17},{2,18},{3,19},{4,20},{5,21},{6,22},{7,23},{8,24},{9,... | collective-permute-start | bytes 884744 | tf_op jit(solution)/shard_map/ppermute | solution.py:675
  299.5 18.1 %collective-permute-start.53 = (f32[1,1,1,2,1,1,4,128]{7,3,2,1,0,6,5,4:T(2,128)S(1)}, f32[1,1,1,2,1,1,4,128]{7,3,2,1,0,6,5,4:T(2,128)S(1)}, u32[]{:S(2)}, u32[]{:S(2)}) collective-permute-start(f32[1,1,1,2,1,1,4,128]{7,3,2,1,0,6,5,4:T(2,128)S(1)} %get-tuple-element.270), channel_id=1, source_target_pairs={{0,4},{1,5},{2,6},{3,7},{4,0},{5,1},{6,2},{7,3},{8,12},{9,13},{10,... | collective-permute-start | bytes 12296 | tf_op jit(solution)/shard_map/ppermute | solution.py:675
  300.4 17.2 %collective-permute-start.55 = (bf16[1,1,1,1,1,4,24,768]{7,6,5,4,3,2,1,0:T(8,128)(2,1)}, bf16[1,1,1,1,1,4,24,768]{7,6,5,4,3,2,1,0:T(8,128)(2,1)}, u32[]{:S(2)}, u32[]{:S(2)}) collective-permute-start(bf16[1,1,1,1,1,4,24,768]{7,6,5,4,3,2,1,0:T(8,128)(2,1)} %add_convert_fusion.35), channel_id=1, source_target_pairs={{0,16},{1,17},{2,18},{3,19},{4,20},{5,21},{6,22},{7,23},{8,24},{9,... | collective-permute-start | bytes 442376 | tf_op jit(solution)/shard_map/ppermute | solution.py:675
  301.5 17.1 %collective-permute-start.52 = (bf16[2,1,1,1,1,4,24,768]{7,6,5,4,3,2,1,0:T(8,128)(2,1)}, bf16[2,1,1,1,1,4,24,768]{7,6,5,4,3,2,1,0:T(8,128)(2,1)}, u32[]{:S(2)}, u32[]{:S(2)}) collective-permute-start(bf16[2,1,1,1,1,4,24,768]{7,6,5,4,3,2,1,0:T(8,128)(2,1)} %get-tuple-element.269), channel_id=1, source_target_pairs={{0,8},{1,9},{2,10},{3,11},{4,12},{5,13},{6,14},{7,15},{8,0},{9,1},... | collective-permute-start | bytes 884744 | tf_op jit(solution)/shard_map/ppermute | solution.py:675
  (92 other events, 560.6 us)

commit v8 on v7

--- a/solution.py
+++ b/solution.py
@@ -878,7 +878,7 @@
     norm_three = tick([g_ffn], norm_three)
     w_in, w_out = g_ffn.result()
     grad_norm, d_in, d_out, sums_ff, result, square_rest = ffn_stage(
-        lengths, core, count, norm_three, grad, bias, w_in, w_out, None, late, vec, batch, block
+        lengths, core, count, norm_three, grad, bias, w_in, w_out, None, late, vec, batch, length
     )
     s_ffn = Scatter([d_in, d_out], count)
     grad_norm = tick([s_ffn], grad_norm)

time: 336 us -> 328 us (0.976)
  Pallas kernels: 119 us -> 111 us
    pallas_call x20, Pallas kernels: 119 us -> 111 us  [run(): pl.pallas_call(body, name=name, grid=grid, in_specs=in_specs, out_specs=[...]
where the time goes in v8:
time: 328 us; the launch traced here: 322 us
  Pallas kernels  111 us (34%)
  waiting for transfers between devices  82.9 us (25%)
  starting transfers between devices  59 us (18%)
  other arithmetic  35.7 us (11%)
  local copies, waits for them, and re-layouts  29.4 us (9%)
  between operations  3.62 us (1%)
    pallas_call x20, Pallas kernels, run(): pl.pallas_call(body, name=name, grid=grid, in_specs=in_specs, out_specs=[...  111 us
    ppermute x58, waiting for transfers between devices, swap(): lax.ppermute(values, 'fsdp', [(i, i ^ 1 << bit) for i in range(count)])  82.9 us
    ppermute x58, starting transfers between devices, swap(): lax.ppermute(values, 'fsdp', [(i, i ^ 1 << bit) for i in range(count)])  59 us
    convert_element_type x18, other arithmetic, total(): return (pair[0].astype(WIDE) + pair[1].astype(WIDE)).astype(kind)  21.1 us
    select_n x22, other arithmetic, land(): jnp.where(own_bit(bit) == 0, jnp.concatenate([held, other], axis), jnp.co...  8.39 us
    unnamed x132, local copies, waits for them, and re-layouts  7.26 us
  transfers between devices with their start and end apart: 58, of which 29 were waited for; matrix products, arithmetic and copies ran while one was open for 14% of the time, Pallas kernels for 23%

profile of v8, /device:TPU:0, one launch (start us, length us, event | category | flops | bytes accessed | tf_op | source)
XLA Modules:
  0.0 322.0 jit_solution(2993637498239402064)
XLA Ops:
  4.7 4.1 %collective-permute-start = (bf16[1,1,1,1,1,4,24,768]{7,6,5,4,3,2,1,0:T(8,128)(2,1)S(1)}, bf16[1,1,1,1,1,4,24,768]{7,6,5,4,3,2,1,0:T(8,128)(2,1)S(1)}, u32[]{:S(2)}, u32[]{:S(2)}) collective-permute-start(bf16[1,1,1,1,1,4,24,768]{7,6,5,4,3,2,1,0:T(8,128)(2,1)S(1)} %maximum_bitcast_fusion.1), channel_id=1, source_target_pairs={{0,16},{1,17},{2,18},{3,19},{4,20},{5,21},{6,22},{7,23},{8,24},{9,... | collective-permute-start | bytes 442376 | tf_op jit(solution)/shard_map/ppermute | solution.py:675
  12.4 3.4 %collective-permute-done = bf16[1,1,1,1,1,4,24,768]{7,6,5,4,3,2,1,0:T(8,128)(2,1)S(1)} collective-permute-done((bf16[1,1,1,1,1,4,24,768]{7,6,5,4,3,2,1,0:T(8,128)(2,1)S(1)}, bf16[1,1,1,1,1,4,24,768]{7,6,5,4,3,2,1,0:T(8,128)(2,1)S(1)}, u32[]{:S(2)}, u32[]{:S(2)}) %collective-permute-start) | collective-permute-done | bytes 147488 | tf_op jit(solution)/shard_map/ppermute | solution.py:675
  20.8 3.2 %collective-permute-done.2 = bf16[2,1,1,1,1,4,24,768]{7,6,5,4,3,2,1,0:T(8,128)(2,1)S(1)} collective-permute-done((bf16[2,1,1,1,1,4,24,768]{7,6,5,4,3,2,1,0:T(8,128)(2,1)S(1)}, bf16[2,1,1,1,1,4,24,768]{7,6,5,4,3,2,1,0:T(8,128)(2,1)S(1)}, u32[]{:S(2)}, u32[]{:S(2)}) %collective-permute-start.2) | collective-permute-done | bytes 294944 | tf_op jit(solution)/shard_map/ppermute | solution.py:675
  24.2 3.2 collective-permute-start.6
  30.6 5.8 %collective-permute-done.7 = bf16[1,1,1,1,1,4,24,768]{7,6,5,4,3,2,1,0:T(8,128)(2,1)S(1)} collective-permute-done((bf16[1,1,1,1,1,4,24,768]{7,6,5,4,3,2,1,0:T(8,128)(2,1)S(1)}, bf16[1,1,1,1,1,4,24,768]{7,6,5,4,3,2,1,0:T(8,128)(2,1)S(1)}, u32[]{:S(2)}, u32[]{:S(2)}) %collective-permute-start.7) | collective-permute-done | bytes 147488 | tf_op jit(solution)/shard_map/ppermute | solution.py:675
  38.4 2.6 collective-permute-start.12
  43.6 7.5 %collective-permute-done.10 = bf16[2,1,2,2,1,1,4,128]{7,6,5,4,3,2,1,0:T(4,128)(2,1)S(1)} collective-permute-done((bf16[2,1,2,2,1,1,4,128]{7,6,5,4,3,2,1,0:T(4,128)(2,1)S(1)}, bf16[2,1,2,2,1,1,4,128]{7,6,5,4,3,2,1,0:T(4,128)(2,1)S(1)}, u32[]{:S(2)}, u32[]{:S(2)}) %collective-permute-start.10) | collective-permute-done | bytes 8224 | tf_op jit(solution)/shard_map/ppermute | solution.py:675
  63.0 2.9 collective-permute-done.14
  75.4 3.8 %qkv.1 = (bf16[640,768]{1,0:T(8,128)(2,1)S(1)}, bf16[640,768]{1,0:T(8,128)(2,1)S(1)}, bf16[640,768]{1,0:T(8,128)(2,1)S(1)}, bf16[640,768]{1,0:T(8,128)(2,1)S(1)}) custom-call(bf16[640,768]{1,0:T(8,128)(2,1)S(1)} %bitcast.120, f32[16,768]{1,0:T(8,128)S(1)} %pad.13.vec_ref.refs_1_, bf16[2,768,768]{2,1,0:T(8,128)(2,1)S(1)} %bitcast.110, ...), custom_call_target="tpu_custom_call" | custom-call | flops 2264924160 | bytes 12042240 | tf_op jit(solution)/shard_map/qkv/pallas_call | solution.py:41
  82.7 3.6 %collective-permute-done.21 = bf16[2,2,2,1,1,2,24,768]{7,6,5,4,3,2,1,0:T(8,128)(2,1)S(1)} collective-permute-done((bf16[2,2,2,1,1,2,24,768]{7,6,5,4,3,2,1,0:T(8,128)(2,1)S(1)}, bf16[2,2,2,1,1,2,24,768]{7,6,5,4,3,2,1,0:T(8,128)(2,1)S(1)}, u32[]{:S(2)}, u32[]{:S(2)}) %collective-permute-start.21) | collective-permute-done | bytes 589856 | tf_op jit(solution)/shard_map/ppermute | solution.py:675
  87.0 5.4 %attend_self.1.a_ref.refs_2_ = bf16[640,768]{1,0:T(8,128)(2,1)S(1)} custom-call(bf16[640,768]{1,0:T(8,128)(2,1)S(1)} %get-tuple-element.172.q_ref, bf16[640,768]{1,0:T(8,128)(2,1)S(1)} %get-tuple-element.173.k_ref, bf16[640,768]{1,0:T(8,128)(2,1)S(1)} %get-tuple-element.174.v_ref), custom_call_target="tpu_custom_call" | custom-call | flops 629145600 | bytes 3932160 | tf_op jit(solution)/shard_map/attend_self/pallas_call | solution.py:41
  92.4 3.0 mid_stage.1
  103.2 3.2 attend_cross.1.a_ref.refs_2_
  106.5 4.0 %late_stage.1 = (f32[640,768]{1,0:T(8,128)}, bf16[640,768]{1,0:T(8,128)(2,1)S(1)}, f32[8,768]{1,0:T(8,128)S(1)}) custom-call(s32[2]{0:T(128)S(1)} %copy-done.34, bf16[640,768]{1,0:T(8,128)(2,1)S(1)} %attend_cross.1.a_ref.refs_2_, f32[640,768]{1,0:T(8,128)S(1)} %get-tuple-element.187.mid_ref, f32[16,768]{1,0:T(8,128)S(1)} %pad.13.vec_ref.refs_1_, ...), custom_call_target="tpu_custom_call" | custom-call | flops 754974720 | bytes 8331272 | tf_op jit(solution)/shard_map/late_stage/pallas_call | solution.py:41
  110.5 13.8 %collective-permute-done.23 = bf16[2,2,2,1,1,4,24,768]{7,6,5,4,3,2,1,0:T(8,128)(2,1)S(1)} collective-permute-done((bf16[2,2,2,1,1,4,24,768]{7,6,5,4,3,2,1,0:T(8,128)(2,1)S(1)}, bf16[2,2,2,1,1,4,24,768]{7,6,5,4,3,2,1,0:T(8,128)(2,1)S(1)}, u32[]{:S(2)}, u32[]{:S(2)}) %collective-permute-start.23) | collective-permute-done | bytes 1179680 | tf_op jit(solution)/shard_map/ppermute | solution.py:675
  132.7 3.4 %collective-permute-done.28 = bf16[2,2,2,2,1,4,24,768]{7,6,5,4,3,2,1,0:T(8,128)(2,1)} collective-permute-done((bf16[2,2,2,2,1,4,24,768]{7,6,5,4,3,2,1,0:T(8,128)(2,1)}, bf16[2,2,2,2,1,4,24,768]{7,6,5,4,3,2,1,0:T(8,128)(2,1)}, u32[]{:S(2)}, u32[]{:S(2)}) %collective-permute-start.28) | collective-permute-done | bytes 2359328 | tf_op jit(solution)/shard_map/ppermute | solution.py:675
  136.0 4.9 %weave.5 = (bf16[4,16,2,24,768]{4,3,2,1,0:T(8,128)(2,1)S(1)}, bf16[4,16,2,24,768]{4,3,2,1,0:T(8,128)(2,1)S(1)}) custom-call(s32[1]{0:T(128)} %bitcast.core_ref, bf16[16,4,24,768]{3,2,1,0:T(8,128)(2,1)} %bitcast.25.refs_0_, bf16[16,4,24,768]{3,2,1,0:T(8,128)(2,1)} %bitcast.26.refs_1_, bf16[16,4,24,768]{3,2,1,0:T(8,128)(2,1)} %bitcast.27.refs_2_, ...), custom_call_target="tpu_custom_call" | custom-call | bytes 18874372 | tf_op jit(solution)/shard_map/weave/pallas_call | solution.py:41
  140.9 31.9 %ffn_stage.1 = (f32[640,768]{1,0:T(8,128)}, bf16[16,4,24,768]{3,2,1,0:T(8,128)(2,1)}, bf16[16,4,24,768]{3,2,1,0:T(8,128)(2,1)}, bf16[16,4,24,768]{3,2,1,0:T(8,12...) custom-call(s32[2]{0:T(128)S(1)} %copy-done.34, ...), custom_call_target="tpu_custom_call" | custom-call | flops 18119393280 | bytes 25853964 | tf_op jit(solution)/shard_map/ffn_stage/pallas_call | solution.py:41
  173.4 5.4 %late_back.1 = (f32[640,768]{1,0:T(8,128)S(1)}, bf16[640,768]{1,0:T(8,128)(2,1)S(1)}, bf16[640,768]{1,0:T(8,128)(2,1)S(1)}, f32[8,768]{1,0:T(8,128)S(1)}) custom-call(f32[640,768]{1,0:T(8,128)} %get-tuple-element.204.gn_ref, f32[640,768]{1,0:T(8,128)} %get-tuple-element.194.refs_0_.late_ref, bf16[640,768]{1,0:T(8,128)(2,1)S(1)} %bitcast.119, ...), custom_call_target="tpu_custom_call" | custom-call | flops 754974720 | bytes 11280384 | tf_op jit(solution)/shard_map/late_back/pallas_call | solution.py:41
  186.5 5.4 %attend_cross_back.1 = (bf16[640,768]{1,0:T(8,128)(2,1)S(1)}, bf16[256,768]{1,0:T(8,128)(2,1)S(1)}, bf16[256,768]{1,0:T(8,128)(2,1)S(1)}) custom-call(bf16[640,768]{1,0:T(8,128)(2,1)S(1)} %copy-done.14, bf16[256,768]{1,0:T(8,128)(2,1)S(1)} %copy-done.19, bf16[256,768]{1,0:T(8,128)(2,1)S(1)} %copy-done.21, bf16[640,768]{1,0:T(8,128)(2,1)S(1)} %get-tuple-element.206.g_ref), custom_call_target="tpu_custom_call" | custom-call | flops 629145600 | bytes 4521984 | tf_op jit(solution)/shard_map/attend_cross_back/pallas_call | solution.py:41
  193.9 3.7 %weight_grads.4 = (bf16[16,2,24,768]{3,2,1,0:T(8,128)(2,1)S(1)}, bf16[16,2,24,768]{3,2,1,0:T(8,128)(2,1)S(1)}) custom-call(s32[1]{0:T(128)} %bitcast.core_ref, bf16[640,768]{1,0:T(8,128)(2,1)S(1)} %copy-done.31, bf16[640,768]{1,0:T(8,128)(2,1)S(1)} %get-tuple-element.219.refs_1_.gq, bf16[640,768]{1,0:T(8,128)(2,1)S(1)} %copy-done.12, ...), custom_call_target="tpu_custom_call" | custom-call | flops 1509949440 | bytes 6291460 | tf_op jit(solution)/shard_map/weight_grads/pallas_call | solution.py:41
  198.2 2.7 frames_back.1
  201.5 5.4 %mid_back.1 = (f32[640,768]{1,0:T(8,128)S(1)}, bf16[640,768]{1,0:T(8,128)(2,1)S(1)}, bf16[640,768]{1,0:T(8,128)(2,1)S(1)}, f32[8,768]{1,0:T(8,128)S(1)}) custom-call(bf16[640,768]{1,0:T(8,128)(2,1)S(1)} %get-tuple-element.219.refs_1_.gq, bf16[2,768,768]{2,1,0:T(8,128)(2,1)S(1)} %bitcast.101, f32[640,768]{1,0:T(8,128)S(1)} %copy-done.8, ...), custom_call_target="tpu_custom_call" | custom-call | flops 1509949440 | bytes 13639680 | tf_op jit(solution)/shard_map/mid_back/pallas_call | solution.py:41
  207.9 4.0 %collective-permute-done.33 = bf16[2,2,2,1,1,4,24,768]{7,6,5,4,3,2,1,0:T(8,128)(2,1)S(1)} collective-permute-done((bf16[2,2,2,1,1,4,24,768]{7,6,5,4,3,2,1,0:T(8,128)(2,1)S(1)}, bf16[2,2,2,1,1,4,24,768]{7,6,5,4,3,2,1,0:T(8,128)(2,1)S(1)}, u32[]{:S(2)}, u32[]{:S(2)}) %collective-permute-start.33) | collective-permute-done | bytes 1179680 | tf_op jit(solution)/shard_map/ppermute | solution.py:675
  225.0 10.0 %attend_self_back.1 = (bf16[640,768]{1,0:T(8,128)(2,1)S(1)}, bf16[640,768]{1,0:T(8,128)(2,1)S(1)}, bf16[640,768]{1,0:T(8,128)(2,1)S(1)}) custom-call(bf16[640,768]{1,0:T(8,128)(2,1)S(1)} %copy-done.45, bf16[640,768]{1,0:T(8,128)(2,1)S(1)} %copy-done.47, bf16[640,768]{1,0:T(8,128)(2,1)S(1)} %copy-done.49, bf16[640,768]{1,0:T(8,128)(2,1)S(1)} %copy-done.39), custom_call_target="tpu_custom_call" | custom-call | flops 1572864000 | bytes 6881280 | tf_op jit(solution)/shard_map/attend_self_back/pallas_call | solution.py:41
  235.1 4.5 %weight_grads.7 = (bf16[16,2,24,768]{3,2,1,0:T(8,128)(2,1)}, bf16[16,2,24,768]{3,2,1,0:T(8,128)(2,1)S(1)}) custom-call(s32[1]{0:T(128)} %bitcast.core_ref, bf16[640,768]{1,0:T(8,128)(2,1)S(1)} %copy-done.43, bf16[640,768]{1,0:T(8,128)(2,1)S(1)} %get-tuple-element.248.refs_1_.gv, bf16[640,768]{1,0:T(8,128)(2,1)S(1)} %copy-done.23, bf16[640,768]{1,0:T(8,128)(2,1)S(1)} %copy-done.37), custom_call_target="tpu_custom_call" | custom-call | flops 1509949440 | bytes 6291460 | tf_op jit(solution)/shard_map/weight_grads/pallas_call | solution.py:41
  239.6 4.7 %weight_grads.6 = (bf16[16,2,24,768]{3,2,1,0:T(8,128)(2,1)}, bf16[16,2,24,768]{3,2,1,0:T(8,128)(2,1)S(1)}) custom-call(s32[1]{0:T(128)} %bitcast.core_ref, bf16[640,768]{1,0:T(8,128)(2,1)S(1)} %copy-done.43, bf16[640,768]{1,0:T(8,128)(2,1)S(1)} %get-tuple-element.246.refs_1_.gq, bf16[640,768]{1,0:T(8,128)(2,1)S(1)} %copy-done.43, ...), custom_call_target="tpu_custom_call" | custom-call | flops 1509949440 | bytes 6291460 | tf_op jit(solution)/shard_map/weight_grads/pallas_call | solution.py:41
  262.3 6.9 %in_back.1 = (bf16[640,768]{1,0:T(8,128)(2,1)}, f32[8,768]{1,0:T(8,128)S(1)}) custom-call(bf16[640,768]{1,0:T(8,128)(2,1)S(1)} %copy-done.25, bf16[640,768]{1,0:T(8,128)(2,1)S(1)} %copy-done.27, bf16[640,768]{1,0:T(8,128)(2,1)S(1)} %copy-done.29, bf16[2,768,768]{2,1,0:T(8,128)(2,1)S(1)} %bitcast.112, bf16[2,768,768]{2,1,0:T(8,128)(2,1)S(1)} %bitcast.113, ...), custom_call_target="tpu_custom_call" | custom-call | flops 2264924160 | bytes 14032896 | tf_op jit(solution)/shard_map/in_back/pallas_call | solution.py:41
  269.3 4.5 %collective-permute-done.41 = bf16[2,2,2,1,1,2,24,768]{7,6,5,4,3,2,1,0:T(8,128)(2,1)S(1)} collective-permute-done((bf16[2,2,2,1,1,2,24,768]{7,6,5,4,3,2,1,0:T(8,128)(2,1)S(1)}, bf16[2,2,2,1,1,2,24,768]{7,6,5,4,3,2,1,0:T(8,128)(2,1)S(1)}, u32[]{:S(2)}, u32[]{:S(2)}) %collective-permute-start.41) | collective-permute-done | bytes 589856 | tf_op jit(solution)/shard_map/ppermute | solution.py:675
  295.1 8.6 %collective-permute-done.56 = bf16[1,1,1,1,1,8,24,768]{7,6,5,4,3,2,1,0:T(8,128)(2,1)S(1)} collective-permute-done((bf16[1,1,1,1,1,8,24,768]{7,6,5,4,3,2,1,0:T(8,128)(2,1)S(1)}, bf16[1,1,1,1,1,8,24,768]{7,6,5,4,3,2,1,0:T(8,128)(2,1)S(1)}, u32[]{:S(2)}, u32[]{:S(2)}) %collective-permute-start.56) | collective-permute-done | bytes 294944 | tf_op jit(solution)/shard_map/ppermute | solution.py:675
  307.1 2.5 reshape.1462
  312.4 2.9 collective-permute-done.57
  (359 shorter events, 137.4 us)
Async XLA Ops:
  4.7 11.1 %collective-permute-start = (bf16[1,1,1,1,1,4,24,768]{7,6,5,4,3,2,1,0:T(8,128)(2,1)S(1)}, bf16[1,1,1,1,1,4,24,768]{7,6,5,4,3,2,1,0:T(8,128)(2,1)S(1)}, u32[]{:S(2)}, u32[]{:S(2)}) collective-permute-start(bf16[1,1,1,1,1,4,24,768]{7,6,5,4,3,2,1,0:T(8,128)(2,1)S(1)} %maximum_bitcast_fusion.1), channel_id=1, source_target_pairs={{0,16},{1,17},{2,18},{3,19},{4,20},{5,21},{6,22},{7,23},{8,24},{9,... | collective-permute-start | bytes 442376 | tf_op jit(solution)/shard_map/ppermute | solution.py:675
  36.9 14.2 %collective-permute-start.11 = (bf16[2,1,1,1,1,4,24,768]{7,6,5,4,3,2,1,0:T(8,128)(2,1)S(1)}, bf16[2,1,1,1,1,4,24,768]{7,6,5,4,3,2,1,0:T(8,128)(2,1)S(1)}, u32[]{:S(2)}, u32[]{:S(2)}) collective-permute-start(bf16[2,1,1,1,1,4,24,768]{7,6,5,4,3,2,1,0:T(8,128)(2,1)S(1)} %maximum_select_fusion.17), channel_id=1, source_target_pairs={{0,8},{1,9},{2,10},{3,11},{4,12},{5,13},{6,14},{7,15},{8,0},{9,1},... | collective-permute-start | bytes 884744 | tf_op jit(solution)/shard_map/ppermute | solution.py:675
  38.4 13.7 %collective-permute-start.12 = (bf16[1,1,1,1,1,8,24,768]{7,6,5,4,3,2,1,0:T(8,128)(2,1)S(1)}, bf16[1,1,1,1,1,8,24,768]{7,6,5,4,3,2,1,0:T(8,128)(2,1)S(1)}, u32[]{:S(2)}, u32[]{:S(2)}) collective-permute-start(bf16[1,1,1,1,1,8,24,768]{7,6,5,4,3,2,1,0:T(8,128)(2,1)S(1)} %maximum_bitcast_fusion), channel_id=1, source_target_pairs={{0,16},{1,17},{2,18},{3,19},{4,20},{5,21},{6,22},{7,23},{8,24},{9,... | collective-permute-start | bytes 884744 | tf_op jit(solution)/shard_map/ppermute | solution.py:675
  41.6 12.1 %collective-permute-start.8 = (bf16[2,2,2,1,1,2,24,768]{7,6,5,4,3,2,1,0:T(8,128)(2,1)S(1)}, bf16[2,2,2,1,1,2,24,768]{7,6,5,4,3,2,1,0:T(8,128)(2,1)S(1)}, u32[]{:S(2)}, u32[]{:S(2)}) collective-permute-start(bf16[2,2,2,1,1,2,24,768]{7,6,5,4,3,2,1,0:T(8,128)(2,1)S(1)} %maximum_select_fusion.10), channel_id=1, source_target_pairs={{0,2},{1,3},{2,0},{3,1},{4,6},{5,7},{6,4},{7,5},{8,10},{9,11},{10,... | collective-permute-start | bytes 1769480 | tf_op jit(solution)/shard_map/ppermute | solution.py:675
  43.1 11.9 %collective-permute-start.9 = (bf16[2,2,1,2,1,2,24,768]{7,6,5,4,3,2,1,0:T(8,128)(2,1)S(1)}, bf16[2,2,1,2,1,2,24,768]{7,6,5,4,3,2,1,0:T(8,128)(2,1)S(1)}, u32[]{:S(2)}, u32[]{:S(2)}) collective-permute-start(bf16[2,2,1,2,1,2,24,768]{7,6,5,4,3,2,1,0:T(8,128)(2,1)S(1)} %maximum_select_fusion.11), channel_id=1, source_target_pairs={{0,4},{1,5},{2,6},{3,7},{4,0},{5,1},{6,2},{7,3},{8,12},{9,13},{10,... | collective-permute-start | bytes 1769480 | tf_op jit(solution)/shard_map/ppermute | solution.py:675
  55.0 18.2 %collective-permute-start.17 = (bf16[2,2,2,2,1,2,24,768]{7,6,5,4,3,2,1,0:T(8,128)(2,1)S(1)}, bf16[2,2,2,2,1,2,24,768]{7,6,5,4,3,2,1,0:T(8,128)(2,1)}, u32[]{:S(2)}, u32[]{:S(2)}) collective-permute-start(bf16[2,2,2,2,1,2,24,768]{7,6,5,4,3,2,1,0:T(8,128)(2,1)S(1)} %maximum_select_fusion.2), channel_id=1, source_target_pairs={{0,1},{1,0},{2,3},{3,2},{4,5},{5,4},{6,7},{7,6},{8,9},{9,8},{10,11... | collective-permute-start | bytes 3538952 | tf_op jit(solution)/shard_map/ppermute | solution.py:675
  55.1 18.2 %collective-permute-start.18 = (bf16[2,2,2,2,1,2,24,768]{7,6,5,4,3,2,1,0:T(8,128)(2,1)S(1)}, bf16[2,2,2,2,1,2,24,768]{7,6,5,4,3,2,1,0:T(8,128)(2,1)}, u32[]{:S(2)}, u32[]{:S(2)}) collective-permute-start(bf16[2,2,2,2,1,2,24,768]{7,6,5,4,3,2,1,0:T(8,128)(2,1)S(1)} %maximum_select_fusion.3), channel_id=1, source_target_pairs={{0,1},{1,0},{2,3},{3,2},{4,5},{5,4},{6,7},{7,6},{8,9},{9,8},{10,11... | collective-permute-start | bytes 3538952 | tf_op jit(solution)/shard_map/ppermute | solution.py:675
  55.6 16.1 %collective-permute-start.13 = (bf16[2,1,1,1,1,8,24,768]{7,6,5,4,3,2,1,0:T(8,128)(2,1)S(1)}, bf16[2,1,1,1,1,8,24,768]{7,6,5,4,3,2,1,0:T(8,128)(2,1)}, u32[]{:S(2)}, u32[]{:S(2)}) collective-permute-start(bf16[2,1,1,1,1,8,24,768]{7,6,5,4,3,2,1,0:T(8,128)(2,1)S(1)} %maximum_select_fusion.13), channel_id=1, source_target_pairs={{0,8},{1,9},{2,10},{3,11},{4,12},{5,13},{6,14},{7,15},{8,0},{9,1},... | collective-permute-start | bytes 1769480 | tf_op jit(solution)/shard_map/ppermute | solution.py:675
  70.1 16.3 %collective-permute-start.21 = (bf16[2,2,2,1,1,2,24,768]{7,6,5,4,3,2,1,0:T(8,128)(2,1)S(1)}, bf16[2,2,2,1,1,2,24,768]{7,6,5,4,3,2,1,0:T(8,128)(2,1)S(1)}, u32[]{:S(2)}, u32[]{:S(2)}) collective-permute-start(bf16[2,2,2,1,1,2,24,768]{7,6,5,4,3,2,1,0:T(8,128)(2,1)S(1)} %maximum_select_fusion.14), channel_id=1, source_target_pairs={{0,2},{1,3},{2,0},{3,1},{4,6},{5,7},{6,4},{7,5},{8,10},{9,11},{10,... | collective-permute-start | bytes 1769480 | tf_op jit(solution)/shard_map/ppermute | solution.py:675
  70.7 16.2 %collective-permute-start.22 = (bf16[2,2,1,2,1,2,24,768]{7,6,5,4,3,2,1,0:T(8,128)(2,1)S(1)}, bf16[2,2,1,2,1,2,24,768]{7,6,5,4,3,2,1,0:T(8,128)(2,1)S(1)}, u32[]{:S(2)}, u32[]{:S(2)}) collective-permute-start(bf16[2,2,1,2,1,2,24,768]{7,6,5,4,3,2,1,0:T(8,128)(2,1)S(1)} %maximum_select_fusion.15), channel_id=1, source_target_pairs={{0,4},{1,5},{2,6},{3,7},{4,0},{5,1},{6,2},{7,3},{8,12},{9,13},{10,... | collective-permute-start | bytes 1769480 | tf_op jit(solution)/shard_map/ppermute | solution.py:675
  80.3 17.3 %collective-permute-start.19 = (bf16[2,2,1,1,1,4,24,768]{7,6,5,4,3,2,1,0:T(8,128)(2,1)S(1)}, bf16[2,2,1,1,1,4,24,768]{7,6,5,4,3,2,1,0:T(8,128)(2,1)S(1)}, u32[]{:S(2)}, u32[]{:S(2)}) collective-permute-start(bf16[2,2,1,1,1,4,24,768]{7,6,5,4,3,2,1,0:T(8,128)(2,1)S(1)} %get-tuple-element.168), channel_id=1, source_target_pairs={{0,4},{1,5},{2,6},{3,7},{4,0},{5,1},{6,2},{7,3},{8,12},{9,13},{10,... | collective-permute-start | bytes 1769480 | tf_op jit(solution)/shard_map/ppermute | solution.py:675
  81.2 16.4 %collective-permute-start.20 = (bf16[2,2,1,1,1,4,24,768]{7,6,5,4,3,2,1,0:T(8,128)(2,1)S(1)}, bf16[2,2,1,1,1,4,24,768]{7,6,5,4,3,2,1,0:T(8,128)(2,1)S(1)}, u32[]{:S(2)}, u32[]{:S(2)}) collective-permute-start(bf16[2,2,1,1,1,4,24,768]{7,6,5,4,3,2,1,0:T(8,128)(2,1)S(1)} %get-tuple-element.169), channel_id=1, source_target_pairs={{0,2},{1,3},{2,0},{3,1},{4,6},{5,7},{6,4},{7,5},{8,10},{9,11},{10,... | collective-permute-start | bytes 1769480 | tf_op jit(solution)/shard_map/ppermute | solution.py:675
  97.8 26.6 %collective-permute-start.23 = (bf16[2,2,2,1,1,4,24,768]{7,6,5,4,3,2,1,0:T(8,128)(2,1)S(1)}, bf16[2,2,2,1,1,4,24,768]{7,6,5,4,3,2,1,0:T(8,128)(2,1)S(1)}, u32[]{:S(2)}, u32[]{:S(2)}) collective-permute-start(bf16[2,2,2,1,1,4,24,768]{7,6,5,4,3,2,1,0:T(8,128)(2,1)S(1)} %maximum_select_fusion.5), channel_id=1, source_target_pairs={{0,2},{1,3},{2,0},{3,1},{4,6},{5,7},{6,4},{7,5},{8,10},{9,11},{10,... | collective-permute-start | bytes 3538952 | tf_op jit(solution)/shard_map/ppermute | solution.py:675
  99.3 26.6 %collective-permute-start.24 = (bf16[2,2,1,2,1,4,24,768]{7,6,5,4,3,2,1,0:T(8,128)(2,1)S(1)}, bf16[2,2,1,2,1,4,24,768]{7,6,5,4,3,2,1,0:T(8,128)(2,1)S(1)}, u32[]{:S(2)}, u32[]{:S(2)}) collective-permute-start(bf16[2,2,1,2,1,4,24,768]{7,6,5,4,3,2,1,0:T(8,128)(2,1)S(1)} %maximum_select_fusion.6), channel_id=1, source_target_pairs={{0,4},{1,5},{2,6},{3,7},{4,0},{5,1},{6,2},{7,3},{8,12},{9,13},{10,... | collective-permute-start | bytes 3538952 | tf_op jit(solution)/shard_map/ppermute | solution.py:675
  183.8 28.1 %collective-permute-start.33 = (bf16[2,2,2,1,1,4,24,768]{7,6,5,4,3,2,1,0:T(8,128)(2,1)S(1)}, bf16[2,2,2,1,1,4,24,768]{7,6,5,4,3,2,1,0:T(8,128)(2,1)S(1)}, u32[]{:S(2)}, u32[]{:S(2)}) collective-permute-start(bf16[2,2,2,1,1,4,24,768]{7,6,5,4,3,2,1,0:T(8,128)(2,1)S(1)} %get-tuple-element.217), channel_id=1, source_target_pairs={{0,2},{1,3},{2,0},{3,1},{4,6},{5,7},{6,4},{7,5},{8,10},{9,11},{10,... | collective-permute-start | bytes 3538952 | tf_op jit(solution)/shard_map/ppermute | solution.py:675
  185.4 27.8 %collective-permute-start.34 = (bf16[2,2,1,2,1,4,24,768]{7,6,5,4,3,2,1,0:T(8,128)(2,1)S(1)}, bf16[2,2,1,2,1,4,24,768]{7,6,5,4,3,2,1,0:T(8,128)(2,1)S(1)}, u32[]{:S(2)}, u32[]{:S(2)}) collective-permute-start(bf16[2,2,1,2,1,4,24,768]{7,6,5,4,3,2,1,0:T(8,128)(2,1)S(1)} %get-tuple-element.218), channel_id=1, source_target_pairs={{0,4},{1,5},{2,6},{3,7},{4,0},{5,1},{6,2},{7,3},{8,12},{9,13},{10,... | collective-permute-start | bytes 3538952 | tf_op jit(solution)/shard_map/ppermute | solution.py:675
  197.7 16.9 %collective-permute-start.32 = (bf16[2,2,2,2,1,2,24,768]{7,6,5,4,3,2,1,0:T(8,128)(2,1)S(1)}, bf16[2,2,2,2,1,2,24,768]{7,6,5,4,3,2,1,0:T(8,128)(2,1)S(1)}, u32[]{:S(2)}, u32[]{:S(2)}) collective-permute-start(bf16[2,2,2,2,1,2,24,768]{7,6,5,4,3,2,1,0:T(8,128)(2,1)S(1)} %bitcast.135), channel_id=1, source_target_pairs={{0,1},{1,0},{2,3},{3,2},{4,5},{5,4},{6,7},{7,6},{8,9},{9,8},{10,11... | collective-permute-start | bytes 3538952 | tf_op jit(solution)/shard_map/ppermute | solution.py:675
  197.7 18.2 %collective-permute-start.31 = (bf16[2,2,2,2,1,2,24,768]{7,6,5,4,3,2,1,0:T(8,128)(2,1)S(1)}, bf16[2,2,2,2,1,2,24,768]{7,6,5,4,3,2,1,0:T(8,128)(2,1)S(1)}, u32[]{:S(2)}, u32[]{:S(2)}) collective-permute-start(bf16[2,2,2,2,1,2,24,768]{7,6,5,4,3,2,1,0:T(8,128)(2,1)S(1)} %bitcast.134), channel_id=1, source_target_pairs={{0,1},{1,0},{2,3},{3,2},{4,5},{5,4},{6,7},{7,6},{8,9},{9,8},{10,11... | collective-permute-start | bytes 3538952 | tf_op jit(solution)/shard_map/ppermute | solution.py:675
  217.1 27.2 %collective-permute-start.39 = (bf16[2,2,1,1,1,4,24,768]{7,6,5,4,3,2,1,0:T(8,128)(2,1)}, bf16[2,2,1,1,1,4,24,768]{7,6,5,4,3,2,1,0:T(8,128)(2,1)}, u32[]{:S(2)}, u32[]{:S(2)}) collective-permute-start(bf16[2,2,1,1,1,4,24,768]{7,6,5,4,3,2,1,0:T(8,128)(2,1)} %get-tuple-element.238), channel_id=1, source_target_pairs={{0,4},{1,5},{2,6},{3,7},{4,0},{5,1},{6,2},{7,3},{8,12},{9,13},{10,... | collective-permute-start | bytes 1769480 | tf_op jit(solution)/shard_map/ppermute | solution.py:675
  219.5 26.9 %collective-permute-start.37 = (bf16[2,2,2,1,1,2,24,768]{7,6,5,4,3,2,1,0:T(8,128)(2,1)}, bf16[2,2,2,1,1,2,24,768]{7,6,5,4,3,2,1,0:T(8,128)(2,1)}, u32[]{:S(2)}, u32[]{:S(2)}) collective-permute-start(bf16[2,2,2,1,1,2,24,768]{7,6,5,4,3,2,1,0:T(8,128)(2,1)} %get-tuple-element.236), channel_id=1, source_target_pairs={{0,2},{1,3},{2,0},{3,1},{4,6},{5,7},{6,4},{7,5},{8,10},{9,11},{10,... | collective-permute-start | bytes 1769480 | tf_op jit(solution)/shard_map/ppermute | solution.py:675
  221.1 26.7 %collective-permute-start.38 = (bf16[2,2,1,2,1,2,24,768]{7,6,5,4,3,2,1,0:T(8,128)(2,1)}, bf16[2,2,1,2,1,2,24,768]{7,6,5,4,3,2,1,0:T(8,128)(2,1)}, u32[]{:S(2)}, u32[]{:S(2)}) collective-permute-start(bf16[2,2,1,2,1,2,24,768]{7,6,5,4,3,2,1,0:T(8,128)(2,1)} %get-tuple-element.237), channel_id=1, source_target_pairs={{0,4},{1,5},{2,6},{3,7},{4,0},{5,1},{6,2},{7,3},{8,12},{9,13},{10,... | collective-permute-start | bytes 1769480 | tf_op jit(solution)/shard_map/ppermute | solution.py:675
  222.0 27.1 %collective-permute-start.40 = (bf16[2,2,1,1,1,4,24,768]{7,6,5,4,3,2,1,0:T(8,128)(2,1)}, bf16[2,2,1,1,1,4,24,768]{7,6,5,4,3,2,1,0:T(8,128)(2,1)}, u32[]{:S(2)}, u32[]{:S(2)}) collective-permute-start(bf16[2,2,1,1,1,4,24,768]{7,6,5,4,3,2,1,0:T(8,128)(2,1)} %get-tuple-element.239), channel_id=1, source_target_pairs={{0,2},{1,3},{2,0},{3,1},{4,6},{5,7},{6,4},{7,5},{8,10},{9,11},{10,... | collective-permute-start | bytes 1769480 | tf_op jit(solution)/shard_map/ppermute | solution.py:675
  244.2 11.4 %collective-permute-start.36 = (bf16[2,2,2,2,1,2,24,768]{7,6,5,4,3,2,1,0:T(8,128)(2,1)}, bf16[2,2,2,2,1,2,24,768]{7,6,5,4,3,2,1,0:T(8,128)(2,1)}, u32[]{:S(2)}, u32[]{:S(2)}) collective-permute-start(bf16[2,2,2,2,1,2,24,768]{7,6,5,4,3,2,1,0:T(8,128)(2,1)} %bitcast.57), channel_id=1, source_target_pairs={{0,1},{1,0},{2,3},{3,2},{4,5},{5,4},{6,7},{7,6},{8,9},{9,8},{10,11... | collective-permute-start | bytes 3538952 | tf_op jit(solution)/shard_map/ppermute | solution.py:675
  244.3 13.0 %collective-permute-start.35 = (bf16[2,2,2,2,1,2,24,768]{7,6,5,4,3,2,1,0:T(8,128)(2,1)}, bf16[2,2,2,2,1,2,24,768]{7,6,5,4,3,2,1,0:T(8,128)(2,1)}, u32[]{:S(2)}, u32[]{:S(2)}) collective-permute-start(bf16[2,2,2,2,1,2,24,768]{7,6,5,4,3,2,1,0:T(8,128)(2,1)} %bitcast.54), channel_id=1, source_target_pairs={{0,1},{1,0},{2,3},{3,2},{4,5},{5,4},{6,7},{7,6},{8,9},{9,8},{10,11... | collective-permute-start | bytes 3538952 | tf_op jit(solution)/shard_map/ppermute | solution.py:675
  253.9 15.3 %collective-permute-start.45 = (bf16[2,1,1,1,1,8,24,768]{7,6,5,4,3,2,1,0:T(8,128)(2,1)S(1)}, bf16[2,1,1,1,1,8,24,768]{7,6,5,4,3,2,1,0:T(8,128)(2,1)S(1)}, u32[]{:S(2)}, u32[]{:S(2)}) collective-permute-start(bf16[2,1,1,1,1,8,24,768]{7,6,5,4,3,2,1,0:T(8,128)(2,1)S(1)} %get-tuple-element.256), channel_id=1, source_target_pairs={{0,8},{1,9},{2,10},{3,11},{4,12},{5,13},{6,14},{7,15},{8,0},{9,1},... | collective-permute-start | bytes 1769480 | tf_op jit(solution)/shard_map/ppermute | solution.py:675
  259.1 14.7 %collective-permute-start.41 = (bf16[2,2,2,1,1,2,24,768]{7,6,5,4,3,2,1,0:T(8,128)(2,1)S(1)}, bf16[2,2,2,1,1,2,24,768]{7,6,5,4,3,2,1,0:T(8,128)(2,1)S(1)}, u32[]{:S(2)}, u32[]{:S(2)}) collective-permute-start(bf16[2,2,2,1,1,2,24,768]{7,6,5,4,3,2,1,0:T(8,128)(2,1)S(1)} %get-tuple-element.252), channel_id=1, source_target_pairs={{0,2},{1,3},{2,0},{3,1},{4,6},{5,7},{6,4},{7,5},{8,10},{9,11},{10,... | collective-permute-start | bytes 1769480 | tf_op jit(solution)/shard_map/ppermute | solution.py:675
  259.7 15.0 %collective-permute-start.42 = (bf16[2,2,1,2,1,2,24,768]{7,6,5,4,3,2,1,0:T(8,128)(2,1)S(1)}, bf16[2,2,1,2,1,2,24,768]{7,6,5,4,3,2,1,0:T(8,128)(2,1)S(1)}, u32[]{:S(2)}, u32[]{:S(2)}) collective-permute-start(bf16[2,2,1,2,1,2,24,768]{7,6,5,4,3,2,1,0:T(8,128)(2,1)S(1)} %get-tuple-element.253), channel_id=1, source_target_pairs={{0,4},{1,5},{2,6},{3,7},{4,0},{5,1},{6,2},{7,3},{8,12},{9,13},{10,... | collective-permute-start | bytes 1769480 | tf_op jit(solution)/shard_map/ppermute | solution.py:675
  275.6 11.1 %collective-permute-start.46 = (bf16[2,2,1,1,1,2,24,768]{7,6,5,4,3,2,1,0:T(8,128)(2,1)}, bf16[2,2,1,1,1,2,24,768]{7,6,5,4,3,2,1,0:T(8,128)(2,1)S(1)}, u32[]{:S(2)}, u32[]{:S(2)}) collective-permute-start(bf16[2,2,1,1,1,2,24,768]{7,6,5,4,3,2,1,0:T(8,128)(2,1)} %get-tuple-element.258), channel_id=1, source_target_pairs={{0,4},{1,5},{2,6},{3,7},{4,0},{5,1},{6,2},{7,3},{8,12},{9,13},{10,... | collective-permute-start | bytes 884744 | tf_op jit(solution)/shard_map/ppermute | solution.py:675
  284.2 19.6 %collective-permute-start.56 = (bf16[1,1,1,1,1,8,24,768]{7,6,5,4,3,2,1,0:T(8,128)(2,1)S(1)}, bf16[1,1,1,1,1,8,24,768]{7,6,5,4,3,2,1,0:T(8,128)(2,1)S(1)}, u32[]{:S(2)}, u32[]{:S(2)}) collective-permute-start(bf16[1,1,1,1,1,8,24,768]{7,6,5,4,3,2,1,0:T(8,128)(2,1)S(1)} %add_convert_fusion.22), channel_id=1, source_target_pairs={{0,16},{1,17},{2,18},{3,19},{4,20},{5,21},{6,22},{7,23},{8,24},{9,... | collective-permute-start | bytes 884744 | tf_op jit(solution)/shard_map/ppermute | solution.py:675
  291.5 18.1 %collective-permute-start.53 = (f32[1,1,1,2,1,1,4,128]{7,3,2,1,0,6,5,4:T(2,128)S(1)}, f32[1,1,1,2,1,1,4,128]{7,3,2,1,0,6,5,4:T(2,128)S(1)}, u32[]{:S(2)}, u32[]{:S(2)}) collective-permute-start(f32[1,1,1,2,1,1,4,128]{7,3,2,1,0,6,5,4:T(2,128)S(1)} %get-tuple-element.270), channel_id=1, source_target_pairs={{0,4},{1,5},{2,6},{3,7},{4,0},{5,1},{6,2},{7,3},{8,12},{9,13},{10,... | collective-permute-start | bytes 12296 | tf_op jit(solution)/shard_map/ppermute | solution.py:675
  292.4 17.2 %collective-permute-start.55 = (bf16[1,1,1,1,1,4,24,768]{7,6,5,4,3,2,1,0:T(8,128)(2,1)}, bf16[1,1,1,1,1,4,24,768]{7,6,5,4,3,2,1,0:T(8,128)(2,1)}, u32[]{:S(2)}, u32[]{:S(2)}) collective-permute-start(bf16[1,1,1,1,1,4,24,768]{7,6,5,4,3,2,1,0:T(8,128)(2,1)} %add_convert_fusion.35), channel_id=1, source_target_pairs={{0,16},{1,17},{2,18},{3,19},{4,20},{5,21},{6,22},{7,23},{8,24},{9,... | collective-permute-start | bytes 442376 | tf_op jit(solution)/shard_map/ppermute | solution.py:675
  293.5 17.1 %collective-permute-start.52 = (bf16[2,1,1,1,1,4,24,768]{7,6,5,4,3,2,1,0:T(8,128)(2,1)}, bf16[2,1,1,1,1,4,24,768]{7,6,5,4,3,2,1,0:T(8,128)(2,1)}, u32[]{:S(2)}, u32[]{:S(2)}) collective-permute-start(bf16[2,1,1,1,1,4,24,768]{7,6,5,4,3,2,1,0:T(8,128)(2,1)} %get-tuple-element.269), channel_id=1, source_target_pairs={{0,8},{1,9},{2,10},{3,11},{4,12},{5,13},{6,14},{7,15},{8,0},{9,1},... | collective-permute-start | bytes 884744 | tf_op jit(solution)/shard_map/ppermute | solution.py:675
  (92 other events, 561.0 us)
